TPU v7x, 512 devices: a whole 4x4x16 slice. The times are simulated.
512 devices in a mesh: obs: 16 (over x, y), patch: 32 (over z, core).
Axes of the slice: x: 4, y: 4, z: 16, core: 2. Of those that a mesh axis runs over, the one named last changes fastest.
Arguments:
- green: float32 [20480, 20480], P('obs', 'patch'), may hold values from -0.0390625 to 0.0390625
- data: float32 [20480, 128], P('obs'), may hold values from -6 to 6
- neighbours: int32 [3, 20480], P(None, 'patch'), may hold values from 0 to 20479, as said below
- reg_weight: float32 [128], replicated, may hold values from 0.5 to 2
Outputs:
- slip: float32 [20480, 128], P('patch')
Inputs may be any that keep to these rules, and one draw needn't show every extreme that they name: `neighbours`: entry (k, i) is a patch within 128 of i; an entry equal to i is padding. Distance 128 is reached in every draw.
All inputs are finite; a program needn't handle non-finite values.
Results may differ from a plain program's by a relative error of at most 0.0001.
Values sent between devices are 32-bit elements; how exact they have to be, the bound alone decides.
No kernel may reach another device: no remote copies, remote signals or barrier semaphores. Data moves between devices by JAX's collectives and lax.ppermute only.
A program may use at most 64 MiB of HBM per device.

v0:
```python
import jax
import jax.numpy as jnp
from jax import lax
from jax.sharding import Mesh
from jax.sharding import PartitionSpec as P

BAND = 128
ITERS = 3
PATCH = ("patch_0", "patch_1")
OBS = ("obs_0", "obs_1")
OBS_PATCH = ("obs_0", "obs_1", "patch_0", "patch_1")


def extended_2(shard, sides, width):
    for axis, dim in sides:
        size, length = (lax.axis_size(axis), shard.shape[dim])
        up = [(i, (i + 1) % size) for i in range(size - 1)]
        down = [(j, i) for i, j in up]
        last = lax.slice_in_dim(shard, length - width, length, axis=dim)
        first = lax.slice_in_dim(shard, 0, width, axis=dim)
        before = lax.ppermute(last, axis, up)
        after = lax.ppermute(first, axis, down)
        shard = jnp.concatenate([before, shard, after], axis=dim)
    return shard


def shifted(value, axis, steps):
    count = lax.axis_size(axis)
    first, last = (max(0, -steps), min(count, count - steps))
    return lax.ppermute(value, axis, [(source, source + steps) for source in range(first, last)])


def cut_along(shard, dim, length):
    before, after = (shard.shape[:dim], shard.shape[dim + 1 :])
    return jnp.moveaxis(shard.reshape(*before, length, -1, *after), dim, 0)


def summed_on_arrival(shard, axis, dim):
    length = lax.axis_size(axis)
    pieces = lax.all_to_all(cut_along(shard, dim, length), axis, 0, 0, tiled=True)
    return jnp.sum(pieces, axis=0)


def joined_along(pieces, dim):
    dims = list(pieces.shape[1:])
    dims[dim] *= pieces.shape[0]
    return jnp.moveaxis(pieces, 0, dim).reshape(dims)


def all_blocks(shard, axes, sequence):
    pieces = shard[None]
    for k in sequence:
        pieces = lax.all_gather(pieces, axes[k], axis=0, tiled=True)
    block = [lax.axis_size(axes[k]) for k in reversed(sequence)]
    pieces = pieces.reshape(*block, *shard.shape)
    turned = sorted(range(len(sequence)), key=lambda place: sequence[len(sequence) - 1 - place])
    return pieces.transpose(*turned, *range(len(sequence), pieces.ndim)).reshape(-1, *shard.shape)


def gather_axes(shard, axes, sequence, dim):
    return joined_along(all_blocks(shard, axes, sequence), dim)


def total_of_pieces(shard, axis):
    pieces = lax.all_gather(shard, axis)
    return pieces.sum(axis=0)


def sent_to_all(shard, axis):
    length = lax.axis_size(axis)
    return lax.all_to_all(
        jnp.broadcast_to(shard[None], (length, *shard.shape)), axis, 0, 0, tiled=True
    )


def taken_together(shard, axis):
    everything = sent_to_all(shard, axis)
    return jnp.sum(everything, axis=0)


def over_axes_2(shard, axes):
    for axis in axes:
        shard = lax.psum(shard, axis)
    return shard


def back_product(block, residual):
    return lax.dot_general(
        block,
        residual,
        (((0,), (0,)), ((), ())),
        precision=lax.Precision.HIGHEST,
        preferred_element_type=jnp.float32,
    )


def shards(green, data, neighbours, reg_weight):
    highest = lax.Precision.HIGHEST
    row_count, col_count = green.shape
    epochs = data.shape[1]
    n_patch = lax.axis_size(PATCH)
    offset = lax.axis_index(PATCH) * col_count
    local_ids = neighbours - offset + BAND
    obs_first = lax.axis_index(OBS) == 0
    share = row_count // n_patch
    residual = lax.dynamic_slice_in_dim(data, lax.axis_index(PATCH) * share, share, 0)

    def back_partial(residual):
        return back_product(green, gather_axes(residual, PATCH, (0, 1), 0))

    def gradient_of(residual):
        return total_of_pieces(back_partial(residual), OBS)

    def squared_norm(gradient):
        return taken_together(jnp.sum(gradient * gradient, axis=0), PATCH)

    slip = jnp.zeros((col_count, epochs), jnp.float32)
    reg_resid = jnp.zeros((col_count, epochs), jnp.float32)
    gradient = gradient_of(residual)
    grad_norm = squared_norm(gradient)
    direction = gradient
    for iteration in range(ITERS):
        image = summed_on_arrival(
            jnp.dot(green, direction, precision=highest, preferred_element_type=jnp.float32),
            PATCH,
            0,
        )
        image, image_sq = (image, jnp.sum(image * image, axis=0))
        extended = extended_2(direction, ((PATCH, 0),), BAND)
        reg_image = reg_weight * (
            4.0 * direction
            - extended[local_ids[0]]
            - extended[local_ids[1]]
            - extended[local_ids[2]]
        )
        reg_sq = jnp.where(obs_first, jnp.sum(reg_image * reg_image, axis=0), 0.0)
        curvature = over_axes_2(image_sq + reg_sq, OBS_PATCH)
        step_size = grad_norm / curvature
        slip = slip + step_size * direction
        if iteration + 1 < ITERS:
            residual = residual - step_size * image
            reg_resid = reg_resid - step_size * reg_image
            spread = jnp.zeros((col_count + 2 * BAND, epochs), jnp.float32)
            for slot in range(3):
                spread = spread.at[local_ids[slot]].add(reg_resid)
            from_left = shifted(spread[BAND + col_count :], PATCH, 1)
            from_right = shifted(spread[:BAND], PATCH, -1)
            filler = jnp.zeros((col_count - BAND, epochs), jnp.float32)
            inside = (
                spread[BAND : BAND + col_count]
                + jnp.concatenate([from_left, filler], 0)
                + jnp.concatenate([filler, from_right], 0)
            )
            gradient = gradient_of(residual) + reg_weight * (4.0 * reg_resid - inside)
            next_norm = squared_norm(gradient)
            direction = gradient + next_norm / grad_norm * direction
            grad_norm = next_norm
    return slip


def solution(mesh):
    split = Mesh(mesh.devices.reshape(4, 4, 16, 2), ("obs_0", "obs_1", "patch_0", "patch_1"))
    in_specs = (P(OBS, PATCH), P(OBS, None), P(None, PATCH), P())
    out_specs = P(PATCH, None)
    return jax.shard_map(
        shards, mesh=split, in_specs=in_specs, out_specs=out_specs, check_vma=False
    )
```

profile of v0, /device:TPU:1, one launch (start us, length us, event | category | flops | bytes accessed | tf_op | source)
XLA Modules:
  0.0 751.5 jit_solution(1936652341242088612)
XLA Ops:
  7.4 30.9 %all-gather = f32[640,128]{1,0:T(8,128)S(1)} all-gather(f32[40,128]{1,0:T(8,128)S(1)} %constant_dynamic-slice_fusion), channel_id=2, replica_groups=mesh['obs_0'=4,'obs_1'=4,'patch_0'=16,'patch_1'=2] {'patch_0'}, dimensions={0}, use_global_device_ids=true | all-gather | bytes 348160 | tf_op jit(solution)/shard_map/all_gather | solution.py:53
  38.3 9.9 %all_gather.37 = f32[32,40,128]{2,1,0:T(8,128)S(1)} all-gather(f32[16,40,128]{2,1,0:T(8,128)S(1)} %bitcast.84), channel_id=1, replica_groups=mesh['obs_0'=4,'obs_1'=4,'patch_0'=16,'patch_1'=2] {'patch_1'}, dimensions={0}, use_global_device_ids=true | all-gather | bytes 983040 | tf_op jit(solution)/shard_map/all_gather | solution.py:53
  51.3 67.2 %all-gather.10.cloned.1.call-done = f32[10240,128]{0,1:T(8,128)} async-done(((f32[640,128]{0,1:T(8,128)}), f32[10240,128]{0,1:T(8,128)}) %all-gather.10.cloned.1.call-update) | async-done | bytes 5242896 | tf_op jit(solution)/shard_map/all_gather | solution.py:65
  118.4 3.4 copy.59
  124.1 13.2 %all-to-all-start = ((f32[32,1,128]{2,1,0:T(1,128)}), f32[32,1,128]{2,1,0:T(1,128)S(1)}, u32[]{:S(2)}, u32[]{:S(2)}) async-start(f32[32,1,128]{2,1,0:T(1,128)} %broadcast_in_dim.21), calls=%async_computation | async-start | bytes 32768 | tf_op jit(solution)/shard_map/all_to_all | solution.py:71
  137.3 5.3 convolution_bitcast_fusion.2
  144.8 4.3 all-to-all-done
  149.1 7.9 %all-to-all-start.1 = ((f32[32,40,128]{2,1,0:T(8,128)}), f32[32,40,128]{2,1,0:T(8,128)}, u32[]{:S(2)}, u32[]{:S(2)}) async-start(f32[32,40,128]{2,1,0:T(8,128)} %bitcast.75), calls=%async_computation.1 | async-start | bytes 1310720 | tf_op jit(solution)/shard_map/all_to_all | solution.py:40
  160.5 3.5 collective-permute-start
  166.0 16.8 %collective-permute-done = f32[128,128]{1,0:T(8,128)S(1)} collective-permute-done((f32[128,128]{1,0:T(8,128)}, f32[128,128]{1,0:T(8,128)S(1)}, u32[]{:S(2)}, u32[]{:S(2)}) %collective-permute-start) | collective-permute-done | bytes 65568 | tf_op jit(solution)/shard_map/ppermute | solution.py:21
  182.8 4.5 collective-permute-done.1
  202.1 8.4 %psum.84 = f32[128]{0:T(128)S(1)} all-reduce(f32[128]{0:T(128)S(1)} %fusion.23), channel_id=1, replica_groups=mesh['obs_0'=4,'obs_1'=4,'patch_0'=16,'patch_1'=2] {'obs_0'}, use_global_device_ids=true, to_apply=%region_6.7 | all-reduce | flops 128 | bytes 1024 | tf_op jit(solution)/shard_map/psum | solution.py:83
  210.5 6.5 psum.85
  217.0 24.1 %psum.86 = f32[128]{0:T(128)S(1)} all-reduce(f32[128]{0:T(128)S(1)} %psum.85), channel_id=1, replica_groups=mesh['obs_0'=4,'obs_1'=4,'patch_0'=16,'patch_1'=2] {'patch_0'}, use_global_device_ids=true, to_apply=%region_8.9 | all-reduce | flops 128 | bytes 1024 | tf_op jit(solution)/shard_map/psum | solution.py:83
  241.2 13.6 %psum.87 = f32[128]{0:T(128)S(1)} all-reduce(f32[128]{0:T(128)S(1)} %psum.86), channel_id=1, replica_groups=mesh['obs_0'=4,'obs_1'=4,'patch_0'=16,'patch_1'=2] {'patch_1'}, use_global_device_ids=true, to_apply=%region_9.10 | all-reduce | flops 128 | bytes 1024 | tf_op jit(solution)/shard_map/psum | solution.py:83
  255.5 21.6 %all-gather.2 = f32[640,128]{1,0:T(8,128)S(1)} all-gather(f32[40,128]{1,0:T(8,128)S(1)} %multiply_subtract_fusion.6), channel_id=4, replica_groups=mesh['obs_0'=4,'obs_1'=4,'patch_0'=16,'patch_1'=2] {'patch_0'}, dimensions={0}, use_global_device_ids=true | all-gather | bytes 348160 | tf_op jit(solution)/shard_map/all_gather | solution.py:53
  277.1 9.2 %all_gather.41 = f32[32,40,128]{2,1,0:T(8,128)S(1)} all-gather(f32[16,40,128]{2,1,0:T(8,128)S(1)} %bitcast.86), channel_id=1, replica_groups=mesh['obs_0'=4,'obs_1'=4,'patch_0'=16,'patch_1'=2] {'patch_1'}, dimensions={0}, use_global_device_ids=true | all-gather | bytes 983040 | tf_op jit(solution)/shard_map/all_gather | solution.py:53
  289.4 7.2 scatter_custom_fusion
  296.6 7.7 %scatter_custom_fusion.1 = f32[896,128]{1,0:T(8,128)} fusion(f32[896,128]{1,0:T(8,128)} %scatter_custom_fusion, s32[640]{0:T(1024)S(1)} %get-tuple-element.7, f32[640,128]{1,0:T(8,128)} %get-tuple-element.15, f32[]{:T(128)} %constant.8.clone.1, f32[128]{0:T(128)S(1)} %div.23), kind=kCustom, calls=%fused_computation.55 | custom fusion | flops 245760 | bytes 787456 | tf_op jit(solution)/shard_map/scatter-add | solution.py:145
  304.3 7.7 %scatter_custom_fusion.2 = f32[896,128]{1,0:T(8,128)} fusion(f32[896,128]{1,0:T(8,128)} %scatter_custom_fusion.1, s32[640]{0:T(1024)S(1)} %get-tuple-element.6, f32[640,128]{1,0:T(8,128)} %get-tuple-element.15, f32[]{:T(128)} %constant.8.clone.1, f32[128]{0:T(128)S(1)} %div.23), kind=kCustom, calls=%fused_computation.54 | custom fusion | flops 245760 | bytes 787456 | tf_op jit(solution)/shard_map/scatter-add | solution.py:145
  319.1 35.6 %all-gather.12.cloned.1.call-done = f32[10240,128]{0,1:T(8,128)} async-done(((f32[640,128]{0,1:T(8,128)}), f32[10240,128]{0,1:T(8,128)}) %all-gather.12.cloned.1.call-update) | async-done | bytes 5242896 | tf_op jit(solution)/shard_map/all_gather | solution.py:65
  363.5 24.8 %all_to_all.33 = f32[32,1,128]{2,1,0:T(1,128)S(1)} all-to-all(f32[32,1,128]{2,1,0:T(1,128)S(1)} %broadcast_in_dim.25), channel_id=1, replica_groups=mesh['obs_0'=4,'obs_1'=4,'patch_0'=16,'patch_1'=2] {'patch_0','patch_1'}, dimensions={0} | all-to-all | bytes 32768 | tf_op jit(solution)/shard_map/all_to_all | solution.py:71
  390.2 4.3 convolution_bitcast_fusion.1
  396.7 5.1 all-to-all-start.3
  402.7 3.5 collective-permute-start.4
  408.2 19.1 %collective-permute-done.4 = f32[128,128]{1,0:T(8,128)S(1)} collective-permute-done((f32[128,128]{1,0:T(8,128)S(1)}, f32[128,128]{1,0:T(8,128)S(1)}, u32[]{:S(2)}, u32[]{:S(2)}) %collective-permute-start.4) | collective-permute-done | bytes 65568 | tf_op jit(solution)/shard_map/ppermute | solution.py:21
  427.3 5.0 collective-permute-done.5
  447.1 8.4 %psum.88 = f32[128]{0:T(128)S(1)} all-reduce(f32[128]{0:T(128)S(1)} %fusion.24), channel_id=1, replica_groups=mesh['obs_0'=4,'obs_1'=4,'patch_0'=16,'patch_1'=2] {'obs_0'}, use_global_device_ids=true, to_apply=%region_19.20 | all-reduce | flops 128 | bytes 1024 | tf_op jit(solution)/shard_map/psum | solution.py:83
  455.5 6.5 psum.89
  462.1 23.9 %psum.90 = f32[128]{0:T(128)S(1)} all-reduce(f32[128]{0:T(128)S(1)} %psum.89), channel_id=1, replica_groups=mesh['obs_0'=4,'obs_1'=4,'patch_0'=16,'patch_1'=2] {'patch_0'}, use_global_device_ids=true, to_apply=%region_21.22 | all-reduce | flops 128 | bytes 1024 | tf_op jit(solution)/shard_map/psum | solution.py:83
  486.0 13.6 %psum.91 = f32[128]{0:T(128)S(1)} all-reduce(f32[128]{0:T(128)S(1)} %psum.90), channel_id=1, replica_groups=mesh['obs_0'=4,'obs_1'=4,'patch_0'=16,'patch_1'=2] {'patch_1'}, use_global_device_ids=true, to_apply=%region_22.23 | all-reduce | flops 128 | bytes 1024 | tf_op jit(solution)/shard_map/psum | solution.py:83
  499.5 21.6 %all-gather.4 = f32[640,128]{1,0:T(8,128)S(1)} all-gather(f32[40,128]{1,0:T(8,128)S(1)} %multiply_subtract_fusion.5), channel_id=6, replica_groups=mesh['obs_0'=4,'obs_1'=4,'patch_0'=16,'patch_1'=2] {'patch_0'}, dimensions={0}, use_global_device_ids=true | all-gather | bytes 348160 | tf_op jit(solution)/shard_map/all_gather | solution.py:53
  521.1 9.2 %all_gather.45 = f32[32,40,128]{2,1,0:T(8,128)S(1)} all-gather(f32[16,40,128]{2,1,0:T(8,128)S(1)} %bitcast.85), channel_id=1, replica_groups=mesh['obs_0'=4,'obs_1'=4,'patch_0'=16,'patch_1'=2] {'patch_1'}, dimensions={0}, use_global_device_ids=true | all-gather | bytes 983040 | tf_op jit(solution)/shard_map/all_gather | solution.py:53
  535.3 7.2 scatter_custom_fusion.3
  542.5 7.6 %scatter_fusion = f32[896,128]{1,0:T(8,128)} fusion(f32[896,128]{1,0:T(8,128)} %scatter_custom_fusion.3, s32[640]{0:T(1024)S(1)} %get-tuple-element.7, f32[640,128]{1,0:T(8,128)} %multiply_subtract_fusion), kind=kCustom, calls=%fused_computation.13 | custom fusion | flops 81920 | bytes 985600 | tf_op jit(solution)/shard_map/scatter-add | solution.py:145
  550.1 7.6 %scatter_fusion.1 = f32[896,128]{1,0:T(8,128)} fusion(f32[896,128]{1,0:T(8,128)} %scatter_fusion, s32[640]{0:T(1024)S(1)} %get-tuple-element.6, f32[640,128]{1,0:T(8,128)} %multiply_subtract_fusion), kind=kCustom, calls=%fused_computation.14 | custom fusion | flops 81920 | bytes 985600 | tf_op jit(solution)/shard_map/scatter-add | solution.py:145
  564.7 34.0 %all-gather.14.cloned.1.call-done = f32[10240,128]{0,1:T(8,128)} async-done(((f32[640,128]{0,1:T(8,128)}), f32[10240,128]{0,1:T(8,128)}) %all-gather.14.cloned.1.call-update) | async-done | bytes 5242896 | tf_op jit(solution)/shard_map/all_gather | solution.py:65
  598.7 3.4 copy.61
  607.5 24.8 %all_to_all.34 = f32[32,1,128]{2,1,0:T(1,128)S(1)} all-to-all(f32[32,1,128]{2,1,0:T(1,128)S(1)} %broadcast_in_dim.27), channel_id=1, replica_groups=mesh['obs_0'=4,'obs_1'=4,'patch_0'=16,'patch_1'=2] {'patch_0','patch_1'}, dimensions={0} | all-to-all | bytes 32768 | tf_op jit(solution)/shard_map/all_to_all | solution.py:71
  634.2 4.3 convolution_bitcast_fusion
  640.7 5.1 all-to-all-start.5
  646.7 3.5 collective-permute-start.8
  652.2 19.2 %collective-permute-done.8 = f32[128,128]{1,0:T(8,128)S(1)} collective-permute-done((f32[128,128]{1,0:T(8,128)S(1)}, f32[128,128]{1,0:T(8,128)S(1)}, u32[]{:S(2)}, u32[]{:S(2)}) %collective-permute-start.8) | collective-permute-done | bytes 65568 | tf_op jit(solution)/shard_map/ppermute | solution.py:21
  671.3 5.0 collective-permute-done.9
  690.4 8.4 %psum.92 = f32[128]{0:T(128)S(1)} all-reduce(f32[128]{0:T(128)S(1)} %fusion.25), channel_id=1, replica_groups=mesh['obs_0'=4,'obs_1'=4,'patch_0'=16,'patch_1'=2] {'obs_0'}, use_global_device_ids=true, to_apply=%region_32.33 | all-reduce | flops 128 | bytes 1024 | tf_op jit(solution)/shard_map/psum | solution.py:83
  698.8 6.8 psum.93
  705.6 23.7 %psum.94 = f32[128]{0:T(128)S(1)} all-reduce(f32[128]{0:T(128)S(1)} %psum.93), channel_id=1, replica_groups=mesh['obs_0'=4,'obs_1'=4,'patch_0'=16,'patch_1'=2] {'patch_0'}, use_global_device_ids=true, to_apply=%region_34.35 | all-reduce | flops 128 | bytes 1024 | tf_op jit(solution)/shard_map/psum | solution.py:83
  729.3 13.6 %psum.95 = f32[128]{0:T(128)S(1)} all-reduce(f32[128]{0:T(128)S(1)} %psum.94), channel_id=1, replica_groups=mesh['obs_0'=4,'obs_1'=4,'patch_0'=16,'patch_1'=2] {'patch_1'}, use_global_device_ids=true, to_apply=%region_35.36 | all-reduce | flops 128 | bytes 1024 | tf_op jit(solution)/shard_map/psum | solution.py:83
  (102 shorter events, 110.3 us)
Async XLA Ops:
  6.5 41.7 %copy-start = (f32[1280,640]{1,0:T(8,128)S(1)}, f32[1280,640]{1,0:T(8,128)}, u32[]{:S(2)}) copy-start(f32[1280,640]{1,0:T(8,128)} %param.4) | copy-start | bytes 9830404
  6.5 111.9 %all-gather.10.cloned.1.call-start = ((), (), s32[]{:S(2)}) async-start(), calls=%async_computation.6 | async-start | bytes 5570560 | tf_op jit(solution)/shard_map/all_gather | solution.py:65
  122.7 0.7 copy-start.3
  124.1 24.9 %all-to-all-start = ((f32[32,1,128]{2,1,0:T(1,128)}), f32[32,1,128]{2,1,0:T(1,128)S(1)}, u32[]{:S(2)}, u32[]{:S(2)}) async-start(f32[32,1,128]{2,1,0:T(1,128)} %broadcast_in_dim.21), calls=%async_computation | async-start | bytes 32768 | tf_op jit(solution)/shard_map/all_to_all | solution.py:71
  137.3 19.7 %copy-start.5 = (s32[3,640]{1,0:T(4,128)S(1)}, s32[3,640]{1,0:T(4,128)}, u32[]{:S(2)}) copy-start(s32[3,640]{1,0:T(4,128)} %param.6) | copy-start | bytes 23044
  149.1 51.8 %all-to-all-start.1 = ((f32[32,40,128]{2,1,0:T(8,128)}), f32[32,40,128]{2,1,0:T(8,128)}, u32[]{:S(2)}, u32[]{:S(2)}) async-start(f32[32,40,128]{2,1,0:T(8,128)} %bitcast.75), calls=%async_computation.1 | async-start | bytes 1310720 | tf_op jit(solution)/shard_map/all_to_all | solution.py:40
  157.0 197.7 %all-gather.12.cloned.1.call-start = ((), (), s32[]{:S(2)}) async-start(), calls=%async_computation.7 | async-start | bytes 5570560 | tf_op jit(solution)/shard_map/all_gather | solution.py:65
  160.5 22.3 %collective-permute-start = (f32[128,128]{1,0:T(8,128)}, f32[128,128]{1,0:T(8,128)S(1)}, u32[]{:S(2)}, u32[]{:S(2)}) collective-permute-start(f32[128,128]{1,0:T(8,128)} %get-tuple-element.24), channel_id=1, source_target_pairs={{0,1},{1,2},{2,3},{3,4},{4,5},{5,6},{6,7},{7,8},{8,9},{9,10},{10,1... | collective-permute-start | bytes 196616 | tf_op jit(solution)/shard_map/ppermute | solution.py:21
  164.1 23.2 %collective-permute-start.1 = (f32[128,128]{1,0:T(8,128)S(1)}, f32[128,128]{1,0:T(8,128)S(1)}, u32[]{:S(2)}, u32[]{:S(2)}) collective-permute-start(f32[128,128]{1,0:T(8,128)S(1)} %get-tuple-element.25), channel_id=1, source_target_pairs={{1,0},{2,1},{3,2},{4,3},{5,4},{6,5},{7,6},{8,7},{9,8},{10,9},{11,1... | collective-permute-start | bytes 196616 | tf_op jit(solution)/shard_map/ppermute | solution.py:22
  192.3 6.5 copy-start.4
  313.5 48.0 %collective-permute-start.2 = (f32[128,128]{1,0:T(8,128)}, f32[128,128]{1,0:T(8,128)S(1)}, u32[]{:S(2)}, u32[]{:S(2)}) collective-permute-start(f32[128,128]{1,0:T(8,128)} %get-tuple-element.18), channel_id=1, source_target_pairs={{0,1},{1,2},{2,3},{3,4},{4,5},{5,6},{6,7},{7,8},{8,9},{9,10},{10,1... | collective-permute-start | bytes 196616 | tf_op jit(solution)/shard_map/ppermute | solution.py:30
  316.8 44.7 %collective-permute-start.3 = (f32[128,128]{1,0:T(8,128)S(1)}, f32[128,128]{1,0:T(8,128)S(1)}, u32[]{:S(2)}, u32[]{:S(2)}) collective-permute-start(f32[128,128]{1,0:T(8,128)S(1)} %get-tuple-element.19), channel_id=1, source_target_pairs={{1,0},{2,1},{3,2},{4,3},{5,4},{6,5},{7,6},{8,7},{9,8},{10,9},{11,1... | collective-permute-start | bytes 196616 | tf_op jit(solution)/shard_map/ppermute | solution.py:30
  389.5 0.7 copy-start.1
  396.7 49.3 %all-to-all-start.3 = ((f32[32,40,128]{2,1,0:T(8,128)}), f32[32,40,128]{2,1,0:T(8,128)}, u32[]{:S(2)}, u32[]{:S(2)}) async-start(f32[32,40,128]{2,1,0:T(8,128)} %bitcast.76), calls=%async_computation.3 | async-start | bytes 1310720 | tf_op jit(solution)/shard_map/all_to_all | solution.py:40
  401.8 196.9 %all-gather.14.cloned.1.call-start = ((), (), s32[]{:S(2)}) async-start(), calls=%async_computation.8 | async-start | bytes 5570560 | tf_op jit(solution)/shard_map/all_gather | solution.py:65
  402.7 24.6 %collective-permute-start.4 = (f32[128,128]{1,0:T(8,128)S(1)}, f32[128,128]{1,0:T(8,128)S(1)}, u32[]{:S(2)}, u32[]{:S(2)}) collective-permute-start(f32[128,128]{1,0:T(8,128)S(1)} %get-tuple-element.22), channel_id=1, source_target_pairs={{0,1},{1,2},{2,3},{3,4},{4,5},{5,6},{6,7},{7,8},{8,9},{9,10},{10,1... | collective-permute-start | bytes 196616 | tf_op jit(solution)/shard_map/ppermute | solution.py:21
  406.3 26.0 %collective-permute-start.5 = (f32[128,128]{1,0:T(8,128)S(1)}, f32[128,128]{1,0:T(8,128)S(1)}, u32[]{:S(2)}, u32[]{:S(2)}) collective-permute-start(f32[128,128]{1,0:T(8,128)S(1)} %get-tuple-element.23), channel_id=1, source_target_pairs={{1,0},{2,1},{3,2},{4,3},{5,4},{6,5},{7,6},{8,7},{9,8},{10,9},{11,1... | collective-permute-start | bytes 196616 | tf_op jit(solution)/shard_map/ppermute | solution.py:22
  559.2 46.3 %collective-permute-start.6 = (f32[128,128]{1,0:T(8,128)}, f32[128,128]{1,0:T(8,128)S(1)}, u32[]{:S(2)}, u32[]{:S(2)}) collective-permute-start(f32[128,128]{1,0:T(8,128)} %get-tuple-element.16), channel_id=1, source_target_pairs={{0,1},{1,2},{2,3},{3,4},{4,5},{5,6},{6,7},{7,8},{8,9},{9,10},{10,1... | collective-permute-start | bytes 196616 | tf_op jit(solution)/shard_map/ppermute | solution.py:30
  562.5 43.0 %collective-permute-start.7 = (f32[128,128]{1,0:T(8,128)S(1)}, f32[128,128]{1,0:T(8,128)S(1)}, u32[]{:S(2)}, u32[]{:S(2)}) collective-permute-start(f32[128,128]{1,0:T(8,128)S(1)} %get-tuple-element.17), channel_id=1, source_target_pairs={{1,0},{2,1},{3,2},{4,3},{5,4},{6,5},{7,6},{8,7},{9,8},{10,9},{11,1... | collective-permute-start | bytes 196616 | tf_op jit(solution)/shard_map/ppermute | solution.py:30
  633.5 0.7 copy-start.2
  640.7 48.6 %all-to-all-start.5 = ((f32[32,40,128]{2,1,0:T(8,128)}), f32[32,40,128]{2,1,0:T(8,128)}, u32[]{:S(2)}, u32[]{:S(2)}) async-start(f32[32,40,128]{2,1,0:T(8,128)} %bitcast.77), calls=%async_computation.5 | async-start | bytes 1310720 | tf_op jit(solution)/shard_map/all_to_all | solution.py:40
  646.7 24.7 %collective-permute-start.8 = (f32[128,128]{1,0:T(8,128)S(1)}, f32[128,128]{1,0:T(8,128)S(1)}, u32[]{:S(2)}, u32[]{:S(2)}) collective-permute-start(f32[128,128]{1,0:T(8,128)S(1)} %get-tuple-element.20), channel_id=1, source_target_pairs={{0,1},{1,2},{2,3},{3,4},{4,5},{5,6},{6,7},{7,8},{8,9},{9,10},{10,1... | collective-permute-start | bytes 196616 | tf_op jit(solution)/shard_map/ppermute | solution.py:21
  650.2 26.1 %collective-permute-start.9 = (f32[128,128]{1,0:T(8,128)S(1)}, f32[128,128]{1,0:T(8,128)S(1)}, u32[]{:S(2)}, u32[]{:S(2)}) collective-permute-start(f32[128,128]{1,0:T(8,128)S(1)} %get-tuple-element.21), channel_id=1, source_target_pairs={{1,0},{2,1},{3,2},{4,3},{5,4},{6,5},{7,6},{8,7},{9,8},{10,9},{11,1... | collective-permute-start | bytes 196616 | tf_op jit(solution)/shard_map/ppermute | solution.py:22
Sparse Core Ops, SparseCore 0:
  51.4 66.9 all-gather.9
  289.5 65.0 all-gather.11
  533.5 65.1 all-gather.13
where the time goes:
time: 762 us; the launch traced here: 752 us
  blocking collectives  309 us (41%)
  waiting for transfers between devices  211 us (28%)
  other arithmetic  74.5 us (10%)
  local copies, waits for them, and re-layouts  61.7 us (8%)
  starting transfers between devices  58.8 us (8%)
  matrix products  22.9 us (3%)
  between operations  13.6 us (2%)
    psum x12, blocking collectives, over_axes_2(): shard = lax.psum(shard, axis)  157 us
    all_gather x3, waiting for transfers between devices, total_of_pieces(): pieces = lax.all_gather(shard, axis)  137 us
    all_gather x6, blocking collectives, all_blocks(): pieces = lax.all_gather(pieces, axes[k], axis=0, tiled=True)  102 us
    ppermute x3, waiting for transfers between devices, extended_2(): before = lax.ppermute(last, axis, up)  55.1 us
    all_to_all x2, blocking collectives, sent_to_all(): lax.all_to_all(jnp.broadcast_to(shard[None], (length, *shard.shape)), axi...  49.6 us
    scatter-add x6, other arithmetic, shards(): spread = spread.at[local_ids[slot]].add(reg_resid)  45 us
    all_to_all x3, starting transfers between devices, summed_on_arrival(): lax.all_to_all(cut_along(shard, dim, length), axis, 0, 0, tiled=True)  18.1 us
  transfers between devices with their start and end apart: 17, of which 10 were waited for; matrix products, arithmetic and copies ran while one was open for 15% of the time, Pallas kernels for 0%

commit v1 on v0

v1 whole, which is shorter than its diff:
```python
import jax
import jax.numpy as jnp
from jax import lax
from jax.sharding import Mesh
from jax.sharding import PartitionSpec as P

BAND = 128
ITERS = 3
OBS = ("x", "y")
PATCH = ("z", "c")
PREC = lax.Precision.HIGH
TILE = 8


def dot(a, b):
    return jnp.dot(a, b, precision=PREC, preferred_element_type=jnp.float32)


def dot_t(a, b):
    dims = (((0,), (0,)), ((), ()))
    return lax.dot_general(a, b, dims, precision=PREC, preferred_element_type=jnp.float32)


def total(x):
    return jnp.sum(x, axis=0, keepdims=True)


def rows_of(parts, epochs):
    pad = jnp.zeros((TILE - len(parts), epochs), jnp.float32)
    return jnp.concatenate([*parts, pad], 0)


def exchanged(pieces, axis):
    return lax.all_to_all(pieces, axis, 0, 0, tiled=True)


def broadcast(block, axis, count):
    return exchanged(jnp.broadcast_to(block[None], (count, *block.shape)), axis)


def to_neighbours(last, first, axis):
    count = lax.axis_size(axis)
    up = [(i, i + 1) for i in range(count - 1)]
    down = [(i + 1, i) for i in range(count - 1)]
    return lax.ppermute(last, axis, up), lax.ppermute(first, axis, down)


def laplace_square(neighbours, col_count, n_patch_blocks):
    block = lax.axis_index(PATCH)
    before, after = to_neighbours(neighbours[:, col_count - BAND :], neighbours[:, :BAND], PATCH)
    ids = jnp.concatenate([before, neighbours, after], 1) - (block * col_count - 2 * BAND)
    height, width = col_count + 2 * BAND, col_count + 4 * BAND
    row = lax.broadcasted_iota(jnp.int32, (height, width), 0)
    col = lax.broadcasted_iota(jnp.int32, (height, width), 1)
    entry = jnp.where(col == row + BAND, 4.0, 0.0)
    for slot in range(3):
        entry = entry - jnp.where(col == ids[slot][:, None], 1.0, 0.0)
    here = row + (block * col_count - BAND)
    inside = (here >= 0) & (here < col_count * n_patch_blocks)
    rows = jnp.where(inside, entry, 0.0).astype(jnp.bfloat16)
    own = rows[:, 2 * BAND : 2 * BAND + col_count]
    dims = (((0,), (0,)), ((), ()))
    return lax.dot_general(own, rows, dims, preferred_element_type=jnp.float32)


def shards(green, data, neighbours, reg_weight):
    row_count, col_count = green.shape
    epochs = data.shape[1]
    n_obs, n_z, n_core = lax.axis_size(OBS), lax.axis_size("z"), lax.axis_size("c")
    n_patch = n_z * n_core
    half = row_count // n_core
    core = lax.axis_index("c")
    share = row_count // n_patch
    piece = col_count // n_obs
    square = laplace_square(neighbours, col_count, n_patch)
    weight_sq = (reg_weight * reg_weight)[None]

    def image_share(field):
        partial = dot(green, field)
        keep = lax.dynamic_slice_in_dim(partial, core * half, half, 0)
        send = lax.dynamic_slice_in_dim(partial, (1 - core) * half, half, 0)
        other = lax.ppermute(send, "c", [(0, 1), (1, 0)])
        pieces = exchanged((keep + other).reshape(n_z, share, epochs), "z")
        return jnp.sum(pieces, axis=0)

    def over_patches(block, tail):
        every = lax.all_gather(jnp.concatenate([block, tail], 0), PATCH)
        image = every[:, :share].reshape(n_z, n_core, share, epochs)
        image = image.transpose(1, 0, 2, 3).reshape(row_count, epochs)
        return image, jnp.sum(every[:, share:], axis=0)

    def back(field, tail):
        partial = dot_t(green, field).reshape(n_obs, piece, epochs)
        part = jnp.sum(exchanged(partial, OBS), axis=0)
        every = broadcast(jnp.concatenate([part, tail], 0), OBS, n_obs)
        return every[:, :piece].reshape(col_count, epochs), jnp.sum(every[:, piece:], axis=0)

    def squared_laplace(field):
        before, after = to_neighbours(field[col_count - 2 * BAND :], field[: 2 * BAND], PATCH)
        return weight_sq * dot(square, jnp.concatenate([before, field, after], 0))

    gradient, _ = back(data, rows_of([], epochs))
    norm = image = smooth = direction = slip = None
    for iteration in range(ITERS):
        first, last = iteration == 0, iteration + 1 == ITERS
        part = image_share(gradient)
        fresh = squared_laplace(gradient)
        sums = [total(gradient * gradient), total(gradient * fresh)]
        if not first:
            sums.append(total(gradient * smooth))
        if last:
            place = (core * half + lax.axis_index("z") * share, 0)
            old = lax.dynamic_slice(image, place, (share, epochs))
            sums = [*sums, total(part * part), total(part * old)]
            tail = broadcast(rows_of(sums, epochs), OBS, n_obs)
            crossed = jnp.sum(tail, axis=0)
            tail = jnp.concatenate([tail[0, :3], crossed[3:]], 0)
            tail = jnp.sum(broadcast(tail, PATCH, n_patch), axis=0)
        else:
            new_image, tail = over_patches(part, rows_of(sums, epochs))
        new_norm = tail[0:1]
        if first:
            ratio = None
            direction, image, smooth = gradient, new_image, fresh
            reg_sq = tail[1:2]
        else:
            ratio = new_norm / norm
            reg_sq = tail[1:2] + ratio * (2.0 * tail[2:3] + ratio * reg_sq)
            direction = gradient + ratio * direction
            if not last:
                image = new_image + ratio * image
                smooth = fresh + ratio * smooth
        norm = new_norm
        if last:
            curvature = tail[3:4] + ratio * (2.0 * tail[4:5] + ratio * image_sq) + reg_sq
            return slip + norm / curvature * direction
        moved, tail = back(image, rows_of([total(image * image)], epochs))
        image_sq = tail[0:1]
        step = norm / (image_sq + reg_sq)
        slip = step * direction if first else slip + step * direction
        gradient = gradient - step * (moved + smooth)


def solution(mesh):
    split = Mesh(mesh.devices.reshape(4, 4, 16, 2), (*OBS, *PATCH))
    in_specs = (P(OBS, PATCH), P(OBS, None), P(None, PATCH), P())
    return jax.shard_map(
        shards, mesh=split, in_specs=in_specs, out_specs=P(PATCH, None), check_vma=False
    )
```

time: 762 us -> 352 us (0.46); the launches traced: 752 us -> 350 us
  blocking collectives: 309 us -> 133 us
  waiting for transfers between devices: 211 us -> 54.1 us
  other arithmetic: 74.5 us -> 24.9 us
  local copies, waits for them, and re-layouts: 61.7 us -> 26 us
  starting transfers between devices: 58.8 us -> 86.9 us
  between operations: 13.6 us -> 0.54 us
    psum x12 -> x0, blocking collectives: 157 us -> none  [over_axes_2(): shard = lax.psum(shard, axis)]
    all_gather x3 -> x0, waiting for transfers between devices: 137 us -> none  [total_of_pieces(): pieces = lax.all_gather(shard, axis)]
    scatter-add x6 -> x0, other arithmetic: 45 us -> none  [shards(): spread = spread.at[local_ids[slot]].add(reg_resid)]
    ppermute x10 -> x11, waiting for transfers between devices: 69.5 us -> 32.4 us  [the longest x8 28.6 us: to_neighbours(): return (lax.ppermute(last, axis, up), lax.ppermute(first, axis, down))]
    all_gather x6 -> x2, blocking collectives: 102 us -> 67.9 us  [over_patches(): every = lax.all_gather(jnp.concatenate([block, tail], 0), PATCH)]
    gather x9 -> x0, local copies, waits for them, and re-layouts: 29.4 us -> none  [the longest x3 9.8 us: shards(): extended[local_ids[1]]]
    all_to_all x4 -> x7, waiting for transfers between devices: 4.33 us -> 21.6 us  [exchanged(): return lax.all_to_all(pieces, axis, 0, 0, tiled=True)]
    all_to_all x2 -> x4, blocking collectives: 49.6 us -> 65.1 us  [exchanged(): return lax.all_to_all(pieces, axis, 0, 0, tiled=True)]
  transfers between devices with their start and end apart: 17 -> 18, of which waited for: 10 -> 10; matrix products, arithmetic and copies ran while one was open for 15% -> 7% of each run, Pallas kernels for 0% -> 0%
where the time goes in v1:
time: 352 us; the launch traced here: 350 us
  blocking collectives  133 us (38%)
  starting transfers between devices  86.9 us (25%)
  waiting for transfers between devices  54.1 us (15%)
  local copies, waits for them, and re-layouts  26 us (7%)
  other arithmetic  24.9 us (7%)
  matrix products  24.4 us (7%)
    all_gather x2, blocking collectives, over_patches(): every = lax.all_gather(jnp.concatenate([block, tail], 0), PATCH)  67.9 us
    all_to_all x4, blocking collectives, exchanged(): return lax.all_to_all(pieces, axis, 0, 0, tiled=True)  65.1 us
    all_to_all x7, starting transfers between devices, exchanged(): return lax.all_to_all(pieces, axis, 0, 0, tiled=True)  45.4 us
    ppermute x8, waiting for transfers between devices, to_neighbours(): return (lax.ppermute(last, axis, up), lax.ppermute(first, axis, down))  28.6 us
    ppermute x8, starting transfers between devices, to_neighbours(): return (lax.ppermute(last, axis, up), lax.ppermute(first, axis, down))  25.7 us
    all_to_all x7, waiting for transfers between devices, exchanged(): return lax.all_to_all(pieces, axis, 0, 0, tiled=True)  21.6 us
    ppermute x3, starting transfers between devices, image_share(): other = lax.ppermute(send, 'c', [(0, 1), (1, 0)])  15.8 us
    dot_general x6, matrix products, dot(): return jnp.dot(a, b, precision=PREC, preferred_element_type=jnp.float32)  14.8 us
  transfers between devices with their start and end apart: 18, of which 10 were waited for; matrix products, arithmetic and copies ran while one was open for 7% of the time, Pallas kernels for 0%

profile of v1, /device:TPU:1, one launch (start us, length us, event | category | flops | bytes accessed | tf_op | source)
XLA Modules:
  0.0 349.7 jit_solution(4886285840628946409)
XLA Ops:
  0.0 1.9 copy-done
  1.9 3.8 %fusion.37 = f32[640,128]{1,0:T(8,128)S(1)} fusion(f32[1280,640]{1,0:T(8,128)S(1)} %copy-done, f32[1280,128]{1,0:T(8,128)} %param.5), kind=kOutput, calls=%fused_computation.89 | convolution fusion | flops 629145600 | bytes 4259840 | tf_op jit(solution)/shard_map/dot_general | solution.py:21
  5.7 15.2 %all_to_all.55 = f32[16,40,128]{2,1,0:T(8,128)} all-to-all(f32[16,40,128]{2,1,0:T(8,128)S(1)} %bitcast.102), channel_id=1, replica_groups=mesh['x'=4,'y'=4,'z'=16,'c'=2] {'x','y'}, dimensions={0} | all-to-all | bytes 655360 | tf_op jit(solution)/shard_map/all_to_all | solution.py:34
  22.7 4.3 %all-to-all-start.1 = ((f32[16,48,128]{2,1,0:T(8,128)}), f32[16,48,128]{2,1,0:T(8,128)}, u32[]{:S(2)}, u32[]{:S(2)}) async-start(f32[16,48,128]{2,1,0:T(8,128)} %broadcast_in_dim.95), calls=%async_computation.1 | async-start | bytes 786432 | tf_op jit(solution)/shard_map/all_to_all | solution.py:34
  27.1 5.6 %collective-permute-start.2 = (s32[3,128]{1,0:T(4,128)S(1)}, s32[3,128]{1,0:T(4,128)S(1)}, u32[]{:S(2)}, u32[]{:S(2)}) collective-permute-start(s32[3,128]{1,0:T(4,128)S(1)} %get-tuple-element.29), channel_id=1, source_target_pairs={{1,0},{2,1},{3,2},{4,3},{5,4},{6,5},{7,6},{8,7},{9,8},{10,9},{11,1... | collective-permute-start | bytes 4616 | tf_op jit(solution)/shard_map/ppermute | solution.py:45
  32.7 2.1 collective-permute-start.1
  40.0 6.7 %collective-permute-start = (f32[640,128]{0,1:T(8,128)}, f32[640,128]{0,1:T(8,128)}, u32[]{:S(2)}, u32[]{:S(2)}) collective-permute-start(f32[640,128]{0,1:T(8,128)} %dynamic-slice_bitcast_fusion.2), channel_id=1, source_target_pairs={{0,1},{1,0},{2,3},{3,2},{4,5},{5,4},{6,7},{7,6},{8,9},{9,8},{10,11... | collective-permute-start | bytes 983048 | tf_op jit(solution)/shard_map/ppermute | solution.py:82
  48.4 1.8 bitcast_add_fusion.5
  50.2 1.9 copy.17
  52.0 13.6 %all-to-all-start.2 = ((f32[16,40,128]{2,1,0:T(8,128)}), f32[16,40,128]{2,1,0:T(8,128)}, u32[]{:S(2)}, u32[]{:S(2)}) async-start(f32[16,40,128]{2,1,0:T(8,128)} %bitcast.104), calls=%async_computation.2 | async-start | bytes 655360 | tf_op jit(solution)/shard_map/all_to_all | solution.py:34
  65.7 2.5 select_convert_fusion
  69.2 2.6 collective-permute-start.4
  71.8 3.5 %collective-permute-start.3 = (f32[256,128]{1,0:T(8,128)S(1)}, f32[256,128]{1,0:T(8,128)S(1)}, u32[]{:S(2)}, u32[]{:S(2)}) collective-permute-start(f32[256,128]{1,0:T(8,128)S(1)} %get-tuple-element.26), channel_id=1, source_target_pairs={{0,1},{1,2},{2,3},{3,4},{4,5},{5,6},{6,7},{7,8},{8,9},{9,10},{10,1... | collective-permute-start | bytes 393224 | tf_op jit(solution)/shard_map/ppermute | solution.py:45
  75.3 1.9 fusion.1
  77.2 6.7 %collective-permute-done.4 = f32[256,128]{1,0:T(8,128)S(1)} collective-permute-done((f32[256,128]{1,0:T(8,128)S(1)}, f32[256,128]{1,0:T(8,128)S(1)}, u32[]{:S(2)}, u32[]{:S(2)}) %collective-permute-start.4) | collective-permute-done | bytes 131104 | tf_op jit(solution)/shard_map/ppermute | solution.py:45
  83.9 2.1 multiply_reduce_fusion.7
  87.1 34.9 %all-gather = f32[1536,128]{1,0:T(8,128)S(1)} all-gather(f32[48,128]{1,0:T(8,128)S(1)} %maximum_maximum_fusion), channel_id=2, replica_groups=mesh['x'=4,'y'=4,'z'=16,'c'=2] {'z','c'}, dimensions={0}, use_global_device_ids=true | all-gather | bytes 811008 | tf_op jit(solution)/shard_map/all_gather | solution.py:87
  124.0 2.0 convolution_bitcast_fusion.1
  125.9 1.9 copy.19
  127.8 4.2 %all-to-all-start.3 = ((f32[16,40,128]{2,1,0:T(8,128)}), f32[16,40,128]{2,1,0:T(8,128)}, u32[]{:S(2)}, u32[]{:S(2)}) async-start(f32[16,40,128]{2,1,0:T(8,128)} %bitcast.106), calls=%async_computation.3 | async-start | bytes 655360 | tf_op jit(solution)/shard_map/all_to_all | solution.py:34
  133.4 7.2 %all-to-all-done.3 = f32[16,40,128]{2,1,0:T(8,128)} async-done(((f32[16,40,128]{2,1,0:T(8,128)}), f32[16,40,128]{2,1,0:T(8,128)}, u32[]{:S(2)}, u32[]{:S(2)}) %all-to-all-start.3) | async-done | bytes 327712 | tf_op jit(solution)/shard_map/all_to_all | solution.py:34
  142.4 4.4 %all-to-all-start.4 = ((f32[16,48,128]{2,1,0:T(8,128)}), f32[16,48,128]{2,1,0:T(8,128)}, u32[]{:S(2)}, u32[]{:S(2)}) async-start(f32[16,48,128]{2,1,0:T(8,128)} %broadcast_in_dim.103), calls=%async_computation.4 | async-start | bytes 786432 | tf_op jit(solution)/shard_map/all_to_all | solution.py:34
  147.7 7.2 %all-to-all-done.4 = f32[16,48,128]{2,1,0:T(8,128)} async-done(((f32[16,48,128]{2,1,0:T(8,128)}), f32[16,48,128]{2,1,0:T(8,128)}, u32[]{:S(2)}, u32[]{:S(2)}) %all-to-all-start.4) | async-done | bytes 393248 | tf_op jit(solution)/shard_map/all_to_all | solution.py:34
  160.3 4.5 %collective-permute-start.5 = (f32[640,128]{0,1:T(8,128)S(1)}, f32[640,128]{0,1:T(8,128)S(1)}, u32[]{:S(2)}, u32[]{:S(2)}) collective-permute-start(f32[640,128]{0,1:T(8,128)S(1)} %dynamic-slice_bitcast_fusion.1), channel_id=1, source_target_pairs={{0,1},{1,0},{2,3},{3,2},{4,5},{5,4},{6,7},{7,6},{8,9},{9,8},{10,11... | collective-permute-start | bytes 983048 | tf_op jit(solution)/shard_map/ppermute | solution.py:82
  166.8 1.9 copy.20
  168.7 6.3 %all-to-all-start.5 = ((f32[16,40,128]{2,1,0:T(8,128)}), f32[16,40,128]{2,1,0:T(8,128)}, u32[]{:S(2)}, u32[]{:S(2)}) async-start(f32[16,40,128]{2,1,0:T(8,128)} %bitcast.105), calls=%async_computation.5 | async-start | bytes 655360 | tf_op jit(solution)/shard_map/all_to_all | solution.py:34
  176.0 2.6 collective-permute-start.7
  178.6 3.4 collective-permute-start.6
  182.0 11.3 %collective-permute-done.7 = f32[256,128]{1,0:T(8,128)S(1)} collective-permute-done((f32[256,128]{1,0:T(8,128)S(1)}, f32[256,128]{1,0:T(8,128)S(1)}, u32[]{:S(2)}, u32[]{:S(2)}) %collective-permute-start.7) | collective-permute-done | bytes 131104 | tf_op jit(solution)/shard_map/ppermute | solution.py:45
  193.2 4.1 %multiply_reduce_fusion.4 = (f32[128]{0:T(128)S(1)}, f32[128]{0:T(128)S(1)}, f32[128]{0:T(128)S(1)}, f32[640,128]{1,0:T(8,128)}) fusion(f32[640,128]{1,0:T(8,128)} %copy-done.4, f32[640,128]{1,0:T(8,128)} %get-tuple-element.31, f32[640,1152]{1,0:T(8,128)} %copy-done.1, f32[256,128]{1,0:T(8,128)S(1)} %collective-permute-done.7, ...), kind=kOutput, calls=%fused_computation.46 | convolution fusion | flops 567099008 | bytes 4196352 | tf_op jit(solution)/shard_map/dot_general | solution.py:16
  198.4 33.0 %all-gather.1 = f32[1536,128]{1,0:T(8,128)S(1)} all-gather(f32[48,128]{1,0:T(8,128)S(1)} %concatenate.39), channel_id=3, replica_groups=mesh['x'=4,'y'=4,'z'=16,'c'=2] {'z','c'}, dimensions={0}, use_global_device_ids=true | all-gather | bytes 811008 | tf_op jit(solution)/shard_map/all_gather | solution.py:87
  233.3 2.0 convolution_bitcast_fusion
  235.3 1.9 copy.22
  237.2 4.2 %all-to-all-start.6 = ((f32[16,40,128]{2,1,0:T(8,128)}), f32[16,40,128]{2,1,0:T(8,128)}, u32[]{:S(2)}, u32[]{:S(2)}) async-start(f32[16,40,128]{2,1,0:T(8,128)} %bitcast.107), calls=%async_computation.6 | async-start | bytes 655360 | tf_op jit(solution)/shard_map/all_to_all | solution.py:34
  242.9 7.0 %all-to-all-done.6 = f32[16,40,128]{2,1,0:T(8,128)} async-done(((f32[16,40,128]{2,1,0:T(8,128)}), f32[16,40,128]{2,1,0:T(8,128)}, u32[]{:S(2)}, u32[]{:S(2)}) %all-to-all-start.6) | async-done | bytes 327712 | tf_op jit(solution)/shard_map/all_to_all | solution.py:34
  251.0 11.9 %all_to_all.56 = f32[16,48,128]{2,1,0:T(8,128)S(1)} all-to-all(f32[16,48,128]{2,1,0:T(8,128)S(1)} %broadcast_in_dim.109), channel_id=1, replica_groups=mesh['x'=4,'y'=4,'z'=16,'c'=2] {'x','y'}, dimensions={0} | all-to-all | bytes 786432 | tf_op jit(solution)/shard_map/all_to_all | solution.py:34
  263.5 1.9 multiply_reduce_fusion.2
  267.8 4.5 %collective-permute-start.10 = (f32[640,128]{0,1:T(8,128)S(1)}, f32[640,128]{0,1:T(8,128)S(1)}, u32[]{:S(2)}, u32[]{:S(2)}) collective-permute-start(f32[640,128]{0,1:T(8,128)S(1)} %dynamic-slice_bitcast_fusion), channel_id=1, source_target_pairs={{0,1},{1,0},{2,3},{3,2},{4,5},{5,4},{6,7},{7,6},{8,9},{9,8},{10,11... | collective-permute-start | bytes 983048 | tf_op jit(solution)/shard_map/ppermute | solution.py:82
  274.3 1.9 copy.23
  276.2 8.3 %all-to-all-start.8 = ((f32[16,40,128]{2,1,0:T(8,128)}), f32[16,40,128]{2,1,0:T(8,128)}, u32[]{:S(2)}, u32[]{:S(2)}) async-start(f32[16,40,128]{2,1,0:T(8,128)} %bitcast.103), calls=%async_computation.8 | async-start | bytes 655360 | tf_op jit(solution)/shard_map/all_to_all | solution.py:34
  284.5 1.7 fusion.33
  286.2 2.5 collective-permute-start.9
  288.7 3.4 collective-permute-start.8
  292.1 10.6 %collective-permute-done.9 = f32[256,128]{1,0:T(8,128)S(1)} collective-permute-done((f32[256,128]{1,0:T(8,128)}, f32[256,128]{1,0:T(8,128)S(1)}, u32[]{:S(2)}, u32[]{:S(2)}) %collective-permute-start.9) | collective-permute-done | bytes 131104 | tf_op jit(solution)/shard_map/ppermute | solution.py:45
  302.7 3.8 %fusion.3 = f32[128]{0:T(128)} fusion(f32[640,128]{1,0:T(8,128)} %copy-done.5, f32[640,1152]{1,0:T(8,128)} %copy-done.1, f32[256,128]{1,0:T(8,128)S(1)} %collective-permute-done.9, f32[256,128]{1,0:T(8,128)S(1)} %collective-permute-done.8, f32[128]{0:T(128)} %copy-done.14), kind=kOutput, calls=%fused_computation.13 | convolution fusion | flops 566771584 | bytes 3539968 | tf_op jit(solution)/shard_map/dot_general | solution.py:16
  309.0 9.7 %all_to_all.57 = f32[16,8,128]{2,1,0:T(8,128)S(1)} all-to-all(f32[16,8,128]{2,1,0:T(8,128)S(1)} %broadcast_in_dim.116), channel_id=1, replica_groups=mesh['x'=4,'y'=4,'z'=16,'c'=2] {'x','y'}, dimensions={0} | all-to-all | bytes 131072 | tf_op jit(solution)/shard_map/all_to_all | solution.py:34
  318.8 28.2 %all_to_all.58 = f32[32,8,128]{2,1,0:T(8,128)S(1)} all-to-all(f32[32,8,128]{2,1,0:T(8,128)S(1)} %broadcast_in_dim.117), channel_id=1, replica_groups=mesh['x'=4,'y'=4,'z'=16,'c'=2] {'z','c'}, dimensions={0} | all-to-all | bytes 262144 | tf_op jit(solution)/shard_map/all_to_all | solution.py:34
  347.7 2.0 multiply_add_fusion
  (109 shorter events, 38.5 us)
Async XLA Ops:
  0.0 1.9 copy-start
  0.0 27.1 %copy-start.13 = (s32[3,640]{1,0:T(4,128)S(1)}, s32[3,640]{1,0:T(4,128)}, u32[]{:S(2)}) copy-start(s32[3,640]{1,0:T(4,128)} %param.6) | copy-start | bytes 23044
  22.7 24.1 %copy-start.16 = (f32[128]{0:T(128)S(1)}, f32[128]{0:T(128)}, u32[]{:S(2)}) copy-start(f32[128]{0:T(128)} %param.7) | copy-start | bytes 1540
  22.7 12.3 %all-to-all-start.1 = ((f32[16,48,128]{2,1,0:T(8,128)}), f32[16,48,128]{2,1,0:T(8,128)}, u32[]{:S(2)}, u32[]{:S(2)}) async-start(f32[16,48,128]{2,1,0:T(8,128)} %broadcast_in_dim.95), calls=%async_computation.1 | async-start | bytes 786432 | tf_op jit(solution)/shard_map/all_to_all | solution.py:34
  27.1 19.8 %collective-permute-start.2 = (s32[3,128]{1,0:T(4,128)S(1)}, s32[3,128]{1,0:T(4,128)S(1)}, u32[]{:S(2)}, u32[]{:S(2)}) collective-permute-start(s32[3,128]{1,0:T(4,128)S(1)} %get-tuple-element.29), channel_id=1, source_target_pairs={{1,0},{2,1},{3,2},{4,3},{5,4},{6,5},{7,6},{8,7},{9,8},{10,9},{11,1... | collective-permute-start | bytes 4616 | tf_op jit(solution)/shard_map/ppermute | solution.py:45
  32.7 14.2 %collective-permute-start.1 = (s32[3,128]{1,0:T(4,128)S(1)}, s32[3,128]{1,0:T(4,128)S(1)}, u32[]{:S(2)}, u32[]{:S(2)}) collective-permute-start(s32[3,128]{1,0:T(4,128)S(1)} %get-tuple-element.28), channel_id=1, source_target_pairs={{0,1},{1,2},{2,3},{3,4},{4,5},{5,6},{6,7},{7,8},{8,9},{9,10},{10,1... | collective-permute-start | bytes 4616 | tf_op jit(solution)/shard_map/ppermute | solution.py:45
  36.1 0.7 copy-start.2
  38.4 0.8 copy-start.12
  40.0 8.3 %collective-permute-start = (f32[640,128]{0,1:T(8,128)}, f32[640,128]{0,1:T(8,128)}, u32[]{:S(2)}, u32[]{:S(2)}) collective-permute-start(f32[640,128]{0,1:T(8,128)} %dynamic-slice_bitcast_fusion.2), channel_id=1, source_target_pairs={{0,1},{1,0},{2,3},{3,2},{4,5},{5,4},{6,7},{7,6},{8,9},{9,8},{10,11... | collective-permute-start | bytes 983048 | tf_op jit(solution)/shard_map/ppermute | solution.py:82
  46.8 146.4 %copy-start.14 = (f32[128]{0:T(128)}, f32[128]{0:T(128)S(1)}, u32[]{:S(2)}) copy-start(f32[128]{0:T(128)S(1)} %mul.194) | copy-start | bytes 1540
  52.0 34.0 %all-to-all-start.2 = ((f32[16,40,128]{2,1,0:T(8,128)}), f32[16,40,128]{2,1,0:T(8,128)}, u32[]{:S(2)}, u32[]{:S(2)}) async-start(f32[16,40,128]{2,1,0:T(8,128)} %bitcast.104), calls=%async_computation.2 | async-start | bytes 655360 | tf_op jit(solution)/shard_map/all_to_all | solution.py:34
  69.2 14.7 %collective-permute-start.4 = (f32[256,128]{1,0:T(8,128)S(1)}, f32[256,128]{1,0:T(8,128)S(1)}, u32[]{:S(2)}, u32[]{:S(2)}) collective-permute-start(f32[256,128]{1,0:T(8,128)S(1)} %get-tuple-element.27), channel_id=1, source_target_pairs={{1,0},{2,1},{3,2},{4,3},{5,4},{6,5},{7,6},{8,7},{9,8},{10,9},{11,1... | collective-permute-start | bytes 393224 | tf_op jit(solution)/shard_map/ppermute | solution.py:45
  71.8 12.1 %copy-start.3 = (f32[16,40,128]{2,1,0:T(8,128)S(1)}, f32[16,40,128]{2,1,0:T(8,128)}, u32[]{:S(2)}) copy-start(f32[16,40,128]{2,1,0:T(8,128)} %copy-done.2) | copy-start | bytes 983044
  71.8 12.1 %collective-permute-start.3 = (f32[256,128]{1,0:T(8,128)S(1)}, f32[256,128]{1,0:T(8,128)S(1)}, u32[]{:S(2)}, u32[]{:S(2)}) collective-permute-start(f32[256,128]{1,0:T(8,128)S(1)} %get-tuple-element.26), channel_id=1, source_target_pairs={{0,1},{1,2},{2,3},{3,4},{4,5},{5,6},{6,7},{7,8},{8,9},{9,10},{10,1... | collective-permute-start | bytes 393224 | tf_op jit(solution)/shard_map/ppermute | solution.py:45
  77.2 6.8 %copy-start.1 = (f32[640,1152]{1,0:T(8,128)}, f32[640,1152]{1,0:T(8,128)S(1)}, u32[]{:S(2)}) copy-start(f32[640,1152]{1,0:T(8,128)S(1)} %fusion.1) | copy-start | bytes 8847364
  122.0 1.1 copy-start.10
  122.0 0.9 copy-start.6
  123.1 0.8 copy-start.8
  127.8 12.7 %all-to-all-start.3 = ((f32[16,40,128]{2,1,0:T(8,128)}), f32[16,40,128]{2,1,0:T(8,128)}, u32[]{:S(2)}, u32[]{:S(2)}) async-start(f32[16,40,128]{2,1,0:T(8,128)} %bitcast.106), calls=%async_computation.3 | async-start | bytes 655360 | tf_op jit(solution)/shard_map/all_to_all | solution.py:34
  142.4 12.6 %all-to-all-start.4 = ((f32[16,48,128]{2,1,0:T(8,128)}), f32[16,48,128]{2,1,0:T(8,128)}, u32[]{:S(2)}, u32[]{:S(2)}) async-start(f32[16,48,128]{2,1,0:T(8,128)} %broadcast_in_dim.103), calls=%async_computation.4 | async-start | bytes 786432 | tf_op jit(solution)/shard_map/all_to_all | solution.py:34
  155.8 4.5 %copy-start.15 = (f32[128]{0:T(128)}, f32[128]{0:T(128)S(1)}, u32[]{:S(2)}) copy-start(f32[128]{0:T(128)S(1)} %fusion.26) | copy-start | bytes 1540
  158.0 0.7 copy-start.4
  160.3 5.7 %collective-permute-start.5 = (f32[640,128]{0,1:T(8,128)S(1)}, f32[640,128]{0,1:T(8,128)S(1)}, u32[]{:S(2)}, u32[]{:S(2)}) collective-permute-start(f32[640,128]{0,1:T(8,128)S(1)} %dynamic-slice_bitcast_fusion.1), channel_id=1, source_target_pairs={{0,1},{1,0},{2,3},{3,2},{4,5},{5,4},{6,7},{7,6},{8,9},{9,8},{10,11... | collective-permute-start | bytes 983048 | tf_op jit(solution)/shard_map/ppermute | solution.py:82
  168.7 28.7 %all-to-all-start.5 = ((f32[16,40,128]{2,1,0:T(8,128)}), f32[16,40,128]{2,1,0:T(8,128)}, u32[]{:S(2)}, u32[]{:S(2)}) async-start(f32[16,40,128]{2,1,0:T(8,128)} %bitcast.105), calls=%async_computation.5 | async-start | bytes 655360 | tf_op jit(solution)/shard_map/all_to_all | solution.py:34
  176.0 17.2 %collective-permute-start.7 = (f32[256,128]{1,0:T(8,128)S(1)}, f32[256,128]{1,0:T(8,128)S(1)}, u32[]{:S(2)}, u32[]{:S(2)}) collective-permute-start(f32[256,128]{1,0:T(8,128)S(1)} %get-tuple-element.25), channel_id=1, source_target_pairs={{1,0},{2,1},{3,2},{4,3},{5,4},{6,5},{7,6},{8,7},{9,8},{10,9},{11,1... | collective-permute-start | bytes 393224 | tf_op jit(solution)/shard_map/ppermute | solution.py:45
  178.6 14.7 %collective-permute-start.6 = (f32[256,128]{1,0:T(8,128)S(1)}, f32[256,128]{1,0:T(8,128)S(1)}, u32[]{:S(2)}, u32[]{:S(2)}) collective-permute-start(f32[256,128]{1,0:T(8,128)S(1)} %get-tuple-element.24), channel_id=1, source_target_pairs={{0,1},{1,2},{2,3},{3,4},{4,5},{5,6},{6,7},{7,8},{8,9},{9,10},{10,1... | collective-permute-start | bytes 393224 | tf_op jit(solution)/shard_map/ppermute | solution.py:45
  198.4 34.0 %copy-start.9 = (f32[2,16,40,128]{3,2,1,0:T(8,128)S(1)}, f32[2,16,40,128]{3,2,1,0:T(8,128)}, u32[]{:S(2)}) copy-start(f32[2,16,40,128]{3,2,1,0:T(8,128)} %copy-done.8) | copy-start | bytes 1966084
  231.5 0.9 copy-start.7
  232.5 0.8 copy-start.11
  237.2 12.7 %all-to-all-start.6 = ((f32[16,40,128]{2,1,0:T(8,128)}), f32[16,40,128]{2,1,0:T(8,128)}, u32[]{:S(2)}, u32[]{:S(2)}) async-start(f32[16,40,128]{2,1,0:T(8,128)} %bitcast.107), calls=%async_computation.6 | async-start | bytes 655360 | tf_op jit(solution)/shard_map/all_to_all | solution.py:34
  265.4 0.7 copy-start.5
  267.8 5.8 %collective-permute-start.10 = (f32[640,128]{0,1:T(8,128)S(1)}, f32[640,128]{0,1:T(8,128)S(1)}, u32[]{:S(2)}, u32[]{:S(2)}) collective-permute-start(f32[640,128]{0,1:T(8,128)S(1)} %dynamic-slice_bitcast_fusion), channel_id=1, source_target_pairs={{0,1},{1,0},{2,3},{3,2},{4,5},{5,4},{6,7},{7,6},{8,9},{9,8},{10,11... | collective-permute-start | bytes 983048 | tf_op jit(solution)/shard_map/ppermute | solution.py:82
  276.2 30.4 %all-to-all-start.8 = ((f32[16,40,128]{2,1,0:T(8,128)}), f32[16,40,128]{2,1,0:T(8,128)}, u32[]{:S(2)}, u32[]{:S(2)}) async-start(f32[16,40,128]{2,1,0:T(8,128)} %bitcast.103), calls=%async_computation.8 | async-start | bytes 655360 | tf_op jit(solution)/shard_map/all_to_all | solution.py:34
  286.2 16.5 %collective-permute-start.9 = (f32[256,128]{1,0:T(8,128)}, f32[256,128]{1,0:T(8,128)S(1)}, u32[]{:S(2)}, u32[]{:S(2)}) collective-permute-start(f32[256,128]{1,0:T(8,128)} %get-tuple-element.23), channel_id=1, source_target_pairs={{1,0},{2,1},{3,2},{4,3},{5,4},{6,5},{7,6},{8,7},{9,8},{10,9},{11,1... | collective-permute-start | bytes 393224 | tf_op jit(solution)/shard_map/ppermute | solution.py:45
  288.7 14.0 %collective-permute-start.8 = (f32[256,128]{1,0:T(8,128)}, f32[256,128]{1,0:T(8,128)S(1)}, u32[]{:S(2)}, u32[]{:S(2)}) collective-permute-start(f32[256,128]{1,0:T(8,128)} %get-tuple-element.22), channel_id=1, source_target_pairs={{0,1},{1,2},{2,3},{3,4},{4,5},{5,6},{6,7},{7,8},{8,9},{9,10},{10,1... | collective-permute-start | bytes 393224 | tf_op jit(solution)/shard_map/ppermute | solution.py:45

commit v2 on v1

v2 whole, which is shorter than its diff:
```python
import jax
import jax.numpy as jnp
from jax import lax
from jax.experimental import pallas as pl
from jax.experimental.pallas import tpu as pltpu
from jax.sharding import Mesh
from jax.sharding import PartitionSpec as P

BAND = 128
ITERS = 3
OBS = ("x", "y")
PATCH = ("z", "c")
TILE = 8
F32, BF16 = jnp.float32, jnp.bfloat16


def local_call(body, outs, *args, scalars=(), scratch=(), mib=24):
    vmem = pl.BlockSpec(memory_space=pltpu.VMEM)
    smem = pl.BlockSpec(memory_space=pltpu.SMEM)
    return pl.pallas_call(
        body,
        out_shape=[jax.ShapeDtypeStruct(shape, kind) for shape, kind in outs],
        in_specs=[smem] * len(scalars) + [vmem] * len(args),
        out_specs=[vmem] * len(outs),
        scratch_shapes=list(scratch),
        compiler_params=pltpu.CompilerParams(vmem_limit_bytes=mib << 20),
        name=body.__name__,
    )(*scalars, *args)


def halves(x):
    high = x.astype(BF16)
    return high, (x - high.astype(F32)).astype(BF16)


def store_halves(ref, start, x):
    high, low = halves(x)
    ref[start : start + x.shape[0], : x.shape[1]] = high
    ref[start : start + x.shape[0], x.shape[1] :] = low


def product(high_ref, low_ref, wide):
    width = wide.shape[1] // 2
    both = jnp.dot(high_ref[...], wide, preferred_element_type=F32)
    both = both + jnp.dot(low_ref[...], wide, preferred_element_type=F32)
    return both[:, :width] + both[:, width:]


def total(x):
    return jnp.sum(x, axis=0, keepdims=True)


def put_rows(ref, rows):
    ref[...] = jnp.zeros_like(ref)
    for place, row in enumerate(rows):
        ref[place : place + 1, :] = row


def summed(pieces_ref):
    value = pieces_ref[0]
    for k in range(1, pieces_ref.shape[0]):
        value = value + pieces_ref[k]
    return value


def first_back(green, data, high, low, moved, wide):
    for k in range(green.shape[0] // 128):
        high[:, 128 * k : 128 * (k + 1)], low[:, 128 * k : 128 * (k + 1)] = halves(
            green[128 * k : 128 * (k + 1), :].T
        )
    store_halves(wide, 0, data[...])
    moved[...] = product(high, low, wide[...])


def split_forward(keep, other, high, low):
    width = keep.shape[1]
    high[:, :width], low[:, :width] = halves(keep[...])
    high[:, width:], low[:, width:] = halves(other[...])


def split_square(square, high, low):
    high[...], low[...] = halves(square[...])


def forward(core, field, other, edge, weight_sq, smooth, f_high, f_low, m_high, m_low, part, fresh, sums, wide, near):
    rows, reach = field.shape[0], 2 * BAND
    own = field[...]
    store_halves(wide, 0, own)
    store_halves(wide, rows, other[...])
    part[...] = product(f_high, f_low, wide[...])
    is_first = core[0] == 0
    outer = edge[...]
    store_halves(near, 0, jnp.where(is_first, outer, other[rows - reach :, :]))
    store_halves(near, reach, own)
    store_halves(near, reach + rows, jnp.where(is_first, other[:reach, :], outer))
    new = weight_sq[...] * product(m_high, m_low, near[...])
    fresh[...] = new
    put_rows(sums, [total(own * own), total(own * new), total(own * smooth[...])])


def collect(pieces, sums, out):
    share = pieces.shape[1]
    out[:share, :] = summed(pieces)
    out[share:, :] = sums[...]


def backward(every, field, fresh, old_image, old_smooth, old_way, old_scalars, high, low, moved, image, tail, smooth, way, scalars, wide):
    count = every.shape[0]
    share = every.shape[1] - TILE
    sums = every[0, share:, :]
    for k in range(1, count):
        sums = sums + every[k, share:, :]
    norm = sums[0:1]
    has_old = old_scalars[2:3, :] > 0.0
    ratio = jnp.where(has_old, norm / old_scalars[0:1, :], 0.0)
    square = jnp.zeros((TILE, every.shape[2]), F32)
    for k in range(0, count, 2):
        rows = slice(share * k, share * (k + 2))
        piece = jnp.concatenate([every[k, :share, :], every[k + 1, :share, :]], 0)
        piece = piece + ratio * old_image[rows, :]
        image[rows, :] = piece
        store_halves(wide, share * k, piece)
        for t in range(2 * share // TILE):
            block = piece[TILE * t : TILE * (t + 1)]
            square = square + block * block
    moved[...] = product(high, low, wide[...])
    put_rows(tail, [total(square)])
    smooth[...] = fresh[...] + ratio * old_smooth[...]
    way[...] = field[...] + ratio * old_way[...]
    reg_sq = sums[1:2] + ratio * (2.0 * sums[2:3] + ratio * old_scalars[1:2, :])
    put_rows(scalars, [norm, reg_sq, jnp.ones_like(norm)])


def spread(pieces, tail, out):
    share = pieces.shape[1]
    value, last = summed(pieces), tail[...]
    for k in range(out.shape[0]):
        out[k, :share, :] = value
        out[k, share:, :] = last


def start_field(every, field):
    share = every.shape[1] - TILE
    for k in range(every.shape[0]):
        field[share * k : share * (k + 1), :] = every[k, :share, :]


def update(every, scalars, smooth, way, old_field, old_slip, field, slip, kept):
    count = every.shape[0]
    share = every.shape[1] - TILE
    image_sq = every[0, share : share + 1, :]
    for k in range(1, count):
        image_sq = image_sq + every[k, share : share + 1, :]
    step = scalars[0:1, :] / (image_sq + scalars[1:2, :])
    for k in range(count):
        rows = slice(share * k, share * (k + 1))
        field[rows, :] = old_field[rows, :] - step * (every[k, :share, :] + smooth[rows, :])
    slip[...] = old_slip[...] + step * way[...]
    put_rows(kept, [scalars[0:1, :], scalars[1:2, :], scalars[2:3, :], image_sq])


def last_sums(place, pieces, image, sums, out):
    share = pieces.shape[1]
    part = summed(pieces)
    start = pl.multiple_of(place[0] * share, TILE)
    old = image[pl.ds(start, share), :]
    new = total(part * part)
    cross = total(part * old)
    for k in range(out.shape[0]):
        out[k] = sums[...]
        out[k, 3:4, :] = new
        out[k, 4:5, :] = cross


def last_spread(every, out):
    sums = summed(every)
    for k in range(out.shape[0]):
        out[k] = sums
        out[k, 0:3, :] = every[0, 0:3, :]


def last_update(every, kept, field, way, old_slip, slip):
    sums = summed(every)
    norm, old_norm, reg_sq, image_sq = sums[0:1], kept[0:1, :], kept[1:2, :], kept[3:4, :]
    ratio = norm / old_norm
    reg_sq = sums[1:2] + ratio * (2.0 * sums[2:3] + ratio * reg_sq)
    image_sq = sums[3:4] + ratio * (2.0 * sums[4:5] + ratio * image_sq)
    step = norm / (image_sq + reg_sq)
    slip[...] = old_slip[...] + step * (field[...] + ratio * way[...])


def to_neighbours(last, first, axis):
    count = lax.axis_size(axis)
    up = [(i, i + 1) for i in range(count - 1)]
    down = [(i + 1, i) for i in range(count - 1)]
    return lax.ppermute(last, axis, up), lax.ppermute(first, axis, down)


def laplace_square(neighbours, col_count, n_patch_blocks):
    block = lax.axis_index(PATCH)
    before, after = to_neighbours(neighbours[:, col_count - BAND :], neighbours[:, :BAND], PATCH)
    ids = jnp.concatenate([before, neighbours, after], 1) - (block * col_count - 2 * BAND)
    height, width = col_count + 2 * BAND, col_count + 4 * BAND
    row = lax.broadcasted_iota(jnp.int32, (height, width), 0)
    col = lax.broadcasted_iota(jnp.int32, (height, width), 1)
    entry = jnp.where(col == row + BAND, 4.0, 0.0)
    for slot in range(3):
        entry = entry - jnp.where(col == ids[slot][:, None], 1.0, 0.0)
    here = row + (block * col_count - BAND)
    inside = (here >= 0) & (here < col_count * n_patch_blocks)
    rows = jnp.where(inside, entry, 0.0).astype(BF16)
    own = rows[:, 2 * BAND : 2 * BAND + col_count]
    dims = (((0,), (0,)), ((), ()))
    return lax.dot_general(own, rows, dims, preferred_element_type=F32)


def exchanged(pieces, axis):
    return lax.all_to_all(pieces, axis, 0, 0, tiled=True)


def shards(green, data, neighbours, reg_weight):
    row_count, col_count = green.shape
    epochs = data.shape[1]
    n_obs, n_z, n_core = lax.axis_size(OBS), lax.axis_size("z"), lax.axis_size("c")
    n_patch = n_z * n_core
    core = lax.axis_index("c")
    share = row_count // n_patch
    piece = col_count // n_obs
    half = row_count // n_core
    weight_sq = (reg_weight * reg_weight)[None]
    core_scalar = core.astype(jnp.int32)[None]
    place_scalar = lax.axis_index(PATCH).astype(jnp.int32)[None]
    swap = [(0, 1), (1, 0)]
    outward = [(2 * z + 1, 2 * z + 2) for z in range(n_z - 1)]
    outward = outward + [(b, a) for a, b in outward]

    field_shape = ((col_count, epochs), F32)
    image_shape = ((row_count, epochs), F32)
    tail_shape = ((TILE, epochs), F32)
    wide = pltpu.VMEM((row_count, 2 * epochs), BF16)

    matrix = ((col_count, row_count), BF16)
    b_high, b_low, moved = local_call(
        first_back, [matrix, matrix, field_shape], green, data, scratch=[wide]
    )
    pieces = exchanged(moved.reshape(n_obs, piece, epochs), OBS)

    by_core = green.reshape(n_z, n_core, share, col_count)
    keep = lax.dynamic_index_in_dim(by_core, core, 1, False).reshape(half, col_count)
    send = lax.dynamic_index_in_dim(by_core, 1 - core, 1, False).reshape(half, col_count)
    matrix = ((half, n_core * col_count), BF16)
    f_high, f_low = local_call(split_forward, [matrix, matrix], keep, lax.ppermute(send, "c", swap))
    square = laplace_square(neighbours, col_count, n_patch)
    matrix = (square.shape, BF16)
    m_high, m_low = local_call(split_square, [matrix, matrix], square)

    zero_tail = jnp.zeros((TILE, epochs), F32)
    zero_field = jnp.zeros((col_count, epochs), F32)
    spread_shape = ((n_obs, piece + TILE, epochs), F32)
    (out,) = local_call(spread, [spread_shape], pieces, zero_tail)
    (field,) = local_call(start_field, [field_shape], exchanged(out, OBS))

    kept, slip, smooth, way = zero_tail, zero_field, zero_field, zero_field
    image = jnp.zeros((row_count, epochs), F32)
    for iteration in range(ITERS):
        other = lax.ppermute(field, "c", swap)
        reach = 2 * BAND
        edge = jnp.where(core == 0, field[:reach], field[col_count - reach :])
        edge = lax.ppermute(edge, PATCH, outward)
        near = pltpu.VMEM((col_count + 2 * reach, 2 * epochs), BF16)
        part, fresh, sums = local_call(
            forward,
            [((half, epochs), F32), field_shape, tail_shape],
            field, other, edge, weight_sq, smooth, f_high, f_low, m_high, m_low,
            scalars=[core_scalar],
            scratch=[wide, near],
        )
        pieces = exchanged(part.reshape(n_z, share, epochs), "z")
        if iteration + 1 == ITERS:
            shape = ((n_obs, TILE, epochs), F32)
            (out,) = local_call(last_sums, [shape], pieces, image, sums, scalars=[place_scalar])
            shape = ((n_patch, TILE, epochs), F32)
            (out,) = local_call(last_spread, [shape], exchanged(out, OBS))
            (slip,) = local_call(
                last_update, [field_shape], exchanged(out, PATCH), kept, field, way, slip
            )
            return slip
        (out,) = local_call(collect, [((share + TILE, epochs), F32)], pieces, sums)
        every = lax.all_gather(out, PATCH)
        moved, image, tail, smooth, way, scalars = local_call(
            backward,
            [field_shape, image_shape, tail_shape, field_shape, field_shape, tail_shape],
            every, field, fresh, image, smooth, way, kept, b_high, b_low,
            scratch=[wide],
        )
        pieces = exchanged(moved.reshape(n_obs, piece, epochs), OBS)
        (out,) = local_call(spread, [spread_shape], pieces, tail)
        field, slip, kept = local_call(
            update, [field_shape, field_shape, tail_shape],
            exchanged(out, OBS), scalars, smooth, way, field, slip,
        )


def solution(mesh):
    split = Mesh(mesh.devices.reshape(4, 4, 16, 2), (*OBS, *PATCH))
    in_specs = (P(OBS, PATCH), P(OBS, None), P(None, PATCH), P())
    return jax.shard_map(
        shards, mesh=split, in_specs=in_specs, out_specs=P(PATCH, None), check_vma=False
    )
```

time: 352 us -> 330 us (0.938)
  blocking collectives: 133 us -> 235 us
  starting transfers between devices: 86.9 us -> 40.9 us
  waiting for transfers between devices: 54.1 us -> 21.9 us
  other arithmetic: 24.9 us -> 3.55 us
  matrix products: 24.4 us -> 3.8 us
  local copies, waits for them, and re-layouts: 26 us -> 7.21 us
  Pallas kernels: 0 us -> 16.2 us
    all_to_all x4 -> x9, blocking collectives: 65.1 us -> 155 us  [exchanged(): return lax.all_to_all(pieces, axis, 0, 0, tiled=True)]
    all_to_all x7 -> x2, starting transfers between devices: 45.4 us -> 8.43 us  [exchanged(): return lax.all_to_all(pieces, axis, 0, 0, tiled=True)]
    ppermute x8 -> x2, waiting for transfers between devices: 28.6 us -> 0.01 us  [to_neighbours(): return (lax.ppermute(last, axis, up), lax.ppermute(first, axis, down))]
    dot_general x10 -> x1, matrix products: 24.4 us -> 3.8 us  [laplace_square(): return lax.dot_general(own, rows, dims, preferred_element_type=F32)]
    pallas_call x0 -> x19, Pallas kernels: none -> 16.2 us  [local_call(): pl.pallas_call(body, out_shape=[jax.ShapeDtypeStruct(shape, kind) for sha...]
    ppermute x8 -> x2, starting transfers between devices: 25.7 us -> 10 us  [to_neighbours(): return (lax.ppermute(last, axis, up), lax.ppermute(first, axis, down))]
    reduce_sum x17 -> x0, other arithmetic: 14.4 us -> none  [the longest x5 6.45 us: total(): return jnp.sum(x, axis=0, keepdims=True)]
    all_gather x2, blocking collectives: 67.9 us -> 79.4 us  [shards(): every = lax.all_gather(out, PATCH)]
  transfers between devices with their start and end apart: 18 -> 11, of which waited for: 10 -> 4; matrix products, arithmetic and copies ran while one was open for 7% -> 3% of each run, Pallas kernels for 0% -> 2%
where the time goes in v2:
time: 330 us; the launch traced here: 329 us
  blocking collectives  235 us (71%)
  starting transfers between devices  40.9 us (12%)
  waiting for transfers between devices  21.9 us (7%)
  Pallas kernels  16.2 us (5%)
  local copies, waits for them, and re-layouts  7.21 us (2%)
  matrix products  3.8 us (1%)
  other arithmetic  3.55 us (1%)
    all_to_all x9, blocking collectives, exchanged(): return lax.all_to_all(pieces, axis, 0, 0, tiled=True)  155 us
    all_gather x2, blocking collectives, shards(): every = lax.all_gather(out, PATCH)  79.4 us
    pallas_call x19, Pallas kernels, local_call(): pl.pallas_call(body, out_shape=[jax.ShapeDtypeStruct(shape, kind) for sha...  16.2 us
    ppermute x3, starting transfers between devices, shards(): other = lax.ppermute(field, 'c', swap)  13.6 us
    all_to_all x2, waiting for transfers between devices, exchanged(): return lax.all_to_all(pieces, axis, 0, 0, tiled=True)  13.2 us
    ppermute x2, starting transfers between devices, to_neighbours(): return (lax.ppermute(last, axis, up), lax.ppermute(first, axis, down))  10 us
    ppermute x3, waiting for transfers between devices, shards(): edge = lax.ppermute(edge, PATCH, outward)  8.72 us
    all_to_all x2, starting transfers between devices, exchanged(): return lax.all_to_all(pieces, axis, 0, 0, tiled=True)  8.43 us
  transfers between devices with their start and end apart: 11, of which 4 were waited for; matrix products, arithmetic and copies ran while one was open for 3% of the time, Pallas kernels for 2%

profile of v2, /device:TPU:1, one launch (start us, length us, event | category | flops | bytes accessed | tf_op | source)
XLA Modules:
  0.0 328.6 jit_solution(8353928697090584739)
XLA Ops:
  0.0 0.7 fusion.5
  0.7 4.9 %collective-permute-start.3 = (s32[3,128]{1,0:T(4,128)S(1)}, s32[3,128]{1,0:T(4,128)S(1)}, u32[]{:S(2)}, u32[]{:S(2)}) collective-permute-start(s32[3,128]{1,0:T(4,128)S(1)} %get-tuple-element.76), channel_id=1, source_target_pairs={{0,1},{1,2},{2,3},{3,4},{4,5},{5,6},{6,7},{7,8},{8,9},{9,10},{10,1... | collective-permute-start | bytes 4616 | tf_op jit(solution)/shard_map/ppermute | solution.py:196
  5.6 5.1 %collective-permute-start.4 = (s32[3,128]{1,0:T(4,128)S(1)}, s32[3,128]{1,0:T(4,128)S(1)}, u32[]{:S(2)}, u32[]{:S(2)}) collective-permute-start(s32[3,128]{1,0:T(4,128)S(1)} %get-tuple-element.77), channel_id=1, source_target_pairs={{1,0},{2,1},{3,2},{4,3},{5,4},{6,5},{7,6},{8,7},{9,8},{10,9},{11,1... | collective-permute-start | bytes 4616 | tf_op jit(solution)/shard_map/ppermute | solution.py:196
  10.7 0.0 copy-start
  10.8 0.0 copy-start.3
  10.8 4.0 %constant_dynamic-slice_fusion = (f32[16,1,40,640]{3,2,1,0:T(8,128)}, f32[16,1,40,640]{3,2,1,0:T(8,128)}) fusion(f32[16,2,40,640]{3,2,1,0:T(8,128)} %bitcast.20, s32[]{:T(128)S(6)} %select_n.43, s32[]{:T(128)S(6)} %select_n.42), kind=kLoop, calls=%fused_computation.20 | loop fusion | bytes 6553608 | tf_op jit(solution)/shard_map/jit(dynamic_index_in_dim)/dynamic_slice | solution.py:250
  14.8 2.0 collective-permute-start.2
  16.9 1.4 first_back.1
  18.3 0.7 copy-done.4
  19.0 4.2 %all-to-all-start = ((f32[16,40,128]{2,1,0:T(8,128)}), f32[16,40,128]{2,1,0:T(8,128)}, u32[]{:S(2)}, u32[]{:S(2)}) async-start(f32[16,40,128]{2,1,0:T(8,128)} %bitcast.24), calls=%async_computation | async-start | bytes 655360 | tf_op jit(solution)/shard_map/all_to_all | solution.py:218
  23.4 8.5 %all-to-all-done.pieces = f32[16,40,128]{2,1,0:T(8,128)} async-done(((f32[16,40,128]{2,1,0:T(8,128)}), f32[16,40,128]{2,1,0:T(8,128)}, u32[]{:S(2)}, u32[]{:S(2)}) %all-to-all-start) | async-done | bytes 327712 | tf_op jit(solution)/shard_map/all_to_all | solution.py:218
  31.8 1.0 spread.3
  32.9 0.7 copy-done.2
  33.6 4.2 %all-to-all-start.1 = ((f32[16,48,128]{2,1,0:T(8,128)}), f32[16,48,128]{2,1,0:T(8,128)}, u32[]{:S(2)}, u32[]{:S(2)}) async-start(f32[16,48,128]{2,1,0:T(8,128)} %copy-done.2), calls=%async_computation.1 | async-start | bytes 786432 | tf_op jit(solution)/shard_map/all_to_all | solution.py:218
  37.8 3.5 %select_convert_fusion = bf16[896,1152]{1,0:T(8,128)(2,1)} fusion(s32[896]{0:T(1024)S(1)} %get-tuple-element.72, s32[896]{0:T(1024)S(1)} %get-tuple-element.73, s32[896]{0:T(1024)S(1)} %get-tuple-element.71, s32[896]{0:T(1024)S(1)} %iota_add_fusion, pred[896]{0:T(1024)(128)(4,1)S(1)} %fusion.4), kind=kLoop, calls=%fused_computation | loop fusion | flops 13418496 | bytes 2079616 | tf_op jit(solution)/shard_map/convert_element_type | solution.py:211
  41.3 4.7 %all-to-all-done.1.every = f32[16,48,128]{2,1,0:T(8,128)} async-done(((f32[16,48,128]{2,1,0:T(8,128)}), f32[16,48,128]{2,1,0:T(8,128)}, u32[]{:S(2)}, u32[]{:S(2)}) %all-to-all-start.1) | async-done | bytes 393248 | tf_op jit(solution)/shard_map/all_to_all | solution.py:218
  46.0 1.0 start_field.1.field.old_field
  47.0 4.5 %collective-permute-start = (f32[640,128]{1,0:T(8,128)S(1)}, f32[640,128]{1,0:T(8,128)S(1)}, u32[]{:S(2)}, u32[]{:S(2)}) collective-permute-start(f32[640,128]{1,0:T(8,128)S(1)} %start_field.1.field.old_field), channel_id=1, source_target_pairs={{0,1},{1,0},{2,3},{3,2},{4,5},{5,4},{6,7},{7,6},{8,9},{9,8},{10,11... | collective-permute-start | bytes 983048 | tf_op jit(solution)/shard_map/ppermute | solution.py:266
  51.6 3.0 collective-permute-start.1
  54.5 3.8 %fusion.square = f32[640,1152]{1,0:T(8,128)S(1)} fusion(bf16[896,1152]{1,0:T(8,128)(2,1)} %select_convert_fusion), kind=kOutput, calls=%fused_computation.5 | convolution fusion | flops 1321205760 | bytes 6160384 | tf_op jit(solution)/shard_map/dot_general | solution.py:214
  58.3 0.5 split_square.1
  58.9 0.9 copy-done.1
  59.8 1.9 split_forward.1
  61.7 2.0 forward.3
  63.7 29.9 %all_to_all.55.pieces = f32[16,40,128]{2,1,0:T(8,128)S(1)} all-to-all(f32[16,40,128]{2,1,0:T(8,128)S(1)} %bitcast.28), channel_id=1, replica_groups=mesh['x'=4,'y'=4,'z'=16,'c'=2] {'z'}, dimensions={0} | all-to-all | bytes 655360 | tf_op jit(solution)/shard_map/all_to_all | solution.py:218
  93.7 39.5 %all-gather = f32[1536,128]{1,0:T(8,128)S(1)} all-gather(f32[48,128]{1,0:T(8,128)S(1)} %collect.2), channel_id=2, replica_groups=mesh['x'=4,'y'=4,'z'=16,'c'=2] {'z','c'}, dimensions={0}, use_global_device_ids=true | all-gather | bytes 811008 | tf_op jit(solution)/shard_map/all_gather | solution.py:289
  133.2 1.2 backward.2
  134.5 11.4 %all_to_all.56.pieces = f32[16,40,128]{2,1,0:T(8,128)S(1)} all-to-all(f32[16,40,128]{2,1,0:T(8,128)S(1)} %bitcast.27), channel_id=1, replica_groups=mesh['x'=4,'y'=4,'z'=16,'c'=2] {'x','y'}, dimensions={0} | all-to-all | bytes 655360 | tf_op jit(solution)/shard_map/all_to_all | solution.py:218
  145.9 12.0 %all_to_all.57.every = f32[16,48,128]{2,1,0:T(8,128)S(1)} all-to-all(f32[16,48,128]{2,1,0:T(8,128)S(1)} %spread.4), channel_id=1, replica_groups=mesh['x'=4,'y'=4,'z'=16,'c'=2] {'x','y'}, dimensions={0} | all-to-all | bytes 786432 | tf_op jit(solution)/shard_map/all_to_all | solution.py:218
  157.9 0.1 update.2
  158.0 4.5 %collective-permute-start.5 = (f32[640,128]{1,0:T(8,128)S(1)}, f32[640,128]{1,0:T(8,128)S(1)}, u32[]{:S(2)}, u32[]{:S(2)}) collective-permute-start(f32[640,128]{1,0:T(8,128)S(1)} %get-tuple-element.53.field.old_field), channel_id=1, source_target_pairs={{0,1},{1,0},{2,3},{3,2},{4,5},{5,4},{6,7},{7,6},{8,9},{9,8},{10,11... | collective-permute-start | bytes 983048 | tf_op jit(solution)/shard_map/ppermute | solution.py:266
  162.6 1.9 collective-permute-start.6
  164.5 4.4 %collective-permute-done.6.edge = f32[256,128]{1,0:T(8,128)S(1)} collective-permute-done((f32[256,128]{1,0:T(8,128)S(1)}, f32[256,128]{1,0:T(8,128)S(1)}, u32[]{:S(2)}, u32[]{:S(2)}) %collective-permute-start.6) | collective-permute-done | bytes 131104 | tf_op jit(solution)/shard_map/ppermute | solution.py:269
  168.9 2.0 forward.4
  170.9 19.3 %all_to_all.58.pieces = f32[16,40,128]{2,1,0:T(8,128)S(1)} all-to-all(f32[16,40,128]{2,1,0:T(8,128)S(1)} %bitcast.29), channel_id=1, replica_groups=mesh['x'=4,'y'=4,'z'=16,'c'=2] {'z'}, dimensions={0} | all-to-all | bytes 655360 | tf_op jit(solution)/shard_map/all_to_all | solution.py:218
  190.2 39.9 %all-gather.1 = f32[1536,128]{1,0:T(8,128)S(1)} all-gather(f32[48,128]{1,0:T(8,128)S(1)} %collect.3), channel_id=3, replica_groups=mesh['x'=4,'y'=4,'z'=16,'c'=2] {'z','c'}, dimensions={0}, use_global_device_ids=true | all-gather | bytes 811008 | tf_op jit(solution)/shard_map/all_gather | solution.py:289
  230.1 1.2 backward.3
  231.3 11.4 %all_to_all.59.pieces = f32[16,40,128]{2,1,0:T(8,128)S(1)} all-to-all(f32[16,40,128]{2,1,0:T(8,128)S(1)} %bitcast.25), channel_id=1, replica_groups=mesh['x'=4,'y'=4,'z'=16,'c'=2] {'x','y'}, dimensions={0} | all-to-all | bytes 655360 | tf_op jit(solution)/shard_map/all_to_all | solution.py:218
  242.8 12.0 %all_to_all.60.every = f32[16,48,128]{2,1,0:T(8,128)S(1)} all-to-all(f32[16,48,128]{2,1,0:T(8,128)S(1)} %spread.5), channel_id=1, replica_groups=mesh['x'=4,'y'=4,'z'=16,'c'=2] {'x','y'}, dimensions={0} | all-to-all | bytes 786432 | tf_op jit(solution)/shard_map/all_to_all | solution.py:218
  254.8 0.1 update.3
  254.9 4.5 %collective-permute-start.7 = (f32[640,128]{1,0:T(8,128)S(1)}, f32[640,128]{1,0:T(8,128)S(1)}, u32[]{:S(2)}, u32[]{:S(2)}) collective-permute-start(f32[640,128]{1,0:T(8,128)S(1)} %get-tuple-element.65.field), channel_id=1, source_target_pairs={{0,1},{1,0},{2,3},{3,2},{4,5},{5,4},{6,7},{7,6},{8,9},{9,8},{10,11... | collective-permute-start | bytes 983048 | tf_op jit(solution)/shard_map/ppermute | solution.py:266
  259.5 1.9 collective-permute-start.8
  261.4 4.4 %collective-permute-done.8.edge = f32[256,128]{1,0:T(8,128)S(1)} collective-permute-done((f32[256,128]{1,0:T(8,128)S(1)}, f32[256,128]{1,0:T(8,128)S(1)}, u32[]{:S(2)}, u32[]{:S(2)}) %collective-permute-start.8) | collective-permute-done | bytes 131104 | tf_op jit(solution)/shard_map/ppermute | solution.py:269
  265.7 2.7 forward.5
  268.5 19.3 %all_to_all.61.pieces = f32[16,40,128]{2,1,0:T(8,128)S(1)} all-to-all(f32[16,40,128]{2,1,0:T(8,128)S(1)} %bitcast.26), channel_id=1, replica_groups=mesh['x'=4,'y'=4,'z'=16,'c'=2] {'z'}, dimensions={0} | all-to-all | bytes 655360 | tf_op jit(solution)/shard_map/all_to_all | solution.py:218
  287.9 9.8 %all_to_all.62.every = f32[16,8,128]{2,1,0:T(8,128)S(1)} all-to-all(f32[16,8,128]{2,1,0:T(8,128)S(1)} %last_sums.1), channel_id=1, replica_groups=mesh['x'=4,'y'=4,'z'=16,'c'=2] {'x','y'}, dimensions={0} | all-to-all | bytes 131072 | tf_op jit(solution)/shard_map/all_to_all | solution.py:218
  297.7 30.1 %all_to_all.63.every = f32[32,8,128]{2,1,0:T(8,128)S(1)} all-to-all(f32[32,8,128]{2,1,0:T(8,128)S(1)} %last_spread.1), channel_id=1, replica_groups=mesh['x'=4,'y'=4,'z'=16,'c'=2] {'z','c'}, dimensions={0} | all-to-all | bytes 262144 | tf_op jit(solution)/shard_map/all_to_all | solution.py:218
  327.7 0.8 last_update.1
  (33 shorter events, 0.4 us)
Async XLA Ops:
  0.7 22.6 %collective-permute-start.3 = (s32[3,128]{1,0:T(4,128)S(1)}, s32[3,128]{1,0:T(4,128)S(1)}, u32[]{:S(2)}, u32[]{:S(2)}) collective-permute-start(s32[3,128]{1,0:T(4,128)S(1)} %get-tuple-element.76), channel_id=1, source_target_pairs={{0,1},{1,2},{2,3},{3,4},{4,5},{5,6},{6,7},{7,8},{8,9},{9,10},{10,1... | collective-permute-start | bytes 4616 | tf_op jit(solution)/shard_map/ppermute | solution.py:196
  5.6 17.7 %collective-permute-start.4 = (s32[3,128]{1,0:T(4,128)S(1)}, s32[3,128]{1,0:T(4,128)S(1)}, u32[]{:S(2)}, u32[]{:S(2)}) collective-permute-start(s32[3,128]{1,0:T(4,128)S(1)} %get-tuple-element.77), channel_id=1, source_target_pairs={{1,0},{2,1},{3,2},{4,3},{5,4},{6,5},{7,6},{8,7},{9,8},{10,9},{11,1... | collective-permute-start | bytes 4616 | tf_op jit(solution)/shard_map/ppermute | solution.py:196
  10.7 6.1 %copy-start = (f32[1280,640]{1,0:T(8,128)S(1)}, f32[1280,640]{1,0:T(8,128)}, u32[]{:S(2)}) copy-start(f32[1280,640]{1,0:T(8,128)} %green.1) | copy-start | bytes 9830404
  10.8 6.1 %copy-start.3 = (f32[1280,128]{1,0:T(8,128)S(1)}, f32[1280,128]{1,0:T(8,128)}, u32[]{:S(2)}) copy-start(f32[1280,128]{1,0:T(8,128)} %data.1) | copy-start | bytes 1966084
  14.8 8.4 %copy-start.6 = (f32[128]{0:T(128)S(1)}, f32[128]{0:T(128)}, u32[]{:S(2)}) copy-start(f32[128]{0:T(128)} %param.7) | copy-start | bytes 1540
  14.8 8.5 %copy-start.5 = (s32[3,640]{1,0:T(4,128)S(1)}, s32[3,640]{1,0:T(4,128)}, u32[]{:S(2)}) copy-start(s32[3,640]{1,0:T(4,128)} %param.6) | copy-start | bytes 23044
  14.8 44.0 %collective-permute-start.2 = (f32[640,640]{1,0:T(8,128)}, f32[640,640]{1,0:T(8,128)}, u32[]{:S(2)}, u32[]{:S(2)}) collective-permute-start(f32[640,640]{1,0:T(8,128)} %bitcast.6), channel_id=1, source_target_pairs={{0,1},{1,0},{2,3},{3,2},{4,5},{5,4},{6,7},{7,6},{8,9},{9,8},{10,11... | collective-permute-start | bytes 4915208 | tf_op jit(solution)/shard_map/ppermute | solution.py:252
  18.3 0.7 copy-start.4
  19.0 12.8 %all-to-all-start = ((f32[16,40,128]{2,1,0:T(8,128)}), f32[16,40,128]{2,1,0:T(8,128)}, u32[]{:S(2)}, u32[]{:S(2)}) async-start(f32[16,40,128]{2,1,0:T(8,128)} %bitcast.24), calls=%async_computation | async-start | bytes 655360 | tf_op jit(solution)/shard_map/all_to_all | solution.py:218
  32.9 0.8 copy-start.2
  33.6 12.4 %all-to-all-start.1 = ((f32[16,48,128]{2,1,0:T(8,128)}), f32[16,48,128]{2,1,0:T(8,128)}, u32[]{:S(2)}, u32[]{:S(2)}) async-start(f32[16,48,128]{2,1,0:T(8,128)} %copy-done.2), calls=%async_computation.1 | async-start | bytes 786432 | tf_op jit(solution)/shard_map/all_to_all | solution.py:218
  47.0 14.7 %collective-permute-start = (f32[640,128]{1,0:T(8,128)S(1)}, f32[640,128]{1,0:T(8,128)S(1)}, u32[]{:S(2)}, u32[]{:S(2)}) collective-permute-start(f32[640,128]{1,0:T(8,128)S(1)} %start_field.1.field.old_field), channel_id=1, source_target_pairs={{0,1},{1,0},{2,3},{3,2},{4,5},{5,4},{6,7},{7,6},{8,9},{9,8},{10,11... | collective-permute-start | bytes 983048 | tf_op jit(solution)/shard_map/ppermute | solution.py:266
  51.6 10.1 %collective-permute-start.1 = (f32[256,128]{1,0:T(8,128)S(1)}, f32[256,128]{1,0:T(8,128)S(1)}, u32[]{:S(2)}, u32[]{:S(2)}) collective-permute-start(f32[256,128]{1,0:T(8,128)S(1)} %slice_select_fusion), channel_id=1, source_target_pairs={{1,2},{3,4},{5,6},{7,8},{9,10},{11,12},{13,14},{15,16},{17,18},{19... | collective-permute-start | bytes 393224 | tf_op jit(solution)/shard_map/ppermute | solution.py:269
  58.3 1.4 copy-start.1
  158.0 10.9 %collective-permute-start.5 = (f32[640,128]{1,0:T(8,128)S(1)}, f32[640,128]{1,0:T(8,128)S(1)}, u32[]{:S(2)}, u32[]{:S(2)}) collective-permute-start(f32[640,128]{1,0:T(8,128)S(1)} %get-tuple-element.53.field.old_field), channel_id=1, source_target_pairs={{0,1},{1,0},{2,3},{3,2},{4,5},{5,4},{6,7},{7,6},{8,9},{9,8},{10,11... | collective-permute-start | bytes 983048 | tf_op jit(solution)/shard_map/ppermute | solution.py:266
  162.6 6.3 %collective-permute-start.6 = (f32[256,128]{1,0:T(8,128)S(1)}, f32[256,128]{1,0:T(8,128)S(1)}, u32[]{:S(2)}, u32[]{:S(2)}) collective-permute-start(f32[256,128]{1,0:T(8,128)S(1)} %slice_select_fusion.2), channel_id=1, source_target_pairs={{1,2},{3,4},{5,6},{7,8},{9,10},{11,12},{13,14},{15,16},{17,18},{19... | collective-permute-start | bytes 393224 | tf_op jit(solution)/shard_map/ppermute | solution.py:269
  254.9 10.9 %collective-permute-start.7 = (f32[640,128]{1,0:T(8,128)S(1)}, f32[640,128]{1,0:T(8,128)S(1)}, u32[]{:S(2)}, u32[]{:S(2)}) collective-permute-start(f32[640,128]{1,0:T(8,128)S(1)} %get-tuple-element.65.field), channel_id=1, source_target_pairs={{0,1},{1,0},{2,3},{3,2},{4,5},{5,4},{6,7},{7,6},{8,9},{9,8},{10,11... | collective-permute-start | bytes 983048 | tf_op jit(solution)/shard_map/ppermute | solution.py:266
  259.5 6.3 %collective-permute-start.8 = (f32[256,128]{1,0:T(8,128)S(1)}, f32[256,128]{1,0:T(8,128)S(1)}, u32[]{:S(2)}, u32[]{:S(2)}) collective-permute-start(f32[256,128]{1,0:T(8,128)S(1)} %slice_select_fusion.1), channel_id=1, source_target_pairs={{1,2},{3,4},{5,6},{7,8},{9,10},{11,12},{13,14},{15,16},{17,18},{19... | collective-permute-start | bytes 393224 | tf_op jit(solution)/shard_map/ppermute | solution.py:269

commit v3 on v2

--- a/solution.py
+++ b/solution.py
@@ -1,3 +1,5 @@
+import functools
+
 import jax
 import jax.numpy as jnp
 from jax import lax
@@ -14,17 +16,16 @@
 F32, BF16 = jnp.float32, jnp.bfloat16
 
 
-def local_call(body, outs, *args, scalars=(), scratch=(), mib=24):
+def local_call(body, outs, *args, scalars=(), scratch=(), mib=24, **options):
     vmem = pl.BlockSpec(memory_space=pltpu.VMEM)
     smem = pl.BlockSpec(memory_space=pltpu.SMEM)
     return pl.pallas_call(
-        body,
+        functools.partial(body, **options),
         out_shape=[jax.ShapeDtypeStruct(shape, kind) for shape, kind in outs],
         in_specs=[smem] * len(scalars) + [vmem] * len(args),
         out_specs=[vmem] * len(outs),
         scratch_shapes=list(scratch),
         compiler_params=pltpu.CompilerParams(vmem_limit_bytes=mib << 20),
-        name=body.__name__,
     )(*scalars, *args)
 
 
@@ -63,31 +64,83 @@
     return value
 
 
-def first_back(green, data, high, low, moved, wide):
+def turned(green, high, low):
     for k in range(green.shape[0] // 128):
         high[:, 128 * k : 128 * (k + 1)], low[:, 128 * k : 128 * (k + 1)] = halves(
             green[128 * k : 128 * (k + 1), :].T
         )
+
+
+def first_back(green, data, moved, high, low, wide):
+    turned(green, high, low)
     store_halves(wide, 0, data[...])
     moved[...] = product(high, low, wide[...])
 
 
-def split_forward(keep, other, high, low):
-    width = keep.shape[1]
-    high[:, :width], low[:, :width] = halves(keep[...])
-    high[:, width:], low[:, width:] = halves(other[...])
-
-
-def split_square(square, high, low):
-    high[...], low[...] = halves(square[...])
-
-
-def forward(core, field, other, edge, weight_sq, smooth, f_high, f_low, m_high, m_low, part, fresh, sums, wide, near):
+def pick(core, green, ids, moved, send, last_ids, first_ids, *, share):
+    last_ids[...] = ids[:, ids.shape[1] - BAND :]
+    first_ids[...] = ids[:, :BAND]
+    for k in range(send.shape[0] // share):
+        theirs = pl.multiple_of((2 * k + 1 - core[0]) * share, TILE)
+        send[share * k : share * (k + 1), :] = green[pl.ds(theirs, share), :]
+
+
+def prepare(core, green, other, back_high, back_low, high, low, far_high, far_low, *, share):
+    for z in range(0, high.shape[0] // share, 2):
+        mine = [
+            green[pl.ds(pl.multiple_of((2 * k + core[0]) * share, TILE), share), :]
+            for k in (z, z + 1)
+        ]
+        rows = slice(share * z, share * (z + 2))
+        high[rows, :], low[rows, :] = halves(jnp.concatenate(mine, 0))
+    far_high[...], far_low[...] = halves(other[...])
+    turned(green, back_high, back_low)
+
+
+def laplace_square(block, before, ids, after, high, low, rows, own, ids_col):
+    col_count = ids.shape[1]
+    height, width = rows.shape
+    total_cols = block[1] * col_count
+    start = block[0] * col_count
+    relative = jnp.concatenate([before[...], ids[...], after[...]], 1) - (start - 2 * BAND)
+    pad = jnp.zeros((TILE - 3, height), jnp.int32)
+    ids_col[...] = jnp.concatenate([relative, pad], 0).T
+    here = lax.broadcasted_iota(jnp.int32, (1, height), 1) + (start - BAND)
+    inside = jnp.where((here >= 0) & (here < total_cols), 1.0, 0.0)
+
+    def fill_rows(i, carry):
+        at = pl.multiple_of(i * 128, 128)
+        row = lax.broadcasted_iota(jnp.int32, (128, width), 0) + at
+        col = lax.broadcasted_iota(jnp.int32, (128, width), 1)
+        entry = jnp.where(col == row + BAND, 4.0, 0.0)
+        for slot in range(3):
+            entry = entry - jnp.where(col == ids_col[pl.ds(at, 128), slot : slot + 1], 1.0, 0.0)
+        rows[pl.ds(at, 128), :] = entry.astype(BF16)
+        return carry
+
+    lax.fori_loop(0, height // 128, fill_rows, 0)
+
+    def fill_out(i, carry):
+        at = pl.multiple_of(i * 128, 128)
+        col = lax.broadcasted_iota(jnp.int32, (128, height), 0) + at
+        row = lax.broadcasted_iota(jnp.int32, (128, height), 1)
+        entry = jnp.where(row == col + BAND, 4.0, 0.0)
+        for slot in range(3):
+            entry = entry - jnp.where(col + 2 * BAND == relative[slot : slot + 1, :], 1.0, 0.0)
+        own[...] = (entry * inside).astype(BF16)
+        square = jnp.dot(own[...], rows[...], preferred_element_type=F32)
+        high[pl.ds(at, 128), :], low[pl.ds(at, 128), :] = halves(square)
+        return carry
+
+    lax.fori_loop(0, col_count // 128, fill_out, 0)
+
+
+def forward(core, field, other, edge, weight_sq, smooth, own_high, own_low, far_high, far_low, m_high, m_low, part, sums, fresh, wide, near):
     rows, reach = field.shape[0], 2 * BAND
     own = field[...]
     store_halves(wide, 0, own)
     store_halves(wide, rows, other[...])
-    part[...] = product(f_high, f_low, wide[...])
+    part[...] = product(own_high, own_low, wide[:rows, :]) + product(far_high, far_low, wide[rows:, :])
     is_first = core[0] == 0
     outer = edge[...]
     store_halves(near, 0, jnp.where(is_first, outer, other[rows - reach :, :]))
@@ -139,7 +192,7 @@
         out[k, share:, :] = last
 
 
-def start_field(every, field):
+def start_field(every, m_high, far_high, field):
     share = every.shape[1] - TILE
     for k in range(every.shape[0]):
         field[share * k : share * (k + 1), :] = every[k, :share, :]
@@ -164,19 +217,16 @@
     part = summed(pieces)
     start = pl.multiple_of(place[0] * share, TILE)
     old = image[pl.ds(start, share), :]
-    new = total(part * part)
-    cross = total(part * old)
+    first = jnp.concatenate([sums[0:3, :], total(part * part), total(part * old), sums[5:, :]], 0)
     for k in range(out.shape[0]):
-        out[k] = sums[...]
-        out[k, 3:4, :] = new
-        out[k, 4:5, :] = cross
+        out[k] = first
 
 
 def last_spread(every, out):
-    sums = summed(every)
+    sums, pair = summed(every), every[0] + every[1]
+    first = jnp.concatenate([pair[0:3], sums[3:]], 0)
     for k in range(out.shape[0]):
-        out[k] = sums
-        out[k, 0:3, :] = every[0, 0:3, :]
+        out[k] = first
 
 
 def last_update(every, kept, field, way, old_slip, slip):
@@ -196,24 +246,6 @@
     return lax.ppermute(last, axis, up), lax.ppermute(first, axis, down)
 
 
-def laplace_square(neighbours, col_count, n_patch_blocks):
-    block = lax.axis_index(PATCH)
-    before, after = to_neighbours(neighbours[:, col_count - BAND :], neighbours[:, :BAND], PATCH)
-    ids = jnp.concatenate([before, neighbours, after], 1) - (block * col_count - 2 * BAND)
-    height, width = col_count + 2 * BAND, col_count + 4 * BAND
-    row = lax.broadcasted_iota(jnp.int32, (height, width), 0)
-    col = lax.broadcasted_iota(jnp.int32, (height, width), 1)
-    entry = jnp.where(col == row + BAND, 4.0, 0.0)
-    for slot in range(3):
-        entry = entry - jnp.where(col == ids[slot][:, None], 1.0, 0.0)
-    here = row + (block * col_count - BAND)
-    inside = (here >= 0) & (here < col_count * n_patch_blocks)
-    rows = jnp.where(inside, entry, 0.0).astype(BF16)
-    own = rows[:, 2 * BAND : 2 * BAND + col_count]
-    dims = (((0,), (0,)), ((), ()))
-    return lax.dot_general(own, rows, dims, preferred_element_type=F32)
-
-
 def exchanged(pieces, axis):
     return lax.all_to_all(pieces, axis, 0, 0, tiled=True)
 
@@ -224,12 +256,14 @@
     n_obs, n_z, n_core = lax.axis_size(OBS), lax.axis_size("z"), lax.axis_size("c")
     n_patch = n_z * n_core
     core = lax.axis_index("c")
-    share = row_count // n_patch
     piece = col_count // n_obs
     half = row_count // n_core
+    reach = 2 * BAND
     weight_sq = (reg_weight * reg_weight)[None]
+    share = row_count // n_patch
     core_scalar = core.astype(jnp.int32)[None]
     place_scalar = lax.axis_index(PATCH).astype(jnp.int32)[None]
+    block_scalars = jnp.stack([lax.axis_index(PATCH).astype(jnp.int32), jnp.int32(n_patch)])
     swap = [(0, 1), (1, 0)]
     outward = [(2 * z + 1, 2 * z + 2) for z in range(n_z - 1)]
     outward = outward + [(b, a) for a, b in outward]
@@ -238,51 +272,66 @@
     image_shape = ((row_count, epochs), F32)
     tail_shape = ((TILE, epochs), F32)
     wide = pltpu.VMEM((row_count, 2 * epochs), BF16)
-
-    matrix = ((col_count, row_count), BF16)
-    b_high, b_low, moved = local_call(
-        first_back, [matrix, matrix, field_shape], green, data, scratch=[wide]
+    near = pltpu.VMEM((col_count + 2 * reach, 2 * epochs), BF16)
+
+    back_matrix = ((col_count, row_count), BF16)
+    (moved,) = local_call(
+        first_back, [field_shape], green, data,
+        scratch=[pltpu.VMEM(*back_matrix), pltpu.VMEM(*back_matrix), wide],
     )
     pieces = exchanged(moved.reshape(n_obs, piece, epochs), OBS)
-
-    by_core = green.reshape(n_z, n_core, share, col_count)
-    keep = lax.dynamic_index_in_dim(by_core, core, 1, False).reshape(half, col_count)
-    send = lax.dynamic_index_in_dim(by_core, 1 - core, 1, False).reshape(half, col_count)
-    matrix = ((half, n_core * col_count), BF16)
-    f_high, f_low = local_call(split_forward, [matrix, matrix], keep, lax.ppermute(send, "c", swap))
-    square = laplace_square(neighbours, col_count, n_patch)
-    matrix = (square.shape, BF16)
-    m_high, m_low = local_call(split_square, [matrix, matrix], square)
+    matrix = ((half, col_count), BF16)
+    ids_shape = ((3, BAND), jnp.int32)
+    send, last_ids, first_ids = local_call(
+        pick, [((half, col_count), F32), ids_shape, ids_shape],
+        green, neighbours, moved, scalars=[core_scalar], share=share,
+    )
+    far = lax.ppermute(send, "c", swap)
+    before, after = to_neighbours(last_ids, first_ids, PATCH)
 
     zero_tail = jnp.zeros((TILE, epochs), F32)
     zero_field = jnp.zeros((col_count, epochs), F32)
     spread_shape = ((n_obs, piece + TILE, epochs), F32)
     (out,) = local_call(spread, [spread_shape], pieces, zero_tail)
-    (field,) = local_call(start_field, [field_shape], exchanged(out, OBS))
+    every = exchanged(out, OBS)
+    b_high, b_low, own_high, own_low, far_high, far_low = local_call(
+        prepare, [back_matrix, back_matrix, matrix, matrix, matrix, matrix],
+        green, far, scalars=[core_scalar], share=share,
+    )
+    height, width = col_count + 2 * BAND, col_count + 4 * BAND
+    m_matrix = ((col_count, width), BF16)
+    m_high, m_low = local_call(
+        laplace_square, [m_matrix, m_matrix], before, neighbours, after,
+        scalars=[block_scalars],
+        scratch=[
+            pltpu.VMEM((height, width), BF16),
+            pltpu.VMEM((128, height), BF16),
+            pltpu.VMEM((height, TILE), jnp.int32),
+        ],
+    )
+    (field,) = local_call(start_field, [field_shape], every, m_high, far_high)
 
     kept, slip, smooth, way = zero_tail, zero_field, zero_field, zero_field
     image = jnp.zeros((row_count, epochs), F32)
     for iteration in range(ITERS):
         other = lax.ppermute(field, "c", swap)
-        reach = 2 * BAND
         edge = jnp.where(core == 0, field[:reach], field[col_count - reach :])
         edge = lax.ppermute(edge, PATCH, outward)
-        near = pltpu.VMEM((col_count + 2 * reach, 2 * epochs), BF16)
-        part, fresh, sums = local_call(
-            forward,
-            [((half, epochs), F32), field_shape, tail_shape],
-            field, other, edge, weight_sq, smooth, f_high, f_low, m_high, m_low,
+        part, sums, fresh = local_call(
+            forward, [((half, epochs), F32), tail_shape, field_shape],
+            field, other, edge, weight_sq, smooth,
+            own_high, own_low, far_high, far_low, m_high, m_low,
             scalars=[core_scalar],
             scratch=[wide, near],
         )
         pieces = exchanged(part.reshape(n_z, share, epochs), "z")
         if iteration + 1 == ITERS:
-            shape = ((n_obs, TILE, epochs), F32)
+            shape = ((n_obs * n_core, TILE, epochs), F32)
             (out,) = local_call(last_sums, [shape], pieces, image, sums, scalars=[place_scalar])
-            shape = ((n_patch, TILE, epochs), F32)
-            (out,) = local_call(last_spread, [shape], exchanged(out, OBS))
+            every = exchanged(out, (*OBS, "c"))
+            (out,) = local_call(last_spread, [((n_z, TILE, epochs), F32)], every)
             (slip,) = local_call(
-                last_update, [field_shape], exchanged(out, PATCH), kept, field, way, slip
+                last_update, [field_shape], exchanged(out, "z"), kept, field, way, slip
             )
             return slip
         (out,) = local_call(collect, [((share + TILE, epochs), F32)], pieces, sums)
@@ -304,6 +353,7 @@
 def solution(mesh):
     split = Mesh(mesh.devices.reshape(4, 4, 16, 2), (*OBS, *PATCH))
     in_specs = (P(OBS, PATCH), P(OBS, None), P(None, PATCH), P())
+
     return jax.shard_map(
         shards, mesh=split, in_specs=in_specs, out_specs=P(PATCH, None), check_vma=False
     )

time: 330 us -> 341 us (1.033)
  blocking collectives: 235 us -> 246 us
  local copies, waits for them, and re-layouts: 7.21 us -> 18.1 us
  Pallas kernels: 16.2 us -> 24.1 us
  waiting for transfers between devices: 21.9 us -> 14.6 us
  matrix products: 3.8 us -> 0 us
  starting transfers between devices: 40.9 us -> 37.2 us
  other arithmetic: 3.55 us -> 0.13 us
    unnamed x14 -> x54, local copies, waits for them, and re-layouts: 2.38 us -> 18.1 us
    all_to_all x2 -> x1, waiting for transfers between devices: 13.2 us -> 0.01 us  [exchanged(): return lax.all_to_all(pieces, axis, 0, 0, tiled=True)]
    all_to_all x9 -> x10, blocking collectives: 155 us -> 166 us  [exchanged(): return lax.all_to_all(pieces, axis, 0, 0, tiled=True)]
    pallas_call x19 -> x20, Pallas kernels: 16.2 us -> 24.1 us  [local_call(): pl.pallas_call(functools.partial(body, **options), out_shape=[jax.ShapeDt...]
    ppermute x1, starting transfers between devices: 2.04 us -> 8.87 us  [shards(): far = lax.ppermute(send, 'c', swap)]
    ppermute x2, starting transfers between devices: 10 us -> 5.57 us  [to_neighbours(): return (lax.ppermute(last, axis, up), lax.ppermute(first, axis, down))]
    all_to_all x2 -> x1, starting transfers between devices: 8.43 us -> 4.2 us  [exchanged(): return lax.all_to_all(pieces, axis, 0, 0, tiled=True)]
    dynamic_slice x1 -> x0, local copies, waits for them, and re-layouts: 4.04 us -> none  [shards(): lax.dynamic_index_in_dim(by_core, 1 - core, 1, False)]
  transfers between devices with their start and end apart: 11 -> 10, of which waited for: 4 -> 4; matrix products, arithmetic and copies ran while one was open for 3% -> 0% of each run, Pallas kernels for 2% -> 3%
where the time goes in v3:
time: 341 us; the launch traced here: 340 us
  blocking collectives  246 us (72%)
  starting transfers between devices  37.2 us (11%)
  Pallas kernels  24.1 us (7%)
  local copies, waits for them, and re-layouts  18.1 us (5%)
  waiting for transfers between devices  14.6 us (4%)
    all_to_all x10, blocking collectives, exchanged(): return lax.all_to_all(pieces, axis, 0, 0, tiled=True)  166 us
    all_gather x2, blocking collectives, shards(): every = lax.all_gather(out, PATCH)  79.2 us
    pallas_call x20, Pallas kernels, local_call(): pl.pallas_call(functools.partial(body, **options), out_shape=[jax.ShapeDt...  24.1 us
    unnamed x54, local copies, waits for them, and re-layouts  18.1 us
    ppermute x3, waiting for transfers between devices, shards(): edge = lax.ppermute(edge, PATCH, outward)  11.3 us
    ppermute x3, starting transfers between devices, shards(): other = lax.ppermute(field, 'c', swap)  11 us
    ppermute x1, starting transfers between devices, shards(): far = lax.ppermute(send, 'c', swap)  8.87 us
    ppermute x3, starting transfers between devices, shards(): edge = lax.ppermute(edge, PATCH, outward)  7.51 us
  transfers between devices with their start and end apart: 10, of which 4 were waited for; matrix products, arithmetic and copies ran while one was open for 0% of the time, Pallas kernels for 3%

profile of v3, /device:TPU:1, one launch (start us, length us, event | category | flops | bytes accessed | tf_op | source)
XLA Modules:
  0.0 340.2 jit_solution(2393255546074179686)
XLA Ops:
  0.0 1.9 copy-done
  1.9 1.1 copy-done.24
  3.0 1.4 shard_map.46.moved
  4.4 1.3 shard_map.48
  5.7 8.9 %collective-permute-start.2 = (f32[640,640]{1,0:T(8,128)}, f32[640,640]{1,0:T(8,128)}, u32[]{:S(2)}, u32[]{:S(2)}) collective-permute-start(f32[640,640]{1,0:T(8,128)} %get-tuple-element.45), channel_id=1, source_target_pairs={{0,1},{1,0},{2,3},{3,2},{4,5},{5,4},{6,7},{7,6},{8,9},{9,8},{10,11... | collective-permute-start | bytes 4915208 | tf_op jit(solution)/shard_map/ppermute | solution.py:289
  14.6 11.1 %all_to_all.55.pieces = f32[16,40,128]{2,1,0:T(8,128)S(1)} all-to-all(f32[16,40,128]{2,1,0:T(8,128)S(1)} %bitcast.14), channel_id=1, replica_groups=mesh['x'=4,'y'=4,'z'=16,'c'=2] {'x','y'}, dimensions={0} | all-to-all | bytes 655360 | tf_op jit(solution)/shard_map/all_to_all | solution.py:250
  26.5 4.2 %all-to-all-start.1 = ((f32[16,48,128]{2,1,0:T(8,128)}), f32[16,48,128]{2,1,0:T(8,128)}, u32[]{:S(2)}, u32[]{:S(2)}) async-start(f32[16,48,128]{2,1,0:T(8,128)} %copy-done.23), calls=%async_computation.1 | async-start | bytes 786432 | tf_op jit(solution)/shard_map/all_to_all | solution.py:250
  30.7 3.6 %collective-permute-start = (s32[3,128]{1,0:T(4,128)S(1)}, s32[3,128]{1,0:T(4,128)S(1)}, u32[]{:S(2)}, u32[]{:S(2)}) collective-permute-start(s32[3,128]{1,0:T(4,128)S(1)} %get-tuple-element.42), channel_id=1, source_target_pairs={{0,1},{1,2},{2,3},{3,4},{4,5},{5,6},{6,7},{7,8},{8,9},{9,10},{10,1... | collective-permute-start | bytes 4616 | tf_op jit(solution)/shard_map/ppermute | solution.py:246
  34.4 1.9 collective-permute-start.1
  36.4 3.3 collective-permute-done.1.after
  39.7 6.2 %shard_map.49 = (bf16[640,1152]{1,0:T(8,128)(2,1)S(1)}, bf16[640,1152]{1,0:T(8,128)(2,1)S(1)}) custom-call(s32[2]{0:T(128)S(1)} %pad_add_fusion.block, s32[3,128]{1,0:T(4,128)S(1)} %collective-permute-done.before, s32[3,640]{1,0:T(4,128)S(1)} %copy-done.25, s32[3,128]{1,0:T(4,128)S(1)} %collective-permute-done.1.after), custom_call_target="tpu_custom_call" | custom-call | tf_op jit(solution)/shard_map/pallas_call | solution.py:22
  45.9 1.1 copy-done.2
  47.0 1.2 copy-done.5
  48.2 3.0 shard_map.50
  53.0 1.0 copy-done.13
  54.9 1.2 copy-done.19
  56.1 1.2 copy-done.21
  57.2 1.4 copy-done.3
  58.6 1.1 copy-done.8
  59.8 1.2 shard_map.51.field.old_field
  60.9 1.9 collective-permute-start.3
  62.9 3.7 %collective-permute-start.4 = (f32[256,128]{1,0:T(8,128)S(1)}, f32[256,128]{1,0:T(8,128)S(1)}, u32[]{:S(2)}, u32[]{:S(2)}) collective-permute-start(f32[256,128]{1,0:T(8,128)S(1)} %slice_select_fusion), channel_id=1, source_target_pairs={{1,2},{3,4},{5,6},{7,8},{9,10},{11,12},{13,14},{15,16},{17,18},{19... | collective-permute-start | bytes 393224 | tf_op jit(solution)/shard_map/ppermute | solution.py:319
  66.6 2.6 collective-permute-done.4.edge
  69.3 1.1 copy-done.11
  70.4 1.1 copy-done.14
  71.5 1.1 copy-done.17
  72.7 2.2 shard_map.52
  74.9 31.0 %all_to_all.56.pieces = f32[16,40,128]{2,1,0:T(8,128)S(1)} all-to-all(f32[16,40,128]{2,1,0:T(8,128)S(1)} %bitcast.18), channel_id=1, replica_groups=mesh['x'=4,'y'=4,'z'=16,'c'=2] {'z'}, dimensions={0} | all-to-all | bytes 655360 | tf_op jit(solution)/shard_map/all_to_all | solution.py:250
  106.0 39.3 %all-gather = f32[1536,128]{1,0:T(8,128)S(1)} all-gather(f32[48,128]{1,0:T(8,128)S(1)} %shard_map.53), channel_id=2, replica_groups=mesh['x'=4,'y'=4,'z'=16,'c'=2] {'z','c'}, dimensions={0}, use_global_device_ids=true | all-gather | bytes 811008 | tf_op jit(solution)/shard_map/all_gather | solution.py:338
  145.3 1.2 shard_map.54
  146.5 15.0 %all_to_all.57.pieces = f32[16,40,128]{2,1,0:T(8,128)S(1)} all-to-all(f32[16,40,128]{2,1,0:T(8,128)S(1)} %bitcast.17), channel_id=1, replica_groups=mesh['x'=4,'y'=4,'z'=16,'c'=2] {'x','y'}, dimensions={0} | all-to-all | bytes 655360 | tf_op jit(solution)/shard_map/all_to_all | solution.py:250
  161.6 12.3 %all_to_all.58.every = f32[16,48,128]{2,1,0:T(8,128)S(1)} all-to-all(f32[16,48,128]{2,1,0:T(8,128)S(1)} %shard_map.55), channel_id=1, replica_groups=mesh['x'=4,'y'=4,'z'=16,'c'=2] {'x','y'}, dimensions={0} | all-to-all | bytes 786432 | tf_op jit(solution)/shard_map/all_to_all | solution.py:250
  173.9 4.5 %collective-permute-start.5 = (f32[640,128]{1,0:T(8,128)S(1)}, f32[640,128]{1,0:T(8,128)S(1)}, u32[]{:S(2)}, u32[]{:S(2)}) collective-permute-start(f32[640,128]{1,0:T(8,128)S(1)} %get-tuple-element.61.field.old_field), channel_id=1, source_target_pairs={{0,1},{1,0},{2,3},{3,2},{4,5},{5,4},{6,7},{7,6},{8,9},{9,8},{10,11... | collective-permute-start | bytes 983048 | tf_op jit(solution)/shard_map/ppermute | solution.py:317
  178.5 1.9 collective-permute-start.6
  180.4 4.4 %collective-permute-done.6.edge = f32[256,128]{1,0:T(8,128)S(1)} collective-permute-done((f32[256,128]{1,0:T(8,128)S(1)}, f32[256,128]{1,0:T(8,128)S(1)}, u32[]{:S(2)}, u32[]{:S(2)}) %collective-permute-start.6) | collective-permute-done | bytes 131104 | tf_op jit(solution)/shard_map/ppermute | solution.py:319
  184.8 2.2 shard_map.57
  187.1 19.1 %all_to_all.59.pieces = f32[16,40,128]{2,1,0:T(8,128)S(1)} all-to-all(f32[16,40,128]{2,1,0:T(8,128)S(1)} %bitcast.19), channel_id=1, replica_groups=mesh['x'=4,'y'=4,'z'=16,'c'=2] {'z'}, dimensions={0} | all-to-all | bytes 655360 | tf_op jit(solution)/shard_map/all_to_all | solution.py:250
  206.2 39.9 %all-gather.1 = f32[1536,128]{1,0:T(8,128)S(1)} all-gather(f32[48,128]{1,0:T(8,128)S(1)} %shard_map.58), channel_id=3, replica_groups=mesh['x'=4,'y'=4,'z'=16,'c'=2] {'z','c'}, dimensions={0}, use_global_device_ids=true | all-gather | bytes 811008 | tf_op jit(solution)/shard_map/all_gather | solution.py:338
  246.1 1.2 shard_map.59
  247.3 11.4 %all_to_all.60.pieces = f32[16,40,128]{2,1,0:T(8,128)S(1)} all-to-all(f32[16,40,128]{2,1,0:T(8,128)S(1)} %bitcast.15), channel_id=1, replica_groups=mesh['x'=4,'y'=4,'z'=16,'c'=2] {'x','y'}, dimensions={0} | all-to-all | bytes 655360 | tf_op jit(solution)/shard_map/all_to_all | solution.py:250
  258.8 12.0 %all_to_all.61.every = f32[16,48,128]{2,1,0:T(8,128)S(1)} all-to-all(f32[16,48,128]{2,1,0:T(8,128)S(1)} %shard_map.60), channel_id=1, replica_groups=mesh['x'=4,'y'=4,'z'=16,'c'=2] {'x','y'}, dimensions={0} | all-to-all | bytes 786432 | tf_op jit(solution)/shard_map/all_to_all | solution.py:250
  270.9 4.5 %collective-permute-start.7 = (f32[640,128]{1,0:T(8,128)S(1)}, f32[640,128]{1,0:T(8,128)S(1)}, u32[]{:S(2)}, u32[]{:S(2)}) collective-permute-start(f32[640,128]{1,0:T(8,128)S(1)} %get-tuple-element.73.field), channel_id=1, source_target_pairs={{0,1},{1,0},{2,3},{3,2},{4,5},{5,4},{6,7},{7,6},{8,9},{9,8},{10,11... | collective-permute-start | bytes 983048 | tf_op jit(solution)/shard_map/ppermute | solution.py:317
  275.4 1.9 collective-permute-start.8
  277.4 4.4 %collective-permute-done.8.edge = f32[256,128]{1,0:T(8,128)S(1)} collective-permute-done((f32[256,128]{1,0:T(8,128)S(1)}, f32[256,128]{1,0:T(8,128)S(1)}, u32[]{:S(2)}, u32[]{:S(2)}) %collective-permute-start.8) | collective-permute-done | bytes 131104 | tf_op jit(solution)/shard_map/ppermute | solution.py:319
  281.7 2.9 shard_map.62
  284.6 19.4 %all_to_all.62.pieces = f32[16,40,128]{2,1,0:T(8,128)S(1)} all-to-all(f32[16,40,128]{2,1,0:T(8,128)S(1)} %bitcast.16), channel_id=1, replica_groups=mesh['x'=4,'y'=4,'z'=16,'c'=2] {'z'}, dimensions={0} | all-to-all | bytes 655360 | tf_op jit(solution)/shard_map/all_to_all | solution.py:250
  304.0 18.0 %all_to_all.63.every = f32[32,8,128]{2,1,0:T(8,128)S(1)} all-to-all(f32[32,8,128]{2,1,0:T(8,128)S(1)} %shard_map.63), channel_id=1, replica_groups=mesh['x'=4,'y'=4,'z'=16,'c'=2] {'x','y','c'}, dimensions={0} | all-to-all | bytes 262144 | tf_op jit(solution)/shard_map/all_to_all | solution.py:250
  322.1 17.3 %all_to_all.64.every = f32[16,8,128]{2,1,0:T(8,128)S(1)} all-to-all(f32[16,8,128]{2,1,0:T(8,128)S(1)} %shard_map.64), channel_id=1, replica_groups=mesh['x'=4,'y'=4,'z'=16,'c'=2] {'z'}, dimensions={0} | all-to-all | bytes 131072 | tf_op jit(solution)/shard_map/all_to_all | solution.py:250
  (66 shorter events, 5.0 us)
Async XLA Ops:
  0.0 1.9 copy-start
  1.9 1.1 copy-start.24
  3.0 1.4 copy-start.25
  4.4 43.7 %copy-start.1 = (f32[1280,640]{1,0:T(8,128)S(1)}, f32[1280,640]{1,0:T(8,128)}, u32[]{:S(2)}) copy-start(f32[1280,640]{1,0:T(8,128)} %green.5) | copy-start | bytes 9830404
  5.7 42.4 %collective-permute-start.2 = (f32[640,640]{1,0:T(8,128)}, f32[640,640]{1,0:T(8,128)}, u32[]{:S(2)}, u32[]{:S(2)}) collective-permute-start(f32[640,640]{1,0:T(8,128)} %get-tuple-element.45), channel_id=1, source_target_pairs={{0,1},{1,0},{2,3},{3,2},{4,5},{5,4},{6,7},{7,6},{8,9},{9,8},{10,11... | collective-permute-start | bytes 4915208 | tf_op jit(solution)/shard_map/ppermute | solution.py:289
  25.8 0.8 copy-start.23
  26.5 30.7 %all-to-all-start.1 = ((f32[16,48,128]{2,1,0:T(8,128)}), f32[16,48,128]{2,1,0:T(8,128)}, u32[]{:S(2)}, u32[]{:S(2)}) async-start(f32[16,48,128]{2,1,0:T(8,128)} %copy-done.23), calls=%async_computation.1 | async-start | bytes 786432 | tf_op jit(solution)/shard_map/all_to_all | solution.py:250
  30.7 5.7 %collective-permute-start = (s32[3,128]{1,0:T(4,128)S(1)}, s32[3,128]{1,0:T(4,128)S(1)}, u32[]{:S(2)}, u32[]{:S(2)}) collective-permute-start(s32[3,128]{1,0:T(4,128)S(1)} %get-tuple-element.42), channel_id=1, source_target_pairs={{0,1},{1,2},{2,3},{3,4},{4,5},{5,6},{6,7},{7,8},{8,9},{9,10},{10,1... | collective-permute-start | bytes 4616 | tf_op jit(solution)/shard_map/ppermute | solution.py:246
  34.4 5.3 %collective-permute-start.1 = (s32[3,128]{1,0:T(4,128)S(1)}, s32[3,128]{1,0:T(4,128)S(1)}, u32[]{:S(2)}, u32[]{:S(2)}) collective-permute-start(s32[3,128]{1,0:T(4,128)S(1)} %get-tuple-element.43), channel_id=1, source_target_pairs={{1,0},{2,1},{3,2},{4,3},{5,4},{6,5},{7,6},{8,7},{9,8},{10,9},{11,1... | collective-permute-start | bytes 4616 | tf_op jit(solution)/shard_map/ppermute | solution.py:246
  45.9 1.1 copy-start.2
  47.0 1.2 copy-start.5
  51.2 0.9 copy-start.7
  52.1 0.9 copy-start.10
  53.0 1.0 copy-start.13
  54.0 0.9 copy-start.16
  54.9 1.2 copy-start.19
  56.1 1.2 copy-start.21
  57.2 1.4 copy-start.3
  58.6 1.1 copy-start.8
  59.8 6.8 %copy-start.26 = (f32[128]{0:T(128)S(1)}, f32[128]{0:T(128)}, u32[]{:S(2)}) copy-start(f32[128]{0:T(128)} %param.7) | copy-start | bytes 1540
  59.8 9.5 %copy-start.4 = (bf16[640,1152]{1,0:T(8,128)(2,1)S(1)}, bf16[640,1152]{1,0:T(8,128)(2,1)}, u32[]{:S(2)}) copy-start(bf16[640,1152]{1,0:T(8,128)(2,1)} %copy-done.2) | copy-start | bytes 4423684
  59.8 9.5 %copy-start.6 = (bf16[640,1152]{1,0:T(8,128)(2,1)S(1)}, bf16[640,1152]{1,0:T(8,128)(2,1)}, u32[]{:S(2)}) copy-start(bf16[640,1152]{1,0:T(8,128)(2,1)} %copy-done.5) | copy-start | bytes 4423684
  60.9 8.3 %collective-permute-start.3 = (f32[640,128]{1,0:T(8,128)S(1)}, f32[640,128]{1,0:T(8,128)S(1)}, u32[]{:S(2)}, u32[]{:S(2)}) collective-permute-start(f32[640,128]{1,0:T(8,128)S(1)} %shard_map.51.field.old_field), channel_id=1, source_target_pairs={{0,1},{1,0},{2,3},{3,2},{4,5},{5,4},{6,7},{7,6},{8,9},{9,8},{10,11... | collective-permute-start | bytes 983048 | tf_op jit(solution)/shard_map/ppermute | solution.py:317
  62.9 6.3 %collective-permute-start.4 = (f32[256,128]{1,0:T(8,128)S(1)}, f32[256,128]{1,0:T(8,128)S(1)}, u32[]{:S(2)}, u32[]{:S(2)}) collective-permute-start(f32[256,128]{1,0:T(8,128)S(1)} %slice_select_fusion), channel_id=1, source_target_pairs={{1,2},{3,4},{5,6},{7,8},{9,10},{11,12},{13,14},{15,16},{17,18},{19... | collective-permute-start | bytes 393224 | tf_op jit(solution)/shard_map/ppermute | solution.py:319
  69.3 1.1 copy-start.11
  70.4 1.1 copy-start.14
  71.5 1.1 copy-start.17
  72.7 72.6 %copy-start.22 = (bf16[640,1280]{1,0:T(8,128)(2,1)S(1)}, bf16[640,1280]{1,0:T(8,128)(2,1)}, u32[]{:S(2)}) copy-start(bf16[640,1280]{1,0:T(8,128)(2,1)} %copy-done.21) | copy-start | bytes 4915204
  74.9 70.4 %copy-start.20 = (bf16[640,1280]{1,0:T(8,128)(2,1)S(1)}, bf16[640,1280]{1,0:T(8,128)(2,1)}, u32[]{:S(2)}) copy-start(bf16[640,1280]{1,0:T(8,128)(2,1)} %copy-done.19) | copy-start | bytes 4915204
  161.5 23.3 %copy-start.9 = (bf16[640,640]{1,0:T(8,128)(2,1)S(1)}, bf16[640,640]{1,0:T(8,128)(2,1)}, u32[]{:S(2)}) copy-start(bf16[640,640]{1,0:T(8,128)(2,1)} %copy-done.7) | copy-start | bytes 2457604
  161.5 23.3 %copy-start.12 = (bf16[640,640]{1,0:T(8,128)(2,1)S(1)}, bf16[640,640]{1,0:T(8,128)(2,1)}, u32[]{:S(2)}) copy-start(bf16[640,640]{1,0:T(8,128)(2,1)} %copy-done.10) | copy-start | bytes 2457604
  161.5 23.3 %copy-start.15 = (bf16[640,640]{1,0:T(8,128)(2,1)S(1)}, bf16[640,640]{1,0:T(8,128)(2,1)}, u32[]{:S(2)}) copy-start(bf16[640,640]{1,0:T(8,128)(2,1)} %copy-done.13) | copy-start | bytes 2457604
  161.5 23.3 %copy-start.18 = (bf16[640,640]{1,0:T(8,128)(2,1)S(1)}, bf16[640,640]{1,0:T(8,128)(2,1)}, u32[]{:S(2)}) copy-start(bf16[640,640]{1,0:T(8,128)(2,1)} %copy-done.16) | copy-start | bytes 2457604
  173.9 10.9 %collective-permute-start.5 = (f32[640,128]{1,0:T(8,128)S(1)}, f32[640,128]{1,0:T(8,128)S(1)}, u32[]{:S(2)}, u32[]{:S(2)}) collective-permute-start(f32[640,128]{1,0:T(8,128)S(1)} %get-tuple-element.61.field.old_field), channel_id=1, source_target_pairs={{0,1},{1,0},{2,3},{3,2},{4,5},{5,4},{6,7},{7,6},{8,9},{9,8},{10,11... | collective-permute-start | bytes 983048 | tf_op jit(solution)/shard_map/ppermute | solution.py:317
  178.5 6.3 %collective-permute-start.6 = (f32[256,128]{1,0:T(8,128)S(1)}, f32[256,128]{1,0:T(8,128)S(1)}, u32[]{:S(2)}, u32[]{:S(2)}) collective-permute-start(f32[256,128]{1,0:T(8,128)S(1)} %slice_select_fusion.2), channel_id=1, source_target_pairs={{1,2},{3,4},{5,6},{7,8},{9,10},{11,12},{13,14},{15,16},{17,18},{19... | collective-permute-start | bytes 393224 | tf_op jit(solution)/shard_map/ppermute | solution.py:319
  270.9 10.9 %collective-permute-start.7 = (f32[640,128]{1,0:T(8,128)S(1)}, f32[640,128]{1,0:T(8,128)S(1)}, u32[]{:S(2)}, u32[]{:S(2)}) collective-permute-start(f32[640,128]{1,0:T(8,128)S(1)} %get-tuple-element.73.field), channel_id=1, source_target_pairs={{0,1},{1,0},{2,3},{3,2},{4,5},{5,4},{6,7},{7,6},{8,9},{9,8},{10,11... | collective-permute-start | bytes 983048 | tf_op jit(solution)/shard_map/ppermute | solution.py:317
  275.4 6.3 %collective-permute-start.8 = (f32[256,128]{1,0:T(8,128)S(1)}, f32[256,128]{1,0:T(8,128)S(1)}, u32[]{:S(2)}, u32[]{:S(2)}) collective-permute-start(f32[256,128]{1,0:T(8,128)S(1)} %slice_select_fusion.1), channel_id=1, source_target_pairs={{1,2},{3,4},{5,6},{7,8},{9,10},{11,12},{13,14},{15,16},{17,18},{19... | collective-permute-start | bytes 393224 | tf_op jit(solution)/shard_map/ppermute | solution.py:319

commit v4 on v3

--- a/solution.py
+++ b/solution.py
@@ -26,6 +26,7 @@
         out_specs=[vmem] * len(outs),
         scratch_shapes=list(scratch),
         compiler_params=pltpu.CompilerParams(vmem_limit_bytes=mib << 20),
+        name=body.__name__,
     )(*scalars, *args)
 
 
@@ -64,42 +65,30 @@
     return value
 
 
-def turned(green, high, low):
+def first_back(core, green, data, moved, back_high, back_low, high, low, send, wide, *, share):
     for k in range(green.shape[0] // 128):
-        high[:, 128 * k : 128 * (k + 1)], low[:, 128 * k : 128 * (k + 1)] = halves(
-            green[128 * k : 128 * (k + 1), :].T
-        )
-
-
-def first_back(green, data, moved, high, low, wide):
-    turned(green, high, low)
+        at = slice(128 * k, 128 * (k + 1))
+        back_high[:, at], back_low[:, at] = halves(green[at, :].T)
     store_halves(wide, 0, data[...])
-    moved[...] = product(high, low, wide[...])
-
-
-def pick(core, green, ids, moved, send, last_ids, first_ids, *, share):
-    last_ids[...] = ids[:, ids.shape[1] - BAND :]
-    first_ids[...] = ids[:, :BAND]
-    for k in range(send.shape[0] // share):
-        theirs = pl.multiple_of((2 * k + 1 - core[0]) * share, TILE)
-        send[share * k : share * (k + 1), :] = green[pl.ds(theirs, share), :]
-
-
-def prepare(core, green, other, back_high, back_low, high, low, far_high, far_low, *, share):
-    for z in range(0, high.shape[0] // share, 2):
-        mine = [
-            green[pl.ds(pl.multiple_of((2 * k + core[0]) * share, TILE), share), :]
-            for k in (z, z + 1)
-        ]
+    moved[...] = product(back_high, back_low, wide[...])
+    for z in range(0, send.shape[0] // share, 2):
+        mine = []
+        for k in (z, z + 1):
+            start = pl.multiple_of((2 * k + core[0]) * share, TILE)
+            mine.append(green[pl.ds(start, share), :])
+            start = pl.multiple_of((2 * k + 1 - core[0]) * share, TILE)
+            send[share * k : share * (k + 1), :] = green[pl.ds(start, share), :]
         rows = slice(share * z, share * (z + 2))
         high[rows, :], low[rows, :] = halves(jnp.concatenate(mine, 0))
-    far_high[...], far_low[...] = halves(other[...])
-    turned(green, back_high, back_low)
+
+
+def split_other(other, high, low):
+    high[...], low[...] = halves(other[...])
 
 
 def laplace_square(block, before, ids, after, high, low, rows, own, ids_col):
     col_count = ids.shape[1]
-    height, width = rows.shape
+    height = rows.shape[0]
     total_cols = block[1] * col_count
     start = block[0] * col_count
     relative = jnp.concatenate([before[...], ids[...], after[...]], 1) - (start - 2 * BAND)
@@ -107,32 +96,30 @@
     ids_col[...] = jnp.concatenate([relative, pad], 0).T
     here = lax.broadcasted_iota(jnp.int32, (1, height), 1) + (start - BAND)
     inside = jnp.where((here >= 0) & (here < total_cols), 1.0, 0.0)
-
-    def fill_rows(i, carry):
-        at = pl.multiple_of(i * 128, 128)
-        row = lax.broadcasted_iota(jnp.int32, (128, width), 0) + at
-        col = lax.broadcasted_iota(jnp.int32, (128, width), 1)
+    rows[...] = jnp.zeros_like(rows)
+    wide = 128 + 2 * BAND
+    for i in range(height // 128):
+        at = 128 * i
+        row = lax.broadcasted_iota(jnp.int32, (128, wide), 0) + at
+        col = lax.broadcasted_iota(jnp.int32, (128, wide), 1) + at
         entry = jnp.where(col == row + BAND, 4.0, 0.0)
         for slot in range(3):
-            entry = entry - jnp.where(col == ids_col[pl.ds(at, 128), slot : slot + 1], 1.0, 0.0)
-        rows[pl.ds(at, 128), :] = entry.astype(BF16)
-        return carry
-
-    lax.fori_loop(0, height // 128, fill_rows, 0)
-
-    def fill_out(i, carry):
-        at = pl.multiple_of(i * 128, 128)
-        col = lax.broadcasted_iota(jnp.int32, (128, height), 0) + at
-        row = lax.broadcasted_iota(jnp.int32, (128, height), 1)
+            entry = entry - jnp.where(col == ids_col[at : at + 128, slot : slot + 1], 1.0, 0.0)
+        rows[at : at + 128, at : at + wide] = entry.astype(BF16)
+    high[...] = jnp.zeros_like(high)
+    low[...] = jnp.zeros_like(low)
+    for i in range(col_count // 128):
+        at = 128 * i
+        col = lax.broadcasted_iota(jnp.int32, (128, wide), 0) + at
+        row = lax.broadcasted_iota(jnp.int32, (128, wide), 1) + at
         entry = jnp.where(row == col + BAND, 4.0, 0.0)
         for slot in range(3):
-            entry = entry - jnp.where(col + 2 * BAND == relative[slot : slot + 1, :], 1.0, 0.0)
-        own[...] = (entry * inside).astype(BF16)
-        square = jnp.dot(own[...], rows[...], preferred_element_type=F32)
-        high[pl.ds(at, 128), :], low[pl.ds(at, 128), :] = halves(square)
-        return carry
-
-    lax.fori_loop(0, col_count // 128, fill_out, 0)
+            target = relative[slot : slot + 1, at : at + wide]
+            entry = entry - jnp.where(col + 2 * BAND == target, 1.0, 0.0)
+        own[...] = (entry * inside[:, at : at + wide]).astype(BF16)
+        reach = slice(at, at + 128 + 4 * BAND)
+        square = jnp.dot(own[...], rows[at : at + wide, reach], preferred_element_type=F32)
+        high[at : at + 128, reach], low[at : at + 128, reach] = halves(square)
 
 
 def forward(core, field, other, edge, weight_sq, smooth, own_high, own_low, far_high, far_low, m_high, m_low, part, sums, fresh, wide, near):
@@ -192,13 +179,21 @@
         out[k, share:, :] = last
 
 
-def start_field(every, m_high, far_high, field):
+def put_edge(core, field, edge):
+    reach = edge.shape[0]
+    edge[...] = jnp.where(core[0] == 0, field[:reach, :], field[field.shape[0] - reach :, :])
+
+
+def start_field(core, every, ids, field, edge, last_ids, first_ids):
+    last_ids[...] = ids[:, ids.shape[1] - BAND :]
+    first_ids[...] = ids[:, :BAND]
     share = every.shape[1] - TILE
     for k in range(every.shape[0]):
         field[share * k : share * (k + 1), :] = every[k, :share, :]
-
-
-def update(every, scalars, smooth, way, old_field, old_slip, field, slip, kept):
+    put_edge(core, field, edge)
+
+
+def update(core, every, scalars, smooth, way, old_field, old_slip, field, edge, slip, kept):
     count = every.shape[0]
     share = every.shape[1] - TILE
     image_sq = every[0, share : share + 1, :]
@@ -208,6 +203,7 @@
     for k in range(count):
         rows = slice(share * k, share * (k + 1))
         field[rows, :] = old_field[rows, :] - step * (every[k, :share, :] + smooth[rows, :])
+    put_edge(core, field, edge)
     slip[...] = old_slip[...] + step * way[...]
     put_rows(kept, [scalars[0:1, :], scalars[1:2, :], scalars[2:3, :], image_sq])
 
@@ -275,29 +271,26 @@
     near = pltpu.VMEM((col_count + 2 * reach, 2 * epochs), BF16)
 
     back_matrix = ((col_count, row_count), BF16)
-    (moved,) = local_call(
-        first_back, [field_shape], green, data,
-        scratch=[pltpu.VMEM(*back_matrix), pltpu.VMEM(*back_matrix), wide],
-    )
-    pieces = exchanged(moved.reshape(n_obs, piece, epochs), OBS)
     matrix = ((half, col_count), BF16)
     ids_shape = ((3, BAND), jnp.int32)
-    send, last_ids, first_ids = local_call(
-        pick, [((half, col_count), F32), ids_shape, ids_shape],
-        green, neighbours, moved, scalars=[core_scalar], share=share,
+    moved, b_high, b_low, own_high, own_low, send = local_call(
+        first_back,
+        [field_shape, back_matrix, back_matrix, matrix, matrix, ((half, col_count), F32)],
+        green, data, scalars=[core_scalar], scratch=[wide], share=share,
     )
     far = lax.ppermute(send, "c", swap)
-    before, after = to_neighbours(last_ids, first_ids, PATCH)
-
+    pieces = exchanged(moved.reshape(n_obs, piece, epochs), OBS)
     zero_tail = jnp.zeros((TILE, epochs), F32)
     zero_field = jnp.zeros((col_count, epochs), F32)
     spread_shape = ((n_obs, piece + TILE, epochs), F32)
     (out,) = local_call(spread, [spread_shape], pieces, zero_tail)
     every = exchanged(out, OBS)
-    b_high, b_low, own_high, own_low, far_high, far_low = local_call(
-        prepare, [back_matrix, back_matrix, matrix, matrix, matrix, matrix],
-        green, far, scalars=[core_scalar], share=share,
+    edge_shape = ((reach, epochs), F32)
+    field, edge, last_ids, first_ids = local_call(
+        start_field, [field_shape, edge_shape, ids_shape, ids_shape], every, neighbours,
+        scalars=[core_scalar],
     )
+    before, after = to_neighbours(last_ids, first_ids, PATCH)
     height, width = col_count + 2 * BAND, col_count + 4 * BAND
     m_matrix = ((col_count, width), BF16)
     m_high, m_low = local_call(
@@ -305,17 +298,16 @@
         scalars=[block_scalars],
         scratch=[
             pltpu.VMEM((height, width), BF16),
-            pltpu.VMEM((128, height), BF16),
+            pltpu.VMEM((128, 128 + 2 * BAND), BF16),
             pltpu.VMEM((height, TILE), jnp.int32),
         ],
     )
-    (field,) = local_call(start_field, [field_shape], every, m_high, far_high)
+    far_high, far_low = local_call(split_other, [matrix, matrix], far)
 
     kept, slip, smooth, way = zero_tail, zero_field, zero_field, zero_field
     image = jnp.zeros((row_count, epochs), F32)
     for iteration in range(ITERS):
         other = lax.ppermute(field, "c", swap)
-        edge = jnp.where(core == 0, field[:reach], field[col_count - reach :])
         edge = lax.ppermute(edge, PATCH, outward)
         part, sums, fresh = local_call(
             forward, [((half, epochs), F32), tail_shape, field_shape],
@@ -344,16 +336,16 @@
         )
         pieces = exchanged(moved.reshape(n_obs, piece, epochs), OBS)
         (out,) = local_call(spread, [spread_shape], pieces, tail)
-        field, slip, kept = local_call(
-            update, [field_shape, field_shape, tail_shape],
+        field, edge, slip, kept = local_call(
+            update, [field_shape, edge_shape, field_shape, tail_shape],
             exchanged(out, OBS), scalars, smooth, way, field, slip,
+            scalars=[core_scalar],
         )
 
 
 def solution(mesh):
     split = Mesh(mesh.devices.reshape(4, 4, 16, 2), (*OBS, *PATCH))
     in_specs = (P(OBS, PATCH), P(OBS, None), P(None, PATCH), P())
-
     return jax.shard_map(
         shards, mesh=split, in_specs=in_specs, out_specs=P(PATCH, None), check_vma=False
     )

time: 341 us -> 325 us (0.953)
  local copies, waits for them, and re-layouts: 18.1 us -> 4.3 us
  blocking collectives: 246 us -> 252 us
    unnamed x54 -> x12, local copies, waits for them, and re-layouts: 18.1 us -> 4.23 us
    all_to_all x10 -> x11, blocking collectives: 166 us -> 175 us  [exchanged(): return lax.all_to_all(pieces, axis, 0, 0, tiled=True)]
    all_to_all x1 -> x0, starting transfers between devices: 4.2 us -> none  [exchanged(): return lax.all_to_all(pieces, axis, 0, 0, tiled=True)]
    pallas_call x20 -> x19, Pallas kernels: 24.1 us -> 21.8 us  [local_call(): pl.pallas_call(functools.partial(body, **options), out_shape=[jax.ShapeDt...]
  transfers between devices with their start and end apart: 10 -> 9, of which waited for: 4 -> 3; matrix products, arithmetic and copies ran while one was open for 0% -> 0% of each run, Pallas kernels for 3% -> 1%
where the time goes in v4:
time: 325 us; the launch traced here: 324 us
  blocking collectives  252 us (78%)
  starting transfers between devices  34.1 us (10%)
  Pallas kernels  21.8 us (7%)
  waiting for transfers between devices  11.6 us (4%)
  local copies, waits for them, and re-layouts  4.3 us (1%)
    all_to_all x11, blocking collectives, exchanged(): return lax.all_to_all(pieces, axis, 0, 0, tiled=True)  175 us
    all_gather x2, blocking collectives, shards(): every = lax.all_gather(out, PATCH)  77.6 us
    pallas_call x19, Pallas kernels, local_call(): pl.pallas_call(functools.partial(body, **options), out_shape=[jax.ShapeDt...  21.8 us
    ppermute x3, starting transfers between devices, shards(): other = lax.ppermute(field, 'c', swap)  11 us
    ppermute x1, starting transfers between devices, shards(): far = lax.ppermute(send, 'c', swap)  8.86 us
    ppermute x3, waiting for transfers between devices, shards(): edge = lax.ppermute(edge, PATCH, outward)  8.72 us
    ppermute x3, starting transfers between devices, shards(): edge = lax.ppermute(edge, PATCH, outward)  8.36 us
  transfers between devices with their start and end apart: 9, of which 3 were waited for; matrix products, arithmetic and copies ran while one was open for 0% of the time, Pallas kernels for 1%

profile of v4, /device:TPU:1, one launch (start us, length us, event | category | flops | bytes accessed | tf_op | source)
XLA Modules:
  0.0 324.3 jit_solution(1741029623823461819)
XLA Ops:
  0.0 1.9 copy-done.2
  1.9 1.1 copy-done.3
  3.0 2.8 first_back.1
  5.8 1.2 copy-done
  7.1 8.9 %collective-permute-start.2 = (f32[640,640]{1,0:T(8,128)}, f32[640,640]{1,0:T(8,128)}, u32[]{:S(2)}, u32[]{:S(2)}) collective-permute-start(f32[640,640]{1,0:T(8,128)} %get-tuple-element.52), channel_id=1, source_target_pairs={{0,1},{1,0},{2,3},{3,2},{4,5},{5,4},{6,7},{7,6},{8,9},{9,8},{10,11... | collective-permute-start | bytes 4915208 | tf_op jit(solution)/shard_map/ppermute | solution.py:281
  15.9 11.1 %all_to_all.55.pieces = f32[16,40,128]{2,1,0:T(8,128)S(1)} all-to-all(f32[16,40,128]{2,1,0:T(8,128)S(1)} %bitcast.16), channel_id=1, replica_groups=mesh['x'=4,'y'=4,'z'=16,'c'=2] {'x','y'}, dimensions={0} | all-to-all | bytes 655360 | tf_op jit(solution)/shard_map/all_to_all | solution.py:246
  27.1 11.9 %all_to_all.56.every = f32[16,48,128]{2,1,0:T(8,128)S(1)} all-to-all(f32[16,48,128]{2,1,0:T(8,128)S(1)} %spread.3), channel_id=1, replica_groups=mesh['x'=4,'y'=4,'z'=16,'c'=2] {'x','y'}, dimensions={0} | all-to-all | bytes 786432 | tf_op jit(solution)/shard_map/all_to_all | solution.py:246
  39.0 0.8 start_field.1
  39.8 4.5 %collective-permute-start.1 = (f32[256,128]{1,0:T(8,128)}, f32[256,128]{1,0:T(8,128)S(1)}, u32[]{:S(2)}, u32[]{:S(2)}) collective-permute-start(f32[256,128]{1,0:T(8,128)} %get-tuple-element.49), channel_id=1, source_target_pairs={{1,2},{3,4},{5,6},{7,8},{9,10},{11,12},{13,14},{15,16},{17,18},{19... | collective-permute-start | bytes 393224 | tf_op jit(solution)/shard_map/ppermute | solution.py:311
  44.3 1.9 collective-permute-start
  46.3 3.9 %collective-permute-start.3 = (s32[3,128]{1,0:T(4,128)S(1)}, s32[3,128]{1,0:T(4,128)S(1)}, u32[]{:S(2)}, u32[]{:S(2)}) collective-permute-start(s32[3,128]{1,0:T(4,128)S(1)} %get-tuple-element.55), channel_id=1, source_target_pairs={{0,1},{1,2},{2,3},{3,4},{4,5},{5,6},{6,7},{7,8},{8,9},{9,10},{10,1... | collective-permute-start | bytes 4616 | tf_op jit(solution)/shard_map/ppermute | solution.py:242
  50.2 1.9 collective-permute-start.4
  52.2 0.1 pad_add_fusion.block
  52.2 0.0 collective-permute-done.3.before
  52.2 2.9 collective-permute-done.4.after
  55.1 2.2 laplace_square.1
  57.4 0.0 collective-permute-done.2.other
  57.4 1.7 split_other.1
  59.1 0.0 collective-permute-done.1.edge
  59.1 0.0 collective-permute-done.other
  59.1 3.4 %forward.3 = (f32[640,128]{1,0:T(8,128)S(1)}, f32[8,128]{1,0:T(8,128)S(1)}, f32[640,128]{1,0:T(8,128)S(1)}) custom-call(s32[1]{0:T(128)} %bitcast.1.core, f32[640,128]{1,0:T(8,128)} %get-tuple-element.48.field.old_field, f32[640,128]{1,0:T(8,128)} %collective-permute-done.other, f32[256,128]{1,0:T(8,128)S(1)} %collective-permute-done.1.edge, ...), custom_call_target="tpu_custom_call" | custom-call | tf_op jit(solution)/shard_map/forward/pallas_call | solution.py:22
  62.5 31.0 %all_to_all.57.pieces = f32[16,40,128]{2,1,0:T(8,128)S(1)} all-to-all(f32[16,40,128]{2,1,0:T(8,128)S(1)} %bitcast.18), channel_id=1, replica_groups=mesh['x'=4,'y'=4,'z'=16,'c'=2] {'z'}, dimensions={0} | all-to-all | bytes 655360 | tf_op jit(solution)/shard_map/all_to_all | solution.py:246
  93.5 37.8 %all-gather = f32[1536,128]{1,0:T(8,128)S(1)} all-gather(f32[48,128]{1,0:T(8,128)S(1)} %collect.2), channel_id=2, replica_groups=mesh['x'=4,'y'=4,'z'=16,'c'=2] {'z','c'}, dimensions={0}, use_global_device_ids=true | all-gather | bytes 811008 | tf_op jit(solution)/shard_map/all_gather | solution.py:330
  131.3 0.0 copy-done.1
  131.4 2.2 backward.2
  133.6 11.4 %all_to_all.58.pieces = f32[16,40,128]{2,1,0:T(8,128)S(1)} all-to-all(f32[16,40,128]{2,1,0:T(8,128)S(1)} %bitcast.17), channel_id=1, replica_groups=mesh['x'=4,'y'=4,'z'=16,'c'=2] {'x','y'}, dimensions={0} | all-to-all | bytes 655360 | tf_op jit(solution)/shard_map/all_to_all | solution.py:246
  145.0 12.0 %all_to_all.59.every = f32[16,48,128]{2,1,0:T(8,128)S(1)} all-to-all(f32[16,48,128]{2,1,0:T(8,128)S(1)} %spread.4), channel_id=1, replica_groups=mesh['x'=4,'y'=4,'z'=16,'c'=2] {'x','y'}, dimensions={0} | all-to-all | bytes 786432 | tf_op jit(solution)/shard_map/all_to_all | solution.py:246
  157.0 1.1 update.2
  158.1 4.5 %collective-permute-start.5 = (f32[640,128]{1,0:T(8,128)S(1)}, f32[640,128]{1,0:T(8,128)S(1)}, u32[]{:S(2)}, u32[]{:S(2)}) collective-permute-start(f32[640,128]{1,0:T(8,128)S(1)} %get-tuple-element.69.field.old_field), channel_id=1, source_target_pairs={{0,1},{1,0},{2,3},{3,2},{4,5},{5,4},{6,7},{7,6},{8,9},{9,8},{10,11... | collective-permute-start | bytes 983048 | tf_op jit(solution)/shard_map/ppermute | solution.py:310
  162.7 1.9 collective-permute-start.6
  164.6 4.4 %collective-permute-done.6.edge = f32[256,128]{1,0:T(8,128)S(1)} collective-permute-done((f32[256,128]{1,0:T(8,128)S(1)}, f32[256,128]{1,0:T(8,128)S(1)}, u32[]{:S(2)}, u32[]{:S(2)}) %collective-permute-start.6) | collective-permute-done | bytes 131104 | tf_op jit(solution)/shard_map/ppermute | solution.py:311
  169.0 0.0 collective-permute-done.5.other
  169.0 2.3 forward.4
  171.2 19.1 %all_to_all.60.pieces = f32[16,40,128]{2,1,0:T(8,128)S(1)} all-to-all(f32[16,40,128]{2,1,0:T(8,128)S(1)} %bitcast.19), channel_id=1, replica_groups=mesh['x'=4,'y'=4,'z'=16,'c'=2] {'z'}, dimensions={0} | all-to-all | bytes 655360 | tf_op jit(solution)/shard_map/all_to_all | solution.py:246
  190.4 39.7 %all-gather.1 = f32[1536,128]{1,0:T(8,128)S(1)} all-gather(f32[48,128]{1,0:T(8,128)S(1)} %collect.3), channel_id=3, replica_groups=mesh['x'=4,'y'=4,'z'=16,'c'=2] {'z','c'}, dimensions={0}, use_global_device_ids=true | all-gather | bytes 811008 | tf_op jit(solution)/shard_map/all_gather | solution.py:330
  230.1 1.2 backward.3
  231.4 11.4 %all_to_all.61.pieces = f32[16,40,128]{2,1,0:T(8,128)S(1)} all-to-all(f32[16,40,128]{2,1,0:T(8,128)S(1)} %bitcast.14), channel_id=1, replica_groups=mesh['x'=4,'y'=4,'z'=16,'c'=2] {'x','y'}, dimensions={0} | all-to-all | bytes 655360 | tf_op jit(solution)/shard_map/all_to_all | solution.py:246
  242.8 12.0 %all_to_all.62.every = f32[16,48,128]{2,1,0:T(8,128)S(1)} all-to-all(f32[16,48,128]{2,1,0:T(8,128)S(1)} %spread.5), channel_id=1, replica_groups=mesh['x'=4,'y'=4,'z'=16,'c'=2] {'x','y'}, dimensions={0} | all-to-all | bytes 786432 | tf_op jit(solution)/shard_map/all_to_all | solution.py:246
  254.8 0.1 update.3
  254.9 4.5 %collective-permute-start.7 = (f32[640,128]{1,0:T(8,128)S(1)}, f32[640,128]{1,0:T(8,128)S(1)}, u32[]{:S(2)}, u32[]{:S(2)}) collective-permute-start(f32[640,128]{1,0:T(8,128)S(1)} %get-tuple-element.82.field), channel_id=1, source_target_pairs={{0,1},{1,0},{2,3},{3,2},{4,5},{5,4},{6,7},{7,6},{8,9},{9,8},{10,11... | collective-permute-start | bytes 983048 | tf_op jit(solution)/shard_map/ppermute | solution.py:310
  259.5 1.9 collective-permute-start.8
  261.4 4.4 %collective-permute-done.8.edge = f32[256,128]{1,0:T(8,128)S(1)} collective-permute-done((f32[256,128]{1,0:T(8,128)S(1)}, f32[256,128]{1,0:T(8,128)S(1)}, u32[]{:S(2)}, u32[]{:S(2)}) %collective-permute-start.8) | collective-permute-done | bytes 131104 | tf_op jit(solution)/shard_map/ppermute | solution.py:311
  265.8 0.0 collective-permute-done.7.other
  265.8 2.9 forward.5
  268.7 19.4 %all_to_all.63.pieces = f32[16,40,128]{2,1,0:T(8,128)S(1)} all-to-all(f32[16,40,128]{2,1,0:T(8,128)S(1)} %bitcast.15), channel_id=1, replica_groups=mesh['x'=4,'y'=4,'z'=16,'c'=2] {'z'}, dimensions={0} | all-to-all | bytes 655360 | tf_op jit(solution)/shard_map/all_to_all | solution.py:246
  288.2 18.0 %all_to_all.64.every = f32[32,8,128]{2,1,0:T(8,128)S(1)} all-to-all(f32[32,8,128]{2,1,0:T(8,128)S(1)} %last_sums.1), channel_id=1, replica_groups=mesh['x'=4,'y'=4,'z'=16,'c'=2] {'x','y','c'}, dimensions={0} | all-to-all | bytes 262144 | tf_op jit(solution)/shard_map/all_to_all | solution.py:246
  306.2 17.3 %all_to_all.65.every = f32[16,8,128]{2,1,0:T(8,128)S(1)} all-to-all(f32[16,8,128]{2,1,0:T(8,128)S(1)} %last_spread.1), channel_id=1, replica_groups=mesh['x'=4,'y'=4,'z'=16,'c'=2] {'z'}, dimensions={0} | all-to-all | bytes 131072 | tf_op jit(solution)/shard_map/all_to_all | solution.py:246
  323.5 0.8 last_update.1
  (19 shorter events, 0.3 us)
Async XLA Ops:
  0.0 1.9 copy-start.2
  1.9 1.1 copy-start.3
  5.8 1.2 copy-start
  7.0 32.0 %copy-start.4 = (s32[3,640]{1,0:T(4,128)S(1)}, s32[3,640]{1,0:T(4,128)}, u32[]{:S(2)}) copy-start(s32[3,640]{1,0:T(4,128)} %ids.3) | copy-start | bytes 23044
  7.1 39.2 %copy-start.5 = (f32[128]{0:T(128)S(1)}, f32[128]{0:T(128)}, u32[]{:S(2)}) copy-start(f32[128]{0:T(128)} %param.7) | copy-start | bytes 1540
  7.1 50.3 %collective-permute-start.2 = (f32[640,640]{1,0:T(8,128)}, f32[640,640]{1,0:T(8,128)}, u32[]{:S(2)}, u32[]{:S(2)}) collective-permute-start(f32[640,640]{1,0:T(8,128)} %get-tuple-element.52), channel_id=1, source_target_pairs={{0,1},{1,0},{2,3},{3,2},{4,5},{5,4},{6,7},{7,6},{8,9},{9,8},{10,11... | collective-permute-start | bytes 4915208 | tf_op jit(solution)/shard_map/ppermute | solution.py:281
  39.8 19.3 %collective-permute-start.1 = (f32[256,128]{1,0:T(8,128)}, f32[256,128]{1,0:T(8,128)S(1)}, u32[]{:S(2)}, u32[]{:S(2)}) collective-permute-start(f32[256,128]{1,0:T(8,128)} %get-tuple-element.49), channel_id=1, source_target_pairs={{1,2},{3,4},{5,6},{7,8},{9,10},{11,12},{13,14},{15,16},{17,18},{19... | collective-permute-start | bytes 393224 | tf_op jit(solution)/shard_map/ppermute | solution.py:311
  44.3 14.7 %collective-permute-start = (f32[640,128]{1,0:T(8,128)}, f32[640,128]{1,0:T(8,128)}, u32[]{:S(2)}, u32[]{:S(2)}) collective-permute-start(f32[640,128]{1,0:T(8,128)} %get-tuple-element.48.field.old_field), channel_id=1, source_target_pairs={{0,1},{1,0},{2,3},{3,2},{4,5},{5,4},{6,7},{7,6},{8,9},{9,8},{10,11... | collective-permute-start | bytes 983048 | tf_op jit(solution)/shard_map/ppermute | solution.py:310
  46.3 5.9 %collective-permute-start.3 = (s32[3,128]{1,0:T(4,128)S(1)}, s32[3,128]{1,0:T(4,128)S(1)}, u32[]{:S(2)}, u32[]{:S(2)}) collective-permute-start(s32[3,128]{1,0:T(4,128)S(1)} %get-tuple-element.55), channel_id=1, source_target_pairs={{0,1},{1,2},{2,3},{3,4},{4,5},{5,6},{6,7},{7,8},{8,9},{9,10},{10,1... | collective-permute-start | bytes 4616 | tf_op jit(solution)/shard_map/ppermute | solution.py:242
  50.2 4.9 %collective-permute-start.4 = (s32[3,128]{1,0:T(4,128)S(1)}, s32[3,128]{1,0:T(4,128)S(1)}, u32[]{:S(2)}, u32[]{:S(2)}) collective-permute-start(s32[3,128]{1,0:T(4,128)S(1)} %get-tuple-element.56), channel_id=1, source_target_pairs={{1,0},{2,1},{3,2},{4,3},{5,4},{6,5},{7,6},{8,7},{9,8},{10,9},{11,1... | collective-permute-start | bytes 4616 | tf_op jit(solution)/shard_map/ppermute | solution.py:242
  62.5 68.9 %copy-start.1 = (bf16[640,1280]{1,0:T(8,128)(2,1)S(1)}, bf16[640,1280]{1,0:T(8,128)(2,1)}, u32[]{:S(2)}) copy-start(bf16[640,1280]{1,0:T(8,128)(2,1)} %copy-done) | copy-start | bytes 4915204
  158.1 10.8 %collective-permute-start.5 = (f32[640,128]{1,0:T(8,128)S(1)}, f32[640,128]{1,0:T(8,128)S(1)}, u32[]{:S(2)}, u32[]{:S(2)}) collective-permute-start(f32[640,128]{1,0:T(8,128)S(1)} %get-tuple-element.69.field.old_field), channel_id=1, source_target_pairs={{0,1},{1,0},{2,3},{3,2},{4,5},{5,4},{6,7},{7,6},{8,9},{9,8},{10,11... | collective-permute-start | bytes 983048 | tf_op jit(solution)/shard_map/ppermute | solution.py:310
  162.7 6.3 %collective-permute-start.6 = (f32[256,128]{1,0:T(8,128)S(1)}, f32[256,128]{1,0:T(8,128)S(1)}, u32[]{:S(2)}, u32[]{:S(2)}) collective-permute-start(f32[256,128]{1,0:T(8,128)S(1)} %get-tuple-element.70), channel_id=1, source_target_pairs={{1,2},{3,4},{5,6},{7,8},{9,10},{11,12},{13,14},{15,16},{17,18},{19... | collective-permute-start | bytes 393224 | tf_op jit(solution)/shard_map/ppermute | solution.py:311
  254.9 10.8 %collective-permute-start.7 = (f32[640,128]{1,0:T(8,128)S(1)}, f32[640,128]{1,0:T(8,128)S(1)}, u32[]{:S(2)}, u32[]{:S(2)}) collective-permute-start(f32[640,128]{1,0:T(8,128)S(1)} %get-tuple-element.82.field), channel_id=1, source_target_pairs={{0,1},{1,0},{2,3},{3,2},{4,5},{5,4},{6,7},{7,6},{8,9},{9,8},{10,11... | collective-permute-start | bytes 983048 | tf_op jit(solution)/shard_map/ppermute | solution.py:310
  259.5 6.3 %collective-permute-start.8 = (f32[256,128]{1,0:T(8,128)S(1)}, f32[256,128]{1,0:T(8,128)S(1)}, u32[]{:S(2)}, u32[]{:S(2)}) collective-permute-start(f32[256,128]{1,0:T(8,128)S(1)} %get-tuple-element.83), channel_id=1, source_target_pairs={{1,2},{3,4},{5,6},{7,8},{9,10},{11,12},{13,14},{15,16},{17,18},{19... | collective-permute-start | bytes 393224 | tf_op jit(solution)/shard_map/ppermute | solution.py:311

commit v5 on v4

--- a/solution.py
+++ b/solution.py
@@ -26,7 +26,6 @@
         out_specs=[vmem] * len(outs),
         scratch_shapes=list(scratch),
         compiler_params=pltpu.CompilerParams(vmem_limit_bytes=mib << 20),
-        name=body.__name__,
     )(*scalars, *args)
 
 
@@ -65,7 +64,7 @@
     return value
 
 
-def first_back(core, green, data, moved, back_high, back_low, high, low, send, wide, *, share):
+def first_back(core, place, green, data, moved, back_high, back_low, high, low, send, wide, *, share):
     for k in range(green.shape[0] // 128):
         at = slice(128 * k, 128 * (k + 1))
         back_high[:, at], back_low[:, at] = halves(green[at, :].T)
@@ -86,10 +85,10 @@
     high[...], low[...] = halves(other[...])
 
 
-def laplace_square(block, before, ids, after, high, low, rows, own, ids_col):
+def laplace_square(block, before, ids, after, high, low, rows, own, ids_col, *, n_patch):
     col_count = ids.shape[1]
     height = rows.shape[0]
-    total_cols = block[1] * col_count
+    total_cols = n_patch * col_count
     start = block[0] * col_count
     relative = jnp.concatenate([before[...], ids[...], after[...]], 1) - (start - 2 * BAND)
     pad = jnp.zeros((TILE - 3, height), jnp.int32)
@@ -122,26 +121,35 @@
         high[at : at + 128, reach], low[at : at + 128, reach] = halves(square)
 
 
-def forward(core, field, other, edge, weight_sq, smooth, own_high, own_low, far_high, far_low, m_high, m_low, part, sums, fresh, wide, near):
-    rows, reach = field.shape[0], 2 * BAND
-    own = field[...]
-    store_halves(wide, 0, own)
-    store_halves(wide, rows, other[...])
+def forward(core, pair, own_high, own_low, far_high, far_low, part, wide):
+    rows = pair.shape[1]
+    store_halves(wide, 0, pair[core[0]])
+    store_halves(wide, rows, pair[1 - core[0]])
     part[...] = product(own_high, own_low, wide[:rows, :]) + product(far_high, far_low, wide[rows:, :])
+
+
+def regularized(core, pair, edge, weight, m_high, m_low, near):
+    rows, reach = pair.shape[1], 2 * BAND
+    own, other = pair[core[0]], pair[1 - core[0]]
     is_first = core[0] == 0
     outer = edge[...]
-    store_halves(near, 0, jnp.where(is_first, outer, other[rows - reach :, :]))
+    store_halves(near, 0, jnp.where(is_first, outer, other[rows - reach :]))
     store_halves(near, reach, own)
-    store_halves(near, reach + rows, jnp.where(is_first, other[:reach, :], outer))
-    new = weight_sq[...] * product(m_high, m_low, near[...])
+    store_halves(near, reach + rows, jnp.where(is_first, other[:reach], outer))
+    return own, weight[...] * weight[...] * product(m_high, m_low, near[...])
+
+
+def gathered(pieces, part):
+    part[...] = summed(pieces)
+
+
+def collect(core, part, pair, edge, weight, smooth, m_high, m_low, out, fresh, near):
+    share = part.shape[0]
+    out[:share, :] = part[...]
+    own, new = regularized(core, pair, edge, weight, m_high, m_low, near)
     fresh[...] = new
-    put_rows(sums, [total(own * own), total(own * new), total(own * smooth[...])])
-
-
-def collect(pieces, sums, out):
-    share = pieces.shape[1]
-    out[:share, :] = summed(pieces)
-    out[share:, :] = sums[...]
+    rows = [total(own * own), total(own * new), total(own * smooth[...])]
+    out[share:, :] = jnp.concatenate([*rows, jnp.zeros((TILE - 3, own.shape[1]), F32)], 0)
 
 
 def backward(every, field, fresh, old_image, old_smooth, old_way, old_scalars, high, low, moved, image, tail, smooth, way, scalars, wide):
@@ -208,12 +216,15 @@
     put_rows(kept, [scalars[0:1, :], scalars[1:2, :], scalars[2:3, :], image_sq])
 
 
-def last_sums(place, pieces, image, sums, out):
-    share = pieces.shape[1]
-    part = summed(pieces)
+def last_sums(core, place, share_ref, image, pair, edge, weight, smooth, m_high, m_low, out, near):
+    part = share_ref[...]
+    share = part.shape[0]
     start = pl.multiple_of(place[0] * share, TILE)
     old = image[pl.ds(start, share), :]
-    first = jnp.concatenate([sums[0:3, :], total(part * part), total(part * old), sums[5:, :]], 0)
+    own, new = regularized(core, pair, edge, weight, m_high, m_low, near)
+    rows = [total(own * own), total(own * new), total(own * smooth[...])]
+    rows = [*rows, total(part * part), total(part * old)]
+    first = jnp.concatenate([*rows, jnp.zeros((TILE - 5, own.shape[1]), F32)], 0)
     for k in range(out.shape[0]):
         out[k] = first
 
@@ -255,11 +266,10 @@
     piece = col_count // n_obs
     half = row_count // n_core
     reach = 2 * BAND
-    weight_sq = (reg_weight * reg_weight)[None]
+    weight = reg_weight[None]
     share = row_count // n_patch
     core_scalar = core.astype(jnp.int32)[None]
     place_scalar = lax.axis_index(PATCH).astype(jnp.int32)[None]
-    block_scalars = jnp.stack([lax.axis_index(PATCH).astype(jnp.int32), jnp.int32(n_patch)])
     swap = [(0, 1), (1, 0)]
     outward = [(2 * z + 1, 2 * z + 2) for z in range(n_z - 1)]
     outward = outward + [(b, a) for a, b in outward]
@@ -276,7 +286,7 @@
     moved, b_high, b_low, own_high, own_low, send = local_call(
         first_back,
         [field_shape, back_matrix, back_matrix, matrix, matrix, ((half, col_count), F32)],
-        green, data, scalars=[core_scalar], scratch=[wide], share=share,
+        green, data, scalars=[core_scalar, place_scalar], scratch=[wide], share=share,
     )
     far = lax.ppermute(send, "c", swap)
     pieces = exchanged(moved.reshape(n_obs, piece, epochs), OBS)
@@ -295,7 +305,8 @@
     m_matrix = ((col_count, width), BF16)
     m_high, m_low = local_call(
         laplace_square, [m_matrix, m_matrix], before, neighbours, after,
-        scalars=[block_scalars],
+        scalars=[place_scalar],
+        n_patch=n_patch,
         scratch=[
             pltpu.VMEM((height, width), BF16),
             pltpu.VMEM((128, 128 + 2 * BAND), BF16),
@@ -307,26 +318,32 @@
     kept, slip, smooth, way = zero_tail, zero_field, zero_field, zero_field
     image = jnp.zeros((row_count, epochs), F32)
     for iteration in range(ITERS):
-        other = lax.ppermute(field, "c", swap)
         edge = lax.ppermute(edge, PATCH, outward)
-        part, sums, fresh = local_call(
-            forward, [((half, epochs), F32), tail_shape, field_shape],
-            field, other, edge, weight_sq, smooth,
-            own_high, own_low, far_high, far_low, m_high, m_low,
-            scalars=[core_scalar],
-            scratch=[wide, near],
+        pair = lax.all_gather(field, "c")
+        (part,) = local_call(
+            forward, [((half, epochs), F32)],
+            pair, own_high, own_low, far_high, far_low,
+            scalars=[core_scalar], scratch=[wide],
         )
         pieces = exchanged(part.reshape(n_z, share, epochs), "z")
+        (part,) = local_call(gathered, [((share, epochs), F32)], pieces)
+        penalty = (pair, edge, weight, smooth, m_high, m_low)
         if iteration + 1 == ITERS:
             shape = ((n_obs * n_core, TILE, epochs), F32)
-            (out,) = local_call(last_sums, [shape], pieces, image, sums, scalars=[place_scalar])
+            (out,) = local_call(
+                last_sums, [shape], part, image, *penalty,
+                scalars=[core_scalar, place_scalar], scratch=[near],
+            )
             every = exchanged(out, (*OBS, "c"))
             (out,) = local_call(last_spread, [((n_z, TILE, epochs), F32)], every)
             (slip,) = local_call(
                 last_update, [field_shape], exchanged(out, "z"), kept, field, way, slip
             )
             return slip
-        (out,) = local_call(collect, [((share + TILE, epochs), F32)], pieces, sums)
+        out, fresh = local_call(
+            collect, [((share + TILE, epochs), F32), field_shape], part, *penalty,
+            scalars=[core_scalar], scratch=[near],
+        )
         every = lax.all_gather(out, PATCH)
         moved, image, tail, smooth, way, scalars = local_call(
             backward,
@@ -346,6 +363,7 @@
 def solution(mesh):
     split = Mesh(mesh.devices.reshape(4, 4, 16, 2), (*OBS, *PATCH))
     in_specs = (P(OBS, PATCH), P(OBS, None), P(None, PATCH), P())
+
     return jax.shard_map(
         shards, mesh=split, in_specs=in_specs, out_specs=P(PATCH, None), check_vma=False
     )

time: 325 us -> 308 us (0.948)
  blocking collectives: 252 us -> 191 us
  waiting for transfers between devices: 11.6 us -> 36.5 us
  starting transfers between devices: 34.1 us -> 48.6 us
  local copies, waits for them, and re-layouts: 4.3 us -> 10.2 us
    all_to_all x11 -> x8, blocking collectives: 175 us -> 104 us  [exchanged(): return lax.all_to_all(pieces, axis, 0, 0, tiled=True)]
    all_to_all x0 -> x3, starting transfers between devices: none -> 23.6 us  [exchanged(): return lax.all_to_all(pieces, axis, 0, 0, tiled=True)]
    all_to_all x0 -> x3, waiting for transfers between devices: none -> 23.3 us  [exchanged(): return lax.all_to_all(pieces, axis, 0, 0, tiled=True)]
    all_gather x0 -> x3, blocking collectives: none -> 13.6 us  [shards(): pair = lax.all_gather(field, 'c')]
    ppermute x3 -> x0, starting transfers between devices: 11 us -> none  [shards(): other = lax.ppermute(field, 'c', swap)]
    ppermute x2, waiting for transfers between devices: 2.9 us -> 9.87 us  [to_neighbours(): return (lax.ppermute(last, axis, up), lax.ppermute(first, axis, down))]
    unnamed x12 -> x98, local copies, waits for them, and re-layouts: 4.23 us -> 10.2 us
    ppermute x3, waiting for transfers between devices: 8.72 us -> 3.34 us  [shards(): edge = lax.ppermute(edge, PATCH, outward)]
  transfers between devices with their start and end apart: 9 -> 9, of which waited for: 3 -> 6; matrix products, arithmetic and copies ran while one was open for 0% -> 0% of each run, Pallas kernels for 1% -> 2%
where the time goes in v5:
time: 308 us; the launch traced here: 307 us
  blocking collectives  191 us (62%)
  starting transfers between devices  48.6 us (16%)
  waiting for transfers between devices  36.5 us (12%)
  Pallas kernels  20 us (6%)
  local copies, waits for them, and re-layouts  10.2 us (3%)
    all_to_all x8, blocking collectives, exchanged(): return lax.all_to_all(pieces, axis, 0, 0, tiled=True)  104 us
    all_gather x2, blocking collectives, shards(): every = lax.all_gather(out, PATCH)  73.6 us
    all_to_all x3, starting transfers between devices, exchanged(): return lax.all_to_all(pieces, axis, 0, 0, tiled=True)  23.6 us
    all_to_all x3, waiting for transfers between devices, exchanged(): return lax.all_to_all(pieces, axis, 0, 0, tiled=True)  23.3 us
    pallas_call x22, Pallas kernels, local_call(): pl.pallas_call(functools.partial(body, **options), out_shape=[jax.ShapeDt...  20 us
    all_gather x3, blocking collectives, shards(): pair = lax.all_gather(field, 'c')  13.6 us
    ppermute x3, starting transfers between devices, shards(): edge = lax.ppermute(edge, PATCH, outward)  11.8 us
    unnamed x98, local copies, waits for them, and re-layouts  10.2 us
  transfers between devices with their start and end apart: 9, of which 6 were waited for; matrix products, arithmetic and copies ran while one was open for 0% of the time, Pallas kernels for 2%

profile of v5, /device:TPU:1, one launch (start us, length us, event | category | flops | bytes accessed | tf_op | source)
XLA Modules:
  0.0 307.1 jit_solution(10491208750475487181)
XLA Ops:
  0.0 1.9 copy-done.24
  1.9 1.1 copy-done.42
  3.0 1.8 shard_map.46
  4.8 1.2 copy-done.15
  6.0 8.9 %collective-permute-start = (f32[640,640]{1,0:T(8,128)S(1)}, f32[640,640]{1,0:T(8,128)S(1)}, u32[]{:S(2)}, u32[]{:S(2)}) collective-permute-start(f32[640,640]{1,0:T(8,128)S(1)} %get-tuple-element.47), channel_id=1, source_target_pairs={{0,1},{1,0},{2,3},{3,2},{4,5},{5,4},{6,7},{7,6},{8,9},{9,8},{10,11... | collective-permute-start | bytes 4915208 | tf_op jit(solution)/shard_map/ppermute | solution.py:291
  14.9 11.1 %all_to_all.55.pieces = f32[16,40,128]{2,1,0:T(8,128)S(1)} all-to-all(f32[16,40,128]{2,1,0:T(8,128)S(1)} %bitcast.24), channel_id=1, replica_groups=mesh['x'=4,'y'=4,'z'=16,'c'=2] {'x','y'}, dimensions={0} | all-to-all | bytes 655360 | tf_op jit(solution)/shard_map/all_to_all | solution.py:257
  26.1 11.9 %all_to_all.56.every = f32[16,48,128]{2,1,0:T(8,128)S(1)} all-to-all(f32[16,48,128]{2,1,0:T(8,128)S(1)} %shard_map.47), channel_id=1, replica_groups=mesh['x'=4,'y'=4,'z'=16,'c'=2] {'x','y'}, dimensions={0} | all-to-all | bytes 786432 | tf_op jit(solution)/shard_map/all_to_all | solution.py:257
  38.7 4.5 %all-gather = f32[1280,128]{1,0:T(8,128)S(1)} all-gather(f32[640,128]{1,0:T(8,128)S(1)} %get-tuple-element.44.field.old_field), channel_id=2, replica_groups=mesh['x'=4,'y'=4,'z'=16,'c'=2] {'c'}, dimensions={0}, use_global_device_ids=true | all-gather | bytes 983040 | tf_op jit(solution)/shard_map/all_gather | solution.py:322
  43.5 2.0 shard_map.50
  45.5 13.4 %all-to-all-start.2 = ((f32[16,40,128]{2,1,0:T(8,128)}), f32[16,40,128]{2,1,0:T(8,128)}, u32[]{:S(2)}, u32[]{:S(2)}) async-start(f32[16,40,128]{2,1,0:T(8,128)} %bitcast.4), calls=%async_computation.2 | async-start | bytes 655360 | tf_op jit(solution)/shard_map/all_to_all | solution.py:257
  58.9 4.0 %collective-permute-start.1 = (f32[256,128]{1,0:T(8,128)}, f32[256,128]{1,0:T(8,128)S(1)}, u32[]{:S(2)}, u32[]{:S(2)}) collective-permute-start(f32[256,128]{1,0:T(8,128)} %get-tuple-element.50), channel_id=1, source_target_pairs={{1,2},{3,4},{5,6},{7,8},{9,10},{11,12},{13,14},{15,16},{17,18},{19... | collective-permute-start | bytes 393224 | tf_op jit(solution)/shard_map/ppermute | solution.py:321
  63.0 1.9 collective-permute-start.2
  64.9 2.4 collective-permute-start.3
  67.3 5.5 %collective-permute-done.2.before = s32[3,128]{1,0:T(4,128)S(1)} collective-permute-done((s32[3,128]{1,0:T(4,128)S(1)}, s32[3,128]{1,0:T(4,128)S(1)}, u32[]{:S(2)}, u32[]{:S(2)}) %collective-permute-start.2) | collective-permute-done | bytes 1568 | tf_op jit(solution)/shard_map/ppermute | solution.py:253
  72.8 4.4 %collective-permute-done.3.after = s32[3,128]{1,0:T(4,128)S(1)} collective-permute-done((s32[3,128]{1,0:T(4,128)S(1)}, s32[3,128]{1,0:T(4,128)S(1)}, u32[]{:S(2)}, u32[]{:S(2)}) %collective-permute-start.3) | collective-permute-done | bytes 1568 | tf_op jit(solution)/shard_map/ppermute | solution.py:253
  77.2 1.8 shard_map.52
  79.0 1.0 shard_map.51.part
  80.0 1.1 copy-done.21
  81.1 1.2 shard_map.53
  82.3 35.2 %all-gather.1 = f32[1536,128]{1,0:T(8,128)S(1)} all-gather(f32[48,128]{1,0:T(8,128)S(1)} %get-tuple-element.55), channel_id=3, replica_groups=mesh['x'=4,'y'=4,'z'=16,'c'=2] {'z','c'}, dimensions={0}, use_global_device_ids=true | all-gather | bytes 811008 | tf_op jit(solution)/shard_map/all_gather | solution.py:347
  117.6 1.2 shard_map.54
  118.9 11.4 %all_to_all.57.pieces = f32[16,40,128]{2,1,0:T(8,128)S(1)} all-to-all(f32[16,40,128]{2,1,0:T(8,128)S(1)} %bitcast.25), channel_id=1, replica_groups=mesh['x'=4,'y'=4,'z'=16,'c'=2] {'x','y'}, dimensions={0} | all-to-all | bytes 655360 | tf_op jit(solution)/shard_map/all_to_all | solution.py:257
  130.3 12.3 %all_to_all.58.every = f32[16,48,128]{2,1,0:T(8,128)S(1)} all-to-all(f32[16,48,128]{2,1,0:T(8,128)S(1)} %shard_map.55), channel_id=1, replica_groups=mesh['x'=4,'y'=4,'z'=16,'c'=2] {'x','y'}, dimensions={0} | all-to-all | bytes 786432 | tf_op jit(solution)/shard_map/all_to_all | solution.py:257
  142.8 4.5 %all-gather.2 = f32[1280,128]{1,0:T(8,128)S(1)} all-gather(f32[640,128]{1,0:T(8,128)S(1)} %get-tuple-element.64.field.old_field), channel_id=4, replica_groups=mesh['x'=4,'y'=4,'z'=16,'c'=2] {'c'}, dimensions={0}, use_global_device_ids=true | all-gather | bytes 983040 | tf_op jit(solution)/shard_map/all_gather | solution.py:322
  147.3 1.3 shard_map.57
  149.4 6.0 %all-to-all-start.5 = ((f32[16,40,128]{2,1,0:T(8,128)}), f32[16,40,128]{2,1,0:T(8,128)}, u32[]{:S(2)}, u32[]{:S(2)}) async-start(f32[16,40,128]{2,1,0:T(8,128)} %bitcast.22), calls=%async_computation.5 | async-start | bytes 655360 | tf_op jit(solution)/shard_map/all_to_all | solution.py:257
  155.4 4.0 %collective-permute-start.4 = (f32[256,128]{1,0:T(8,128)S(1)}, f32[256,128]{1,0:T(8,128)S(1)}, u32[]{:S(2)}, u32[]{:S(2)}) collective-permute-start(f32[256,128]{1,0:T(8,128)S(1)} %get-tuple-element.65), channel_id=1, source_target_pairs={{1,2},{3,4},{5,6},{7,8},{9,10},{11,12},{13,14},{15,16},{17,18},{19... | collective-permute-start | bytes 393224 | tf_op jit(solution)/shard_map/ppermute | solution.py:321
  159.4 11.5 %all-to-all-done.5.pieces = f32[16,40,128]{2,1,0:T(8,128)} async-done(((f32[16,40,128]{2,1,0:T(8,128)}), f32[16,40,128]{2,1,0:T(8,128)}, u32[]{:S(2)}, u32[]{:S(2)}) %all-to-all-start.5) | async-done | bytes 327712 | tf_op jit(solution)/shard_map/all_to_all | solution.py:257
  170.9 1.0 shard_map.58.part
  171.9 1.7 collective-permute-done.4.edge
  173.6 1.1 copy-done.23
  174.7 1.2 shard_map.59
  175.9 38.4 %all-gather.3 = f32[1536,128]{1,0:T(8,128)S(1)} all-gather(f32[48,128]{1,0:T(8,128)S(1)} %get-tuple-element.66), channel_id=5, replica_groups=mesh['x'=4,'y'=4,'z'=16,'c'=2] {'z','c'}, dimensions={0}, use_global_device_ids=true | all-gather | bytes 811008 | tf_op jit(solution)/shard_map/all_gather | solution.py:347
  214.3 1.2 shard_map.60
  215.6 11.5 %all_to_all.59.pieces = f32[16,40,128]{2,1,0:T(8,128)S(1)} all-to-all(f32[16,40,128]{2,1,0:T(8,128)S(1)} %bitcast.23), channel_id=1, replica_groups=mesh['x'=4,'y'=4,'z'=16,'c'=2] {'x','y'}, dimensions={0} | all-to-all | bytes 655360 | tf_op jit(solution)/shard_map/all_to_all | solution.py:257
  227.2 12.3 %all_to_all.60.every = f32[16,48,128]{2,1,0:T(8,128)S(1)} all-to-all(f32[16,48,128]{2,1,0:T(8,128)S(1)} %shard_map.61), channel_id=1, replica_groups=mesh['x'=4,'y'=4,'z'=16,'c'=2] {'x','y'}, dimensions={0} | all-to-all | bytes 786432 | tf_op jit(solution)/shard_map/all_to_all | solution.py:257
  240.3 4.5 %all-gather.4 = f32[1280,128]{1,0:T(8,128)S(1)} all-gather(f32[640,128]{1,0:T(8,128)S(1)} %get-tuple-element.76.field), channel_id=6, replica_groups=mesh['x'=4,'y'=4,'z'=16,'c'=2] {'c'}, dimensions={0}, use_global_device_ids=true | all-gather | bytes 983040 | tf_op jit(solution)/shard_map/all_gather | solution.py:322
  244.9 2.0 shard_map.63
  246.9 4.2 %all-to-all-start.8 = ((f32[16,40,128]{2,1,0:T(8,128)}), f32[16,40,128]{2,1,0:T(8,128)}, u32[]{:S(2)}, u32[]{:S(2)}) async-start(f32[16,40,128]{2,1,0:T(8,128)} %bitcast.13), calls=%async_computation.8 | async-start | bytes 655360 | tf_op jit(solution)/shard_map/all_to_all | solution.py:257
  251.1 3.7 %collective-permute-start.5 = (f32[256,128]{1,0:T(8,128)S(1)}, f32[256,128]{1,0:T(8,128)S(1)}, u32[]{:S(2)}, u32[]{:S(2)}) collective-permute-start(f32[256,128]{1,0:T(8,128)S(1)} %get-tuple-element.78), channel_id=1, source_target_pairs={{1,2},{3,4},{5,6},{7,8},{9,10},{11,12},{13,14},{15,16},{17,18},{19... | collective-permute-start | bytes 393224 | tf_op jit(solution)/shard_map/ppermute | solution.py:321
  254.9 11.8 %all-to-all-done.8.pieces = f32[16,40,128]{2,1,0:T(8,128)} async-done(((f32[16,40,128]{2,1,0:T(8,128)}), f32[16,40,128]{2,1,0:T(8,128)}, u32[]{:S(2)}, u32[]{:S(2)}) %all-to-all-start.8) | async-done | bytes 327712 | tf_op jit(solution)/shard_map/all_to_all | solution.py:257
  266.7 1.0 shard_map.64.share_ref
  267.7 1.6 collective-permute-done.5.edge
  269.3 1.1 copy-done.19
  270.4 1.1 copy-done.41
  271.5 1.2 shard_map.65
  272.7 18.5 %all_to_all.61.every = f32[32,8,128]{2,1,0:T(8,128)S(1)} all-to-all(f32[32,8,128]{2,1,0:T(8,128)S(1)} %shard_map.65), channel_id=1, replica_groups=mesh['x'=4,'y'=4,'z'=16,'c'=2] {'x','y','c'}, dimensions={0} | all-to-all | bytes 262144 | tf_op jit(solution)/shard_map/all_to_all | solution.py:257
  291.3 15.0 %all_to_all.62.every = f32[16,8,128]{2,1,0:T(8,128)S(1)} all-to-all(f32[16,8,128]{2,1,0:T(8,128)S(1)} %shard_map.66), channel_id=1, replica_groups=mesh['x'=4,'y'=4,'z'=16,'c'=2] {'z'}, dimensions={0} | all-to-all | bytes 131072 | tf_op jit(solution)/shard_map/all_to_all | solution.py:257
  (106 shorter events, 3.8 us)
Async XLA Ops:
  6.0 37.2 %copy-start.12 = (bf16[640,1280]{1,0:T(8,128)(2,1)}, bf16[640,1280]{1,0:T(8,128)(2,1)S(1)}, u32[]{:S(2)}) copy-start(bf16[640,1280]{1,0:T(8,128)(2,1)S(1)} %get-tuple-element.57.high) | copy-start | bytes 4915204
  6.0 37.5 %copy-start = (bf16[640,640]{1,0:T(8,128)(2,1)}, bf16[640,640]{1,0:T(8,128)(2,1)S(1)}, u32[]{:S(2)}) copy-start(bf16[640,640]{1,0:T(8,128)(2,1)S(1)} %get-tuple-element.45.own_high) | copy-start | bytes 2457604
  6.0 37.5 %copy-start.3 = (bf16[640,640]{1,0:T(8,128)(2,1)}, bf16[640,640]{1,0:T(8,128)(2,1)S(1)}, u32[]{:S(2)}) copy-start(bf16[640,640]{1,0:T(8,128)(2,1)S(1)} %get-tuple-element.46.own_low) | copy-start | bytes 2457604
  6.0 32.0 %copy-start.47 = (s32[3,640]{1,0:T(4,128)S(1)}, s32[3,640]{1,0:T(4,128)}, u32[]{:S(2)}) copy-start(s32[3,640]{1,0:T(4,128)} %ids.3) | copy-start | bytes 23044
  6.0 37.2 %collective-permute-start = (f32[640,640]{1,0:T(8,128)S(1)}, f32[640,640]{1,0:T(8,128)S(1)}, u32[]{:S(2)}, u32[]{:S(2)}) collective-permute-start(f32[640,640]{1,0:T(8,128)S(1)} %get-tuple-element.47), channel_id=1, source_target_pairs={{0,1},{1,0},{2,3},{3,2},{4,5},{5,4},{6,7},{7,6},{8,9},{9,8},{10,11... | collective-permute-start | bytes 4915208 | tf_op jit(solution)/shard_map/ppermute | solution.py:291
  43.2 2.3 copy-start.20
  43.5 2.1 copy-start.6
  43.5 2.0 copy-start.9
  43.5 36.5 %copy-start.48 = (f32[128]{0:T(128)S(1)}, f32[128]{0:T(128)}, u32[]{:S(2)}) copy-start(f32[128]{0:T(128)} %param.7) | copy-start | bytes 1540
  45.5 33.4 %all-to-all-start.2 = ((f32[16,40,128]{2,1,0:T(8,128)}), f32[16,40,128]{2,1,0:T(8,128)}, u32[]{:S(2)}, u32[]{:S(2)}) async-start(f32[16,40,128]{2,1,0:T(8,128)} %bitcast.4), calls=%async_computation.2 | async-start | bytes 655360 | tf_op jit(solution)/shard_map/all_to_all | solution.py:257
  58.9 21.0 %collective-permute-start.1 = (f32[256,128]{1,0:T(8,128)}, f32[256,128]{1,0:T(8,128)S(1)}, u32[]{:S(2)}, u32[]{:S(2)}) collective-permute-start(f32[256,128]{1,0:T(8,128)} %get-tuple-element.50), channel_id=1, source_target_pairs={{1,2},{3,4},{5,6},{7,8},{9,10},{11,12},{13,14},{15,16},{17,18},{19... | collective-permute-start | bytes 393224 | tf_op jit(solution)/shard_map/ppermute | solution.py:321
  63.0 9.9 %collective-permute-start.2 = (s32[3,128]{1,0:T(4,128)S(1)}, s32[3,128]{1,0:T(4,128)S(1)}, u32[]{:S(2)}, u32[]{:S(2)}) collective-permute-start(s32[3,128]{1,0:T(4,128)S(1)} %get-tuple-element.51), channel_id=1, source_target_pairs={{0,1},{1,2},{2,3},{3,4},{4,5},{5,6},{6,7},{7,8},{8,9},{9,10},{10,1... | collective-permute-start | bytes 4616 | tf_op jit(solution)/shard_map/ppermute | solution.py:253
  64.9 12.3 %collective-permute-start.3 = (s32[3,128]{1,0:T(4,128)S(1)}, s32[3,128]{1,0:T(4,128)S(1)}, u32[]{:S(2)}, u32[]{:S(2)}) collective-permute-start(s32[3,128]{1,0:T(4,128)S(1)} %get-tuple-element.52), channel_id=1, source_target_pairs={{1,0},{2,1},{3,2},{4,3},{5,4},{6,5},{7,6},{8,7},{9,8},{10,9},{11,1... | collective-permute-start | bytes 4616 | tf_op jit(solution)/shard_map/ppermute | solution.py:253
  81.1 36.5 %copy-start.13 = (bf16[640,1280]{1,0:T(8,128)(2,1)S(1)}, bf16[640,1280]{1,0:T(8,128)(2,1)}, u32[]{:S(2)}) copy-start(bf16[640,1280]{1,0:T(8,128)(2,1)} %copy-done.12) | copy-start | bytes 4915204
  81.1 36.5 %copy-start.16 = (bf16[640,1280]{1,0:T(8,128)(2,1)S(1)}, bf16[640,1280]{1,0:T(8,128)(2,1)}, u32[]{:S(2)}) copy-start(bf16[640,1280]{1,0:T(8,128)(2,1)} %copy-done.15) | copy-start | bytes 4915204
  118.8 23.8 %copy-start.38 = (f32[1280,128]{1,0:T(8,128)}, f32[1280,128]{1,0:T(8,128)S(1)}, u32[]{:S(2)}) copy-start(f32[1280,128]{1,0:T(8,128)S(1)} %get-tuple-element.68.old_image) | copy-start | bytes 1966084
  118.8 23.9 %copy-start.27 = (f32[640,128]{1,0:T(8,128)}, f32[640,128]{1,0:T(8,128)S(1)}, u32[]{:S(2)}) copy-start(f32[640,128]{1,0:T(8,128)S(1)} %get-tuple-element.62.smooth.old_smooth) | copy-start | bytes 983044
  118.9 23.9 %copy-start.30 = (f32[640,128]{1,0:T(8,128)}, f32[640,128]{1,0:T(8,128)S(1)}, u32[]{:S(2)}) copy-start(f32[640,128]{1,0:T(8,128)S(1)} %get-tuple-element.63.way.old_way) | copy-start | bytes 983044
  130.3 17.0 %copy-start.1 = (bf16[640,640]{1,0:T(8,128)(2,1)S(1)}, bf16[640,640]{1,0:T(8,128)(2,1)}, u32[]{:S(2)}) copy-start(bf16[640,640]{1,0:T(8,128)(2,1)} %copy-done) | copy-start | bytes 2457604
  130.3 17.0 %copy-start.4 = (bf16[640,640]{1,0:T(8,128)(2,1)S(1)}, bf16[640,640]{1,0:T(8,128)(2,1)}, u32[]{:S(2)}) copy-start(bf16[640,640]{1,0:T(8,128)(2,1)} %copy-done.3) | copy-start | bytes 2457604
  130.3 17.0 %copy-start.7 = (bf16[640,640]{1,0:T(8,128)(2,1)S(1)}, bf16[640,640]{1,0:T(8,128)(2,1)}, u32[]{:S(2)}) copy-start(bf16[640,640]{1,0:T(8,128)(2,1)} %copy-done.6) | copy-start | bytes 2457604
  130.3 17.0 %copy-start.10 = (bf16[640,640]{1,0:T(8,128)(2,1)S(1)}, bf16[640,640]{1,0:T(8,128)(2,1)}, u32[]{:S(2)}) copy-start(bf16[640,640]{1,0:T(8,128)(2,1)} %copy-done.9) | copy-start | bytes 2457604
  142.7 5.9 %copy-start.25 = (f32[640,128]{1,0:T(8,128)}, f32[640,128]{1,0:T(8,128)S(1)}, u32[]{:S(2)}) copy-start(f32[640,128]{1,0:T(8,128)S(1)} %get-tuple-element.64.field.old_field) | copy-start | bytes 983044
  142.7 5.9 %copy-start.43 = (f32[640,128]{1,0:T(8,128)}, f32[640,128]{1,0:T(8,128)S(1)}, u32[]{:S(2)}) copy-start(f32[640,128]{1,0:T(8,128)S(1)} %get-tuple-element.75.old_slip) | copy-start | bytes 983044
  147.3 26.3 %copy-start.28 = (f32[640,128]{1,0:T(8,128)S(1)}, f32[640,128]{1,0:T(8,128)}, u32[]{:S(2)}) copy-start(f32[640,128]{1,0:T(8,128)} %copy-done.27) | copy-start | bytes 983044
  149.4 21.5 %all-to-all-start.5 = ((f32[16,40,128]{2,1,0:T(8,128)}), f32[16,40,128]{2,1,0:T(8,128)}, u32[]{:S(2)}, u32[]{:S(2)}) async-start(f32[16,40,128]{2,1,0:T(8,128)} %bitcast.22), calls=%async_computation.5 | async-start | bytes 655360 | tf_op jit(solution)/shard_map/all_to_all | solution.py:257
  155.4 18.2 %collective-permute-start.4 = (f32[256,128]{1,0:T(8,128)S(1)}, f32[256,128]{1,0:T(8,128)S(1)}, u32[]{:S(2)}, u32[]{:S(2)}) collective-permute-start(f32[256,128]{1,0:T(8,128)S(1)} %get-tuple-element.65), channel_id=1, source_target_pairs={{1,2},{3,4},{5,6},{7,8},{9,10},{11,12},{13,14},{15,16},{17,18},{19... | collective-permute-start | bytes 393224 | tf_op jit(solution)/shard_map/ppermute | solution.py:321
  171.9 42.4 %copy-start.14 = (bf16[640,1280]{1,0:T(8,128)(2,1)S(1)}, bf16[640,1280]{1,0:T(8,128)(2,1)}, u32[]{:S(2)}) copy-start(bf16[640,1280]{1,0:T(8,128)(2,1)} %copy-done.12) | copy-start | bytes 4915204
  171.9 42.4 %copy-start.17 = (bf16[640,1280]{1,0:T(8,128)(2,1)S(1)}, bf16[640,1280]{1,0:T(8,128)(2,1)}, u32[]{:S(2)}) copy-start(bf16[640,1280]{1,0:T(8,128)(2,1)} %copy-done.15) | copy-start | bytes 4915204
  174.7 39.6 %copy-start.26 = (f32[640,128]{1,0:T(8,128)S(1)}, f32[640,128]{1,0:T(8,128)}, u32[]{:S(2)}) copy-start(f32[640,128]{1,0:T(8,128)} %copy-done.25) | copy-start | bytes 983044
  174.7 39.6 %copy-start.31 = (f32[640,128]{1,0:T(8,128)S(1)}, f32[640,128]{1,0:T(8,128)}, u32[]{:S(2)}) copy-start(f32[640,128]{1,0:T(8,128)} %copy-done.30) | copy-start | bytes 983044
  174.7 39.6 %copy-start.39 = (f32[1280,128]{1,0:T(8,128)S(1)}, f32[1280,128]{1,0:T(8,128)}, u32[]{:S(2)}) copy-start(f32[1280,128]{1,0:T(8,128)} %copy-done.38) | copy-start | bytes 1966084
  215.5 24.0 %copy-start.32 = (f32[640,128]{1,0:T(8,128)}, f32[640,128]{1,0:T(8,128)S(1)}, u32[]{:S(2)}) copy-start(f32[640,128]{1,0:T(8,128)S(1)} %get-tuple-element.73.smooth) | copy-start | bytes 983044
  215.5 24.0 %copy-start.34 = (f32[640,128]{1,0:T(8,128)}, f32[640,128]{1,0:T(8,128)S(1)}, u32[]{:S(2)}) copy-start(f32[640,128]{1,0:T(8,128)S(1)} %get-tuple-element.74.way) | copy-start | bytes 983044
  215.6 24.0 %copy-start.40 = (f32[1280,128]{1,0:T(8,128)}, f32[1280,128]{1,0:T(8,128)S(1)}, u32[]{:S(2)}) copy-start(f32[1280,128]{1,0:T(8,128)S(1)} %get-tuple-element.77.image) | copy-start | bytes 1966084
  215.6 23.9 %copy-start.44 = (f32[640,128]{1,0:T(8,128)S(1)}, f32[640,128]{1,0:T(8,128)}, u32[]{:S(2)}) copy-start(f32[640,128]{1,0:T(8,128)} %copy-done.43) | copy-start | bytes 983044
  227.1 17.7 %copy-start.2 = (bf16[640,640]{1,0:T(8,128)(2,1)S(1)}, bf16[640,640]{1,0:T(8,128)(2,1)}, u32[]{:S(2)}) copy-start(bf16[640,640]{1,0:T(8,128)(2,1)} %copy-done) | copy-start | bytes 2457604
  227.1 17.7 %copy-start.5 = (bf16[640,640]{1,0:T(8,128)(2,1)S(1)}, bf16[640,640]{1,0:T(8,128)(2,1)}, u32[]{:S(2)}) copy-start(bf16[640,640]{1,0:T(8,128)(2,1)} %copy-done.3) | copy-start | bytes 2457604
  227.2 17.7 %copy-start.8 = (bf16[640,640]{1,0:T(8,128)(2,1)S(1)}, bf16[640,640]{1,0:T(8,128)(2,1)}, u32[]{:S(2)}) copy-start(bf16[640,640]{1,0:T(8,128)(2,1)} %copy-done.6) | copy-start | bytes 2457604
  227.2 17.7 %copy-start.11 = (bf16[640,640]{1,0:T(8,128)(2,1)S(1)}, bf16[640,640]{1,0:T(8,128)(2,1)}, u32[]{:S(2)}) copy-start(bf16[640,640]{1,0:T(8,128)(2,1)} %copy-done.9) | copy-start | bytes 2457604
  240.3 6.6 %copy-start.36 = (f32[640,128]{1,0:T(8,128)}, f32[640,128]{1,0:T(8,128)S(1)}, u32[]{:S(2)}) copy-start(f32[640,128]{1,0:T(8,128)S(1)} %get-tuple-element.76.field) | copy-start | bytes 983044
  244.9 2.0 copy-start.18
  244.9 24.4 %copy-start.33 = (f32[640,128]{1,0:T(8,128)S(1)}, f32[640,128]{1,0:T(8,128)}, u32[]{:S(2)}) copy-start(f32[640,128]{1,0:T(8,128)} %copy-done.32) | copy-start | bytes 983044
  246.9 19.8 %all-to-all-start.8 = ((f32[16,40,128]{2,1,0:T(8,128)}), f32[16,40,128]{2,1,0:T(8,128)}, u32[]{:S(2)}, u32[]{:S(2)}) async-start(f32[16,40,128]{2,1,0:T(8,128)} %bitcast.13), calls=%async_computation.8 | async-start | bytes 655360 | tf_op jit(solution)/shard_map/all_to_all | solution.py:257
  251.1 18.2 %collective-permute-start.5 = (f32[256,128]{1,0:T(8,128)S(1)}, f32[256,128]{1,0:T(8,128)S(1)}, u32[]{:S(2)}, u32[]{:S(2)}) collective-permute-start(f32[256,128]{1,0:T(8,128)S(1)} %get-tuple-element.78), channel_id=1, source_target_pairs={{1,2},{3,4},{5,6},{7,8},{9,10},{11,12},{13,14},{15,16},{17,18},{19... | collective-permute-start | bytes 393224 | tf_op jit(solution)/shard_map/ppermute | solution.py:321
  271.5 34.7 %copy-start.35 = (f32[640,128]{1,0:T(8,128)S(1)}, f32[640,128]{1,0:T(8,128)}, u32[]{:S(2)}) copy-start(f32[640,128]{1,0:T(8,128)} %copy-done.34) | copy-start | bytes 983044
  271.5 34.7 %copy-start.37 = (f32[640,128]{1,0:T(8,128)S(1)}, f32[640,128]{1,0:T(8,128)}, u32[]{:S(2)}) copy-start(f32[640,128]{1,0:T(8,128)} %copy-done.36) | copy-start | bytes 983044
  271.5 34.7 %copy-start.46 = (f32[640,128]{1,0:T(8,128)S(1)}, f32[640,128]{1,0:T(8,128)}, u32[]{:S(2)}) copy-start(f32[640,128]{1,0:T(8,128)} %copy-done.45) | copy-start | bytes 983044
  (10 other events, 11.4 us)

commit v6 on v5

--- a/solution.py
+++ b/solution.py
@@ -64,18 +64,19 @@
     return value
 
 
-def first_back(core, place, green, data, moved, back_high, back_low, high, low, send, wide, *, share):
+def first_back(core, place, row, green, data, moved, back_high, back_low, high, low, send, wide, *, share):
     for k in range(green.shape[0] // 128):
         at = slice(128 * k, 128 * (k + 1))
         back_high[:, at], back_low[:, at] = halves(green[at, :].T)
     store_halves(wide, 0, data[...])
     moved[...] = product(back_high, back_low, wide[...])
-    for z in range(0, send.shape[0] // share, 2):
+    half = send.shape[0]
+    for z in range(0, half // share, 2):
         mine = []
         for k in (z, z + 1):
-            start = pl.multiple_of((2 * k + core[0]) * share, TILE)
+            start = pl.multiple_of(core[0] * half + k * share, TILE)
             mine.append(green[pl.ds(start, share), :])
-            start = pl.multiple_of((2 * k + 1 - core[0]) * share, TILE)
+            start = pl.multiple_of((1 - core[0]) * half + k * share, TILE)
             send[share * k : share * (k + 1), :] = green[pl.ds(start, share), :]
         rows = slice(share * z, share * (z + 2))
         high[rows, :], low[rows, :] = halves(jnp.concatenate(mine, 0))
@@ -85,12 +86,18 @@
     high[...], low[...] = halves(other[...])
 
 
-def laplace_square(block, before, ids, after, high, low, rows, own, ids_col, *, n_patch):
+def laplace_square(core, block, pair, edge, ids, high, low, rows, own, ids_col, *, n_patch):
     col_count = ids.shape[1]
     height = rows.shape[0]
     total_cols = n_patch * col_count
     start = block[0] * col_count
-    relative = jnp.concatenate([before[...], ids[...], after[...]], 1) - (start - 2 * BAND)
+    own_rows, edge_rows = pair.shape[1] - TILE, edge.shape[0] - TILE
+    other = pair[1 - core[0]][own_rows:]
+    outer = edge[edge_rows : edge_rows + 3, :]
+    is_first = core[0] == 0
+    before = jnp.where(is_first, outer, other[3:6]).astype(jnp.int32)
+    after = jnp.where(is_first, other[0:3], outer).astype(jnp.int32)
+    relative = jnp.concatenate([before, ids[...], after], 1) - (start - 2 * BAND)
     pad = jnp.zeros((TILE - 3, height), jnp.int32)
     ids_col[...] = jnp.concatenate([relative, pad], 0).T
     here = lax.broadcasted_iota(jnp.int32, (1, height), 1) + (start - BAND)
@@ -122,17 +129,18 @@
 
 
 def forward(core, pair, own_high, own_low, far_high, far_low, part, wide):
-    rows = pair.shape[1]
-    store_halves(wide, 0, pair[core[0]])
-    store_halves(wide, rows, pair[1 - core[0]])
+    rows = wide.shape[0] // 2
+    store_halves(wide, 0, pair[core[0]][:rows])
+    store_halves(wide, rows, pair[1 - core[0]][:rows])
     part[...] = product(own_high, own_low, wide[:rows, :]) + product(far_high, far_low, wide[rows:, :])
 
 
 def regularized(core, pair, edge, weight, m_high, m_low, near):
-    rows, reach = pair.shape[1], 2 * BAND
-    own, other = pair[core[0]], pair[1 - core[0]]
+    reach = 2 * BAND
+    rows = near.shape[0] - 2 * reach
+    own, other = pair[core[0]][:rows], pair[1 - core[0]][:rows]
     is_first = core[0] == 0
-    outer = edge[...]
+    outer = edge[:reach, :]
     store_halves(near, 0, jnp.where(is_first, outer, other[rows - reach :]))
     store_halves(near, reach, own)
     store_halves(near, reach + rows, jnp.where(is_first, other[:reach], outer))
@@ -174,7 +182,7 @@
     moved[...] = product(high, low, wide[...])
     put_rows(tail, [total(square)])
     smooth[...] = fresh[...] + ratio * old_smooth[...]
-    way[...] = field[...] + ratio * old_way[...]
+    way[...] = field[: way.shape[0], :] + ratio * old_way[...]
     reg_sq = sums[1:2] + ratio * (2.0 * sums[2:3] + ratio * old_scalars[1:2, :])
     put_rows(scalars, [norm, reg_sq, jnp.ones_like(norm)])
 
@@ -187,18 +195,21 @@
         out[k, share:, :] = last
 
 
-def put_edge(core, field, edge):
-    reach = edge.shape[0]
-    edge[...] = jnp.where(core[0] == 0, field[:reach, :], field[field.shape[0] - reach :, :])
-
-
-def start_field(core, every, ids, field, edge, last_ids, first_ids):
-    last_ids[...] = ids[:, ids.shape[1] - BAND :]
-    first_ids[...] = ids[:, :BAND]
+def put_edge(core, rows, field, edge):
+    reach = 2 * BAND
+    edge[:reach, :] = jnp.where(core[0] == 0, field[:reach, :], field[rows - reach : rows, :])
+
+
+def start_field(core, every, ids, field, edge):
     share = every.shape[1] - TILE
+    rows, reach = field.shape[0] - TILE, edge.shape[0] - TILE
     for k in range(every.shape[0]):
         field[share * k : share * (k + 1), :] = every[k, :share, :]
-    put_edge(core, field, edge)
+    put_edge(core, rows, field, edge)
+    first, last = ids[:, :BAND].astype(F32), ids[:, ids.shape[1] - BAND :].astype(F32)
+    field[rows:, :] = jnp.concatenate([first, last, jnp.zeros((TILE - 6, BAND), F32)], 0)
+    sent = jnp.where(core[0] == 0, first, last)
+    edge[reach:, :] = jnp.concatenate([sent, jnp.zeros((TILE - 3, BAND), F32)], 0)
 
 
 def update(core, every, scalars, smooth, way, old_field, old_slip, field, edge, slip, kept):
@@ -211,7 +222,7 @@
     for k in range(count):
         rows = slice(share * k, share * (k + 1))
         field[rows, :] = old_field[rows, :] - step * (every[k, :share, :] + smooth[rows, :])
-    put_edge(core, field, edge)
+    put_edge(core, field.shape[0], field, edge)
     slip[...] = old_slip[...] + step * way[...]
     put_rows(kept, [scalars[0:1, :], scalars[1:2, :], scalars[2:3, :], image_sq])
 
@@ -244,13 +255,6 @@
     image_sq = sums[3:4] + ratio * (2.0 * sums[4:5] + ratio * image_sq)
     step = norm / (image_sq + reg_sq)
     slip[...] = old_slip[...] + step * (field[...] + ratio * way[...])
-
-
-def to_neighbours(last, first, axis):
-    count = lax.axis_size(axis)
-    up = [(i, i + 1) for i in range(count - 1)]
-    down = [(i + 1, i) for i in range(count - 1)]
-    return lax.ppermute(last, axis, up), lax.ppermute(first, axis, down)
 
 
 def exchanged(pieces, axis):
@@ -269,6 +273,7 @@
     weight = reg_weight[None]
     share = row_count // n_patch
     core_scalar = core.astype(jnp.int32)[None]
+    row_scalar = (core * n_z + lax.axis_index("z")).astype(jnp.int32)[None]
     place_scalar = lax.axis_index(PATCH).astype(jnp.int32)[None]
     swap = [(0, 1), (1, 0)]
     outward = [(2 * z + 1, 2 * z + 2) for z in range(n_z - 1)]
@@ -282,11 +287,10 @@
 
     back_matrix = ((col_count, row_count), BF16)
     matrix = ((half, col_count), BF16)
-    ids_shape = ((3, BAND), jnp.int32)
     moved, b_high, b_low, own_high, own_low, send = local_call(
         first_back,
         [field_shape, back_matrix, back_matrix, matrix, matrix, ((half, col_count), F32)],
-        green, data, scalars=[core_scalar, place_scalar], scratch=[wide], share=share,
+        green, data, scalars=[core_scalar, place_scalar, row_scalar], scratch=[wide], share=share,
     )
     far = lax.ppermute(send, "c", swap)
     pieces = exchanged(moved.reshape(n_obs, piece, epochs), OBS)
@@ -296,22 +300,9 @@
     (out,) = local_call(spread, [spread_shape], pieces, zero_tail)
     every = exchanged(out, OBS)
     edge_shape = ((reach, epochs), F32)
-    field, edge, last_ids, first_ids = local_call(
-        start_field, [field_shape, edge_shape, ids_shape, ids_shape], every, neighbours,
-        scalars=[core_scalar],
-    )
-    before, after = to_neighbours(last_ids, first_ids, PATCH)
-    height, width = col_count + 2 * BAND, col_count + 4 * BAND
-    m_matrix = ((col_count, width), BF16)
-    m_high, m_low = local_call(
-        laplace_square, [m_matrix, m_matrix], before, neighbours, after,
-        scalars=[place_scalar],
-        n_patch=n_patch,
-        scratch=[
-            pltpu.VMEM((height, width), BF16),
-            pltpu.VMEM((128, 128 + 2 * BAND), BF16),
-            pltpu.VMEM((height, TILE), jnp.int32),
-        ],
+    long_field, long_edge = ((col_count + TILE, epochs), F32), ((reach + TILE, epochs), F32)
+    field, edge = local_call(
+        start_field, [long_field, long_edge], every, neighbours, scalars=[core_scalar]
     )
     far_high, far_low = local_call(split_other, [matrix, matrix], far)
 
@@ -327,12 +318,24 @@
         )
         pieces = exchanged(part.reshape(n_z, share, epochs), "z")
         (part,) = local_call(gathered, [((share, epochs), F32)], pieces)
+        if iteration == 0:
+            m_matrix = ((col_count, col_count + 2 * reach), BF16)
+            m_high, m_low = local_call(
+                laplace_square, [m_matrix, m_matrix], pair, edge, neighbours,
+                scalars=[core_scalar, place_scalar],
+                n_patch=n_patch,
+                scratch=[
+                    pltpu.VMEM((col_count + reach, col_count + 2 * reach), BF16),
+                    pltpu.VMEM((128, 128 + reach), BF16),
+                    pltpu.VMEM((col_count + reach, TILE), jnp.int32),
+                ],
+            )
         penalty = (pair, edge, weight, smooth, m_high, m_low)
         if iteration + 1 == ITERS:
             shape = ((n_obs * n_core, TILE, epochs), F32)
             (out,) = local_call(
                 last_sums, [shape], part, image, *penalty,
-                scalars=[core_scalar, place_scalar], scratch=[near],
+                scalars=[core_scalar, row_scalar], scratch=[near],
             )
             every = exchanged(out, (*OBS, "c"))
             (out,) = local_call(last_spread, [((n_z, TILE, epochs), F32)], every)
@@ -344,7 +347,8 @@
             collect, [((share + TILE, epochs), F32), field_shape], part, *penalty,
             scalars=[core_scalar], scratch=[near],
         )
-        every = lax.all_gather(out, PATCH)
+        every = lax.all_gather(lax.all_gather(out, "z"), "c")
+        every = every.reshape(n_patch, share + TILE, epochs)
         moved, image, tail, smooth, way, scalars = local_call(
             backward,
             [field_shape, image_shape, tail_shape, field_shape, field_shape, tail_shape],

time: 308 us -> 312 us (1.013)
  waiting for transfers between devices: 36.5 us -> 40.9 us
    ppermute x3, waiting for transfers between devices: 3.34 us -> 17.6 us  [shards(): edge = lax.ppermute(edge, PATCH, outward)]
    ppermute x2 -> x0, waiting for transfers between devices: 9.87 us -> none  [to_neighbours(): return (lax.ppermute(last, axis, up), lax.ppermute(first, axis, down))]
    ppermute x2 -> x0, starting transfers between devices: 4.32 us -> none  [to_neighbours(): return (lax.ppermute(last, axis, up), lax.ppermute(first, axis, down))]
    all_gather x2 -> x4, blocking collectives: 73.6 us -> 75.2 us  [shards(): every = lax.all_gather(lax.all_gather(out, 'z'), 'c')]
    unnamed x98 -> x104, local copies, waits for them, and re-layouts: 10.2 us -> 11.3 us
  transfers between devices with their start and end apart: 9 -> 7, of which waited for: 6 -> 5; matrix products, arithmetic and copies ran while one was open for 0% -> 0% of each run, Pallas kernels for 2% -> 1%
where the time goes in v6:
time: 312 us; the launch traced here: 310 us
  blocking collectives  193 us (62%)
  starting transfers between devices  45.6 us (15%)
  waiting for transfers between devices  40.9 us (13%)
  Pallas kernels  19.1 us (6%)
  local copies, waits for them, and re-layouts  11.3 us (4%)
    all_to_all x8, blocking collectives, exchanged(): return lax.all_to_all(pieces, axis, 0, 0, tiled=True)  103 us
    all_gather x4, blocking collectives, shards(): every = lax.all_gather(lax.all_gather(out, 'z'), 'c')  75.2 us
    all_to_all x3, starting transfers between devices, exchanged(): return lax.all_to_all(pieces, axis, 0, 0, tiled=True)  24.9 us
    all_to_all x3, waiting for transfers between devices, exchanged(): return lax.all_to_all(pieces, axis, 0, 0, tiled=True)  23.3 us
    pallas_call x22, Pallas kernels, local_call(): pl.pallas_call(functools.partial(body, **options), out_shape=[jax.ShapeDt...  19.1 us
    ppermute x3, waiting for transfers between devices, shards(): edge = lax.ppermute(edge, PATCH, outward)  17.6 us
    all_gather x3, blocking collectives, shards(): pair = lax.all_gather(field, 'c')  14.2 us
    ppermute x3, starting transfers between devices, shards(): edge = lax.ppermute(edge, PATCH, outward)  11.8 us
  transfers between devices with their start and end apart: 7, of which 5 were waited for; matrix products, arithmetic and copies ran while one was open for 0% of the time, Pallas kernels for 1%

profile of v6, /device:TPU:1, one launch (start us, length us, event | category | flops | bytes accessed | tf_op | source)
XLA Modules:
  0.0 310.2 jit_solution(18370813912900425841)
XLA Ops:
  0.0 1.9 copy-done.25
  1.9 1.1 copy-done.43
  3.0 1.7 shard_map.46
  4.8 1.2 copy-done.18
  6.0 8.9 %collective-permute-start = (f32[640,640]{1,0:T(8,128)S(1)}, f32[640,640]{1,0:T(8,128)S(1)}, u32[]{:S(2)}, u32[]{:S(2)}) collective-permute-start(f32[640,640]{1,0:T(8,128)S(1)} %get-tuple-element.45), channel_id=1, source_target_pairs={{0,1},{1,0},{2,3},{3,2},{4,5},{5,4},{6,7},{7,6},{8,9},{9,8},{10,11... | collective-permute-start | bytes 4915208 | tf_op jit(solution)/shard_map/ppermute | solution.py:295
  14.9 11.1 %all_to_all.55.pieces = f32[16,40,128]{2,1,0:T(8,128)S(1)} all-to-all(f32[16,40,128]{2,1,0:T(8,128)S(1)} %bitcast.24), channel_id=1, replica_groups=mesh['x'=4,'y'=4,'z'=16,'c'=2] {'x','y'}, dimensions={0} | all-to-all | bytes 655360 | tf_op jit(solution)/shard_map/all_to_all | solution.py:261
  26.0 11.9 %all_to_all.56.every = f32[16,48,128]{2,1,0:T(8,128)S(1)} all-to-all(f32[16,48,128]{2,1,0:T(8,128)S(1)} %shard_map.47), channel_id=1, replica_groups=mesh['x'=4,'y'=4,'z'=16,'c'=2] {'x','y'}, dimensions={0} | all-to-all | bytes 786432 | tf_op jit(solution)/shard_map/all_to_all | solution.py:261
  38.0 4.5 %all-gather = f32[1296,128]{1,0:T(8,128)S(1)} all-gather(f32[648,128]{1,0:T(8,128)S(1)} %get-tuple-element.42.field.old_field), channel_id=2, replica_groups=mesh['x'=4,'y'=4,'z'=16,'c'=2] {'c'}, dimensions={0}, use_global_device_ids=true | all-gather | bytes 995328 | tf_op jit(solution)/shard_map/all_gather | solution.py:313
  42.8 2.0 shard_map.50
  44.8 13.4 %all-to-all-start.2 = ((f32[16,40,128]{2,1,0:T(8,128)}), f32[16,40,128]{2,1,0:T(8,128)}, u32[]{:S(2)}, u32[]{:S(2)}) async-start(f32[16,40,128]{2,1,0:T(8,128)} %bitcast.5), calls=%async_computation.2 | async-start | bytes 655360 | tf_op jit(solution)/shard_map/all_to_all | solution.py:261
  58.3 4.0 %collective-permute-start.1 = (f32[264,128]{1,0:T(8,128)S(1)}, f32[264,128]{1,0:T(8,128)S(1)}, u32[]{:S(2)}, u32[]{:S(2)}) collective-permute-start(f32[264,128]{1,0:T(8,128)S(1)} %get-tuple-element.48), channel_id=1, source_target_pairs={{1,2},{3,4},{5,6},{7,8},{9,10},{11,12},{13,14},{15,16},{17,18},{19... | collective-permute-start | bytes 405512 | tf_op jit(solution)/shard_map/ppermute | solution.py:312
  62.3 14.2 %collective-permute-done.1.edge = f32[264,128]{1,0:T(8,128)S(1)} collective-permute-done((f32[264,128]{1,0:T(8,128)S(1)}, f32[264,128]{1,0:T(8,128)S(1)}, u32[]{:S(2)}, u32[]{:S(2)}) %collective-permute-start.1) | collective-permute-done | bytes 135200 | tf_op jit(solution)/shard_map/ppermute | solution.py:312
  76.6 1.1 copy-done.1
  77.7 1.8 shard_map.52
  79.4 1.0 shard_map.51.part
  80.5 1.1 copy-done.2
  81.6 1.2 shard_map.53
  82.8 24.6 %all-gather.1 = f32[768,128]{1,0:T(8,128)S(1)} all-gather(f32[48,128]{1,0:T(8,128)S(1)} %get-tuple-element.51), channel_id=3, replica_groups=mesh['x'=4,'y'=4,'z'=16,'c'=2] {'z'}, dimensions={0}, use_global_device_ids=true | all-gather | bytes 417792 | tf_op jit(solution)/shard_map/all_gather | solution.py:350
  107.3 11.0 %all-gather.2.every = f32[32,48,128]{2,1,0:T(8,128)S(1)} all-gather(f32[16,48,128]{2,1,0:T(8,128)S(1)} %bitcast.29), channel_id=4, replica_groups=mesh['x'=4,'y'=4,'z'=16,'c'=2] {'c'}, dimensions={0}, use_global_device_ids=true | all-gather | bytes 1179648 | tf_op jit(solution)/shard_map/all_gather | solution.py:350
  118.3 1.2 shard_map.54
  119.6 11.2 %all_to_all.57.pieces = f32[16,40,128]{2,1,0:T(8,128)S(1)} all-to-all(f32[16,40,128]{2,1,0:T(8,128)S(1)} %bitcast.25), channel_id=1, replica_groups=mesh['x'=4,'y'=4,'z'=16,'c'=2] {'x','y'}, dimensions={0} | all-to-all | bytes 655360 | tf_op jit(solution)/shard_map/all_to_all | solution.py:261
  130.8 12.1 %all_to_all.58.every = f32[16,48,128]{2,1,0:T(8,128)S(1)} all-to-all(f32[16,48,128]{2,1,0:T(8,128)S(1)} %shard_map.55), channel_id=1, replica_groups=mesh['x'=4,'y'=4,'z'=16,'c'=2] {'x','y'}, dimensions={0} | all-to-all | bytes 786432 | tf_op jit(solution)/shard_map/all_to_all | solution.py:261
  143.1 4.8 %all-gather.3 = f32[1280,128]{1,0:T(8,128)S(1)} all-gather(f32[640,128]{1,0:T(8,128)S(1)} %get-tuple-element.60.field.old_field), channel_id=5, replica_groups=mesh['x'=4,'y'=4,'z'=16,'c'=2] {'c'}, dimensions={0}, use_global_device_ids=true | all-gather | bytes 983040 | tf_op jit(solution)/shard_map/all_gather | solution.py:313
  148.0 1.3 shard_map.57
  150.0 7.2 %all-to-all-start.5 = ((f32[16,40,128]{2,1,0:T(8,128)}), f32[16,40,128]{2,1,0:T(8,128)}, u32[]{:S(2)}, u32[]{:S(2)}) async-start(f32[16,40,128]{2,1,0:T(8,128)} %bitcast.22), calls=%async_computation.5 | async-start | bytes 655360 | tf_op jit(solution)/shard_map/all_to_all | solution.py:261
  157.3 4.0 %collective-permute-start.2 = (f32[256,128]{1,0:T(8,128)}, f32[256,128]{1,0:T(8,128)S(1)}, u32[]{:S(2)}, u32[]{:S(2)}) collective-permute-start(f32[256,128]{1,0:T(8,128)} %copy-done.51), channel_id=1, source_target_pairs={{1,2},{3,4},{5,6},{7,8},{9,10},{11,12},{13,14},{15,16},{17,18},{19... | collective-permute-start | bytes 393224 | tf_op jit(solution)/shard_map/ppermute | solution.py:312
  161.3 11.5 %all-to-all-done.5.pieces = f32[16,40,128]{2,1,0:T(8,128)} async-done(((f32[16,40,128]{2,1,0:T(8,128)}), f32[16,40,128]{2,1,0:T(8,128)}, u32[]{:S(2)}, u32[]{:S(2)}) %all-to-all-start.5) | async-done | bytes 327712 | tf_op jit(solution)/shard_map/all_to_all | solution.py:261
  172.8 1.0 shard_map.58.part
  173.8 1.7 collective-permute-done.2.edge
  175.5 1.1 copy-done.24
  176.6 1.2 shard_map.59
  177.8 26.6 %all-gather.4 = f32[768,128]{1,0:T(8,128)S(1)} all-gather(f32[48,128]{1,0:T(8,128)S(1)} %get-tuple-element.62), channel_id=6, replica_groups=mesh['x'=4,'y'=4,'z'=16,'c'=2] {'z'}, dimensions={0}, use_global_device_ids=true | all-gather | bytes 417792 | tf_op jit(solution)/shard_map/all_gather | solution.py:350
  204.4 13.0 %all-gather.5.every = f32[32,48,128]{2,1,0:T(8,128)S(1)} all-gather(f32[16,48,128]{2,1,0:T(8,128)S(1)} %bitcast.30), channel_id=7, replica_groups=mesh['x'=4,'y'=4,'z'=16,'c'=2] {'c'}, dimensions={0}, use_global_device_ids=true | all-gather | bytes 1179648 | tf_op jit(solution)/shard_map/all_gather | solution.py:350
  217.5 1.2 shard_map.60
  218.7 11.3 %all_to_all.59.pieces = f32[16,40,128]{2,1,0:T(8,128)S(1)} all-to-all(f32[16,40,128]{2,1,0:T(8,128)S(1)} %bitcast.23), channel_id=1, replica_groups=mesh['x'=4,'y'=4,'z'=16,'c'=2] {'x','y'}, dimensions={0} | all-to-all | bytes 655360 | tf_op jit(solution)/shard_map/all_to_all | solution.py:261
  230.1 12.3 %all_to_all.60.every = f32[16,48,128]{2,1,0:T(8,128)S(1)} all-to-all(f32[16,48,128]{2,1,0:T(8,128)S(1)} %shard_map.61), channel_id=1, replica_groups=mesh['x'=4,'y'=4,'z'=16,'c'=2] {'x','y'}, dimensions={0} | all-to-all | bytes 786432 | tf_op jit(solution)/shard_map/all_to_all | solution.py:261
  243.3 4.8 %all-gather.6 = f32[1280,128]{1,0:T(8,128)S(1)} all-gather(f32[640,128]{1,0:T(8,128)S(1)} %get-tuple-element.72.field), channel_id=8, replica_groups=mesh['x'=4,'y'=4,'z'=16,'c'=2] {'c'}, dimensions={0}, use_global_device_ids=true | all-gather | bytes 983040 | tf_op jit(solution)/shard_map/all_gather | solution.py:313
  248.1 2.0 shard_map.63
  250.1 4.2 %all-to-all-start.8 = ((f32[16,40,128]{2,1,0:T(8,128)}), f32[16,40,128]{2,1,0:T(8,128)}, u32[]{:S(2)}, u32[]{:S(2)}) async-start(f32[16,40,128]{2,1,0:T(8,128)} %bitcast.14), calls=%async_computation.8 | async-start | bytes 655360 | tf_op jit(solution)/shard_map/all_to_all | solution.py:261
  254.3 3.7 %collective-permute-start.3 = (f32[256,128]{1,0:T(8,128)}, f32[256,128]{1,0:T(8,128)S(1)}, u32[]{:S(2)}, u32[]{:S(2)}) collective-permute-start(f32[256,128]{1,0:T(8,128)} %copy-done.50), channel_id=1, source_target_pairs={{1,2},{3,4},{5,6},{7,8},{9,10},{11,12},{13,14},{15,16},{17,18},{19... | collective-permute-start | bytes 393224 | tf_op jit(solution)/shard_map/ppermute | solution.py:312
  258.1 11.8 %all-to-all-done.8.pieces = f32[16,40,128]{2,1,0:T(8,128)} async-done(((f32[16,40,128]{2,1,0:T(8,128)}), f32[16,40,128]{2,1,0:T(8,128)}, u32[]{:S(2)}, u32[]{:S(2)}) %all-to-all-start.8) | async-done | bytes 327712 | tf_op jit(solution)/shard_map/all_to_all | solution.py:261
  269.9 1.0 shard_map.64.share_ref
  270.9 1.6 collective-permute-done.3.edge
  272.6 1.1 copy-done.22
  273.6 1.1 copy-done.42
  274.7 1.2 shard_map.65
  275.9 18.5 %all_to_all.61.every = f32[32,8,128]{2,1,0:T(8,128)S(1)} all-to-all(f32[32,8,128]{2,1,0:T(8,128)S(1)} %shard_map.65), channel_id=1, replica_groups=mesh['x'=4,'y'=4,'z'=16,'c'=2] {'x','y','c'}, dimensions={0} | all-to-all | bytes 262144 | tf_op jit(solution)/shard_map/all_to_all | solution.py:261
  294.4 15.0 %all_to_all.62.every = f32[16,8,128]{2,1,0:T(8,128)S(1)} all-to-all(f32[16,8,128]{2,1,0:T(8,128)S(1)} %shard_map.66), channel_id=1, replica_groups=mesh['x'=4,'y'=4,'z'=16,'c'=2] {'z'}, dimensions={0} | all-to-all | bytes 131072 | tf_op jit(solution)/shard_map/all_to_all | solution.py:261
  (110 shorter events, 3.1 us)
Async XLA Ops:
  6.0 36.6 %copy-start.15 = (bf16[640,1280]{1,0:T(8,128)(2,1)}, bf16[640,1280]{1,0:T(8,128)(2,1)S(1)}, u32[]{:S(2)}) copy-start(bf16[640,1280]{1,0:T(8,128)(2,1)S(1)} %get-tuple-element.53.high) | copy-start | bytes 4915204
  6.0 36.8 %copy-start.3 = (bf16[640,640]{1,0:T(8,128)(2,1)}, bf16[640,640]{1,0:T(8,128)(2,1)S(1)}, u32[]{:S(2)}) copy-start(bf16[640,640]{1,0:T(8,128)(2,1)S(1)} %get-tuple-element.43.own_high) | copy-start | bytes 2457604
  6.0 36.8 %copy-start.6 = (bf16[640,640]{1,0:T(8,128)(2,1)}, bf16[640,640]{1,0:T(8,128)(2,1)S(1)}, u32[]{:S(2)}) copy-start(bf16[640,640]{1,0:T(8,128)(2,1)S(1)} %get-tuple-element.44.own_low) | copy-start | bytes 2457604
  6.0 32.0 %copy-start.48 = (s32[3,640]{1,0:T(4,128)S(1)}, s32[3,640]{1,0:T(4,128)}, u32[]{:S(2)}) copy-start(s32[3,640]{1,0:T(4,128)} %ids.3) | copy-start | bytes 23044
  6.0 36.6 %collective-permute-start = (f32[640,640]{1,0:T(8,128)S(1)}, f32[640,640]{1,0:T(8,128)S(1)}, u32[]{:S(2)}, u32[]{:S(2)}) collective-permute-start(f32[640,640]{1,0:T(8,128)S(1)} %get-tuple-element.45), channel_id=1, source_target_pairs={{0,1},{1,0},{2,3},{3,2},{4,5},{5,4},{6,7},{7,6},{8,9},{9,8},{10,11... | collective-permute-start | bytes 4915208 | tf_op jit(solution)/shard_map/ppermute | solution.py:295
  42.6 2.3 copy-start
  42.8 2.0 copy-start.9
  42.8 2.0 copy-start.12
  44.8 35.6 %copy-start.49 = (f32[128]{0:T(128)S(1)}, f32[128]{0:T(128)}, u32[]{:S(2)}) copy-start(f32[128]{0:T(128)} %param.7) | copy-start | bytes 1540
  44.8 34.6 %all-to-all-start.2 = ((f32[16,40,128]{2,1,0:T(8,128)}), f32[16,40,128]{2,1,0:T(8,128)}, u32[]{:S(2)}, u32[]{:S(2)}) async-start(f32[16,40,128]{2,1,0:T(8,128)} %bitcast.5), calls=%async_computation.2 | async-start | bytes 655360 | tf_op jit(solution)/shard_map/all_to_all | solution.py:261
  58.3 18.3 %collective-permute-start.1 = (f32[264,128]{1,0:T(8,128)S(1)}, f32[264,128]{1,0:T(8,128)S(1)}, u32[]{:S(2)}, u32[]{:S(2)}) collective-permute-start(f32[264,128]{1,0:T(8,128)S(1)} %get-tuple-element.48), channel_id=1, source_target_pairs={{1,2},{3,4},{5,6},{7,8},{9,10},{11,12},{13,14},{15,16},{17,18},{19... | collective-permute-start | bytes 405512 | tf_op jit(solution)/shard_map/ppermute | solution.py:312
  81.6 36.8 %copy-start.19 = (bf16[640,1280]{1,0:T(8,128)(2,1)S(1)}, bf16[640,1280]{1,0:T(8,128)(2,1)}, u32[]{:S(2)}) copy-start(bf16[640,1280]{1,0:T(8,128)(2,1)} %copy-done.18) | copy-start | bytes 4915204
  82.8 35.6 %copy-start.16 = (bf16[640,1280]{1,0:T(8,128)(2,1)S(1)}, bf16[640,1280]{1,0:T(8,128)(2,1)}, u32[]{:S(2)}) copy-start(bf16[640,1280]{1,0:T(8,128)(2,1)} %copy-done.15) | copy-start | bytes 4915204
  119.6 23.4 %copy-start.39 = (f32[1280,128]{1,0:T(8,128)}, f32[1280,128]{1,0:T(8,128)S(1)}, u32[]{:S(2)}) copy-start(f32[1280,128]{1,0:T(8,128)S(1)} %get-tuple-element.64.old_image) | copy-start | bytes 1966084
  119.6 23.5 %copy-start.28 = (f32[640,128]{1,0:T(8,128)}, f32[640,128]{1,0:T(8,128)S(1)}, u32[]{:S(2)}) copy-start(f32[640,128]{1,0:T(8,128)S(1)} %get-tuple-element.58.smooth.old_smooth) | copy-start | bytes 983044
  119.6 23.5 %copy-start.31 = (f32[640,128]{1,0:T(8,128)}, f32[640,128]{1,0:T(8,128)S(1)}, u32[]{:S(2)}) copy-start(f32[640,128]{1,0:T(8,128)S(1)} %get-tuple-element.59.way.old_way) | copy-start | bytes 983044
  130.8 17.2 %copy-start.4 = (bf16[640,640]{1,0:T(8,128)(2,1)S(1)}, bf16[640,640]{1,0:T(8,128)(2,1)}, u32[]{:S(2)}) copy-start(bf16[640,640]{1,0:T(8,128)(2,1)} %copy-done.3) | copy-start | bytes 2457604
  130.8 17.1 %copy-start.7 = (bf16[640,640]{1,0:T(8,128)(2,1)S(1)}, bf16[640,640]{1,0:T(8,128)(2,1)}, u32[]{:S(2)}) copy-start(bf16[640,640]{1,0:T(8,128)(2,1)} %copy-done.6) | copy-start | bytes 2457604
  130.8 17.1 %copy-start.10 = (bf16[640,640]{1,0:T(8,128)(2,1)S(1)}, bf16[640,640]{1,0:T(8,128)(2,1)}, u32[]{:S(2)}) copy-start(bf16[640,640]{1,0:T(8,128)(2,1)} %copy-done.9) | copy-start | bytes 2457604
  130.8 17.1 %copy-start.13 = (bf16[640,640]{1,0:T(8,128)(2,1)S(1)}, bf16[640,640]{1,0:T(8,128)(2,1)}, u32[]{:S(2)}) copy-start(bf16[640,640]{1,0:T(8,128)(2,1)} %copy-done.12) | copy-start | bytes 2457604
  143.1 6.2 %copy-start.26 = (f32[640,128]{1,0:T(8,128)}, f32[640,128]{1,0:T(8,128)S(1)}, u32[]{:S(2)}) copy-start(f32[640,128]{1,0:T(8,128)S(1)} %get-tuple-element.60.field.old_field) | copy-start | bytes 983044
  143.1 6.2 %copy-start.44 = (f32[640,128]{1,0:T(8,128)}, f32[640,128]{1,0:T(8,128)S(1)}, u32[]{:S(2)}) copy-start(f32[640,128]{1,0:T(8,128)S(1)} %get-tuple-element.71.old_slip) | copy-start | bytes 983044
  143.1 6.2 %copy-start.51 = (f32[256,128]{1,0:T(8,128)}, f32[256,128]{1,0:T(8,128)S(1)}, u32[]{:S(2)}) copy-start(f32[256,128]{1,0:T(8,128)S(1)} %get-tuple-element.61) | copy-start | bytes 393220
  148.0 27.5 %copy-start.29 = (f32[640,128]{1,0:T(8,128)S(1)}, f32[640,128]{1,0:T(8,128)}, u32[]{:S(2)}) copy-start(f32[640,128]{1,0:T(8,128)} %copy-done.28) | copy-start | bytes 983044
  150.0 22.8 %all-to-all-start.5 = ((f32[16,40,128]{2,1,0:T(8,128)}), f32[16,40,128]{2,1,0:T(8,128)}, u32[]{:S(2)}, u32[]{:S(2)}) async-start(f32[16,40,128]{2,1,0:T(8,128)} %bitcast.22), calls=%async_computation.5 | async-start | bytes 655360 | tf_op jit(solution)/shard_map/all_to_all | solution.py:261
  157.3 18.2 %collective-permute-start.2 = (f32[256,128]{1,0:T(8,128)}, f32[256,128]{1,0:T(8,128)S(1)}, u32[]{:S(2)}, u32[]{:S(2)}) collective-permute-start(f32[256,128]{1,0:T(8,128)} %copy-done.51), channel_id=1, source_target_pairs={{1,2},{3,4},{5,6},{7,8},{9,10},{11,12},{13,14},{15,16},{17,18},{19... | collective-permute-start | bytes 393224 | tf_op jit(solution)/shard_map/ppermute | solution.py:312
  176.6 40.9 %copy-start.17 = (bf16[640,1280]{1,0:T(8,128)(2,1)S(1)}, bf16[640,1280]{1,0:T(8,128)(2,1)}, u32[]{:S(2)}) copy-start(bf16[640,1280]{1,0:T(8,128)(2,1)} %copy-done.15) | copy-start | bytes 4915204
  176.6 40.9 %copy-start.20 = (bf16[640,1280]{1,0:T(8,128)(2,1)S(1)}, bf16[640,1280]{1,0:T(8,128)(2,1)}, u32[]{:S(2)}) copy-start(bf16[640,1280]{1,0:T(8,128)(2,1)} %copy-done.18) | copy-start | bytes 4915204
  177.8 39.7 %copy-start.27 = (f32[640,128]{1,0:T(8,128)S(1)}, f32[640,128]{1,0:T(8,128)}, u32[]{:S(2)}) copy-start(f32[640,128]{1,0:T(8,128)} %copy-done.26) | copy-start | bytes 983044
  177.8 39.7 %copy-start.32 = (f32[640,128]{1,0:T(8,128)S(1)}, f32[640,128]{1,0:T(8,128)}, u32[]{:S(2)}) copy-start(f32[640,128]{1,0:T(8,128)} %copy-done.31) | copy-start | bytes 983044
  177.8 39.7 %copy-start.40 = (f32[1280,128]{1,0:T(8,128)S(1)}, f32[1280,128]{1,0:T(8,128)}, u32[]{:S(2)}) copy-start(f32[1280,128]{1,0:T(8,128)} %copy-done.39) | copy-start | bytes 1966084
  218.7 23.7 %copy-start.41 = (f32[1280,128]{1,0:T(8,128)}, f32[1280,128]{1,0:T(8,128)S(1)}, u32[]{:S(2)}) copy-start(f32[1280,128]{1,0:T(8,128)S(1)} %get-tuple-element.73.image) | copy-start | bytes 1966084
  218.7 23.8 %copy-start.33 = (f32[640,128]{1,0:T(8,128)}, f32[640,128]{1,0:T(8,128)S(1)}, u32[]{:S(2)}) copy-start(f32[640,128]{1,0:T(8,128)S(1)} %get-tuple-element.69.smooth) | copy-start | bytes 983044
  218.7 23.8 %copy-start.35 = (f32[640,128]{1,0:T(8,128)}, f32[640,128]{1,0:T(8,128)S(1)}, u32[]{:S(2)}) copy-start(f32[640,128]{1,0:T(8,128)S(1)} %get-tuple-element.70.way) | copy-start | bytes 983044
  218.7 23.7 %copy-start.45 = (f32[640,128]{1,0:T(8,128)S(1)}, f32[640,128]{1,0:T(8,128)}, u32[]{:S(2)}) copy-start(f32[640,128]{1,0:T(8,128)} %copy-done.44) | copy-start | bytes 983044
  230.1 18.0 %copy-start.5 = (bf16[640,640]{1,0:T(8,128)(2,1)S(1)}, bf16[640,640]{1,0:T(8,128)(2,1)}, u32[]{:S(2)}) copy-start(bf16[640,640]{1,0:T(8,128)(2,1)} %copy-done.3) | copy-start | bytes 2457604
  230.1 18.0 %copy-start.8 = (bf16[640,640]{1,0:T(8,128)(2,1)S(1)}, bf16[640,640]{1,0:T(8,128)(2,1)}, u32[]{:S(2)}) copy-start(bf16[640,640]{1,0:T(8,128)(2,1)} %copy-done.6) | copy-start | bytes 2457604
  230.1 18.0 %copy-start.11 = (bf16[640,640]{1,0:T(8,128)(2,1)S(1)}, bf16[640,640]{1,0:T(8,128)(2,1)}, u32[]{:S(2)}) copy-start(bf16[640,640]{1,0:T(8,128)(2,1)} %copy-done.9) | copy-start | bytes 2457604
  230.1 18.0 %copy-start.14 = (bf16[640,640]{1,0:T(8,128)(2,1)S(1)}, bf16[640,640]{1,0:T(8,128)(2,1)}, u32[]{:S(2)}) copy-start(bf16[640,640]{1,0:T(8,128)(2,1)} %copy-done.12) | copy-start | bytes 2457604
  243.3 6.9 %copy-start.37 = (f32[640,128]{1,0:T(8,128)}, f32[640,128]{1,0:T(8,128)S(1)}, u32[]{:S(2)}) copy-start(f32[640,128]{1,0:T(8,128)S(1)} %get-tuple-element.72.field) | copy-start | bytes 983044
  243.3 6.9 %copy-start.50 = (f32[256,128]{1,0:T(8,128)}, f32[256,128]{1,0:T(8,128)S(1)}, u32[]{:S(2)}) copy-start(f32[256,128]{1,0:T(8,128)S(1)} %get-tuple-element.74) | copy-start | bytes 393220
  248.1 2.0 copy-start.21
  248.1 24.4 %copy-start.34 = (f32[640,128]{1,0:T(8,128)S(1)}, f32[640,128]{1,0:T(8,128)}, u32[]{:S(2)}) copy-start(f32[640,128]{1,0:T(8,128)} %copy-done.33) | copy-start | bytes 983044
  250.1 19.8 %all-to-all-start.8 = ((f32[16,40,128]{2,1,0:T(8,128)}), f32[16,40,128]{2,1,0:T(8,128)}, u32[]{:S(2)}, u32[]{:S(2)}) async-start(f32[16,40,128]{2,1,0:T(8,128)} %bitcast.14), calls=%async_computation.8 | async-start | bytes 655360 | tf_op jit(solution)/shard_map/all_to_all | solution.py:261
  254.3 18.2 %collective-permute-start.3 = (f32[256,128]{1,0:T(8,128)}, f32[256,128]{1,0:T(8,128)S(1)}, u32[]{:S(2)}, u32[]{:S(2)}) collective-permute-start(f32[256,128]{1,0:T(8,128)} %copy-done.50), channel_id=1, source_target_pairs={{1,2},{3,4},{5,6},{7,8},{9,10},{11,12},{13,14},{15,16},{17,18},{19... | collective-permute-start | bytes 393224 | tf_op jit(solution)/shard_map/ppermute | solution.py:312
  274.7 34.7 %copy-start.36 = (f32[640,128]{1,0:T(8,128)S(1)}, f32[640,128]{1,0:T(8,128)}, u32[]{:S(2)}) copy-start(f32[640,128]{1,0:T(8,128)} %copy-done.35) | copy-start | bytes 983044
  274.7 34.7 %copy-start.38 = (f32[640,128]{1,0:T(8,128)S(1)}, f32[640,128]{1,0:T(8,128)}, u32[]{:S(2)}) copy-start(f32[640,128]{1,0:T(8,128)} %copy-done.37) | copy-start | bytes 983044
  274.7 34.7 %copy-start.47 = (f32[640,128]{1,0:T(8,128)S(1)}, f32[640,128]{1,0:T(8,128)}, u32[]{:S(2)}) copy-start(f32[640,128]{1,0:T(8,128)} %copy-done.46) | copy-start | bytes 983044
  (11 other events, 12.5 us)

commit v7 on v6

--- a/solution.py
+++ b/solution.py
@@ -153,11 +153,13 @@
 
 def collect(core, part, pair, edge, weight, smooth, m_high, m_low, out, fresh, near):
     share = part.shape[0]
-    out[:share, :] = part[...]
     own, new = regularized(core, pair, edge, weight, m_high, m_low, near)
     fresh[...] = new
     rows = [total(own * own), total(own * new), total(own * smooth[...])]
-    out[share:, :] = jnp.concatenate([*rows, jnp.zeros((TILE - 3, own.shape[1]), F32)], 0)
+    value, tail = part[...], jnp.concatenate([*rows, jnp.zeros((TILE - 3, own.shape[1]), F32)], 0)
+    for k in range(out.shape[0]):
+        out[k, :share, :] = value
+        out[k, share:, :] = tail
 
 
 def backward(every, field, fresh, old_image, old_smooth, old_way, old_scalars, high, low, moved, image, tail, smooth, way, scalars, wide):
@@ -344,10 +346,10 @@
             )
             return slip
         out, fresh = local_call(
-            collect, [((share + TILE, epochs), F32), field_shape], part, *penalty,
+            collect, [((n_z, share + TILE, epochs), F32), field_shape], part, *penalty,
             scalars=[core_scalar], scratch=[near],
         )
-        every = lax.all_gather(lax.all_gather(out, "z"), "c")
+        every = lax.all_gather(exchanged(out, "z"), "c")
         every = every.reshape(n_patch, share + TILE, epochs)
         moved, image, tail, smooth, way, scalars = local_call(
             backward,

time: 312 us -> 311 us (level)
    all_gather x4 -> x2, blocking collectives: 75.2 us -> 18.5 us  [shards(): every = lax.all_gather(exchanged(out, 'z'), 'c')]
    all_to_all x8 -> x10, blocking collectives: 103 us -> 159 us  [exchanged(): return lax.all_to_all(pieces, axis, 0, 0, tiled=True)]
where the time goes in v7:
time: 311 us; the launch traced here: 309 us
  blocking collectives  192 us (62%)
  starting transfers between devices  45.6 us (15%)
  waiting for transfers between devices  40.6 us (13%)
  Pallas kernels  19.1 us (6%)
  local copies, waits for them, and re-layouts  11.3 us (4%)
    all_to_all x10, blocking collectives, exchanged(): return lax.all_to_all(pieces, axis, 0, 0, tiled=True)  159 us
    all_to_all x3, starting transfers between devices, exchanged(): return lax.all_to_all(pieces, axis, 0, 0, tiled=True)  24.6 us
    all_to_all x3, waiting for transfers between devices, exchanged(): return lax.all_to_all(pieces, axis, 0, 0, tiled=True)  22.9 us
    pallas_call x22, Pallas kernels, local_call(): pl.pallas_call(functools.partial(body, **options), out_shape=[jax.ShapeDt...  19.1 us
    all_gather x2, blocking collectives, shards(): every = lax.all_gather(exchanged(out, 'z'), 'c')  18.5 us
    ppermute x3, waiting for transfers between devices, shards(): edge = lax.ppermute(edge, PATCH, outward)  17.7 us
    all_gather x3, blocking collectives, shards(): pair = lax.all_gather(field, 'c')  14.2 us
    ppermute x3, starting transfers between devices, shards(): edge = lax.ppermute(edge, PATCH, outward)  12.1 us
  transfers between devices with their start and end apart: 7, of which 5 were waited for; matrix products, arithmetic and copies ran while one was open for 0% of the time, Pallas kernels for 1%

profile of v7, /device:TPU:1, one launch (start us, length us, event | category | flops | bytes accessed | tf_op | source)
XLA Modules:
  0.0 309.3 jit_solution(12206284231655337388)
XLA Ops:
  0.0 1.9 copy-done.25
  1.9 1.1 copy-done.43
  3.0 1.7 shard_map.46
  4.8 1.2 copy-done.18
  6.0 8.9 %collective-permute-start = (f32[640,640]{1,0:T(8,128)S(1)}, f32[640,640]{1,0:T(8,128)S(1)}, u32[]{:S(2)}, u32[]{:S(2)}) collective-permute-start(f32[640,640]{1,0:T(8,128)S(1)} %get-tuple-element.45), channel_id=1, source_target_pairs={{0,1},{1,0},{2,3},{3,2},{4,5},{5,4},{6,7},{7,6},{8,9},{9,8},{10,11... | collective-permute-start | bytes 4915208 | tf_op jit(solution)/shard_map/ppermute | solution.py:297
  14.8 11.1 %all_to_all.65.pieces = f32[16,40,128]{2,1,0:T(8,128)S(1)} all-to-all(f32[16,40,128]{2,1,0:T(8,128)S(1)} %bitcast.22), channel_id=1, replica_groups=mesh['x'=4,'y'=4,'z'=16,'c'=2] {'x','y'}, dimensions={0} | all-to-all | bytes 655360 | tf_op jit(solution)/shard_map/all_to_all | solution.py:263
  26.0 11.9 %all_to_all.66.every = f32[16,48,128]{2,1,0:T(8,128)S(1)} all-to-all(f32[16,48,128]{2,1,0:T(8,128)S(1)} %shard_map.47), channel_id=1, replica_groups=mesh['x'=4,'y'=4,'z'=16,'c'=2] {'x','y'}, dimensions={0} | all-to-all | bytes 786432 | tf_op jit(solution)/shard_map/all_to_all | solution.py:263
  38.0 4.5 %all-gather = f32[1296,128]{1,0:T(8,128)S(1)} all-gather(f32[648,128]{1,0:T(8,128)S(1)} %get-tuple-element.42.field.old_field), channel_id=2, replica_groups=mesh['x'=4,'y'=4,'z'=16,'c'=2] {'c'}, dimensions={0}, use_global_device_ids=true | all-gather | bytes 995328 | tf_op jit(solution)/shard_map/all_gather | solution.py:315
  42.8 2.0 shard_map.50
  44.8 13.4 %all-to-all-start.2 = ((f32[16,40,128]{2,1,0:T(8,128)}), f32[16,40,128]{2,1,0:T(8,128)}, u32[]{:S(2)}, u32[]{:S(2)}) async-start(f32[16,40,128]{2,1,0:T(8,128)} %bitcast.5), calls=%async_computation.2 | async-start | bytes 655360 | tf_op jit(solution)/shard_map/all_to_all | solution.py:263
  58.3 4.0 %collective-permute-start.1 = (f32[264,128]{1,0:T(8,128)S(1)}, f32[264,128]{1,0:T(8,128)S(1)}, u32[]{:S(2)}, u32[]{:S(2)}) collective-permute-start(f32[264,128]{1,0:T(8,128)S(1)} %get-tuple-element.48), channel_id=1, source_target_pairs={{1,2},{3,4},{5,6},{7,8},{9,10},{11,12},{13,14},{15,16},{17,18},{19... | collective-permute-start | bytes 405512 | tf_op jit(solution)/shard_map/ppermute | solution.py:314
  62.3 14.2 %collective-permute-done.1.edge = f32[264,128]{1,0:T(8,128)S(1)} collective-permute-done((f32[264,128]{1,0:T(8,128)S(1)}, f32[264,128]{1,0:T(8,128)S(1)}, u32[]{:S(2)}, u32[]{:S(2)}) %collective-permute-start.1) | collective-permute-done | bytes 135200 | tf_op jit(solution)/shard_map/ppermute | solution.py:314
  76.5 1.1 copy-done.1
  77.6 1.8 shard_map.52
  79.4 1.0 shard_map.51.part
  80.4 1.1 copy-done.2
  81.5 1.2 shard_map.53
  82.7 27.8 %all_to_all.67 = f32[16,48,128]{2,1,0:T(8,128)S(1)} all-to-all(f32[16,48,128]{2,1,0:T(8,128)S(1)} %get-tuple-element.51), channel_id=1, replica_groups=mesh['x'=4,'y'=4,'z'=16,'c'=2] {'z'}, dimensions={0} | all-to-all | bytes 786432 | tf_op jit(solution)/shard_map/all_to_all | solution.py:263
  110.5 9.4 %all-gather.1.every = f32[32,48,128]{2,1,0:T(8,128)S(1)} all-gather(f32[16,48,128]{2,1,0:T(8,128)S(1)} %all_to_all.67), channel_id=3, replica_groups=mesh['x'=4,'y'=4,'z'=16,'c'=2] {'c'}, dimensions={0}, use_global_device_ids=true | all-gather | bytes 1179648 | tf_op jit(solution)/shard_map/all_gather | solution.py:352
  120.0 1.2 shard_map.54
  121.3 11.2 %all_to_all.68.pieces = f32[16,40,128]{2,1,0:T(8,128)S(1)} all-to-all(f32[16,40,128]{2,1,0:T(8,128)S(1)} %bitcast.23), channel_id=1, replica_groups=mesh['x'=4,'y'=4,'z'=16,'c'=2] {'x','y'}, dimensions={0} | all-to-all | bytes 655360 | tf_op jit(solution)/shard_map/all_to_all | solution.py:263
  132.5 12.1 %all_to_all.69.every = f32[16,48,128]{2,1,0:T(8,128)S(1)} all-to-all(f32[16,48,128]{2,1,0:T(8,128)S(1)} %shard_map.55), channel_id=1, replica_groups=mesh['x'=4,'y'=4,'z'=16,'c'=2] {'x','y'}, dimensions={0} | all-to-all | bytes 786432 | tf_op jit(solution)/shard_map/all_to_all | solution.py:263
  144.8 4.8 %all-gather.2 = f32[1280,128]{1,0:T(8,128)S(1)} all-gather(f32[640,128]{1,0:T(8,128)S(1)} %get-tuple-element.60.field.old_field), channel_id=4, replica_groups=mesh['x'=4,'y'=4,'z'=16,'c'=2] {'c'}, dimensions={0}, use_global_device_ids=true | all-gather | bytes 983040 | tf_op jit(solution)/shard_map/all_gather | solution.py:315
  149.7 1.3 shard_map.57
  151.7 5.6 %all-to-all-start.6 = ((f32[16,40,128]{2,1,0:T(8,128)}), f32[16,40,128]{2,1,0:T(8,128)}, u32[]{:S(2)}, u32[]{:S(2)}) async-start(f32[16,40,128]{2,1,0:T(8,128)} %bitcast.20), calls=%async_computation.6 | async-start | bytes 655360 | tf_op jit(solution)/shard_map/all_to_all | solution.py:263
  157.3 4.0 %collective-permute-start.2 = (f32[256,128]{1,0:T(8,128)}, f32[256,128]{1,0:T(8,128)S(1)}, u32[]{:S(2)}, u32[]{:S(2)}) collective-permute-start(f32[256,128]{1,0:T(8,128)} %copy-done.51), channel_id=1, source_target_pairs={{1,2},{3,4},{5,6},{7,8},{9,10},{11,12},{13,14},{15,16},{17,18},{19... | collective-permute-start | bytes 393224 | tf_op jit(solution)/shard_map/ppermute | solution.py:314
  161.3 11.5 %all-to-all-done.6.pieces = f32[16,40,128]{2,1,0:T(8,128)} async-done(((f32[16,40,128]{2,1,0:T(8,128)}), f32[16,40,128]{2,1,0:T(8,128)}, u32[]{:S(2)}, u32[]{:S(2)}) %all-to-all-start.6) | async-done | bytes 327712 | tf_op jit(solution)/shard_map/all_to_all | solution.py:263
  172.8 1.0 shard_map.58.part
  173.8 1.7 collective-permute-done.2.edge
  175.5 1.1 copy-done.24
  176.6 1.2 shard_map.59
  177.8 28.1 %all_to_all.70 = f32[16,48,128]{2,1,0:T(8,128)S(1)} all-to-all(f32[16,48,128]{2,1,0:T(8,128)S(1)} %get-tuple-element.62), channel_id=1, replica_groups=mesh['x'=4,'y'=4,'z'=16,'c'=2] {'z'}, dimensions={0} | all-to-all | bytes 786432 | tf_op jit(solution)/shard_map/all_to_all | solution.py:263
  205.9 9.0 %all-gather.3.every = f32[32,48,128]{2,1,0:T(8,128)S(1)} all-gather(f32[16,48,128]{2,1,0:T(8,128)S(1)} %all_to_all.70), channel_id=5, replica_groups=mesh['x'=4,'y'=4,'z'=16,'c'=2] {'c'}, dimensions={0}, use_global_device_ids=true | all-gather | bytes 1179648 | tf_op jit(solution)/shard_map/all_gather | solution.py:352
  215.0 1.2 shard_map.60
  216.2 11.5 %all_to_all.71.pieces = f32[16,40,128]{2,1,0:T(8,128)S(1)} all-to-all(f32[16,40,128]{2,1,0:T(8,128)S(1)} %bitcast.21), channel_id=1, replica_groups=mesh['x'=4,'y'=4,'z'=16,'c'=2] {'x','y'}, dimensions={0} | all-to-all | bytes 655360 | tf_op jit(solution)/shard_map/all_to_all | solution.py:263
  227.8 12.1 %all_to_all.72.every = f32[16,48,128]{2,1,0:T(8,128)S(1)} all-to-all(f32[16,48,128]{2,1,0:T(8,128)S(1)} %shard_map.61), channel_id=1, replica_groups=mesh['x'=4,'y'=4,'z'=16,'c'=2] {'x','y'}, dimensions={0} | all-to-all | bytes 786432 | tf_op jit(solution)/shard_map/all_to_all | solution.py:263
  240.8 4.8 %all-gather.4 = f32[1280,128]{1,0:T(8,128)S(1)} all-gather(f32[640,128]{1,0:T(8,128)S(1)} %get-tuple-element.72.field), channel_id=6, replica_groups=mesh['x'=4,'y'=4,'z'=16,'c'=2] {'c'}, dimensions={0}, use_global_device_ids=true | all-gather | bytes 983040 | tf_op jit(solution)/shard_map/all_gather | solution.py:315
  245.7 2.0 shard_map.63
  247.6 5.6 %all-to-all-start.10 = ((f32[16,40,128]{2,1,0:T(8,128)}), f32[16,40,128]{2,1,0:T(8,128)}, u32[]{:S(2)}, u32[]{:S(2)}) async-start(f32[16,40,128]{2,1,0:T(8,128)} %bitcast.12), calls=%async_computation.10 | async-start | bytes 655360 | tf_op jit(solution)/shard_map/all_to_all | solution.py:263
  253.3 4.0 %collective-permute-start.3 = (f32[256,128]{1,0:T(8,128)}, f32[256,128]{1,0:T(8,128)S(1)}, u32[]{:S(2)}, u32[]{:S(2)}) collective-permute-start(f32[256,128]{1,0:T(8,128)} %copy-done.50), channel_id=1, source_target_pairs={{1,2},{3,4},{5,6},{7,8},{9,10},{11,12},{13,14},{15,16},{17,18},{19... | collective-permute-start | bytes 393224 | tf_op jit(solution)/shard_map/ppermute | solution.py:314
  257.3 11.5 %all-to-all-done.10.pieces = f32[16,40,128]{2,1,0:T(8,128)} async-done(((f32[16,40,128]{2,1,0:T(8,128)}), f32[16,40,128]{2,1,0:T(8,128)}, u32[]{:S(2)}, u32[]{:S(2)}) %all-to-all-start.10) | async-done | bytes 327712 | tf_op jit(solution)/shard_map/all_to_all | solution.py:263
  268.8 1.0 shard_map.64.share_ref
  269.8 1.7 collective-permute-done.3.edge
  271.5 1.1 copy-done.22
  272.6 1.1 copy-done.42
  273.7 1.2 shard_map.65
  274.9 18.5 %all_to_all.73.every = f32[32,8,128]{2,1,0:T(8,128)S(1)} all-to-all(f32[32,8,128]{2,1,0:T(8,128)S(1)} %shard_map.65), channel_id=1, replica_groups=mesh['x'=4,'y'=4,'z'=16,'c'=2] {'x','y','c'}, dimensions={0} | all-to-all | bytes 262144 | tf_op jit(solution)/shard_map/all_to_all | solution.py:263
  293.5 15.0 %all_to_all.74.every = f32[16,8,128]{2,1,0:T(8,128)S(1)} all-to-all(f32[16,8,128]{2,1,0:T(8,128)S(1)} %shard_map.66), channel_id=1, replica_groups=mesh['x'=4,'y'=4,'z'=16,'c'=2] {'z'}, dimensions={0} | all-to-all | bytes 131072 | tf_op jit(solution)/shard_map/all_to_all | solution.py:263
  (110 shorter events, 3.1 us)
Async XLA Ops:
  6.0 36.6 %copy-start.15 = (bf16[640,1280]{1,0:T(8,128)(2,1)}, bf16[640,1280]{1,0:T(8,128)(2,1)S(1)}, u32[]{:S(2)}) copy-start(bf16[640,1280]{1,0:T(8,128)(2,1)S(1)} %get-tuple-element.53.high) | copy-start | bytes 4915204
  6.0 36.8 %copy-start.3 = (bf16[640,640]{1,0:T(8,128)(2,1)}, bf16[640,640]{1,0:T(8,128)(2,1)S(1)}, u32[]{:S(2)}) copy-start(bf16[640,640]{1,0:T(8,128)(2,1)S(1)} %get-tuple-element.43.own_high) | copy-start | bytes 2457604
  6.0 36.8 %copy-start.6 = (bf16[640,640]{1,0:T(8,128)(2,1)}, bf16[640,640]{1,0:T(8,128)(2,1)S(1)}, u32[]{:S(2)}) copy-start(bf16[640,640]{1,0:T(8,128)(2,1)S(1)} %get-tuple-element.44.own_low) | copy-start | bytes 2457604
  6.0 32.0 %copy-start.48 = (s32[3,640]{1,0:T(4,128)S(1)}, s32[3,640]{1,0:T(4,128)}, u32[]{:S(2)}) copy-start(s32[3,640]{1,0:T(4,128)} %ids.3) | copy-start | bytes 23044
  6.0 36.6 %collective-permute-start = (f32[640,640]{1,0:T(8,128)S(1)}, f32[640,640]{1,0:T(8,128)S(1)}, u32[]{:S(2)}, u32[]{:S(2)}) collective-permute-start(f32[640,640]{1,0:T(8,128)S(1)} %get-tuple-element.45), channel_id=1, source_target_pairs={{0,1},{1,0},{2,3},{3,2},{4,5},{5,4},{6,7},{7,6},{8,9},{9,8},{10,11... | collective-permute-start | bytes 4915208 | tf_op jit(solution)/shard_map/ppermute | solution.py:297
  42.5 2.3 copy-start
  42.8 2.0 copy-start.9
  42.8 2.0 copy-start.12
  44.8 35.6 %copy-start.49 = (f32[128]{0:T(128)S(1)}, f32[128]{0:T(128)}, u32[]{:S(2)}) copy-start(f32[128]{0:T(128)} %param.7) | copy-start | bytes 1540
  44.8 34.6 %all-to-all-start.2 = ((f32[16,40,128]{2,1,0:T(8,128)}), f32[16,40,128]{2,1,0:T(8,128)}, u32[]{:S(2)}, u32[]{:S(2)}) async-start(f32[16,40,128]{2,1,0:T(8,128)} %bitcast.5), calls=%async_computation.2 | async-start | bytes 655360 | tf_op jit(solution)/shard_map/all_to_all | solution.py:263
  58.3 18.3 %collective-permute-start.1 = (f32[264,128]{1,0:T(8,128)S(1)}, f32[264,128]{1,0:T(8,128)S(1)}, u32[]{:S(2)}, u32[]{:S(2)}) collective-permute-start(f32[264,128]{1,0:T(8,128)S(1)} %get-tuple-element.48), channel_id=1, source_target_pairs={{1,2},{3,4},{5,6},{7,8},{9,10},{11,12},{13,14},{15,16},{17,18},{19... | collective-permute-start | bytes 405512 | tf_op jit(solution)/shard_map/ppermute | solution.py:314
  81.5 38.5 %copy-start.19 = (bf16[640,1280]{1,0:T(8,128)(2,1)S(1)}, bf16[640,1280]{1,0:T(8,128)(2,1)}, u32[]{:S(2)}) copy-start(bf16[640,1280]{1,0:T(8,128)(2,1)} %copy-done.18) | copy-start | bytes 4915204
  82.7 37.3 %copy-start.16 = (bf16[640,1280]{1,0:T(8,128)(2,1)S(1)}, bf16[640,1280]{1,0:T(8,128)(2,1)}, u32[]{:S(2)}) copy-start(bf16[640,1280]{1,0:T(8,128)(2,1)} %copy-done.15) | copy-start | bytes 4915204
  121.2 23.4 %copy-start.39 = (f32[1280,128]{1,0:T(8,128)}, f32[1280,128]{1,0:T(8,128)S(1)}, u32[]{:S(2)}) copy-start(f32[1280,128]{1,0:T(8,128)S(1)} %get-tuple-element.64.old_image) | copy-start | bytes 1966084
  121.2 23.5 %copy-start.28 = (f32[640,128]{1,0:T(8,128)}, f32[640,128]{1,0:T(8,128)S(1)}, u32[]{:S(2)}) copy-start(f32[640,128]{1,0:T(8,128)S(1)} %get-tuple-element.58.smooth.old_smooth) | copy-start | bytes 983044
  121.3 23.5 %copy-start.31 = (f32[640,128]{1,0:T(8,128)}, f32[640,128]{1,0:T(8,128)S(1)}, u32[]{:S(2)}) copy-start(f32[640,128]{1,0:T(8,128)S(1)} %get-tuple-element.59.way.old_way) | copy-start | bytes 983044
  132.5 17.1 %copy-start.4 = (bf16[640,640]{1,0:T(8,128)(2,1)S(1)}, bf16[640,640]{1,0:T(8,128)(2,1)}, u32[]{:S(2)}) copy-start(bf16[640,640]{1,0:T(8,128)(2,1)} %copy-done.3) | copy-start | bytes 2457604
  132.5 17.1 %copy-start.7 = (bf16[640,640]{1,0:T(8,128)(2,1)S(1)}, bf16[640,640]{1,0:T(8,128)(2,1)}, u32[]{:S(2)}) copy-start(bf16[640,640]{1,0:T(8,128)(2,1)} %copy-done.6) | copy-start | bytes 2457604
  132.5 17.1 %copy-start.10 = (bf16[640,640]{1,0:T(8,128)(2,1)S(1)}, bf16[640,640]{1,0:T(8,128)(2,1)}, u32[]{:S(2)}) copy-start(bf16[640,640]{1,0:T(8,128)(2,1)} %copy-done.9) | copy-start | bytes 2457604
  132.5 17.1 %copy-start.13 = (bf16[640,640]{1,0:T(8,128)(2,1)S(1)}, bf16[640,640]{1,0:T(8,128)(2,1)}, u32[]{:S(2)}) copy-start(bf16[640,640]{1,0:T(8,128)(2,1)} %copy-done.12) | copy-start | bytes 2457604
  144.8 6.2 %copy-start.26 = (f32[640,128]{1,0:T(8,128)}, f32[640,128]{1,0:T(8,128)S(1)}, u32[]{:S(2)}) copy-start(f32[640,128]{1,0:T(8,128)S(1)} %get-tuple-element.60.field.old_field) | copy-start | bytes 983044
  144.8 6.2 %copy-start.44 = (f32[640,128]{1,0:T(8,128)}, f32[640,128]{1,0:T(8,128)S(1)}, u32[]{:S(2)}) copy-start(f32[640,128]{1,0:T(8,128)S(1)} %get-tuple-element.71.old_slip) | copy-start | bytes 983044
  144.8 6.2 %copy-start.51 = (f32[256,128]{1,0:T(8,128)}, f32[256,128]{1,0:T(8,128)S(1)}, u32[]{:S(2)}) copy-start(f32[256,128]{1,0:T(8,128)S(1)} %get-tuple-element.61) | copy-start | bytes 393220
  149.7 25.8 %copy-start.29 = (f32[640,128]{1,0:T(8,128)S(1)}, f32[640,128]{1,0:T(8,128)}, u32[]{:S(2)}) copy-start(f32[640,128]{1,0:T(8,128)} %copy-done.28) | copy-start | bytes 983044
  151.7 21.1 %all-to-all-start.6 = ((f32[16,40,128]{2,1,0:T(8,128)}), f32[16,40,128]{2,1,0:T(8,128)}, u32[]{:S(2)}, u32[]{:S(2)}) async-start(f32[16,40,128]{2,1,0:T(8,128)} %bitcast.20), calls=%async_computation.6 | async-start | bytes 655360 | tf_op jit(solution)/shard_map/all_to_all | solution.py:263
  157.3 18.2 %collective-permute-start.2 = (f32[256,128]{1,0:T(8,128)}, f32[256,128]{1,0:T(8,128)S(1)}, u32[]{:S(2)}, u32[]{:S(2)}) collective-permute-start(f32[256,128]{1,0:T(8,128)} %copy-done.51), channel_id=1, source_target_pairs={{1,2},{3,4},{5,6},{7,8},{9,10},{11,12},{13,14},{15,16},{17,18},{19... | collective-permute-start | bytes 393224 | tf_op jit(solution)/shard_map/ppermute | solution.py:314
  176.6 38.4 %copy-start.20 = (bf16[640,1280]{1,0:T(8,128)(2,1)S(1)}, bf16[640,1280]{1,0:T(8,128)(2,1)}, u32[]{:S(2)}) copy-start(bf16[640,1280]{1,0:T(8,128)(2,1)} %copy-done.18) | copy-start | bytes 4915204
  176.6 38.4 %copy-start.32 = (f32[640,128]{1,0:T(8,128)S(1)}, f32[640,128]{1,0:T(8,128)}, u32[]{:S(2)}) copy-start(f32[640,128]{1,0:T(8,128)} %copy-done.31) | copy-start | bytes 983044
  176.6 38.4 %copy-start.40 = (f32[1280,128]{1,0:T(8,128)S(1)}, f32[1280,128]{1,0:T(8,128)}, u32[]{:S(2)}) copy-start(f32[1280,128]{1,0:T(8,128)} %copy-done.39) | copy-start | bytes 1966084
  177.8 37.2 %copy-start.17 = (bf16[640,1280]{1,0:T(8,128)(2,1)S(1)}, bf16[640,1280]{1,0:T(8,128)(2,1)}, u32[]{:S(2)}) copy-start(bf16[640,1280]{1,0:T(8,128)(2,1)} %copy-done.15) | copy-start | bytes 4915204
  177.8 37.2 %copy-start.27 = (f32[640,128]{1,0:T(8,128)S(1)}, f32[640,128]{1,0:T(8,128)}, u32[]{:S(2)}) copy-start(f32[640,128]{1,0:T(8,128)} %copy-done.26) | copy-start | bytes 983044
  216.2 23.7 %copy-start.41 = (f32[1280,128]{1,0:T(8,128)}, f32[1280,128]{1,0:T(8,128)S(1)}, u32[]{:S(2)}) copy-start(f32[1280,128]{1,0:T(8,128)S(1)} %get-tuple-element.73.image) | copy-start | bytes 1966084
  216.2 23.8 %copy-start.33 = (f32[640,128]{1,0:T(8,128)}, f32[640,128]{1,0:T(8,128)S(1)}, u32[]{:S(2)}) copy-start(f32[640,128]{1,0:T(8,128)S(1)} %get-tuple-element.69.smooth) | copy-start | bytes 983044
  216.2 23.8 %copy-start.35 = (f32[640,128]{1,0:T(8,128)}, f32[640,128]{1,0:T(8,128)S(1)}, u32[]{:S(2)}) copy-start(f32[640,128]{1,0:T(8,128)S(1)} %get-tuple-element.70.way) | copy-start | bytes 983044
  216.2 23.7 %copy-start.45 = (f32[640,128]{1,0:T(8,128)S(1)}, f32[640,128]{1,0:T(8,128)}, u32[]{:S(2)}) copy-start(f32[640,128]{1,0:T(8,128)} %copy-done.44) | copy-start | bytes 983044
  227.8 17.9 %copy-start.5 = (bf16[640,640]{1,0:T(8,128)(2,1)S(1)}, bf16[640,640]{1,0:T(8,128)(2,1)}, u32[]{:S(2)}) copy-start(bf16[640,640]{1,0:T(8,128)(2,1)} %copy-done.3) | copy-start | bytes 2457604
  227.8 17.8 %copy-start.8 = (bf16[640,640]{1,0:T(8,128)(2,1)S(1)}, bf16[640,640]{1,0:T(8,128)(2,1)}, u32[]{:S(2)}) copy-start(bf16[640,640]{1,0:T(8,128)(2,1)} %copy-done.6) | copy-start | bytes 2457604
  227.8 17.8 %copy-start.11 = (bf16[640,640]{1,0:T(8,128)(2,1)S(1)}, bf16[640,640]{1,0:T(8,128)(2,1)}, u32[]{:S(2)}) copy-start(bf16[640,640]{1,0:T(8,128)(2,1)} %copy-done.9) | copy-start | bytes 2457604
  227.8 17.8 %copy-start.14 = (bf16[640,640]{1,0:T(8,128)(2,1)S(1)}, bf16[640,640]{1,0:T(8,128)(2,1)}, u32[]{:S(2)}) copy-start(bf16[640,640]{1,0:T(8,128)(2,1)} %copy-done.12) | copy-start | bytes 2457604
  240.8 6.9 %copy-start.37 = (f32[640,128]{1,0:T(8,128)}, f32[640,128]{1,0:T(8,128)S(1)}, u32[]{:S(2)}) copy-start(f32[640,128]{1,0:T(8,128)S(1)} %get-tuple-element.72.field) | copy-start | bytes 983044
  240.8 6.9 %copy-start.50 = (f32[256,128]{1,0:T(8,128)}, f32[256,128]{1,0:T(8,128)S(1)}, u32[]{:S(2)}) copy-start(f32[256,128]{1,0:T(8,128)S(1)} %get-tuple-element.74) | copy-start | bytes 393220
  245.6 2.0 copy-start.21
  245.6 25.8 %copy-start.34 = (f32[640,128]{1,0:T(8,128)S(1)}, f32[640,128]{1,0:T(8,128)}, u32[]{:S(2)}) copy-start(f32[640,128]{1,0:T(8,128)} %copy-done.33) | copy-start | bytes 983044
  247.6 21.1 %all-to-all-start.10 = ((f32[16,40,128]{2,1,0:T(8,128)}), f32[16,40,128]{2,1,0:T(8,128)}, u32[]{:S(2)}, u32[]{:S(2)}) async-start(f32[16,40,128]{2,1,0:T(8,128)} %bitcast.12), calls=%async_computation.10 | async-start | bytes 655360 | tf_op jit(solution)/shard_map/all_to_all | solution.py:263
  253.3 18.2 %collective-permute-start.3 = (f32[256,128]{1,0:T(8,128)}, f32[256,128]{1,0:T(8,128)S(1)}, u32[]{:S(2)}, u32[]{:S(2)}) collective-permute-start(f32[256,128]{1,0:T(8,128)} %copy-done.50), channel_id=1, source_target_pairs={{1,2},{3,4},{5,6},{7,8},{9,10},{11,12},{13,14},{15,16},{17,18},{19... | collective-permute-start | bytes 393224 | tf_op jit(solution)/shard_map/ppermute | solution.py:314
  273.7 34.8 %copy-start.36 = (f32[640,128]{1,0:T(8,128)S(1)}, f32[640,128]{1,0:T(8,128)}, u32[]{:S(2)}) copy-start(f32[640,128]{1,0:T(8,128)} %copy-done.35) | copy-start | bytes 983044
  273.7 34.8 %copy-start.38 = (f32[640,128]{1,0:T(8,128)S(1)}, f32[640,128]{1,0:T(8,128)}, u32[]{:S(2)}) copy-start(f32[640,128]{1,0:T(8,128)} %copy-done.37) | copy-start | bytes 983044
  273.7 34.8 %copy-start.47 = (f32[640,128]{1,0:T(8,128)S(1)}, f32[640,128]{1,0:T(8,128)}, u32[]{:S(2)}) copy-start(f32[640,128]{1,0:T(8,128)} %copy-done.46) | copy-start | bytes 983044
  (11 other events, 12.4 us)

commit v8 on v6

--- a/solution.py
+++ b/solution.py
@@ -11,7 +11,8 @@
 BAND = 128
 ITERS = 3
 OBS = ("x", "y")
-PATCH = ("z", "c")
+Z = ("zh", "zl")
+PATCH = (*Z, "c")
 TILE = 8
 F32, BF16 = jnp.float32, jnp.bfloat16
 
@@ -74,9 +75,9 @@
     for z in range(0, half // share, 2):
         mine = []
         for k in (z, z + 1):
-            start = pl.multiple_of(core[0] * half + k * share, TILE)
+            start = pl.multiple_of((4 * (k // 2) + 2 * core[0] + k % 2) * share, TILE)
             mine.append(green[pl.ds(start, share), :])
-            start = pl.multiple_of((1 - core[0]) * half + k * share, TILE)
+            start = pl.multiple_of((4 * (k // 2) + 2 * (1 - core[0]) + k % 2) * share, TILE)
             send[share * k : share * (k + 1), :] = green[pl.ds(start, share), :]
         rows = slice(share * z, share * (z + 2))
         high[rows, :], low[rows, :] = halves(jnp.concatenate(mine, 0))
@@ -195,16 +196,22 @@
         out[k, share:, :] = last
 
 
+def spread_first(pieces, out):
+    value = summed(pieces)
+    for k in range(out.shape[0]):
+        out[k] = value
+
+
 def put_edge(core, rows, field, edge):
     reach = 2 * BAND
     edge[:reach, :] = jnp.where(core[0] == 0, field[:reach, :], field[rows - reach : rows, :])
 
 
 def start_field(core, every, ids, field, edge):
-    share = every.shape[1] - TILE
+    share = every.shape[1]
     rows, reach = field.shape[0] - TILE, edge.shape[0] - TILE
     for k in range(every.shape[0]):
-        field[share * k : share * (k + 1), :] = every[k, :share, :]
+        field[share * k : share * (k + 1), :] = every[k]
     put_edge(core, rows, field, edge)
     first, last = ids[:, :BAND].astype(F32), ids[:, ids.shape[1] - BAND :].astype(F32)
     field[rows:, :] = jnp.concatenate([first, last, jnp.zeros((TILE - 6, BAND), F32)], 0)
@@ -264,7 +271,7 @@
 def shards(green, data, neighbours, reg_weight):
     row_count, col_count = green.shape
     epochs = data.shape[1]
-    n_obs, n_z, n_core = lax.axis_size(OBS), lax.axis_size("z"), lax.axis_size("c")
+    n_obs, n_z, n_core = lax.axis_size(OBS), lax.axis_size(Z), lax.axis_size("c")
     n_patch = n_z * n_core
     core = lax.axis_index("c")
     piece = col_count // n_obs
@@ -273,7 +280,7 @@
     weight = reg_weight[None]
     share = row_count // n_patch
     core_scalar = core.astype(jnp.int32)[None]
-    row_scalar = (core * n_z + lax.axis_index("z")).astype(jnp.int32)[None]
+    row_scalar = lax.axis_index(("zh", "c", "zl")).astype(jnp.int32)[None]
     place_scalar = lax.axis_index(PATCH).astype(jnp.int32)[None]
     swap = [(0, 1), (1, 0)]
     outward = [(2 * z + 1, 2 * z + 2) for z in range(n_z - 1)]
@@ -297,7 +304,7 @@
     zero_tail = jnp.zeros((TILE, epochs), F32)
     zero_field = jnp.zeros((col_count, epochs), F32)
     spread_shape = ((n_obs, piece + TILE, epochs), F32)
-    (out,) = local_call(spread, [spread_shape], pieces, zero_tail)
+    (out,) = local_call(spread_first, [((n_obs, piece, epochs), F32)], pieces)
     every = exchanged(out, OBS)
     edge_shape = ((reach, epochs), F32)
     long_field, long_edge = ((col_count + TILE, epochs), F32), ((reach + TILE, epochs), F32)
@@ -316,7 +323,7 @@
             pair, own_high, own_low, far_high, far_low,
             scalars=[core_scalar], scratch=[wide],
         )
-        pieces = exchanged(part.reshape(n_z, share, epochs), "z")
+        pieces = exchanged(part.reshape(n_z, share, epochs), Z)
         (part,) = local_call(gathered, [((share, epochs), F32)], pieces)
         if iteration == 0:
             m_matrix = ((col_count, col_count + 2 * reach), BF16)
@@ -340,14 +347,14 @@
             every = exchanged(out, (*OBS, "c"))
             (out,) = local_call(last_spread, [((n_z, TILE, epochs), F32)], every)
             (slip,) = local_call(
-                last_update, [field_shape], exchanged(out, "z"), kept, field, way, slip
+                last_update, [field_shape], exchanged(out, Z), kept, field, way, slip
             )
             return slip
         out, fresh = local_call(
             collect, [((share + TILE, epochs), F32), field_shape], part, *penalty,
             scalars=[core_scalar], scratch=[near],
         )
-        every = lax.all_gather(lax.all_gather(out, "z"), "c")
+        every = lax.all_gather(lax.all_gather(out, "zl"), ("zh", "c"))
         every = every.reshape(n_patch, share + TILE, epochs)
         moved, image, tail, smooth, way, scalars = local_call(
             backward,
@@ -365,7 +372,7 @@
 
 
 def solution(mesh):
-    split = Mesh(mesh.devices.reshape(4, 4, 16, 2), (*OBS, *PATCH))
+    split = Mesh(mesh.devices.reshape(4, 4, 8, 2, 2), (*OBS, *PATCH))
     in_specs = (P(OBS, PATCH), P(OBS, None), P(None, PATCH), P())
 
     return jax.shard_map(

time: 312 us -> 300 us (0.962)
  blocking collectives: 193 us -> 177 us
  starting transfers between devices: 45.6 us -> 50.6 us
    all_gather x4, blocking collectives: 75.2 us -> 59.7 us  [shards(): every = lax.all_gather(lax.all_gather(out, 'zl'), ('zh', 'c'))]
    all_to_all x3, starting transfers between devices: 24.9 us -> 29.6 us  [exchanged(): return lax.all_to_all(pieces, axis, 0, 0, tiled=True)]
where the time goes in v8:
time: 300 us; the launch traced here: 299 us
  blocking collectives  177 us (59%)
  starting transfers between devices  50.6 us (17%)
  waiting for transfers between devices  40.6 us (14%)
  Pallas kernels  19.2 us (6%)
  local copies, waits for them, and re-layouts  11.3 us (4%)
    all_to_all x8, blocking collectives, exchanged(): return lax.all_to_all(pieces, axis, 0, 0, tiled=True)  104 us
    all_gather x4, blocking collectives, shards(): every = lax.all_gather(lax.all_gather(out, 'zl'), ('zh', 'c'))  59.7 us
    all_to_all x3, starting transfers between devices, exchanged(): return lax.all_to_all(pieces, axis, 0, 0, tiled=True)  29.6 us
    all_to_all x3, waiting for transfers between devices, exchanged(): return lax.all_to_all(pieces, axis, 0, 0, tiled=True)  22.9 us
    pallas_call x22, Pallas kernels, local_call(): pl.pallas_call(functools.partial(body, **options), out_shape=[jax.ShapeDt...  19.2 us
    ppermute x3, waiting for transfers between devices, shards(): edge = lax.ppermute(edge, PATCH, outward)  17.6 us
    all_gather x3, blocking collectives, shards(): pair = lax.all_gather(field, 'c')  13.3 us
    ppermute x3, starting transfers between devices, shards(): edge = lax.ppermute(edge, PATCH, outward)  12.1 us
  transfers between devices with their start and end apart: 7, of which 5 were waited for; matrix products, arithmetic and copies ran while one was open for 0% of the time, Pallas kernels for 1%

profile of v8, /device:TPU:1, one launch (start us, length us, event | category | flops | bytes accessed | tf_op | source)
XLA Modules:
  0.0 298.9 jit_solution(18143700039091409968)
XLA Ops:
  0.0 1.9 copy-done.25
  1.9 1.1 copy-done.43
  3.0 1.8 shard_map.46
  4.8 1.2 copy-done.18
  6.0 8.9 %collective-permute-start = (f32[640,640]{1,0:T(8,128)S(1)}, f32[640,640]{1,0:T(8,128)S(1)}, u32[]{:S(2)}, u32[]{:S(2)}) collective-permute-start(f32[640,640]{1,0:T(8,128)S(1)} %get-tuple-element.45), channel_id=1, source_target_pairs={{0,1},{1,0},{2,3},{3,2},{4,5},{5,4},{6,7},{7,6},{8,9},{9,8},{10,11... | collective-permute-start | bytes 4915208 | tf_op jit(solution)/shard_map/ppermute | solution.py:302
  14.9 11.1 %all_to_all.55.pieces = f32[16,40,128]{2,1,0:T(8,128)S(1)} all-to-all(f32[16,40,128]{2,1,0:T(8,128)S(1)} %bitcast.24), channel_id=1, replica_groups=mesh['x'=4,'y'=4,'zh'=8,'zl'=2,'c'=2] {'x','y'}, dimensions={0} | all-to-all | bytes 655360 | tf_op jit(solution)/shard_map/all_to_all | solution.py:268
  26.0 11.6 %all_to_all.56.every = f32[16,40,128]{2,1,0:T(8,128)S(1)} all-to-all(f32[16,40,128]{2,1,0:T(8,128)S(1)} %shard_map.47), channel_id=1, replica_groups=mesh['x'=4,'y'=4,'zh'=8,'zl'=2,'c'=2] {'x','y'}, dimensions={0} | all-to-all | bytes 655360 | tf_op jit(solution)/shard_map/all_to_all | solution.py:268
  37.7 4.2 %all-gather = f32[1296,128]{1,0:T(8,128)S(1)} all-gather(f32[648,128]{1,0:T(8,128)S(1)} %get-tuple-element.42.field.old_field), channel_id=2, replica_groups=mesh['x'=4,'y'=4,'zh'=8,'zl'=2,'c'=2] {'c'}, dimensions={0}, use_global_device_ids=true | all-gather | bytes 995328 | tf_op jit(solution)/shard_map/all_gather | solution.py:320
  42.2 2.0 shard_map.50
  44.2 13.6 %all-to-all-start.2 = ((f32[16,40,128]{2,1,0:T(8,128)}), f32[16,40,128]{2,1,0:T(8,128)}, u32[]{:S(2)}, u32[]{:S(2)}) async-start(f32[16,40,128]{2,1,0:T(8,128)} %bitcast.5), calls=%async_computation.2 | async-start | bytes 655360 | tf_op jit(solution)/shard_map/all_to_all | solution.py:268
  57.8 4.0 %collective-permute-start.1 = (f32[264,128]{1,0:T(8,128)S(1)}, f32[264,128]{1,0:T(8,128)S(1)}, u32[]{:S(2)}, u32[]{:S(2)}) collective-permute-start(f32[264,128]{1,0:T(8,128)S(1)} %get-tuple-element.48), channel_id=1, source_target_pairs={{1,2},{3,4},{5,6},{7,8},{9,10},{11,12},{13,14},{15,16},{17,18},{19... | collective-permute-start | bytes 405512 | tf_op jit(solution)/shard_map/ppermute | solution.py:319
  61.8 14.2 %collective-permute-done.1.edge = f32[264,128]{1,0:T(8,128)S(1)} collective-permute-done((f32[264,128]{1,0:T(8,128)S(1)}, f32[264,128]{1,0:T(8,128)S(1)}, u32[]{:S(2)}, u32[]{:S(2)}) %collective-permute-start.1) | collective-permute-done | bytes 135200 | tf_op jit(solution)/shard_map/ppermute | solution.py:319
  76.0 1.1 copy-done.1
  77.1 1.8 shard_map.52
  78.9 1.0 shard_map.51.part
  79.9 1.1 copy-done.2
  81.0 1.2 shard_map.53
  82.2 3.3 %all-gather.1 = f32[96,128]{1,0:T(8,128)S(1)} all-gather(f32[48,128]{1,0:T(8,128)S(1)} %get-tuple-element.51), channel_id=3, replica_groups=mesh['x'=4,'y'=4,'zh'=8,'zl'=2,'c'=2] {'zl'}, dimensions={0}, use_global_device_ids=true | all-gather | bytes 73728 | tf_op jit(solution)/shard_map/all_gather | solution.py:357
  85.6 25.0 %all-gather.2.every = f32[32,48,128]{2,1,0:T(8,128)S(1)} all-gather(f32[2,48,128]{2,1,0:T(8,128)S(1)} %bitcast.29), channel_id=4, replica_groups=mesh['x'=4,'y'=4,'zh'=8,'zl'=2,'c'=2] {'zh','c'}, dimensions={0}, use_global_device_ids=true | all-gather | bytes 835584 | tf_op jit(solution)/shard_map/all_gather | solution.py:357
  110.6 1.2 shard_map.54
  111.9 11.3 %all_to_all.57.pieces = f32[16,40,128]{2,1,0:T(8,128)S(1)} all-to-all(f32[16,40,128]{2,1,0:T(8,128)S(1)} %bitcast.25), channel_id=1, replica_groups=mesh['x'=4,'y'=4,'zh'=8,'zl'=2,'c'=2] {'x','y'}, dimensions={0} | all-to-all | bytes 655360 | tf_op jit(solution)/shard_map/all_to_all | solution.py:268
  123.3 12.3 %all_to_all.58.every = f32[16,48,128]{2,1,0:T(8,128)S(1)} all-to-all(f32[16,48,128]{2,1,0:T(8,128)S(1)} %shard_map.55), channel_id=1, replica_groups=mesh['x'=4,'y'=4,'zh'=8,'zl'=2,'c'=2] {'x','y'}, dimensions={0} | all-to-all | bytes 786432 | tf_op jit(solution)/shard_map/all_to_all | solution.py:268
  135.7 4.5 %all-gather.3 = f32[1280,128]{1,0:T(8,128)S(1)} all-gather(f32[640,128]{1,0:T(8,128)S(1)} %get-tuple-element.60.field.old_field), channel_id=5, replica_groups=mesh['x'=4,'y'=4,'zh'=8,'zl'=2,'c'=2] {'c'}, dimensions={0}, use_global_device_ids=true | all-gather | bytes 983040 | tf_op jit(solution)/shard_map/all_gather | solution.py:320
  140.3 1.3 shard_map.57
  142.3 8.7 %all-to-all-start.5 = ((f32[16,40,128]{2,1,0:T(8,128)}), f32[16,40,128]{2,1,0:T(8,128)}, u32[]{:S(2)}, u32[]{:S(2)}) async-start(f32[16,40,128]{2,1,0:T(8,128)} %bitcast.22), calls=%async_computation.5 | async-start | bytes 655360 | tf_op jit(solution)/shard_map/all_to_all | solution.py:268
  151.0 4.0 %collective-permute-start.2 = (f32[256,128]{1,0:T(8,128)}, f32[256,128]{1,0:T(8,128)S(1)}, u32[]{:S(2)}, u32[]{:S(2)}) collective-permute-start(f32[256,128]{1,0:T(8,128)} %copy-done.51), channel_id=1, source_target_pairs={{1,2},{3,4},{5,6},{7,8},{9,10},{11,12},{13,14},{15,16},{17,18},{19... | collective-permute-start | bytes 393224 | tf_op jit(solution)/shard_map/ppermute | solution.py:319
  155.1 11.5 %all-to-all-done.5.pieces = f32[16,40,128]{2,1,0:T(8,128)} async-done(((f32[16,40,128]{2,1,0:T(8,128)}), f32[16,40,128]{2,1,0:T(8,128)}, u32[]{:S(2)}, u32[]{:S(2)}) %all-to-all-start.5) | async-done | bytes 327712 | tf_op jit(solution)/shard_map/all_to_all | solution.py:268
  166.6 1.0 shard_map.58.part
  167.6 1.7 collective-permute-done.2.edge
  169.3 1.1 copy-done.24
  170.4 1.2 shard_map.59
  171.6 5.4 %all-gather.4 = f32[96,128]{1,0:T(8,128)S(1)} all-gather(f32[48,128]{1,0:T(8,128)S(1)} %get-tuple-element.62), channel_id=6, replica_groups=mesh['x'=4,'y'=4,'zh'=8,'zl'=2,'c'=2] {'zl'}, dimensions={0}, use_global_device_ids=true | all-gather | bytes 73728 | tf_op jit(solution)/shard_map/all_gather | solution.py:357
  176.9 26.0 %all-gather.5.every = f32[32,48,128]{2,1,0:T(8,128)S(1)} all-gather(f32[2,48,128]{2,1,0:T(8,128)S(1)} %bitcast.30), channel_id=7, replica_groups=mesh['x'=4,'y'=4,'zh'=8,'zl'=2,'c'=2] {'zh','c'}, dimensions={0}, use_global_device_ids=true | all-gather | bytes 835584 | tf_op jit(solution)/shard_map/all_gather | solution.py:357
  203.0 1.2 shard_map.60
  204.2 11.5 %all_to_all.59.pieces = f32[16,40,128]{2,1,0:T(8,128)S(1)} all-to-all(f32[16,40,128]{2,1,0:T(8,128)S(1)} %bitcast.23), channel_id=1, replica_groups=mesh['x'=4,'y'=4,'zh'=8,'zl'=2,'c'=2] {'x','y'}, dimensions={0} | all-to-all | bytes 655360 | tf_op jit(solution)/shard_map/all_to_all | solution.py:268
  215.9 12.3 %all_to_all.60.every = f32[16,48,128]{2,1,0:T(8,128)S(1)} all-to-all(f32[16,48,128]{2,1,0:T(8,128)S(1)} %shard_map.61), channel_id=1, replica_groups=mesh['x'=4,'y'=4,'zh'=8,'zl'=2,'c'=2] {'x','y'}, dimensions={0} | all-to-all | bytes 786432 | tf_op jit(solution)/shard_map/all_to_all | solution.py:268
  229.0 4.5 %all-gather.6 = f32[1280,128]{1,0:T(8,128)S(1)} all-gather(f32[640,128]{1,0:T(8,128)S(1)} %get-tuple-element.72.field), channel_id=8, replica_groups=mesh['x'=4,'y'=4,'zh'=8,'zl'=2,'c'=2] {'c'}, dimensions={0}, use_global_device_ids=true | all-gather | bytes 983040 | tf_op jit(solution)/shard_map/all_gather | solution.py:320
  233.6 2.0 shard_map.63
  235.6 7.3 %all-to-all-start.8 = ((f32[16,40,128]{2,1,0:T(8,128)}), f32[16,40,128]{2,1,0:T(8,128)}, u32[]{:S(2)}, u32[]{:S(2)}) async-start(f32[16,40,128]{2,1,0:T(8,128)} %bitcast.14), calls=%async_computation.8 | async-start | bytes 655360 | tf_op jit(solution)/shard_map/all_to_all | solution.py:268
  242.9 4.0 %collective-permute-start.3 = (f32[256,128]{1,0:T(8,128)}, f32[256,128]{1,0:T(8,128)S(1)}, u32[]{:S(2)}, u32[]{:S(2)}) collective-permute-start(f32[256,128]{1,0:T(8,128)} %copy-done.50), channel_id=1, source_target_pairs={{1,2},{3,4},{5,6},{7,8},{9,10},{11,12},{13,14},{15,16},{17,18},{19... | collective-permute-start | bytes 393224 | tf_op jit(solution)/shard_map/ppermute | solution.py:319
  247.0 11.5 %all-to-all-done.8.pieces = f32[16,40,128]{2,1,0:T(8,128)} async-done(((f32[16,40,128]{2,1,0:T(8,128)}), f32[16,40,128]{2,1,0:T(8,128)}, u32[]{:S(2)}, u32[]{:S(2)}) %all-to-all-start.8) | async-done | bytes 327712 | tf_op jit(solution)/shard_map/all_to_all | solution.py:268
  258.4 1.0 shard_map.64.share_ref
  259.4 1.7 collective-permute-done.3.edge
  261.1 1.1 copy-done.22
  262.2 1.1 copy-done.42
  263.3 1.2 shard_map.65
  264.5 18.5 %all_to_all.61.every = f32[32,8,128]{2,1,0:T(8,128)S(1)} all-to-all(f32[32,8,128]{2,1,0:T(8,128)S(1)} %shard_map.65), channel_id=1, replica_groups=mesh['x'=4,'y'=4,'zh'=8,'zl'=2,'c'=2] {'x','y','c'}, dimensions={0} | all-to-all | bytes 262144 | tf_op jit(solution)/shard_map/all_to_all | solution.py:268
  283.1 15.0 %all_to_all.62.every = f32[16,8,128]{2,1,0:T(8,128)S(1)} all-to-all(f32[16,8,128]{2,1,0:T(8,128)S(1)} %shard_map.66), channel_id=1, replica_groups=mesh['x'=4,'y'=4,'zh'=8,'zl'=2,'c'=2] {'zh','zl'}, dimensions={0} | all-to-all | bytes 131072 | tf_op jit(solution)/shard_map/all_to_all | solution.py:268
  (110 shorter events, 3.1 us)
Async XLA Ops:
  6.0 35.9 %copy-start.15 = (bf16[640,1280]{1,0:T(8,128)(2,1)}, bf16[640,1280]{1,0:T(8,128)(2,1)S(1)}, u32[]{:S(2)}) copy-start(bf16[640,1280]{1,0:T(8,128)(2,1)S(1)} %get-tuple-element.53.high) | copy-start | bytes 4915204
  6.0 36.2 %copy-start.3 = (bf16[640,640]{1,0:T(8,128)(2,1)}, bf16[640,640]{1,0:T(8,128)(2,1)S(1)}, u32[]{:S(2)}) copy-start(bf16[640,640]{1,0:T(8,128)(2,1)S(1)} %get-tuple-element.43.own_high) | copy-start | bytes 2457604
  6.0 36.2 %copy-start.6 = (bf16[640,640]{1,0:T(8,128)(2,1)}, bf16[640,640]{1,0:T(8,128)(2,1)S(1)}, u32[]{:S(2)}) copy-start(bf16[640,640]{1,0:T(8,128)(2,1)S(1)} %get-tuple-element.44.own_low) | copy-start | bytes 2457604
  6.0 31.6 %copy-start.48 = (s32[3,640]{1,0:T(4,128)S(1)}, s32[3,640]{1,0:T(4,128)}, u32[]{:S(2)}) copy-start(s32[3,640]{1,0:T(4,128)} %ids.3) | copy-start | bytes 23044
  6.0 35.9 %collective-permute-start = (f32[640,640]{1,0:T(8,128)S(1)}, f32[640,640]{1,0:T(8,128)S(1)}, u32[]{:S(2)}, u32[]{:S(2)}) collective-permute-start(f32[640,640]{1,0:T(8,128)S(1)} %get-tuple-element.45), channel_id=1, source_target_pairs={{0,1},{1,0},{2,3},{3,2},{4,5},{5,4},{6,7},{7,6},{8,9},{9,8},{10,11... | collective-permute-start | bytes 4915208 | tf_op jit(solution)/shard_map/ppermute | solution.py:302
  41.9 2.3 copy-start
  42.1 2.0 copy-start.9
  42.1 2.0 copy-start.12
  44.2 35.8 %copy-start.49 = (f32[128]{0:T(128)S(1)}, f32[128]{0:T(128)}, u32[]{:S(2)}) copy-start(f32[128]{0:T(128)} %param.7) | copy-start | bytes 1540
  44.2 34.7 %all-to-all-start.2 = ((f32[16,40,128]{2,1,0:T(8,128)}), f32[16,40,128]{2,1,0:T(8,128)}, u32[]{:S(2)}, u32[]{:S(2)}) async-start(f32[16,40,128]{2,1,0:T(8,128)} %bitcast.5), calls=%async_computation.2 | async-start | bytes 655360 | tf_op jit(solution)/shard_map/all_to_all | solution.py:268
  57.8 18.3 %collective-permute-start.1 = (f32[264,128]{1,0:T(8,128)S(1)}, f32[264,128]{1,0:T(8,128)S(1)}, u32[]{:S(2)}, u32[]{:S(2)}) collective-permute-start(f32[264,128]{1,0:T(8,128)S(1)} %get-tuple-element.48), channel_id=1, source_target_pairs={{1,2},{3,4},{5,6},{7,8},{9,10},{11,12},{13,14},{15,16},{17,18},{19... | collective-permute-start | bytes 405512 | tf_op jit(solution)/shard_map/ppermute | solution.py:319
  81.0 29.6 %copy-start.16 = (bf16[640,1280]{1,0:T(8,128)(2,1)S(1)}, bf16[640,1280]{1,0:T(8,128)(2,1)}, u32[]{:S(2)}) copy-start(bf16[640,1280]{1,0:T(8,128)(2,1)} %copy-done.15) | copy-start | bytes 4915204
  81.0 29.6 %copy-start.19 = (bf16[640,1280]{1,0:T(8,128)(2,1)S(1)}, bf16[640,1280]{1,0:T(8,128)(2,1)}, u32[]{:S(2)}) copy-start(bf16[640,1280]{1,0:T(8,128)(2,1)} %copy-done.18) | copy-start | bytes 4915204
  111.8 23.7 %copy-start.39 = (f32[1280,128]{1,0:T(8,128)}, f32[1280,128]{1,0:T(8,128)S(1)}, u32[]{:S(2)}) copy-start(f32[1280,128]{1,0:T(8,128)S(1)} %get-tuple-element.64.old_image) | copy-start | bytes 1966084
  111.8 23.8 %copy-start.28 = (f32[640,128]{1,0:T(8,128)}, f32[640,128]{1,0:T(8,128)S(1)}, u32[]{:S(2)}) copy-start(f32[640,128]{1,0:T(8,128)S(1)} %get-tuple-element.58.smooth.old_smooth) | copy-start | bytes 983044
  111.9 23.8 %copy-start.31 = (f32[640,128]{1,0:T(8,128)}, f32[640,128]{1,0:T(8,128)S(1)}, u32[]{:S(2)}) copy-start(f32[640,128]{1,0:T(8,128)S(1)} %get-tuple-element.59.way.old_way) | copy-start | bytes 983044
  123.3 17.0 %copy-start.4 = (bf16[640,640]{1,0:T(8,128)(2,1)S(1)}, bf16[640,640]{1,0:T(8,128)(2,1)}, u32[]{:S(2)}) copy-start(bf16[640,640]{1,0:T(8,128)(2,1)} %copy-done.3) | copy-start | bytes 2457604
  123.3 17.0 %copy-start.7 = (bf16[640,640]{1,0:T(8,128)(2,1)S(1)}, bf16[640,640]{1,0:T(8,128)(2,1)}, u32[]{:S(2)}) copy-start(bf16[640,640]{1,0:T(8,128)(2,1)} %copy-done.6) | copy-start | bytes 2457604
  123.3 17.0 %copy-start.10 = (bf16[640,640]{1,0:T(8,128)(2,1)S(1)}, bf16[640,640]{1,0:T(8,128)(2,1)}, u32[]{:S(2)}) copy-start(bf16[640,640]{1,0:T(8,128)(2,1)} %copy-done.9) | copy-start | bytes 2457604
  123.3 17.0 %copy-start.13 = (bf16[640,640]{1,0:T(8,128)(2,1)S(1)}, bf16[640,640]{1,0:T(8,128)(2,1)}, u32[]{:S(2)}) copy-start(bf16[640,640]{1,0:T(8,128)(2,1)} %copy-done.12) | copy-start | bytes 2457604
  135.7 5.9 %copy-start.26 = (f32[640,128]{1,0:T(8,128)}, f32[640,128]{1,0:T(8,128)S(1)}, u32[]{:S(2)}) copy-start(f32[640,128]{1,0:T(8,128)S(1)} %get-tuple-element.60.field.old_field) | copy-start | bytes 983044
  135.7 5.9 %copy-start.44 = (f32[640,128]{1,0:T(8,128)}, f32[640,128]{1,0:T(8,128)S(1)}, u32[]{:S(2)}) copy-start(f32[640,128]{1,0:T(8,128)S(1)} %get-tuple-element.71.old_slip) | copy-start | bytes 983044
  135.7 5.9 %copy-start.51 = (f32[256,128]{1,0:T(8,128)}, f32[256,128]{1,0:T(8,128)S(1)}, u32[]{:S(2)}) copy-start(f32[256,128]{1,0:T(8,128)S(1)} %get-tuple-element.61) | copy-start | bytes 393220
  140.3 29.0 %copy-start.29 = (f32[640,128]{1,0:T(8,128)S(1)}, f32[640,128]{1,0:T(8,128)}, u32[]{:S(2)}) copy-start(f32[640,128]{1,0:T(8,128)} %copy-done.28) | copy-start | bytes 983044
  142.3 24.2 %all-to-all-start.5 = ((f32[16,40,128]{2,1,0:T(8,128)}), f32[16,40,128]{2,1,0:T(8,128)}, u32[]{:S(2)}, u32[]{:S(2)}) async-start(f32[16,40,128]{2,1,0:T(8,128)} %bitcast.22), calls=%async_computation.5 | async-start | bytes 655360 | tf_op jit(solution)/shard_map/all_to_all | solution.py:268
  151.0 18.2 %collective-permute-start.2 = (f32[256,128]{1,0:T(8,128)}, f32[256,128]{1,0:T(8,128)S(1)}, u32[]{:S(2)}, u32[]{:S(2)}) collective-permute-start(f32[256,128]{1,0:T(8,128)} %copy-done.51), channel_id=1, source_target_pairs={{1,2},{3,4},{5,6},{7,8},{9,10},{11,12},{13,14},{15,16},{17,18},{19... | collective-permute-start | bytes 393224 | tf_op jit(solution)/shard_map/ppermute | solution.py:319
  167.6 35.4 %copy-start.17 = (bf16[640,1280]{1,0:T(8,128)(2,1)S(1)}, bf16[640,1280]{1,0:T(8,128)(2,1)}, u32[]{:S(2)}) copy-start(bf16[640,1280]{1,0:T(8,128)(2,1)} %copy-done.15) | copy-start | bytes 4915204
  167.6 35.4 %copy-start.20 = (bf16[640,1280]{1,0:T(8,128)(2,1)S(1)}, bf16[640,1280]{1,0:T(8,128)(2,1)}, u32[]{:S(2)}) copy-start(bf16[640,1280]{1,0:T(8,128)(2,1)} %copy-done.18) | copy-start | bytes 4915204
  170.4 32.6 %copy-start.27 = (f32[640,128]{1,0:T(8,128)S(1)}, f32[640,128]{1,0:T(8,128)}, u32[]{:S(2)}) copy-start(f32[640,128]{1,0:T(8,128)} %copy-done.26) | copy-start | bytes 983044
  170.4 32.6 %copy-start.32 = (f32[640,128]{1,0:T(8,128)S(1)}, f32[640,128]{1,0:T(8,128)}, u32[]{:S(2)}) copy-start(f32[640,128]{1,0:T(8,128)} %copy-done.31) | copy-start | bytes 983044
  170.4 32.6 %copy-start.40 = (f32[1280,128]{1,0:T(8,128)S(1)}, f32[1280,128]{1,0:T(8,128)}, u32[]{:S(2)}) copy-start(f32[1280,128]{1,0:T(8,128)} %copy-done.39) | copy-start | bytes 1966084
  204.2 24.0 %copy-start.33 = (f32[640,128]{1,0:T(8,128)}, f32[640,128]{1,0:T(8,128)S(1)}, u32[]{:S(2)}) copy-start(f32[640,128]{1,0:T(8,128)S(1)} %get-tuple-element.69.smooth) | copy-start | bytes 983044
  204.2 24.0 %copy-start.35 = (f32[640,128]{1,0:T(8,128)}, f32[640,128]{1,0:T(8,128)S(1)}, u32[]{:S(2)}) copy-start(f32[640,128]{1,0:T(8,128)S(1)} %get-tuple-element.70.way) | copy-start | bytes 983044
  204.2 24.0 %copy-start.41 = (f32[1280,128]{1,0:T(8,128)}, f32[1280,128]{1,0:T(8,128)S(1)}, u32[]{:S(2)}) copy-start(f32[1280,128]{1,0:T(8,128)S(1)} %get-tuple-element.73.image) | copy-start | bytes 1966084
  204.2 23.9 %copy-start.45 = (f32[640,128]{1,0:T(8,128)S(1)}, f32[640,128]{1,0:T(8,128)}, u32[]{:S(2)}) copy-start(f32[640,128]{1,0:T(8,128)} %copy-done.44) | copy-start | bytes 983044
  215.8 17.7 %copy-start.5 = (bf16[640,640]{1,0:T(8,128)(2,1)S(1)}, bf16[640,640]{1,0:T(8,128)(2,1)}, u32[]{:S(2)}) copy-start(bf16[640,640]{1,0:T(8,128)(2,1)} %copy-done.3) | copy-start | bytes 2457604
  215.8 17.7 %copy-start.8 = (bf16[640,640]{1,0:T(8,128)(2,1)S(1)}, bf16[640,640]{1,0:T(8,128)(2,1)}, u32[]{:S(2)}) copy-start(bf16[640,640]{1,0:T(8,128)(2,1)} %copy-done.6) | copy-start | bytes 2457604
  215.9 17.7 %copy-start.11 = (bf16[640,640]{1,0:T(8,128)(2,1)S(1)}, bf16[640,640]{1,0:T(8,128)(2,1)}, u32[]{:S(2)}) copy-start(bf16[640,640]{1,0:T(8,128)(2,1)} %copy-done.9) | copy-start | bytes 2457604
  215.9 17.7 %copy-start.14 = (bf16[640,640]{1,0:T(8,128)(2,1)S(1)}, bf16[640,640]{1,0:T(8,128)(2,1)}, u32[]{:S(2)}) copy-start(bf16[640,640]{1,0:T(8,128)(2,1)} %copy-done.12) | copy-start | bytes 2457604
  229.0 4.5 %copy-start.50 = (f32[256,128]{1,0:T(8,128)}, f32[256,128]{1,0:T(8,128)S(1)}, u32[]{:S(2)}) copy-start(f32[256,128]{1,0:T(8,128)S(1)} %get-tuple-element.74) | copy-start | bytes 393220
  229.0 6.6 %copy-start.37 = (f32[640,128]{1,0:T(8,128)}, f32[640,128]{1,0:T(8,128)S(1)}, u32[]{:S(2)}) copy-start(f32[640,128]{1,0:T(8,128)S(1)} %get-tuple-element.72.field) | copy-start | bytes 983044
  233.5 2.0 copy-start.21
  233.6 27.6 %copy-start.34 = (f32[640,128]{1,0:T(8,128)S(1)}, f32[640,128]{1,0:T(8,128)}, u32[]{:S(2)}) copy-start(f32[640,128]{1,0:T(8,128)} %copy-done.33) | copy-start | bytes 983044
  235.6 22.9 %all-to-all-start.8 = ((f32[16,40,128]{2,1,0:T(8,128)}), f32[16,40,128]{2,1,0:T(8,128)}, u32[]{:S(2)}, u32[]{:S(2)}) async-start(f32[16,40,128]{2,1,0:T(8,128)} %bitcast.14), calls=%async_computation.8 | async-start | bytes 655360 | tf_op jit(solution)/shard_map/all_to_all | solution.py:268
  242.9 18.2 %collective-permute-start.3 = (f32[256,128]{1,0:T(8,128)}, f32[256,128]{1,0:T(8,128)S(1)}, u32[]{:S(2)}, u32[]{:S(2)}) collective-permute-start(f32[256,128]{1,0:T(8,128)} %copy-done.50), channel_id=1, source_target_pairs={{1,2},{3,4},{5,6},{7,8},{9,10},{11,12},{13,14},{15,16},{17,18},{19... | collective-permute-start | bytes 393224 | tf_op jit(solution)/shard_map/ppermute | solution.py:319
  263.3 34.8 %copy-start.36 = (f32[640,128]{1,0:T(8,128)S(1)}, f32[640,128]{1,0:T(8,128)}, u32[]{:S(2)}) copy-start(f32[640,128]{1,0:T(8,128)} %copy-done.35) | copy-start | bytes 983044
  263.3 34.8 %copy-start.38 = (f32[640,128]{1,0:T(8,128)S(1)}, f32[640,128]{1,0:T(8,128)}, u32[]{:S(2)}) copy-start(f32[640,128]{1,0:T(8,128)} %copy-done.37) | copy-start | bytes 983044
  263.3 34.8 %copy-start.47 = (f32[640,128]{1,0:T(8,128)S(1)}, f32[640,128]{1,0:T(8,128)}, u32[]{:S(2)}) copy-start(f32[640,128]{1,0:T(8,128)} %copy-done.46) | copy-start | bytes 983044
  (11 other events, 12.5 us)

commit v9 on v8

--- a/solution.py
+++ b/solution.py
@@ -72,12 +72,13 @@
     store_halves(wide, 0, data[...])
     moved[...] = product(back_high, back_low, wide[...])
     half = send.shape[0]
+    far_count = half // (2 * share)
     for z in range(0, half // share, 2):
         mine = []
         for k in (z, z + 1):
-            start = pl.multiple_of((4 * (k // 2) + 2 * core[0] + k % 2) * share, TILE)
+            start = pl.multiple_of((4 * (k % far_count) + 2 * core[0] + k // far_count) * share, TILE)
             mine.append(green[pl.ds(start, share), :])
-            start = pl.multiple_of((4 * (k // 2) + 2 * (1 - core[0]) + k % 2) * share, TILE)
+            start = pl.multiple_of((4 * (k % far_count) + 2 * (1 - core[0]) + k // far_count) * share, TILE)
             send[share * k : share * (k + 1), :] = green[pl.ds(start, share), :]
         rows = slice(share * z, share * (z + 2))
         high[rows, :], low[rows, :] = halves(jnp.concatenate(mine, 0))
@@ -323,7 +324,9 @@
             pair, own_high, own_low, far_high, far_low,
             scalars=[core_scalar], scratch=[wide],
         )
-        pieces = exchanged(part.reshape(n_z, share, epochs), Z)
+        pieces = exchanged(part.reshape(2, half // 2, epochs), "zl")
+        (part,) = local_call(gathered, [((half // 2, epochs), F32)], pieces)
+        pieces = exchanged(part.reshape(n_z // 2, share, epochs), "zh")
         (part,) = local_call(gathered, [((share, epochs), F32)], pieces)
         if iteration == 0:
             m_matrix = ((col_count, col_count + 2 * reach), BF16)

time: 300 us -> 306 us (1.020)
  blocking collectives: 177 us -> 198 us
  waiting for transfers between devices: 40.6 us -> 28.1 us
  starting transfers between devices: 50.6 us -> 45.7 us
  local copies, waits for them, and re-layouts: 11.3 us -> 14.6 us
    all_to_all x8 -> x11, blocking collectives: 104 us -> 124 us  [exchanged(): return lax.all_to_all(pieces, axis, 0, 0, tiled=True)]
    ppermute x3, waiting for transfers between devices: 17.6 us -> 5.68 us  [shards(): edge = lax.ppermute(edge, PATCH, outward)]
    unnamed x104 -> x110, local copies, waits for them, and re-layouts: 11.3 us -> 14.5 us
    pallas_call x22 -> x25, Pallas kernels: 19.2 us -> 17.6 us  [local_call(): pl.pallas_call(functools.partial(body, **options), out_shape=[jax.ShapeDt...]
  transfers between devices with their start and end apart: 7 -> 7, of which waited for: 5 -> 4; matrix products, arithmetic and copies ran while one was open for 0% -> 0% of each run, Pallas kernels for 1% -> 1%
where the time goes in v9:
time: 306 us; the launch traced here: 305 us
  blocking collectives  198 us (65%)
  starting transfers between devices  45.7 us (15%)
  waiting for transfers between devices  28.1 us (9%)
  Pallas kernels  17.6 us (6%)
  local copies, waits for them, and re-layouts  14.6 us (5%)
    all_to_all x11, blocking collectives, exchanged(): return lax.all_to_all(pieces, axis, 0, 0, tiled=True)  124 us
    all_gather x4, blocking collectives, shards(): every = lax.all_gather(lax.all_gather(out, 'zl'), ('zh', 'c'))  60.3 us
    all_to_all x3, starting transfers between devices, exchanged(): return lax.all_to_all(pieces, axis, 0, 0, tiled=True)  26.7 us
    all_to_all x3, waiting for transfers between devices, exchanged(): return lax.all_to_all(pieces, axis, 0, 0, tiled=True)  22.4 us
    pallas_call x25, Pallas kernels, local_call(): pl.pallas_call(functools.partial(body, **options), out_shape=[jax.ShapeDt...  17.6 us
    unnamed x110, local copies, waits for them, and re-layouts  14.5 us
    all_gather x3, blocking collectives, shards(): pair = lax.all_gather(field, 'c')  13.3 us
    ppermute x3, starting transfers between devices, shards(): edge = lax.ppermute(edge, PATCH, outward)  10.2 us
  transfers between devices with their start and end apart: 7, of which 4 were waited for; matrix products, arithmetic and copies ran while one was open for 0% of the time, Pallas kernels for 1%

profile of v9, /device:TPU:1, one launch (start us, length us, event | category | flops | bytes accessed | tf_op | source)
XLA Modules:
  0.0 304.7 jit_solution(12893273386090735713)
XLA Ops:
  0.0 1.9 copy-done.25
  1.9 1.1 copy-done.44
  3.0 1.8 shard_map.46
  4.8 1.2 copy-done.18
  6.0 8.9 %collective-permute-start = (f32[640,640]{1,0:T(8,128)S(1)}, f32[640,640]{1,0:T(8,128)S(1)}, u32[]{:S(2)}, u32[]{:S(2)}) collective-permute-start(f32[640,640]{1,0:T(8,128)S(1)} %get-tuple-element.45), channel_id=1, source_target_pairs={{0,1},{1,0},{2,3},{3,2},{4,5},{5,4},{6,7},{7,6},{8,9},{9,8},{10,11... | collective-permute-start | bytes 4915208 | tf_op jit(solution)/shard_map/ppermute | solution.py:303
  14.9 11.1 %all_to_all.70.pieces = f32[16,40,128]{2,1,0:T(8,128)S(1)} all-to-all(f32[16,40,128]{2,1,0:T(8,128)S(1)} %bitcast.31), channel_id=1, replica_groups=mesh['x'=4,'y'=4,'zh'=8,'zl'=2,'c'=2] {'x','y'}, dimensions={0} | all-to-all | bytes 655360 | tf_op jit(solution)/shard_map/all_to_all | solution.py:269
  26.0 11.6 %all_to_all.71.every = f32[16,40,128]{2,1,0:T(8,128)S(1)} all-to-all(f32[16,40,128]{2,1,0:T(8,128)S(1)} %shard_map.47), channel_id=1, replica_groups=mesh['x'=4,'y'=4,'zh'=8,'zl'=2,'c'=2] {'x','y'}, dimensions={0} | all-to-all | bytes 655360 | tf_op jit(solution)/shard_map/all_to_all | solution.py:269
  37.7 4.2 %all-gather = f32[1296,128]{1,0:T(8,128)S(1)} all-gather(f32[648,128]{1,0:T(8,128)S(1)} %get-tuple-element.42.field.old_field), channel_id=2, replica_groups=mesh['x'=4,'y'=4,'zh'=8,'zl'=2,'c'=2] {'c'}, dimensions={0}, use_global_device_ids=true | all-gather | bytes 995328 | tf_op jit(solution)/shard_map/all_gather | solution.py:321
  42.2 1.3 shard_map.50
  43.5 8.0 %all_to_all.72.pieces = f32[2,320,128]{2,1,0:T(8,128)S(1)} all-to-all(f32[2,320,128]{2,1,0:T(8,128)S(1)} %bitcast.26), channel_id=1, replica_groups=mesh['x'=4,'y'=4,'zh'=8,'zl'=2,'c'=2] {'zl'}, dimensions={0} | all-to-all | bytes 655360 | tf_op jit(solution)/shard_map/all_to_all | solution.py:269
  52.2 13.4 %all-to-all-start.3 = ((f32[8,40,128]{2,1,0:T(8,128)}), f32[8,40,128]{2,1,0:T(8,128)S(1)}, u32[]{:S(2)}, u32[]{:S(2)}) async-start(f32[8,40,128]{2,1,0:T(8,128)} %bitcast.6), calls=%async_computation.3 | async-start | bytes 327680 | tf_op jit(solution)/shard_map/all_to_all | solution.py:269
  65.6 3.3 %collective-permute-start.1 = (f32[264,128]{1,0:T(8,128)S(1)}, f32[264,128]{1,0:T(8,128)S(1)}, u32[]{:S(2)}, u32[]{:S(2)}) collective-permute-start(f32[264,128]{1,0:T(8,128)S(1)} %get-tuple-element.48), channel_id=1, source_target_pairs={{1,2},{3,4},{5,6},{7,8},{9,10},{11,12},{13,14},{15,16},{17,18},{19... | collective-permute-start | bytes 405512 | tf_op jit(solution)/shard_map/ppermute | solution.py:320
  68.9 5.7 %collective-permute-done.1.edge = f32[264,128]{1,0:T(8,128)S(1)} collective-permute-done((f32[264,128]{1,0:T(8,128)S(1)}, f32[264,128]{1,0:T(8,128)S(1)}, u32[]{:S(2)}, u32[]{:S(2)}) %collective-permute-start.1) | collective-permute-done | bytes 135200 | tf_op jit(solution)/shard_map/ppermute | solution.py:320
  74.6 1.1 copy-done.1
  75.7 1.8 shard_map.53
  78.1 1.7 all-to-all-done.3.pieces
  79.8 1.1 copy-done.2
  80.9 0.9 copy-done.46
  81.8 1.2 shard_map.54
  83.0 3.3 %all-gather.1 = f32[96,128]{1,0:T(8,128)S(1)} all-gather(f32[48,128]{1,0:T(8,128)S(1)} %get-tuple-element.51), channel_id=3, replica_groups=mesh['x'=4,'y'=4,'zh'=8,'zl'=2,'c'=2] {'zl'}, dimensions={0}, use_global_device_ids=true | all-gather | bytes 73728 | tf_op jit(solution)/shard_map/all_gather | solution.py:360
  86.4 26.5 %all-gather.2.every = f32[32,48,128]{2,1,0:T(8,128)S(1)} all-gather(f32[2,48,128]{2,1,0:T(8,128)S(1)} %bitcast.36), channel_id=4, replica_groups=mesh['x'=4,'y'=4,'zh'=8,'zl'=2,'c'=2] {'zh','c'}, dimensions={0}, use_global_device_ids=true | all-gather | bytes 835584 | tf_op jit(solution)/shard_map/all_gather | solution.py:360
  113.0 1.2 shard_map.55
  115.1 11.3 %all_to_all.73.pieces = f32[16,40,128]{2,1,0:T(8,128)S(1)} all-to-all(f32[16,40,128]{2,1,0:T(8,128)S(1)} %bitcast.32), channel_id=1, replica_groups=mesh['x'=4,'y'=4,'zh'=8,'zl'=2,'c'=2] {'x','y'}, dimensions={0} | all-to-all | bytes 655360 | tf_op jit(solution)/shard_map/all_to_all | solution.py:269
  126.5 12.3 %all_to_all.74.every = f32[16,48,128]{2,1,0:T(8,128)S(1)} all-to-all(f32[16,48,128]{2,1,0:T(8,128)S(1)} %shard_map.56), channel_id=1, replica_groups=mesh['x'=4,'y'=4,'zh'=8,'zl'=2,'c'=2] {'x','y'}, dimensions={0} | all-to-all | bytes 786432 | tf_op jit(solution)/shard_map/all_to_all | solution.py:269
  138.9 4.5 %all-gather.3 = f32[1280,128]{1,0:T(8,128)S(1)} all-gather(f32[640,128]{1,0:T(8,128)S(1)} %get-tuple-element.60.field.old_field), channel_id=5, replica_groups=mesh['x'=4,'y'=4,'zh'=8,'zl'=2,'c'=2] {'c'}, dimensions={0}, use_global_device_ids=true | all-gather | bytes 983040 | tf_op jit(solution)/shard_map/all_gather | solution.py:321
  143.5 1.3 shard_map.58
  144.8 8.1 %all_to_all.75.pieces = f32[2,320,128]{2,1,0:T(8,128)S(1)} all-to-all(f32[2,320,128]{2,1,0:T(8,128)S(1)} %bitcast.27), channel_id=1, replica_groups=mesh['x'=4,'y'=4,'zh'=8,'zl'=2,'c'=2] {'zl'}, dimensions={0} | all-to-all | bytes 655360 | tf_op jit(solution)/shard_map/all_to_all | solution.py:269
  153.6 6.9 %all-to-all-start.7 = ((f32[8,40,128]{2,1,0:T(8,128)}), f32[8,40,128]{2,1,0:T(8,128)S(1)}, u32[]{:S(2)}, u32[]{:S(2)}) async-start(f32[8,40,128]{2,1,0:T(8,128)} %bitcast.28), calls=%async_computation.7 | async-start | bytes 327680 | tf_op jit(solution)/shard_map/all_to_all | solution.py:269
  160.5 3.6 %collective-permute-start.2 = (f32[256,128]{1,0:T(8,128)}, f32[256,128]{1,0:T(8,128)}, u32[]{:S(2)}, u32[]{:S(2)}) collective-permute-start(f32[256,128]{1,0:T(8,128)} %copy-done.54), channel_id=1, source_target_pairs={{1,2},{3,4},{5,6},{7,8},{9,10},{11,12},{13,14},{15,16},{17,18},{19... | collective-permute-start | bytes 393224 | tf_op jit(solution)/shard_map/ppermute | solution.py:320
  164.1 9.9 %all-to-all-done.7.pieces = f32[8,40,128]{2,1,0:T(8,128)S(1)} async-done(((f32[8,40,128]{2,1,0:T(8,128)}), f32[8,40,128]{2,1,0:T(8,128)S(1)}, u32[]{:S(2)}, u32[]{:S(2)}) %all-to-all-start.7) | async-done | bytes 163872 | tf_op jit(solution)/shard_map/all_to_all | solution.py:269
  174.0 1.2 copy-done.24
  175.3 2.2 shard_map.61
  177.5 3.6 %all-gather.4 = f32[96,128]{1,0:T(8,128)S(1)} all-gather(f32[48,128]{1,0:T(8,128)S(1)} %get-tuple-element.62), channel_id=6, replica_groups=mesh['x'=4,'y'=4,'zh'=8,'zl'=2,'c'=2] {'zl'}, dimensions={0}, use_global_device_ids=true | all-gather | bytes 73728 | tf_op jit(solution)/shard_map/all_gather | solution.py:360
  181.0 26.9 %all-gather.5.every = f32[32,48,128]{2,1,0:T(8,128)S(1)} all-gather(f32[2,48,128]{2,1,0:T(8,128)S(1)} %bitcast.37), channel_id=7, replica_groups=mesh['x'=4,'y'=4,'zh'=8,'zl'=2,'c'=2] {'zh','c'}, dimensions={0}, use_global_device_ids=true | all-gather | bytes 835584 | tf_op jit(solution)/shard_map/all_gather | solution.py:360
  207.9 1.2 shard_map.62
  210.0 11.5 %all_to_all.76.pieces = f32[16,40,128]{2,1,0:T(8,128)S(1)} all-to-all(f32[16,40,128]{2,1,0:T(8,128)S(1)} %bitcast.30), channel_id=1, replica_groups=mesh['x'=4,'y'=4,'zh'=8,'zl'=2,'c'=2] {'x','y'}, dimensions={0} | all-to-all | bytes 655360 | tf_op jit(solution)/shard_map/all_to_all | solution.py:269
  221.6 12.3 %all_to_all.77.every = f32[16,48,128]{2,1,0:T(8,128)S(1)} all-to-all(f32[16,48,128]{2,1,0:T(8,128)S(1)} %shard_map.63), channel_id=1, replica_groups=mesh['x'=4,'y'=4,'zh'=8,'zl'=2,'c'=2] {'x','y'}, dimensions={0} | all-to-all | bytes 786432 | tf_op jit(solution)/shard_map/all_to_all | solution.py:269
  234.1 4.5 %all-gather.6 = f32[1280,128]{1,0:T(8,128)S(1)} all-gather(f32[640,128]{1,0:T(8,128)S(1)} %get-tuple-element.72.field), channel_id=8, replica_groups=mesh['x'=4,'y'=4,'zh'=8,'zl'=2,'c'=2] {'c'}, dimensions={0}, use_global_device_ids=true | all-gather | bytes 983040 | tf_op jit(solution)/shard_map/all_gather | solution.py:321
  238.6 1.3 shard_map.65
  239.9 8.1 %all_to_all.78.pieces = f32[2,320,128]{2,1,0:T(8,128)S(1)} all-to-all(f32[2,320,128]{2,1,0:T(8,128)S(1)} %bitcast.25), channel_id=1, replica_groups=mesh['x'=4,'y'=4,'zh'=8,'zl'=2,'c'=2] {'zl'}, dimensions={0} | all-to-all | bytes 655360 | tf_op jit(solution)/shard_map/all_to_all | solution.py:269
  248.8 6.4 %all-to-all-start.11 = ((f32[8,40,128]{2,1,0:T(8,128)}), f32[8,40,128]{2,1,0:T(8,128)S(1)}, u32[]{:S(2)}, u32[]{:S(2)}) async-start(f32[8,40,128]{2,1,0:T(8,128)} %bitcast.29), calls=%async_computation.11 | async-start | bytes 327680 | tf_op jit(solution)/shard_map/all_to_all | solution.py:269
  255.1 3.3 %collective-permute-start.3 = (f32[256,128]{1,0:T(8,128)}, f32[256,128]{1,0:T(8,128)}, u32[]{:S(2)}, u32[]{:S(2)}) collective-permute-start(f32[256,128]{1,0:T(8,128)} %copy-done.53), channel_id=1, source_target_pairs={{1,2},{3,4},{5,6},{7,8},{9,10},{11,12},{13,14},{15,16},{17,18},{19... | collective-permute-start | bytes 393224 | tf_op jit(solution)/shard_map/ppermute | solution.py:320
  258.4 10.8 %all-to-all-done.11.pieces = f32[8,40,128]{2,1,0:T(8,128)S(1)} async-done(((f32[8,40,128]{2,1,0:T(8,128)}), f32[8,40,128]{2,1,0:T(8,128)S(1)}, u32[]{:S(2)}, u32[]{:S(2)}) %all-to-all-start.11) | async-done | bytes 163872 | tf_op jit(solution)/shard_map/all_to_all | solution.py:269
  269.3 1.1 copy-done.22
  270.4 1.1 copy-done.41
  271.5 2.2 shard_map.68
  273.7 15.6 %all_to_all.79.every = f32[32,8,128]{2,1,0:T(8,128)S(1)} all-to-all(f32[32,8,128]{2,1,0:T(8,128)S(1)} %shard_map.68), channel_id=1, replica_groups=mesh['x'=4,'y'=4,'zh'=8,'zl'=2,'c'=2] {'x','y','c'}, dimensions={0} | all-to-all | bytes 262144 | tf_op jit(solution)/shard_map/all_to_all | solution.py:269
  289.4 14.5 %all_to_all.80.every = f32[16,8,128]{2,1,0:T(8,128)S(1)} all-to-all(f32[16,8,128]{2,1,0:T(8,128)S(1)} %shard_map.69), channel_id=1, replica_groups=mesh['x'=4,'y'=4,'zh'=8,'zl'=2,'c'=2] {'zh','zl'}, dimensions={0} | all-to-all | bytes 131072 | tf_op jit(solution)/shard_map/all_to_all | solution.py:269
  (122 shorter events, 6.2 us)
Async XLA Ops:
  0.0 1.9 copy-start.25
  6.0 35.9 %copy-start.15 = (bf16[640,1280]{1,0:T(8,128)(2,1)}, bf16[640,1280]{1,0:T(8,128)(2,1)S(1)}, u32[]{:S(2)}) copy-start(bf16[640,1280]{1,0:T(8,128)(2,1)S(1)} %get-tuple-element.53.high) | copy-start | bytes 4915204
  6.0 36.2 %copy-start.3 = (bf16[640,640]{1,0:T(8,128)(2,1)}, bf16[640,640]{1,0:T(8,128)(2,1)S(1)}, u32[]{:S(2)}) copy-start(bf16[640,640]{1,0:T(8,128)(2,1)S(1)} %get-tuple-element.43.own_high) | copy-start | bytes 2457604
  6.0 36.2 %copy-start.6 = (bf16[640,640]{1,0:T(8,128)(2,1)}, bf16[640,640]{1,0:T(8,128)(2,1)S(1)}, u32[]{:S(2)}) copy-start(bf16[640,640]{1,0:T(8,128)(2,1)S(1)} %get-tuple-element.44.own_low) | copy-start | bytes 2457604
  6.0 31.6 %copy-start.51 = (s32[3,640]{1,0:T(4,128)S(1)}, s32[3,640]{1,0:T(4,128)}, u32[]{:S(2)}) copy-start(s32[3,640]{1,0:T(4,128)} %ids.3) | copy-start | bytes 23044
  6.0 35.9 %collective-permute-start = (f32[640,640]{1,0:T(8,128)S(1)}, f32[640,640]{1,0:T(8,128)S(1)}, u32[]{:S(2)}, u32[]{:S(2)}) collective-permute-start(f32[640,640]{1,0:T(8,128)S(1)} %get-tuple-element.45), channel_id=1, source_target_pairs={{0,1},{1,0},{2,3},{3,2},{4,5},{5,4},{6,7},{7,6},{8,9},{9,8},{10,11... | collective-permute-start | bytes 4915208 | tf_op jit(solution)/shard_map/ppermute | solution.py:303
  41.9 1.6 copy-start
  42.2 1.3 copy-start.9
  42.2 1.3 copy-start.12
  43.5 36.3 %copy-start.52 = (f32[128]{0:T(128)S(1)}, f32[128]{0:T(128)}, u32[]{:S(2)}) copy-start(f32[128]{0:T(128)} %param.7) | copy-start | bytes 1540
  52.2 27.6 %all-to-all-start.3 = ((f32[8,40,128]{2,1,0:T(8,128)}), f32[8,40,128]{2,1,0:T(8,128)S(1)}, u32[]{:S(2)}, u32[]{:S(2)}) async-start(f32[8,40,128]{2,1,0:T(8,128)} %bitcast.6), calls=%async_computation.3 | async-start | bytes 327680 | tf_op jit(solution)/shard_map/all_to_all | solution.py:269
  65.6 9.0 %collective-permute-start.1 = (f32[264,128]{1,0:T(8,128)S(1)}, f32[264,128]{1,0:T(8,128)S(1)}, u32[]{:S(2)}, u32[]{:S(2)}) collective-permute-start(f32[264,128]{1,0:T(8,128)S(1)} %get-tuple-element.48), channel_id=1, source_target_pairs={{1,2},{3,4},{5,6},{7,8},{9,10},{11,12},{13,14},{15,16},{17,18},{19... | collective-permute-start | bytes 405512 | tf_op jit(solution)/shard_map/ppermute | solution.py:320
  81.8 31.1 %copy-start.16 = (bf16[640,1280]{1,0:T(8,128)(2,1)S(1)}, bf16[640,1280]{1,0:T(8,128)(2,1)}, u32[]{:S(2)}) copy-start(bf16[640,1280]{1,0:T(8,128)(2,1)} %copy-done.15) | copy-start | bytes 4915204
  81.8 31.1 %copy-start.19 = (bf16[640,1280]{1,0:T(8,128)(2,1)S(1)}, bf16[640,1280]{1,0:T(8,128)(2,1)}, u32[]{:S(2)}) copy-start(bf16[640,1280]{1,0:T(8,128)(2,1)} %copy-done.18) | copy-start | bytes 4915204
  115.1 23.8 %copy-start.28 = (f32[640,128]{1,0:T(8,128)}, f32[640,128]{1,0:T(8,128)S(1)}, u32[]{:S(2)}) copy-start(f32[640,128]{1,0:T(8,128)S(1)} %get-tuple-element.58.smooth.old_smooth) | copy-start | bytes 983044
  115.1 23.8 %copy-start.30 = (f32[640,128]{1,0:T(8,128)}, f32[640,128]{1,0:T(8,128)S(1)}, u32[]{:S(2)}) copy-start(f32[640,128]{1,0:T(8,128)S(1)} %get-tuple-element.59.way.old_way) | copy-start | bytes 983044
  126.4 17.0 %copy-start.4 = (bf16[640,640]{1,0:T(8,128)(2,1)S(1)}, bf16[640,640]{1,0:T(8,128)(2,1)}, u32[]{:S(2)}) copy-start(bf16[640,640]{1,0:T(8,128)(2,1)} %copy-done.3) | copy-start | bytes 2457604
  126.4 17.0 %copy-start.7 = (bf16[640,640]{1,0:T(8,128)(2,1)S(1)}, bf16[640,640]{1,0:T(8,128)(2,1)}, u32[]{:S(2)}) copy-start(bf16[640,640]{1,0:T(8,128)(2,1)} %copy-done.6) | copy-start | bytes 2457604
  126.5 17.0 %copy-start.10 = (bf16[640,640]{1,0:T(8,128)(2,1)S(1)}, bf16[640,640]{1,0:T(8,128)(2,1)}, u32[]{:S(2)}) copy-start(bf16[640,640]{1,0:T(8,128)(2,1)} %copy-done.9) | copy-start | bytes 2457604
  126.5 17.0 %copy-start.13 = (bf16[640,640]{1,0:T(8,128)(2,1)S(1)}, bf16[640,640]{1,0:T(8,128)(2,1)}, u32[]{:S(2)}) copy-start(bf16[640,640]{1,0:T(8,128)(2,1)} %copy-done.12) | copy-start | bytes 2457604
  138.9 5.9 %copy-start.26 = (f32[640,128]{1,0:T(8,128)}, f32[640,128]{1,0:T(8,128)S(1)}, u32[]{:S(2)}) copy-start(f32[640,128]{1,0:T(8,128)S(1)} %get-tuple-element.60.field.old_field) | copy-start | bytes 983044
  138.9 5.9 %copy-start.47 = (f32[640,128]{1,0:T(8,128)}, f32[640,128]{1,0:T(8,128)S(1)}, u32[]{:S(2)}) copy-start(f32[640,128]{1,0:T(8,128)S(1)} %get-tuple-element.71.old_slip) | copy-start | bytes 983044
  138.9 5.9 %copy-start.54 = (f32[256,128]{1,0:T(8,128)}, f32[256,128]{1,0:T(8,128)S(1)}, u32[]{:S(2)}) copy-start(f32[256,128]{1,0:T(8,128)S(1)} %get-tuple-element.61) | copy-start | bytes 393220
  144.8 29.2 %copy-start.29 = (f32[640,128]{1,0:T(8,128)S(1)}, f32[640,128]{1,0:T(8,128)}, u32[]{:S(2)}) copy-start(f32[640,128]{1,0:T(8,128)} %copy-done.28) | copy-start | bytes 983044
  153.6 20.4 %all-to-all-start.7 = ((f32[8,40,128]{2,1,0:T(8,128)}), f32[8,40,128]{2,1,0:T(8,128)S(1)}, u32[]{:S(2)}, u32[]{:S(2)}) async-start(f32[8,40,128]{2,1,0:T(8,128)} %bitcast.28), calls=%async_computation.7 | async-start | bytes 327680 | tf_op jit(solution)/shard_map/all_to_all | solution.py:269
  160.5 13.5 %collective-permute-start.2 = (f32[256,128]{1,0:T(8,128)}, f32[256,128]{1,0:T(8,128)}, u32[]{:S(2)}, u32[]{:S(2)}) collective-permute-start(f32[256,128]{1,0:T(8,128)} %copy-done.54), channel_id=1, source_target_pairs={{1,2},{3,4},{5,6},{7,8},{9,10},{11,12},{13,14},{15,16},{17,18},{19... | collective-permute-start | bytes 393224 | tf_op jit(solution)/shard_map/ppermute | solution.py:320
  174.0 33.9 %copy-start.17 = (bf16[640,1280]{1,0:T(8,128)(2,1)S(1)}, bf16[640,1280]{1,0:T(8,128)(2,1)}, u32[]{:S(2)}) copy-start(bf16[640,1280]{1,0:T(8,128)(2,1)} %copy-done.15) | copy-start | bytes 4915204
  174.0 33.9 %copy-start.20 = (bf16[640,1280]{1,0:T(8,128)(2,1)S(1)}, bf16[640,1280]{1,0:T(8,128)(2,1)}, u32[]{:S(2)}) copy-start(bf16[640,1280]{1,0:T(8,128)(2,1)} %copy-done.18) | copy-start | bytes 4915204
  175.3 32.6 %copy-start.27 = (f32[640,128]{1,0:T(8,128)S(1)}, f32[640,128]{1,0:T(8,128)}, u32[]{:S(2)}) copy-start(f32[640,128]{1,0:T(8,128)} %copy-done.26) | copy-start | bytes 983044
  175.3 32.6 %copy-start.31 = (f32[640,128]{1,0:T(8,128)S(1)}, f32[640,128]{1,0:T(8,128)}, u32[]{:S(2)}) copy-start(f32[640,128]{1,0:T(8,128)} %copy-done.30) | copy-start | bytes 983044
  175.3 32.6 %copy-start.39 = (f32[1280,128]{1,0:T(8,128)S(1)}, f32[1280,128]{1,0:T(8,128)}, u32[]{:S(2)}) copy-start(f32[1280,128]{1,0:T(8,128)} %copy-done.38) | copy-start | bytes 1966084
  210.0 24.0 %copy-start.32 = (f32[640,128]{1,0:T(8,128)}, f32[640,128]{1,0:T(8,128)S(1)}, u32[]{:S(2)}) copy-start(f32[640,128]{1,0:T(8,128)S(1)} %get-tuple-element.69.smooth) | copy-start | bytes 983044
  210.0 24.0 %copy-start.34 = (f32[640,128]{1,0:T(8,128)}, f32[640,128]{1,0:T(8,128)S(1)}, u32[]{:S(2)}) copy-start(f32[640,128]{1,0:T(8,128)S(1)} %get-tuple-element.70.way) | copy-start | bytes 983044
  210.0 23.9 %copy-start.48 = (f32[640,128]{1,0:T(8,128)S(1)}, f32[640,128]{1,0:T(8,128)}, u32[]{:S(2)}) copy-start(f32[640,128]{1,0:T(8,128)} %copy-done.47) | copy-start | bytes 983044
  221.6 17.0 %copy-start.5 = (bf16[640,640]{1,0:T(8,128)(2,1)S(1)}, bf16[640,640]{1,0:T(8,128)(2,1)}, u32[]{:S(2)}) copy-start(bf16[640,640]{1,0:T(8,128)(2,1)} %copy-done.3) | copy-start | bytes 2457604
  221.6 17.0 %copy-start.8 = (bf16[640,640]{1,0:T(8,128)(2,1)S(1)}, bf16[640,640]{1,0:T(8,128)(2,1)}, u32[]{:S(2)}) copy-start(bf16[640,640]{1,0:T(8,128)(2,1)} %copy-done.6) | copy-start | bytes 2457604
  221.6 17.0 %copy-start.11 = (bf16[640,640]{1,0:T(8,128)(2,1)S(1)}, bf16[640,640]{1,0:T(8,128)(2,1)}, u32[]{:S(2)}) copy-start(bf16[640,640]{1,0:T(8,128)(2,1)} %copy-done.9) | copy-start | bytes 2457604
  221.6 17.0 %copy-start.14 = (bf16[640,640]{1,0:T(8,128)(2,1)S(1)}, bf16[640,640]{1,0:T(8,128)(2,1)}, u32[]{:S(2)}) copy-start(bf16[640,640]{1,0:T(8,128)(2,1)} %copy-done.12) | copy-start | bytes 2457604
  234.0 4.6 %copy-start.53 = (f32[256,128]{1,0:T(8,128)}, f32[256,128]{1,0:T(8,128)S(1)}, u32[]{:S(2)}) copy-start(f32[256,128]{1,0:T(8,128)S(1)} %get-tuple-element.74) | copy-start | bytes 393220
  234.0 5.9 %copy-start.36 = (f32[640,128]{1,0:T(8,128)}, f32[640,128]{1,0:T(8,128)S(1)}, u32[]{:S(2)}) copy-start(f32[640,128]{1,0:T(8,128)S(1)} %get-tuple-element.72.field) | copy-start | bytes 983044
  234.0 5.9 %copy-start.49 = (f32[640,128]{1,0:T(8,128)}, f32[640,128]{1,0:T(8,128)S(1)}, u32[]{:S(2)}) copy-start(f32[640,128]{1,0:T(8,128)S(1)} %get-tuple-element.76.old_slip) | copy-start | bytes 983044
  238.6 1.3 copy-start.21
  239.9 29.4 %copy-start.33 = (f32[640,128]{1,0:T(8,128)S(1)}, f32[640,128]{1,0:T(8,128)}, u32[]{:S(2)}) copy-start(f32[640,128]{1,0:T(8,128)} %copy-done.32) | copy-start | bytes 983044
  248.8 20.5 %all-to-all-start.11 = ((f32[8,40,128]{2,1,0:T(8,128)}), f32[8,40,128]{2,1,0:T(8,128)S(1)}, u32[]{:S(2)}, u32[]{:S(2)}) async-start(f32[8,40,128]{2,1,0:T(8,128)} %bitcast.29), calls=%async_computation.11 | async-start | bytes 327680 | tf_op jit(solution)/shard_map/all_to_all | solution.py:269
  255.1 14.2 %collective-permute-start.3 = (f32[256,128]{1,0:T(8,128)}, f32[256,128]{1,0:T(8,128)}, u32[]{:S(2)}, u32[]{:S(2)}) collective-permute-start(f32[256,128]{1,0:T(8,128)} %copy-done.53), channel_id=1, source_target_pairs={{1,2},{3,4},{5,6},{7,8},{9,10},{11,12},{13,14},{15,16},{17,18},{19... | collective-permute-start | bytes 393224 | tf_op jit(solution)/shard_map/ppermute | solution.py:320
  271.5 32.4 %copy-start.35 = (f32[640,128]{1,0:T(8,128)S(1)}, f32[640,128]{1,0:T(8,128)}, u32[]{:S(2)}) copy-start(f32[640,128]{1,0:T(8,128)} %copy-done.34) | copy-start | bytes 983044
  271.5 32.4 %copy-start.37 = (f32[640,128]{1,0:T(8,128)S(1)}, f32[640,128]{1,0:T(8,128)}, u32[]{:S(2)}) copy-start(f32[640,128]{1,0:T(8,128)} %copy-done.36) | copy-start | bytes 983044
  271.5 32.4 %copy-start.50 = (f32[640,128]{1,0:T(8,128)S(1)}, f32[640,128]{1,0:T(8,128)}, u32[]{:S(2)}) copy-start(f32[640,128]{1,0:T(8,128)} %copy-done.49) | copy-start | bytes 983044
  (14 other events, 13.8 us)

commit v10 on v8

--- a/solution.py
+++ b/solution.py
@@ -65,11 +65,10 @@
     return value
 
 
-def first_back(core, place, row, green, data, moved, back_high, back_low, high, low, send, wide, *, share):
+def first_back(core, place, row, green, wide, moved, back_high, back_low, high, low, send, *, share):
     for k in range(green.shape[0] // 128):
         at = slice(128 * k, 128 * (k + 1))
         back_high[:, at], back_low[:, at] = halves(green[at, :].T)
-    store_halves(wide, 0, data[...])
     moved[...] = product(back_high, back_low, wide[...])
     half = send.shape[0]
     for z in range(0, half // share, 2):
@@ -294,10 +293,12 @@
 
     back_matrix = ((col_count, row_count), BF16)
     matrix = ((half, col_count), BF16)
+    rounded = lax.reduce_precision(data, 8, 7)
+    data_wide = jnp.concatenate([rounded, data - rounded], 1).astype(BF16)
     moved, b_high, b_low, own_high, own_low, send = local_call(
         first_back,
         [field_shape, back_matrix, back_matrix, matrix, matrix, ((half, col_count), F32)],
-        green, data, scalars=[core_scalar, place_scalar, row_scalar], scratch=[wide], share=share,
+        green, data_wide, scalars=[core_scalar, place_scalar, row_scalar], share=share,
     )
     far = lax.ppermute(send, "c", swap)
     pieces = exchanged(moved.reshape(n_obs, piece, epochs), OBS)

time: 300 us -> 301 us (level)
    unnamed x104 -> x102, local copies, waits for them, and re-layouts: 11.3 us -> 10.2 us
where the time goes in v10:
time: 301 us; the launch traced here: 299 us
  blocking collectives  177 us (59%)
  starting transfers between devices  50.6 us (17%)
  waiting for transfers between devices  40.6 us (13%)
  Pallas kernels  19.1 us (6%)
  local copies, waits for them, and re-layouts  10.2 us (3%)
    all_to_all x8, blocking collectives, exchanged(): return lax.all_to_all(pieces, axis, 0, 0, tiled=True)  104 us
    all_gather x4, blocking collectives, shards(): every = lax.all_gather(lax.all_gather(out, 'zl'), ('zh', 'c'))  59.9 us
    all_to_all x3, starting transfers between devices, exchanged(): return lax.all_to_all(pieces, axis, 0, 0, tiled=True)  29.6 us
    all_to_all x3, waiting for transfers between devices, exchanged(): return lax.all_to_all(pieces, axis, 0, 0, tiled=True)  22.9 us
    pallas_call x22, Pallas kernels, local_call(): pl.pallas_call(functools.partial(body, **options), out_shape=[jax.ShapeDt...  19.1 us
    ppermute x3, waiting for transfers between devices, shards(): edge = lax.ppermute(edge, PATCH, outward)  17.6 us
    all_gather x3, blocking collectives, shards(): pair = lax.all_gather(field, 'c')  13.3 us
    ppermute x3, starting transfers between devices, shards(): edge = lax.ppermute(edge, PATCH, outward)  12.1 us
  transfers between devices with their start and end apart: 7, of which 5 were waited for; matrix products, arithmetic and copies ran while one was open for 0% of the time, Pallas kernels for 1%

profile of v10, /device:TPU:1, one launch (start us, length us, event | category | flops | bytes accessed | tf_op | source)
XLA Modules:
  0.0 299.3 jit_solution(13200995584438558803)
XLA Ops:
  0.0 1.2 reduce-precision_convert_fusion
  1.3 1.9 copy-done.25
  3.2 1.7 shard_map.46
  5.0 1.2 copy-done.18
  6.2 8.9 %collective-permute-start = (f32[640,640]{1,0:T(8,128)S(1)}, f32[640,640]{1,0:T(8,128)S(1)}, u32[]{:S(2)}, u32[]{:S(2)}) collective-permute-start(f32[640,640]{1,0:T(8,128)S(1)} %get-tuple-element.45), channel_id=1, source_target_pairs={{0,1},{1,0},{2,3},{3,2},{4,5},{5,4},{6,7},{7,6},{8,9},{9,8},{10,11... | collective-permute-start | bytes 4915208 | tf_op jit(solution)/shard_map/ppermute | solution.py:303
  15.1 11.1 %all_to_all.55.pieces = f32[16,40,128]{2,1,0:T(8,128)S(1)} all-to-all(f32[16,40,128]{2,1,0:T(8,128)S(1)} %bitcast.24), channel_id=1, replica_groups=mesh['x'=4,'y'=4,'zh'=8,'zl'=2,'c'=2] {'x','y'}, dimensions={0} | all-to-all | bytes 655360 | tf_op jit(solution)/shard_map/all_to_all | solution.py:267
  26.2 11.6 %all_to_all.56.every = f32[16,40,128]{2,1,0:T(8,128)S(1)} all-to-all(f32[16,40,128]{2,1,0:T(8,128)S(1)} %shard_map.47), channel_id=1, replica_groups=mesh['x'=4,'y'=4,'zh'=8,'zl'=2,'c'=2] {'x','y'}, dimensions={0} | all-to-all | bytes 655360 | tf_op jit(solution)/shard_map/all_to_all | solution.py:267
  37.8 4.2 %all-gather = f32[1296,128]{1,0:T(8,128)S(1)} all-gather(f32[648,128]{1,0:T(8,128)S(1)} %get-tuple-element.42.field.old_field), channel_id=2, replica_groups=mesh['x'=4,'y'=4,'zh'=8,'zl'=2,'c'=2] {'c'}, dimensions={0}, use_global_device_ids=true | all-gather | bytes 995328 | tf_op jit(solution)/shard_map/all_gather | solution.py:321
  42.4 2.0 shard_map.50
  44.4 13.6 %all-to-all-start.2 = ((f32[16,40,128]{2,1,0:T(8,128)}), f32[16,40,128]{2,1,0:T(8,128)}, u32[]{:S(2)}, u32[]{:S(2)}) async-start(f32[16,40,128]{2,1,0:T(8,128)} %bitcast.5), calls=%async_computation.2 | async-start | bytes 655360 | tf_op jit(solution)/shard_map/all_to_all | solution.py:267
  57.9 4.0 %collective-permute-start.1 = (f32[264,128]{1,0:T(8,128)S(1)}, f32[264,128]{1,0:T(8,128)S(1)}, u32[]{:S(2)}, u32[]{:S(2)}) collective-permute-start(f32[264,128]{1,0:T(8,128)S(1)} %get-tuple-element.48), channel_id=1, source_target_pairs={{1,2},{3,4},{5,6},{7,8},{9,10},{11,12},{13,14},{15,16},{17,18},{19... | collective-permute-start | bytes 405512 | tf_op jit(solution)/shard_map/ppermute | solution.py:320
  62.0 14.2 %collective-permute-done.1.edge = f32[264,128]{1,0:T(8,128)S(1)} collective-permute-done((f32[264,128]{1,0:T(8,128)S(1)}, f32[264,128]{1,0:T(8,128)S(1)}, u32[]{:S(2)}, u32[]{:S(2)}) %collective-permute-start.1) | collective-permute-done | bytes 135200 | tf_op jit(solution)/shard_map/ppermute | solution.py:320
  76.2 1.1 copy-done.1
  77.3 1.8 shard_map.52
  79.1 1.0 shard_map.51.part
  80.1 1.1 copy-done.2
  81.2 1.2 shard_map.53
  82.4 3.3 %all-gather.1 = f32[96,128]{1,0:T(8,128)S(1)} all-gather(f32[48,128]{1,0:T(8,128)S(1)} %get-tuple-element.51), channel_id=3, replica_groups=mesh['x'=4,'y'=4,'zh'=8,'zl'=2,'c'=2] {'zl'}, dimensions={0}, use_global_device_ids=true | all-gather | bytes 73728 | tf_op jit(solution)/shard_map/all_gather | solution.py:358
  85.8 25.0 %all-gather.2.every = f32[32,48,128]{2,1,0:T(8,128)S(1)} all-gather(f32[2,48,128]{2,1,0:T(8,128)S(1)} %bitcast.29), channel_id=4, replica_groups=mesh['x'=4,'y'=4,'zh'=8,'zl'=2,'c'=2] {'zh','c'}, dimensions={0}, use_global_device_ids=true | all-gather | bytes 835584 | tf_op jit(solution)/shard_map/all_gather | solution.py:358
  110.8 1.2 shard_map.54
  112.0 11.4 %all_to_all.57.pieces = f32[16,40,128]{2,1,0:T(8,128)S(1)} all-to-all(f32[16,40,128]{2,1,0:T(8,128)S(1)} %bitcast.25), channel_id=1, replica_groups=mesh['x'=4,'y'=4,'zh'=8,'zl'=2,'c'=2] {'x','y'}, dimensions={0} | all-to-all | bytes 655360 | tf_op jit(solution)/shard_map/all_to_all | solution.py:267
  123.5 12.3 %all_to_all.58.every = f32[16,48,128]{2,1,0:T(8,128)S(1)} all-to-all(f32[16,48,128]{2,1,0:T(8,128)S(1)} %shard_map.55), channel_id=1, replica_groups=mesh['x'=4,'y'=4,'zh'=8,'zl'=2,'c'=2] {'x','y'}, dimensions={0} | all-to-all | bytes 786432 | tf_op jit(solution)/shard_map/all_to_all | solution.py:267
  135.9 4.5 %all-gather.3 = f32[1280,128]{1,0:T(8,128)S(1)} all-gather(f32[640,128]{1,0:T(8,128)S(1)} %get-tuple-element.60.field.old_field), channel_id=5, replica_groups=mesh['x'=4,'y'=4,'zh'=8,'zl'=2,'c'=2] {'c'}, dimensions={0}, use_global_device_ids=true | all-gather | bytes 983040 | tf_op jit(solution)/shard_map/all_gather | solution.py:321
  140.5 1.3 shard_map.57
  142.5 8.7 %all-to-all-start.5 = ((f32[16,40,128]{2,1,0:T(8,128)}), f32[16,40,128]{2,1,0:T(8,128)}, u32[]{:S(2)}, u32[]{:S(2)}) async-start(f32[16,40,128]{2,1,0:T(8,128)} %bitcast.22), calls=%async_computation.5 | async-start | bytes 655360 | tf_op jit(solution)/shard_map/all_to_all | solution.py:267
  151.2 4.0 %collective-permute-start.2 = (f32[256,128]{1,0:T(8,128)}, f32[256,128]{1,0:T(8,128)S(1)}, u32[]{:S(2)}, u32[]{:S(2)}) collective-permute-start(f32[256,128]{1,0:T(8,128)} %copy-done.50), channel_id=1, source_target_pairs={{1,2},{3,4},{5,6},{7,8},{9,10},{11,12},{13,14},{15,16},{17,18},{19... | collective-permute-start | bytes 393224 | tf_op jit(solution)/shard_map/ppermute | solution.py:320
  155.3 11.5 %all-to-all-done.5.pieces = f32[16,40,128]{2,1,0:T(8,128)} async-done(((f32[16,40,128]{2,1,0:T(8,128)}), f32[16,40,128]{2,1,0:T(8,128)}, u32[]{:S(2)}, u32[]{:S(2)}) %all-to-all-start.5) | async-done | bytes 327712 | tf_op jit(solution)/shard_map/all_to_all | solution.py:267
  166.7 1.0 shard_map.58.part
  167.7 1.7 collective-permute-done.2.edge
  169.4 1.1 copy-done.24
  170.5 1.2 shard_map.59
  171.7 5.4 %all-gather.4 = f32[96,128]{1,0:T(8,128)S(1)} all-gather(f32[48,128]{1,0:T(8,128)S(1)} %get-tuple-element.62), channel_id=6, replica_groups=mesh['x'=4,'y'=4,'zh'=8,'zl'=2,'c'=2] {'zl'}, dimensions={0}, use_global_device_ids=true | all-gather | bytes 73728 | tf_op jit(solution)/shard_map/all_gather | solution.py:358
  177.1 26.2 %all-gather.5.every = f32[32,48,128]{2,1,0:T(8,128)S(1)} all-gather(f32[2,48,128]{2,1,0:T(8,128)S(1)} %bitcast.30), channel_id=7, replica_groups=mesh['x'=4,'y'=4,'zh'=8,'zl'=2,'c'=2] {'zh','c'}, dimensions={0}, use_global_device_ids=true | all-gather | bytes 835584 | tf_op jit(solution)/shard_map/all_gather | solution.py:358
  203.3 1.2 shard_map.60
  204.6 11.5 %all_to_all.59.pieces = f32[16,40,128]{2,1,0:T(8,128)S(1)} all-to-all(f32[16,40,128]{2,1,0:T(8,128)S(1)} %bitcast.23), channel_id=1, replica_groups=mesh['x'=4,'y'=4,'zh'=8,'zl'=2,'c'=2] {'x','y'}, dimensions={0} | all-to-all | bytes 655360 | tf_op jit(solution)/shard_map/all_to_all | solution.py:267
  216.2 12.3 %all_to_all.60.every = f32[16,48,128]{2,1,0:T(8,128)S(1)} all-to-all(f32[16,48,128]{2,1,0:T(8,128)S(1)} %shard_map.61), channel_id=1, replica_groups=mesh['x'=4,'y'=4,'zh'=8,'zl'=2,'c'=2] {'x','y'}, dimensions={0} | all-to-all | bytes 786432 | tf_op jit(solution)/shard_map/all_to_all | solution.py:267
  229.3 4.5 %all-gather.6 = f32[1280,128]{1,0:T(8,128)S(1)} all-gather(f32[640,128]{1,0:T(8,128)S(1)} %get-tuple-element.72.field), channel_id=8, replica_groups=mesh['x'=4,'y'=4,'zh'=8,'zl'=2,'c'=2] {'c'}, dimensions={0}, use_global_device_ids=true | all-gather | bytes 983040 | tf_op jit(solution)/shard_map/all_gather | solution.py:321
  233.9 2.0 shard_map.63
  235.9 7.4 %all-to-all-start.8 = ((f32[16,40,128]{2,1,0:T(8,128)}), f32[16,40,128]{2,1,0:T(8,128)}, u32[]{:S(2)}, u32[]{:S(2)}) async-start(f32[16,40,128]{2,1,0:T(8,128)} %bitcast.14), calls=%async_computation.8 | async-start | bytes 655360 | tf_op jit(solution)/shard_map/all_to_all | solution.py:267
  243.3 4.0 %collective-permute-start.3 = (f32[256,128]{1,0:T(8,128)}, f32[256,128]{1,0:T(8,128)S(1)}, u32[]{:S(2)}, u32[]{:S(2)}) collective-permute-start(f32[256,128]{1,0:T(8,128)} %copy-done.49), channel_id=1, source_target_pairs={{1,2},{3,4},{5,6},{7,8},{9,10},{11,12},{13,14},{15,16},{17,18},{19... | collective-permute-start | bytes 393224 | tf_op jit(solution)/shard_map/ppermute | solution.py:320
  247.3 11.5 %all-to-all-done.8.pieces = f32[16,40,128]{2,1,0:T(8,128)} async-done(((f32[16,40,128]{2,1,0:T(8,128)}), f32[16,40,128]{2,1,0:T(8,128)}, u32[]{:S(2)}, u32[]{:S(2)}) %all-to-all-start.8) | async-done | bytes 327712 | tf_op jit(solution)/shard_map/all_to_all | solution.py:267
  258.8 1.0 shard_map.64.share_ref
  259.8 1.7 collective-permute-done.3.edge
  261.5 1.1 copy-done.22
  262.6 1.1 copy-done.42
  263.7 1.2 shard_map.65
  264.9 18.5 %all_to_all.61.every = f32[32,8,128]{2,1,0:T(8,128)S(1)} all-to-all(f32[32,8,128]{2,1,0:T(8,128)S(1)} %shard_map.65), channel_id=1, replica_groups=mesh['x'=4,'y'=4,'zh'=8,'zl'=2,'c'=2] {'x','y','c'}, dimensions={0} | all-to-all | bytes 262144 | tf_op jit(solution)/shard_map/all_to_all | solution.py:267
  283.5 15.0 %all_to_all.62.every = f32[16,8,128]{2,1,0:T(8,128)S(1)} all-to-all(f32[16,8,128]{2,1,0:T(8,128)S(1)} %shard_map.66), channel_id=1, replica_groups=mesh['x'=4,'y'=4,'zh'=8,'zl'=2,'c'=2] {'zh','zl'}, dimensions={0} | all-to-all | bytes 131072 | tf_op jit(solution)/shard_map/all_to_all | solution.py:267
  (110 shorter events, 3.2 us)
Async XLA Ops:
  6.2 35.9 %copy-start.15 = (bf16[640,1280]{1,0:T(8,128)(2,1)}, bf16[640,1280]{1,0:T(8,128)(2,1)S(1)}, u32[]{:S(2)}) copy-start(bf16[640,1280]{1,0:T(8,128)(2,1)S(1)} %get-tuple-element.53.high) | copy-start | bytes 4915204
  6.2 36.2 %copy-start.3 = (bf16[640,640]{1,0:T(8,128)(2,1)}, bf16[640,640]{1,0:T(8,128)(2,1)S(1)}, u32[]{:S(2)}) copy-start(bf16[640,640]{1,0:T(8,128)(2,1)S(1)} %get-tuple-element.43.own_high) | copy-start | bytes 2457604
  6.2 36.2 %copy-start.6 = (bf16[640,640]{1,0:T(8,128)(2,1)}, bf16[640,640]{1,0:T(8,128)(2,1)S(1)}, u32[]{:S(2)}) copy-start(bf16[640,640]{1,0:T(8,128)(2,1)S(1)} %get-tuple-element.44.own_low) | copy-start | bytes 2457604
  6.2 31.6 %copy-start.47 = (s32[3,640]{1,0:T(4,128)S(1)}, s32[3,640]{1,0:T(4,128)}, u32[]{:S(2)}) copy-start(s32[3,640]{1,0:T(4,128)} %ids.3) | copy-start | bytes 23044
  6.2 35.9 %collective-permute-start = (f32[640,640]{1,0:T(8,128)S(1)}, f32[640,640]{1,0:T(8,128)S(1)}, u32[]{:S(2)}, u32[]{:S(2)}) collective-permute-start(f32[640,640]{1,0:T(8,128)S(1)} %get-tuple-element.45), channel_id=1, source_target_pairs={{0,1},{1,0},{2,3},{3,2},{4,5},{5,4},{6,7},{7,6},{8,9},{9,8},{10,11... | collective-permute-start | bytes 4915208 | tf_op jit(solution)/shard_map/ppermute | solution.py:303
  42.1 2.3 copy-start
  42.3 2.0 copy-start.9
  42.3 2.0 copy-start.12
  44.4 35.8 %copy-start.48 = (f32[128]{0:T(128)S(1)}, f32[128]{0:T(128)}, u32[]{:S(2)}) copy-start(f32[128]{0:T(128)} %param.7) | copy-start | bytes 1540
  44.4 34.7 %all-to-all-start.2 = ((f32[16,40,128]{2,1,0:T(8,128)}), f32[16,40,128]{2,1,0:T(8,128)}, u32[]{:S(2)}, u32[]{:S(2)}) async-start(f32[16,40,128]{2,1,0:T(8,128)} %bitcast.5), calls=%async_computation.2 | async-start | bytes 655360 | tf_op jit(solution)/shard_map/all_to_all | solution.py:267
  57.9 18.3 %collective-permute-start.1 = (f32[264,128]{1,0:T(8,128)S(1)}, f32[264,128]{1,0:T(8,128)S(1)}, u32[]{:S(2)}, u32[]{:S(2)}) collective-permute-start(f32[264,128]{1,0:T(8,128)S(1)} %get-tuple-element.48), channel_id=1, source_target_pairs={{1,2},{3,4},{5,6},{7,8},{9,10},{11,12},{13,14},{15,16},{17,18},{19... | collective-permute-start | bytes 405512 | tf_op jit(solution)/shard_map/ppermute | solution.py:320
  81.2 29.6 %copy-start.16 = (bf16[640,1280]{1,0:T(8,128)(2,1)S(1)}, bf16[640,1280]{1,0:T(8,128)(2,1)}, u32[]{:S(2)}) copy-start(bf16[640,1280]{1,0:T(8,128)(2,1)} %copy-done.15) | copy-start | bytes 4915204
  81.2 29.6 %copy-start.19 = (bf16[640,1280]{1,0:T(8,128)(2,1)S(1)}, bf16[640,1280]{1,0:T(8,128)(2,1)}, u32[]{:S(2)}) copy-start(bf16[640,1280]{1,0:T(8,128)(2,1)} %copy-done.18) | copy-start | bytes 4915204
  112.0 23.7 %copy-start.39 = (f32[1280,128]{1,0:T(8,128)}, f32[1280,128]{1,0:T(8,128)S(1)}, u32[]{:S(2)}) copy-start(f32[1280,128]{1,0:T(8,128)S(1)} %get-tuple-element.64.old_image) | copy-start | bytes 1966084
  112.0 23.8 %copy-start.28 = (f32[640,128]{1,0:T(8,128)}, f32[640,128]{1,0:T(8,128)S(1)}, u32[]{:S(2)}) copy-start(f32[640,128]{1,0:T(8,128)S(1)} %get-tuple-element.58.smooth.old_smooth) | copy-start | bytes 983044
  112.0 23.8 %copy-start.31 = (f32[640,128]{1,0:T(8,128)}, f32[640,128]{1,0:T(8,128)S(1)}, u32[]{:S(2)}) copy-start(f32[640,128]{1,0:T(8,128)S(1)} %get-tuple-element.59.way.old_way) | copy-start | bytes 983044
  123.4 17.0 %copy-start.4 = (bf16[640,640]{1,0:T(8,128)(2,1)S(1)}, bf16[640,640]{1,0:T(8,128)(2,1)}, u32[]{:S(2)}) copy-start(bf16[640,640]{1,0:T(8,128)(2,1)} %copy-done.3) | copy-start | bytes 2457604
  123.5 17.0 %copy-start.7 = (bf16[640,640]{1,0:T(8,128)(2,1)S(1)}, bf16[640,640]{1,0:T(8,128)(2,1)}, u32[]{:S(2)}) copy-start(bf16[640,640]{1,0:T(8,128)(2,1)} %copy-done.6) | copy-start | bytes 2457604
  123.5 17.0 %copy-start.10 = (bf16[640,640]{1,0:T(8,128)(2,1)S(1)}, bf16[640,640]{1,0:T(8,128)(2,1)}, u32[]{:S(2)}) copy-start(bf16[640,640]{1,0:T(8,128)(2,1)} %copy-done.9) | copy-start | bytes 2457604
  123.5 17.0 %copy-start.13 = (bf16[640,640]{1,0:T(8,128)(2,1)S(1)}, bf16[640,640]{1,0:T(8,128)(2,1)}, u32[]{:S(2)}) copy-start(bf16[640,640]{1,0:T(8,128)(2,1)} %copy-done.12) | copy-start | bytes 2457604
  135.9 5.9 %copy-start.26 = (f32[640,128]{1,0:T(8,128)}, f32[640,128]{1,0:T(8,128)S(1)}, u32[]{:S(2)}) copy-start(f32[640,128]{1,0:T(8,128)S(1)} %get-tuple-element.60.field.old_field) | copy-start | bytes 983044
  135.9 5.9 %copy-start.43 = (f32[640,128]{1,0:T(8,128)}, f32[640,128]{1,0:T(8,128)S(1)}, u32[]{:S(2)}) copy-start(f32[640,128]{1,0:T(8,128)S(1)} %get-tuple-element.71.old_slip) | copy-start | bytes 983044
  135.9 5.9 %copy-start.50 = (f32[256,128]{1,0:T(8,128)}, f32[256,128]{1,0:T(8,128)S(1)}, u32[]{:S(2)}) copy-start(f32[256,128]{1,0:T(8,128)S(1)} %get-tuple-element.61) | copy-start | bytes 393220
  140.5 29.0 %copy-start.29 = (f32[640,128]{1,0:T(8,128)S(1)}, f32[640,128]{1,0:T(8,128)}, u32[]{:S(2)}) copy-start(f32[640,128]{1,0:T(8,128)} %copy-done.28) | copy-start | bytes 983044
  142.5 24.2 %all-to-all-start.5 = ((f32[16,40,128]{2,1,0:T(8,128)}), f32[16,40,128]{2,1,0:T(8,128)}, u32[]{:S(2)}, u32[]{:S(2)}) async-start(f32[16,40,128]{2,1,0:T(8,128)} %bitcast.22), calls=%async_computation.5 | async-start | bytes 655360 | tf_op jit(solution)/shard_map/all_to_all | solution.py:267
  151.2 18.2 %collective-permute-start.2 = (f32[256,128]{1,0:T(8,128)}, f32[256,128]{1,0:T(8,128)S(1)}, u32[]{:S(2)}, u32[]{:S(2)}) collective-permute-start(f32[256,128]{1,0:T(8,128)} %copy-done.50), channel_id=1, source_target_pairs={{1,2},{3,4},{5,6},{7,8},{9,10},{11,12},{13,14},{15,16},{17,18},{19... | collective-permute-start | bytes 393224 | tf_op jit(solution)/shard_map/ppermute | solution.py:320
  167.7 35.6 %copy-start.17 = (bf16[640,1280]{1,0:T(8,128)(2,1)S(1)}, bf16[640,1280]{1,0:T(8,128)(2,1)}, u32[]{:S(2)}) copy-start(bf16[640,1280]{1,0:T(8,128)(2,1)} %copy-done.15) | copy-start | bytes 4915204
  167.7 35.6 %copy-start.20 = (bf16[640,1280]{1,0:T(8,128)(2,1)S(1)}, bf16[640,1280]{1,0:T(8,128)(2,1)}, u32[]{:S(2)}) copy-start(bf16[640,1280]{1,0:T(8,128)(2,1)} %copy-done.18) | copy-start | bytes 4915204
  170.5 32.8 %copy-start.27 = (f32[640,128]{1,0:T(8,128)S(1)}, f32[640,128]{1,0:T(8,128)}, u32[]{:S(2)}) copy-start(f32[640,128]{1,0:T(8,128)} %copy-done.26) | copy-start | bytes 983044
  170.5 32.8 %copy-start.32 = (f32[640,128]{1,0:T(8,128)S(1)}, f32[640,128]{1,0:T(8,128)}, u32[]{:S(2)}) copy-start(f32[640,128]{1,0:T(8,128)} %copy-done.31) | copy-start | bytes 983044
  170.5 32.8 %copy-start.40 = (f32[1280,128]{1,0:T(8,128)S(1)}, f32[1280,128]{1,0:T(8,128)}, u32[]{:S(2)}) copy-start(f32[1280,128]{1,0:T(8,128)} %copy-done.39) | copy-start | bytes 1966084
  204.5 24.0 %copy-start.33 = (f32[640,128]{1,0:T(8,128)}, f32[640,128]{1,0:T(8,128)S(1)}, u32[]{:S(2)}) copy-start(f32[640,128]{1,0:T(8,128)S(1)} %get-tuple-element.69.smooth) | copy-start | bytes 983044
  204.5 24.0 %copy-start.35 = (f32[640,128]{1,0:T(8,128)}, f32[640,128]{1,0:T(8,128)S(1)}, u32[]{:S(2)}) copy-start(f32[640,128]{1,0:T(8,128)S(1)} %get-tuple-element.70.way) | copy-start | bytes 983044
  204.6 24.0 %copy-start.41 = (f32[1280,128]{1,0:T(8,128)}, f32[1280,128]{1,0:T(8,128)S(1)}, u32[]{:S(2)}) copy-start(f32[1280,128]{1,0:T(8,128)S(1)} %get-tuple-element.73.image) | copy-start | bytes 1966084
  204.6 23.9 %copy-start.44 = (f32[640,128]{1,0:T(8,128)S(1)}, f32[640,128]{1,0:T(8,128)}, u32[]{:S(2)}) copy-start(f32[640,128]{1,0:T(8,128)} %copy-done.43) | copy-start | bytes 983044
  216.2 17.7 %copy-start.5 = (bf16[640,640]{1,0:T(8,128)(2,1)S(1)}, bf16[640,640]{1,0:T(8,128)(2,1)}, u32[]{:S(2)}) copy-start(bf16[640,640]{1,0:T(8,128)(2,1)} %copy-done.3) | copy-start | bytes 2457604
  216.2 17.7 %copy-start.8 = (bf16[640,640]{1,0:T(8,128)(2,1)S(1)}, bf16[640,640]{1,0:T(8,128)(2,1)}, u32[]{:S(2)}) copy-start(bf16[640,640]{1,0:T(8,128)(2,1)} %copy-done.6) | copy-start | bytes 2457604
  216.2 17.7 %copy-start.11 = (bf16[640,640]{1,0:T(8,128)(2,1)S(1)}, bf16[640,640]{1,0:T(8,128)(2,1)}, u32[]{:S(2)}) copy-start(bf16[640,640]{1,0:T(8,128)(2,1)} %copy-done.9) | copy-start | bytes 2457604
  216.2 17.7 %copy-start.14 = (bf16[640,640]{1,0:T(8,128)(2,1)S(1)}, bf16[640,640]{1,0:T(8,128)(2,1)}, u32[]{:S(2)}) copy-start(bf16[640,640]{1,0:T(8,128)(2,1)} %copy-done.12) | copy-start | bytes 2457604
  229.3 6.5 %copy-start.37 = (f32[640,128]{1,0:T(8,128)}, f32[640,128]{1,0:T(8,128)S(1)}, u32[]{:S(2)}) copy-start(f32[640,128]{1,0:T(8,128)S(1)} %get-tuple-element.72.field) | copy-start | bytes 983044
  229.3 6.5 %copy-start.49 = (f32[256,128]{1,0:T(8,128)}, f32[256,128]{1,0:T(8,128)S(1)}, u32[]{:S(2)}) copy-start(f32[256,128]{1,0:T(8,128)S(1)} %get-tuple-element.74) | copy-start | bytes 393220
  233.9 2.0 copy-start.21
  233.9 27.6 %copy-start.34 = (f32[640,128]{1,0:T(8,128)S(1)}, f32[640,128]{1,0:T(8,128)}, u32[]{:S(2)}) copy-start(f32[640,128]{1,0:T(8,128)} %copy-done.33) | copy-start | bytes 983044
  235.9 22.9 %all-to-all-start.8 = ((f32[16,40,128]{2,1,0:T(8,128)}), f32[16,40,128]{2,1,0:T(8,128)}, u32[]{:S(2)}, u32[]{:S(2)}) async-start(f32[16,40,128]{2,1,0:T(8,128)} %bitcast.14), calls=%async_computation.8 | async-start | bytes 655360 | tf_op jit(solution)/shard_map/all_to_all | solution.py:267
  243.3 18.2 %collective-permute-start.3 = (f32[256,128]{1,0:T(8,128)}, f32[256,128]{1,0:T(8,128)S(1)}, u32[]{:S(2)}, u32[]{:S(2)}) collective-permute-start(f32[256,128]{1,0:T(8,128)} %copy-done.49), channel_id=1, source_target_pairs={{1,2},{3,4},{5,6},{7,8},{9,10},{11,12},{13,14},{15,16},{17,18},{19... | collective-permute-start | bytes 393224 | tf_op jit(solution)/shard_map/ppermute | solution.py:320
  263.7 34.8 %copy-start.36 = (f32[640,128]{1,0:T(8,128)S(1)}, f32[640,128]{1,0:T(8,128)}, u32[]{:S(2)}) copy-start(f32[640,128]{1,0:T(8,128)} %copy-done.35) | copy-start | bytes 983044
  263.7 34.8 %copy-start.38 = (f32[640,128]{1,0:T(8,128)S(1)}, f32[640,128]{1,0:T(8,128)}, u32[]{:S(2)}) copy-start(f32[640,128]{1,0:T(8,128)} %copy-done.37) | copy-start | bytes 983044
  263.7 34.8 %copy-start.46 = (f32[640,128]{1,0:T(8,128)S(1)}, f32[640,128]{1,0:T(8,128)}, u32[]{:S(2)}) copy-start(f32[640,128]{1,0:T(8,128)} %copy-done.45) | copy-start | bytes 983044
  (10 other events, 11.4 us)

commit v11 on v8

--- a/solution.py
+++ b/solution.py
@@ -161,6 +161,13 @@
     out[share:, :] = jnp.concatenate([*rows, jnp.zeros((TILE - 3, own.shape[1]), F32)], 0)
 
 
+def merged(pair, out):
+    share = pair.shape[1] - TILE
+    out[:share, :] = pair[0, :share, :]
+    out[share : 2 * share, :] = pair[1, :share, :]
+    out[2 * share :, :] = pair[0, share:, :] + pair[1, share:, :]
+
+
 def backward(every, field, fresh, old_image, old_smooth, old_way, old_scalars, high, low, moved, image, tail, smooth, way, scalars, wide):
     count = every.shape[0]
     share = every.shape[1] - TILE
@@ -171,13 +178,12 @@
     has_old = old_scalars[2:3, :] > 0.0
     ratio = jnp.where(has_old, norm / old_scalars[0:1, :], 0.0)
     square = jnp.zeros((TILE, every.shape[2]), F32)
-    for k in range(0, count, 2):
-        rows = slice(share * k, share * (k + 2))
-        piece = jnp.concatenate([every[k, :share, :], every[k + 1, :share, :]], 0)
-        piece = piece + ratio * old_image[rows, :]
+    for k in range(count):
+        rows = slice(share * k, share * (k + 1))
+        piece = every[k, :share, :] + ratio * old_image[rows, :]
         image[rows, :] = piece
         store_halves(wide, share * k, piece)
-        for t in range(2 * share // TILE):
+        for t in range(share // TILE):
             block = piece[TILE * t : TILE * (t + 1)]
             square = square + block * block
     moved[...] = product(high, low, wide[...])
@@ -354,8 +360,8 @@
             collect, [((share + TILE, epochs), F32), field_shape], part, *penalty,
             scalars=[core_scalar], scratch=[near],
         )
-        every = lax.all_gather(lax.all_gather(out, "zl"), ("zh", "c"))
-        every = every.reshape(n_patch, share + TILE, epochs)
+        (out,) = local_call(merged, [((2 * share + TILE, epochs), F32)], lax.all_gather(out, "zl"))
+        every = lax.all_gather(out, ("zh", "c"))
         moved, image, tail, smooth, way, scalars = local_call(
             backward,
             [field_shape, image_shape, tail_shape, field_shape, field_shape, tail_shape],

time: 300 us -> 301 us (level)
    pallas_call x22 -> x24, Pallas kernels: 19.2 us -> 19.1 us  [local_call(): pl.pallas_call(functools.partial(body, **options), out_shape=[jax.ShapeDt...]
where the time goes in v11:
time: 301 us; the launch traced here: 300 us
  blocking collectives  176 us (58%)
  starting transfers between devices  50.3 us (17%)
  waiting for transfers between devices  40.6 us (13%)
  Pallas kernels  19.1 us (6%)
  local copies, waits for them, and re-layouts  13 us (4%)
    all_to_all x8, blocking collectives, exchanged(): return lax.all_to_all(pieces, axis, 0, 0, tiled=True)  104 us
    all_gather x2, blocking collectives, shards(): every = lax.all_gather(out, ('zh', 'c'))  50.6 us
    all_to_all x3, starting transfers between devices, exchanged(): return lax.all_to_all(pieces, axis, 0, 0, tiled=True)  29.3 us
    all_to_all x3, waiting for transfers between devices, exchanged(): return lax.all_to_all(pieces, axis, 0, 0, tiled=True)  22.9 us
    pallas_call x24, Pallas kernels, local_call(): pl.pallas_call(functools.partial(body, **options), out_shape=[jax.ShapeDt...  19.1 us
    ppermute x3, waiting for transfers between devices, shards(): edge = lax.ppermute(edge, PATCH, outward)  17.6 us
    all_gather x3, blocking collectives, shards(): pair = lax.all_gather(field, 'c')  13.3 us
    unnamed x104, local copies, waits for them, and re-layouts  12.9 us
  transfers between devices with their start and end apart: 7, of which 5 were waited for; matrix products, arithmetic and copies ran while one was open for 0% of the time, Pallas kernels for 1%

profile of v11, /device:TPU:1, one launch (start us, length us, event | category | flops | bytes accessed | tf_op | source)
XLA Modules:
  0.0 299.6 jit_solution(1065680841234549196)
XLA Ops:
  0.0 1.9 copy-done.25
  1.9 1.1 copy-done.43
  3.0 1.8 shard_map.46
  4.8 1.2 copy-done.18
  6.0 8.9 %collective-permute-start = (f32[640,640]{1,0:T(8,128)S(1)}, f32[640,640]{1,0:T(8,128)S(1)}, u32[]{:S(2)}, u32[]{:S(2)}) collective-permute-start(f32[640,640]{1,0:T(8,128)S(1)} %get-tuple-element.45), channel_id=1, source_target_pairs={{0,1},{1,0},{2,3},{3,2},{4,5},{5,4},{6,7},{7,6},{8,9},{9,8},{10,11... | collective-permute-start | bytes 4915208 | tf_op jit(solution)/shard_map/ppermute | solution.py:308
  14.9 11.1 %all_to_all.55.pieces = f32[16,40,128]{2,1,0:T(8,128)S(1)} all-to-all(f32[16,40,128]{2,1,0:T(8,128)S(1)} %bitcast.28), channel_id=1, replica_groups=mesh['x'=4,'y'=4,'zh'=8,'zl'=2,'c'=2] {'x','y'}, dimensions={0} | all-to-all | bytes 655360 | tf_op jit(solution)/shard_map/all_to_all | solution.py:274
  26.0 11.6 %all_to_all.56.every = f32[16,40,128]{2,1,0:T(8,128)S(1)} all-to-all(f32[16,40,128]{2,1,0:T(8,128)S(1)} %shard_map.47), channel_id=1, replica_groups=mesh['x'=4,'y'=4,'zh'=8,'zl'=2,'c'=2] {'x','y'}, dimensions={0} | all-to-all | bytes 655360 | tf_op jit(solution)/shard_map/all_to_all | solution.py:274
  37.7 4.2 %all-gather = f32[1296,128]{1,0:T(8,128)S(1)} all-gather(f32[648,128]{1,0:T(8,128)S(1)} %get-tuple-element.42.field.old_field), channel_id=2, replica_groups=mesh['x'=4,'y'=4,'zh'=8,'zl'=2,'c'=2] {'c'}, dimensions={0}, use_global_device_ids=true | all-gather | bytes 995328 | tf_op jit(solution)/shard_map/all_gather | solution.py:326
  42.2 2.0 shard_map.50
  44.2 13.6 %all-to-all-start.2 = ((f32[16,40,128]{2,1,0:T(8,128)}), f32[16,40,128]{2,1,0:T(8,128)}, u32[]{:S(2)}, u32[]{:S(2)}) async-start(f32[16,40,128]{2,1,0:T(8,128)} %bitcast.5), calls=%async_computation.2 | async-start | bytes 655360 | tf_op jit(solution)/shard_map/all_to_all | solution.py:274
  57.8 4.0 %collective-permute-start.1 = (f32[264,128]{1,0:T(8,128)S(1)}, f32[264,128]{1,0:T(8,128)S(1)}, u32[]{:S(2)}, u32[]{:S(2)}) collective-permute-start(f32[264,128]{1,0:T(8,128)S(1)} %get-tuple-element.48), channel_id=1, source_target_pairs={{1,2},{3,4},{5,6},{7,8},{9,10},{11,12},{13,14},{15,16},{17,18},{19... | collective-permute-start | bytes 405512 | tf_op jit(solution)/shard_map/ppermute | solution.py:325
  61.8 14.2 %collective-permute-done.1.edge = f32[264,128]{1,0:T(8,128)S(1)} collective-permute-done((f32[264,128]{1,0:T(8,128)S(1)}, f32[264,128]{1,0:T(8,128)S(1)}, u32[]{:S(2)}, u32[]{:S(2)}) %collective-permute-start.1) | collective-permute-done | bytes 135200 | tf_op jit(solution)/shard_map/ppermute | solution.py:325
  76.0 1.1 copy-done.1
  77.1 1.8 shard_map.52
  78.9 1.0 shard_map.51.part
  79.9 1.1 copy-done.2
  81.0 1.2 shard_map.53
  82.2 3.3 %all-gather.1 = f32[96,128]{1,0:T(8,128)S(1)} all-gather(f32[48,128]{1,0:T(8,128)S(1)} %get-tuple-element.51), channel_id=3, replica_groups=mesh['x'=4,'y'=4,'zh'=8,'zl'=2,'c'=2] {'zl'}, dimensions={0}, use_global_device_ids=true | all-gather | bytes 73728 | tf_op jit(solution)/shard_map/all_gather | solution.py:363
  85.6 24.8 %all-gather.2 = f32[1408,128]{1,0:T(8,128)S(1)} all-gather(f32[88,128]{1,0:T(8,128)S(1)} %shard_map.54), channel_id=4, replica_groups=mesh['x'=4,'y'=4,'zh'=8,'zl'=2,'c'=2] {'zh','c'}, dimensions={0}, use_global_device_ids=true | all-gather | bytes 765952 | tf_op jit(solution)/shard_map/all_gather | solution.py:364
  110.5 1.2 shard_map.55
  111.7 11.3 %all_to_all.57.pieces = f32[16,40,128]{2,1,0:T(8,128)S(1)} all-to-all(f32[16,40,128]{2,1,0:T(8,128)S(1)} %bitcast.29), channel_id=1, replica_groups=mesh['x'=4,'y'=4,'zh'=8,'zl'=2,'c'=2] {'x','y'}, dimensions={0} | all-to-all | bytes 655360 | tf_op jit(solution)/shard_map/all_to_all | solution.py:274
  123.1 12.3 %all_to_all.58.every = f32[16,48,128]{2,1,0:T(8,128)S(1)} all-to-all(f32[16,48,128]{2,1,0:T(8,128)S(1)} %shard_map.56), channel_id=1, replica_groups=mesh['x'=4,'y'=4,'zh'=8,'zl'=2,'c'=2] {'x','y'}, dimensions={0} | all-to-all | bytes 786432 | tf_op jit(solution)/shard_map/all_to_all | solution.py:274
  136.3 4.5 %all-gather.3 = f32[1280,128]{1,0:T(8,128)S(1)} all-gather(f32[640,128]{1,0:T(8,128)S(1)} %get-tuple-element.60.field.old_field), channel_id=5, replica_groups=mesh['x'=4,'y'=4,'zh'=8,'zl'=2,'c'=2] {'c'}, dimensions={0}, use_global_device_ids=true | all-gather | bytes 983040 | tf_op jit(solution)/shard_map/all_gather | solution.py:326
  140.8 1.3 shard_map.58
  142.8 8.4 %all-to-all-start.5 = ((f32[16,40,128]{2,1,0:T(8,128)}), f32[16,40,128]{2,1,0:T(8,128)}, u32[]{:S(2)}, u32[]{:S(2)}) async-start(f32[16,40,128]{2,1,0:T(8,128)} %bitcast.26), calls=%async_computation.5 | async-start | bytes 655360 | tf_op jit(solution)/shard_map/all_to_all | solution.py:274
  151.2 4.0 %collective-permute-start.2 = (f32[256,128]{1,0:T(8,128)}, f32[256,128]{1,0:T(8,128)S(1)}, u32[]{:S(2)}, u32[]{:S(2)}) collective-permute-start(f32[256,128]{1,0:T(8,128)} %copy-done.51), channel_id=1, source_target_pairs={{1,2},{3,4},{5,6},{7,8},{9,10},{11,12},{13,14},{15,16},{17,18},{19... | collective-permute-start | bytes 393224 | tf_op jit(solution)/shard_map/ppermute | solution.py:325
  155.3 11.5 %all-to-all-done.5.pieces = f32[16,40,128]{2,1,0:T(8,128)} async-done(((f32[16,40,128]{2,1,0:T(8,128)}), f32[16,40,128]{2,1,0:T(8,128)}, u32[]{:S(2)}, u32[]{:S(2)}) %all-to-all-start.5) | async-done | bytes 327712 | tf_op jit(solution)/shard_map/all_to_all | solution.py:274
  166.7 1.0 shard_map.59.part
  167.8 1.7 collective-permute-done.2.edge
  169.5 1.1 copy-done.24
  170.6 1.2 shard_map.60
  171.7 5.4 %all-gather.4 = f32[96,128]{1,0:T(8,128)S(1)} all-gather(f32[48,128]{1,0:T(8,128)S(1)} %get-tuple-element.62), channel_id=6, replica_groups=mesh['x'=4,'y'=4,'zh'=8,'zl'=2,'c'=2] {'zl'}, dimensions={0}, use_global_device_ids=true | all-gather | bytes 73728 | tf_op jit(solution)/shard_map/all_gather | solution.py:363
  177.1 25.8 %all-gather.5 = f32[1408,128]{1,0:T(8,128)S(1)} all-gather(f32[88,128]{1,0:T(8,128)S(1)} %shard_map.61), channel_id=7, replica_groups=mesh['x'=4,'y'=4,'zh'=8,'zl'=2,'c'=2] {'zh','c'}, dimensions={0}, use_global_device_ids=true | all-gather | bytes 765952 | tf_op jit(solution)/shard_map/all_gather | solution.py:364
  202.9 1.2 shard_map.62
  205.0 11.5 %all_to_all.59.pieces = f32[16,40,128]{2,1,0:T(8,128)S(1)} all-to-all(f32[16,40,128]{2,1,0:T(8,128)S(1)} %bitcast.27), channel_id=1, replica_groups=mesh['x'=4,'y'=4,'zh'=8,'zl'=2,'c'=2] {'x','y'}, dimensions={0} | all-to-all | bytes 655360 | tf_op jit(solution)/shard_map/all_to_all | solution.py:274
  216.6 12.3 %all_to_all.60.every = f32[16,48,128]{2,1,0:T(8,128)S(1)} all-to-all(f32[16,48,128]{2,1,0:T(8,128)S(1)} %shard_map.63), channel_id=1, replica_groups=mesh['x'=4,'y'=4,'zh'=8,'zl'=2,'c'=2] {'x','y'}, dimensions={0} | all-to-all | bytes 786432 | tf_op jit(solution)/shard_map/all_to_all | solution.py:274
  229.7 4.5 %all-gather.6 = f32[1280,128]{1,0:T(8,128)S(1)} all-gather(f32[640,128]{1,0:T(8,128)S(1)} %get-tuple-element.72.field), channel_id=8, replica_groups=mesh['x'=4,'y'=4,'zh'=8,'zl'=2,'c'=2] {'c'}, dimensions={0}, use_global_device_ids=true | all-gather | bytes 983040 | tf_op jit(solution)/shard_map/all_gather | solution.py:326
  234.3 2.0 shard_map.65
  236.3 7.3 %all-to-all-start.8 = ((f32[16,40,128]{2,1,0:T(8,128)}), f32[16,40,128]{2,1,0:T(8,128)}, u32[]{:S(2)}, u32[]{:S(2)}) async-start(f32[16,40,128]{2,1,0:T(8,128)} %bitcast.16), calls=%async_computation.8 | async-start | bytes 655360 | tf_op jit(solution)/shard_map/all_to_all | solution.py:274
  243.6 4.0 %collective-permute-start.3 = (f32[256,128]{1,0:T(8,128)}, f32[256,128]{1,0:T(8,128)S(1)}, u32[]{:S(2)}, u32[]{:S(2)}) collective-permute-start(f32[256,128]{1,0:T(8,128)} %copy-done.50), channel_id=1, source_target_pairs={{1,2},{3,4},{5,6},{7,8},{9,10},{11,12},{13,14},{15,16},{17,18},{19... | collective-permute-start | bytes 393224 | tf_op jit(solution)/shard_map/ppermute | solution.py:325
  247.7 11.5 %all-to-all-done.8.pieces = f32[16,40,128]{2,1,0:T(8,128)} async-done(((f32[16,40,128]{2,1,0:T(8,128)}), f32[16,40,128]{2,1,0:T(8,128)}, u32[]{:S(2)}, u32[]{:S(2)}) %all-to-all-start.8) | async-done | bytes 327712 | tf_op jit(solution)/shard_map/all_to_all | solution.py:274
  259.1 1.0 shard_map.66.share_ref
  260.1 1.7 collective-permute-done.3.edge
  261.8 1.1 copy-done.22
  262.9 1.1 copy-done.42
  264.0 1.2 shard_map.67
  265.2 18.5 %all_to_all.61.every = f32[32,8,128]{2,1,0:T(8,128)S(1)} all-to-all(f32[32,8,128]{2,1,0:T(8,128)S(1)} %shard_map.67), channel_id=1, replica_groups=mesh['x'=4,'y'=4,'zh'=8,'zl'=2,'c'=2] {'x','y','c'}, dimensions={0} | all-to-all | bytes 262144 | tf_op jit(solution)/shard_map/all_to_all | solution.py:274
  283.8 15.0 %all_to_all.62.every = f32[16,8,128]{2,1,0:T(8,128)S(1)} all-to-all(f32[16,8,128]{2,1,0:T(8,128)S(1)} %shard_map.68), channel_id=1, replica_groups=mesh['x'=4,'y'=4,'zh'=8,'zl'=2,'c'=2] {'zh','zl'}, dimensions={0} | all-to-all | bytes 131072 | tf_op jit(solution)/shard_map/all_to_all | solution.py:274
  (112 shorter events, 4.8 us)
Async XLA Ops:
  0.0 1.9 copy-start.25
  6.0 35.9 %copy-start.15 = (bf16[640,1280]{1,0:T(8,128)(2,1)}, bf16[640,1280]{1,0:T(8,128)(2,1)S(1)}, u32[]{:S(2)}) copy-start(bf16[640,1280]{1,0:T(8,128)(2,1)S(1)} %get-tuple-element.53.high) | copy-start | bytes 4915204
  6.0 36.2 %copy-start.3 = (bf16[640,640]{1,0:T(8,128)(2,1)}, bf16[640,640]{1,0:T(8,128)(2,1)S(1)}, u32[]{:S(2)}) copy-start(bf16[640,640]{1,0:T(8,128)(2,1)S(1)} %get-tuple-element.43.own_high) | copy-start | bytes 2457604
  6.0 36.2 %copy-start.6 = (bf16[640,640]{1,0:T(8,128)(2,1)}, bf16[640,640]{1,0:T(8,128)(2,1)S(1)}, u32[]{:S(2)}) copy-start(bf16[640,640]{1,0:T(8,128)(2,1)S(1)} %get-tuple-element.44.own_low) | copy-start | bytes 2457604
  6.0 31.6 %copy-start.48 = (s32[3,640]{1,0:T(4,128)S(1)}, s32[3,640]{1,0:T(4,128)}, u32[]{:S(2)}) copy-start(s32[3,640]{1,0:T(4,128)} %ids.3) | copy-start | bytes 23044
  6.0 35.9 %collective-permute-start = (f32[640,640]{1,0:T(8,128)S(1)}, f32[640,640]{1,0:T(8,128)S(1)}, u32[]{:S(2)}, u32[]{:S(2)}) collective-permute-start(f32[640,640]{1,0:T(8,128)S(1)} %get-tuple-element.45), channel_id=1, source_target_pairs={{0,1},{1,0},{2,3},{3,2},{4,5},{5,4},{6,7},{7,6},{8,9},{9,8},{10,11... | collective-permute-start | bytes 4915208 | tf_op jit(solution)/shard_map/ppermute | solution.py:308
  41.9 2.3 copy-start
  42.1 2.0 copy-start.9
  42.1 2.0 copy-start.12
  44.2 35.8 %copy-start.49 = (f32[128]{0:T(128)S(1)}, f32[128]{0:T(128)}, u32[]{:S(2)}) copy-start(f32[128]{0:T(128)} %param.7) | copy-start | bytes 1540
  44.2 34.7 %all-to-all-start.2 = ((f32[16,40,128]{2,1,0:T(8,128)}), f32[16,40,128]{2,1,0:T(8,128)}, u32[]{:S(2)}, u32[]{:S(2)}) async-start(f32[16,40,128]{2,1,0:T(8,128)} %bitcast.5), calls=%async_computation.2 | async-start | bytes 655360 | tf_op jit(solution)/shard_map/all_to_all | solution.py:274
  57.8 18.3 %collective-permute-start.1 = (f32[264,128]{1,0:T(8,128)S(1)}, f32[264,128]{1,0:T(8,128)S(1)}, u32[]{:S(2)}, u32[]{:S(2)}) collective-permute-start(f32[264,128]{1,0:T(8,128)S(1)} %get-tuple-element.48), channel_id=1, source_target_pairs={{1,2},{3,4},{5,6},{7,8},{9,10},{11,12},{13,14},{15,16},{17,18},{19... | collective-permute-start | bytes 405512 | tf_op jit(solution)/shard_map/ppermute | solution.py:325
  81.0 29.4 %copy-start.16 = (bf16[640,1280]{1,0:T(8,128)(2,1)S(1)}, bf16[640,1280]{1,0:T(8,128)(2,1)}, u32[]{:S(2)}) copy-start(bf16[640,1280]{1,0:T(8,128)(2,1)} %copy-done.15) | copy-start | bytes 4915204
  81.0 29.4 %copy-start.19 = (bf16[640,1280]{1,0:T(8,128)(2,1)S(1)}, bf16[640,1280]{1,0:T(8,128)(2,1)}, u32[]{:S(2)}) copy-start(bf16[640,1280]{1,0:T(8,128)(2,1)} %copy-done.18) | copy-start | bytes 4915204
  111.6 23.7 %copy-start.39 = (f32[1280,128]{1,0:T(8,128)}, f32[1280,128]{1,0:T(8,128)S(1)}, u32[]{:S(2)}) copy-start(f32[1280,128]{1,0:T(8,128)S(1)} %get-tuple-element.64.old_image) | copy-start | bytes 1966084
  111.7 23.8 %copy-start.28 = (f32[640,128]{1,0:T(8,128)}, f32[640,128]{1,0:T(8,128)S(1)}, u32[]{:S(2)}) copy-start(f32[640,128]{1,0:T(8,128)S(1)} %get-tuple-element.58.smooth.old_smooth) | copy-start | bytes 983044
  111.7 23.8 %copy-start.31 = (f32[640,128]{1,0:T(8,128)}, f32[640,128]{1,0:T(8,128)S(1)}, u32[]{:S(2)}) copy-start(f32[640,128]{1,0:T(8,128)S(1)} %get-tuple-element.59.way.old_way) | copy-start | bytes 983044
  123.1 17.7 %copy-start.4 = (bf16[640,640]{1,0:T(8,128)(2,1)S(1)}, bf16[640,640]{1,0:T(8,128)(2,1)}, u32[]{:S(2)}) copy-start(bf16[640,640]{1,0:T(8,128)(2,1)} %copy-done.3) | copy-start | bytes 2457604
  123.1 17.7 %copy-start.7 = (bf16[640,640]{1,0:T(8,128)(2,1)S(1)}, bf16[640,640]{1,0:T(8,128)(2,1)}, u32[]{:S(2)}) copy-start(bf16[640,640]{1,0:T(8,128)(2,1)} %copy-done.6) | copy-start | bytes 2457604
  123.1 17.7 %copy-start.10 = (bf16[640,640]{1,0:T(8,128)(2,1)S(1)}, bf16[640,640]{1,0:T(8,128)(2,1)}, u32[]{:S(2)}) copy-start(bf16[640,640]{1,0:T(8,128)(2,1)} %copy-done.9) | copy-start | bytes 2457604
  123.1 17.7 %copy-start.13 = (bf16[640,640]{1,0:T(8,128)(2,1)S(1)}, bf16[640,640]{1,0:T(8,128)(2,1)}, u32[]{:S(2)}) copy-start(bf16[640,640]{1,0:T(8,128)(2,1)} %copy-done.12) | copy-start | bytes 2457604
  136.3 5.8 %copy-start.26 = (f32[640,128]{1,0:T(8,128)}, f32[640,128]{1,0:T(8,128)S(1)}, u32[]{:S(2)}) copy-start(f32[640,128]{1,0:T(8,128)S(1)} %get-tuple-element.60.field.old_field) | copy-start | bytes 983044
  136.3 5.8 %copy-start.51 = (f32[256,128]{1,0:T(8,128)}, f32[256,128]{1,0:T(8,128)S(1)}, u32[]{:S(2)}) copy-start(f32[256,128]{1,0:T(8,128)S(1)} %get-tuple-element.61) | copy-start | bytes 393220
  140.8 1.3 copy-start.23
  140.8 28.7 %copy-start.29 = (f32[640,128]{1,0:T(8,128)S(1)}, f32[640,128]{1,0:T(8,128)}, u32[]{:S(2)}) copy-start(f32[640,128]{1,0:T(8,128)} %copy-done.28) | copy-start | bytes 983044
  142.8 23.9 %all-to-all-start.5 = ((f32[16,40,128]{2,1,0:T(8,128)}), f32[16,40,128]{2,1,0:T(8,128)}, u32[]{:S(2)}, u32[]{:S(2)}) async-start(f32[16,40,128]{2,1,0:T(8,128)} %bitcast.26), calls=%async_computation.5 | async-start | bytes 655360 | tf_op jit(solution)/shard_map/all_to_all | solution.py:274
  151.2 18.2 %collective-permute-start.2 = (f32[256,128]{1,0:T(8,128)}, f32[256,128]{1,0:T(8,128)S(1)}, u32[]{:S(2)}, u32[]{:S(2)}) collective-permute-start(f32[256,128]{1,0:T(8,128)} %copy-done.51), channel_id=1, source_target_pairs={{1,2},{3,4},{5,6},{7,8},{9,10},{11,12},{13,14},{15,16},{17,18},{19... | collective-permute-start | bytes 393224 | tf_op jit(solution)/shard_map/ppermute | solution.py:325
  167.7 35.1 %copy-start.17 = (bf16[640,1280]{1,0:T(8,128)(2,1)S(1)}, bf16[640,1280]{1,0:T(8,128)(2,1)}, u32[]{:S(2)}) copy-start(bf16[640,1280]{1,0:T(8,128)(2,1)} %copy-done.15) | copy-start | bytes 4915204
  167.8 35.1 %copy-start.20 = (bf16[640,1280]{1,0:T(8,128)(2,1)S(1)}, bf16[640,1280]{1,0:T(8,128)(2,1)}, u32[]{:S(2)}) copy-start(bf16[640,1280]{1,0:T(8,128)(2,1)} %copy-done.18) | copy-start | bytes 4915204
  170.6 32.3 %copy-start.27 = (f32[640,128]{1,0:T(8,128)S(1)}, f32[640,128]{1,0:T(8,128)}, u32[]{:S(2)}) copy-start(f32[640,128]{1,0:T(8,128)} %copy-done.26) | copy-start | bytes 983044
  170.6 32.3 %copy-start.32 = (f32[640,128]{1,0:T(8,128)S(1)}, f32[640,128]{1,0:T(8,128)}, u32[]{:S(2)}) copy-start(f32[640,128]{1,0:T(8,128)} %copy-done.31) | copy-start | bytes 983044
  170.6 32.4 %copy-start.40 = (f32[1280,128]{1,0:T(8,128)S(1)}, f32[1280,128]{1,0:T(8,128)}, u32[]{:S(2)}) copy-start(f32[1280,128]{1,0:T(8,128)} %copy-done.39) | copy-start | bytes 1966084
  205.0 24.0 %copy-start.33 = (f32[640,128]{1,0:T(8,128)}, f32[640,128]{1,0:T(8,128)S(1)}, u32[]{:S(2)}) copy-start(f32[640,128]{1,0:T(8,128)S(1)} %get-tuple-element.69.smooth) | copy-start | bytes 983044
  205.0 24.0 %copy-start.35 = (f32[640,128]{1,0:T(8,128)}, f32[640,128]{1,0:T(8,128)S(1)}, u32[]{:S(2)}) copy-start(f32[640,128]{1,0:T(8,128)S(1)} %get-tuple-element.70.way) | copy-start | bytes 983044
  205.0 23.9 %copy-start.45 = (f32[640,128]{1,0:T(8,128)S(1)}, f32[640,128]{1,0:T(8,128)}, u32[]{:S(2)}) copy-start(f32[640,128]{1,0:T(8,128)} %copy-done.44) | copy-start | bytes 983044
  216.6 17.7 %copy-start.5 = (bf16[640,640]{1,0:T(8,128)(2,1)S(1)}, bf16[640,640]{1,0:T(8,128)(2,1)}, u32[]{:S(2)}) copy-start(bf16[640,640]{1,0:T(8,128)(2,1)} %copy-done.3) | copy-start | bytes 2457604
  216.6 17.7 %copy-start.8 = (bf16[640,640]{1,0:T(8,128)(2,1)S(1)}, bf16[640,640]{1,0:T(8,128)(2,1)}, u32[]{:S(2)}) copy-start(bf16[640,640]{1,0:T(8,128)(2,1)} %copy-done.6) | copy-start | bytes 2457604
  216.6 17.7 %copy-start.11 = (bf16[640,640]{1,0:T(8,128)(2,1)S(1)}, bf16[640,640]{1,0:T(8,128)(2,1)}, u32[]{:S(2)}) copy-start(bf16[640,640]{1,0:T(8,128)(2,1)} %copy-done.9) | copy-start | bytes 2457604
  216.6 17.7 %copy-start.14 = (bf16[640,640]{1,0:T(8,128)(2,1)S(1)}, bf16[640,640]{1,0:T(8,128)(2,1)}, u32[]{:S(2)}) copy-start(bf16[640,640]{1,0:T(8,128)(2,1)} %copy-done.12) | copy-start | bytes 2457604
  229.7 4.5 %copy-start.50 = (f32[256,128]{1,0:T(8,128)}, f32[256,128]{1,0:T(8,128)S(1)}, u32[]{:S(2)}) copy-start(f32[256,128]{1,0:T(8,128)S(1)} %get-tuple-element.74) | copy-start | bytes 393220
  229.7 6.6 %copy-start.37 = (f32[640,128]{1,0:T(8,128)}, f32[640,128]{1,0:T(8,128)S(1)}, u32[]{:S(2)}) copy-start(f32[640,128]{1,0:T(8,128)S(1)} %get-tuple-element.72.field) | copy-start | bytes 983044
  234.3 2.0 copy-start.21
  234.3 27.5 %copy-start.34 = (f32[640,128]{1,0:T(8,128)S(1)}, f32[640,128]{1,0:T(8,128)}, u32[]{:S(2)}) copy-start(f32[640,128]{1,0:T(8,128)} %copy-done.33) | copy-start | bytes 983044
  236.3 22.8 %all-to-all-start.8 = ((f32[16,40,128]{2,1,0:T(8,128)}), f32[16,40,128]{2,1,0:T(8,128)}, u32[]{:S(2)}, u32[]{:S(2)}) async-start(f32[16,40,128]{2,1,0:T(8,128)} %bitcast.16), calls=%async_computation.8 | async-start | bytes 655360 | tf_op jit(solution)/shard_map/all_to_all | solution.py:274
  243.6 18.2 %collective-permute-start.3 = (f32[256,128]{1,0:T(8,128)}, f32[256,128]{1,0:T(8,128)S(1)}, u32[]{:S(2)}, u32[]{:S(2)}) collective-permute-start(f32[256,128]{1,0:T(8,128)} %copy-done.50), channel_id=1, source_target_pairs={{1,2},{3,4},{5,6},{7,8},{9,10},{11,12},{13,14},{15,16},{17,18},{19... | collective-permute-start | bytes 393224 | tf_op jit(solution)/shard_map/ppermute | solution.py:325
  264.0 34.8 %copy-start.36 = (f32[640,128]{1,0:T(8,128)S(1)}, f32[640,128]{1,0:T(8,128)}, u32[]{:S(2)}) copy-start(f32[640,128]{1,0:T(8,128)} %copy-done.35) | copy-start | bytes 983044
  264.0 34.8 %copy-start.38 = (f32[640,128]{1,0:T(8,128)S(1)}, f32[640,128]{1,0:T(8,128)}, u32[]{:S(2)}) copy-start(f32[640,128]{1,0:T(8,128)} %copy-done.37) | copy-start | bytes 983044
  264.0 34.8 %copy-start.47 = (f32[640,128]{1,0:T(8,128)S(1)}, f32[640,128]{1,0:T(8,128)}, u32[]{:S(2)}) copy-start(f32[640,128]{1,0:T(8,128)} %copy-done.46) | copy-start | bytes 983044
  (11 other events, 10.9 us)
